TPU v7x, 32 devices: a whole 2x2x4 slice. The times are simulated.
32 devices in a mesh: img: 16 (over z, x, core), seq: 2 (over y).
Axes of the slice: x: 2, y: 2, z: 4, core: 2. Of those that a mesh axis runs over, the one named last changes fastest.
Arguments:
- tokens: bfloat16 [16, 512, 768], P('img', 'seq'), may hold values from -6 to 6
- w_query: bfloat16 [768, 768], replicated, may hold values from -0.21875 to 0.21875
- w_key: bfloat16 [768, 768], replicated, may hold values from -0.21875 to 0.21875
- w_value: bfloat16 [768, 768], replicated, may hold values from -0.21875 to 0.21875
- w_output: bfloat16 [768, 768], replicated, may hold values from -1.75 to 1.75
- w_up: bfloat16 [768, 3072], replicated, may hold values from -0.21875 to 0.21875
- w_down: bfloat16 [3072, 768], replicated, may hold values from -0.109375 to 0.109375
- first_gain: float32 [768], replicated, may hold values from 0.1 to 1.9
- second_gain: float32 [768], replicated, may hold values from 0.1 to 1.9
- final_gain: float32 [768], replicated, may hold values from 0.1 to 1.9
- probe: float32 [768], replicated, may hold values from -6 to 6
- pool_query: bfloat16 [768, 768], replicated, may hold values from -0.21875 to 0.21875
- pool_key: bfloat16 [768, 768], replicated, may hold values from -0.21875 to 0.21875
- pool_value: bfloat16 [768, 768], replicated, may hold values from -0.21875 to 0.21875
- pool_output: bfloat16 [768, 768], replicated, may hold values from -0.21875 to 0.21875
- captions: float32 [80, 768], P('img'), may hold values from -6 to 6
- positive_pairs: int32 [16, 80], P('img'), may hold values from 0 to 1, as said below
- caption_counts: int32 [16], P('img'), may hold values from 2 to 5
- log_temp: float32 [], replicated, may hold values from 1.5 to 3
- pair_bias: float32 [], replicated, may hold values from -12 to -8
Outputs:
- block_out: bfloat16 [16, 512, 768], P('img', 'seq')
- input_grad: float32 [16, 512, 768], P('img', 'seq')
- grad_query: float32 [768, 768], P('img', 'seq')
- grad_key: float32 [768, 768], P('img', 'seq')
- grad_value: float32 [768, 768], P('img', 'seq')
- grad_output: float32 [768, 768], P('img', 'seq')
- grad_up: float32 [768, 3072], P('img', 'seq')
- grad_down: float32 [3072, 768], P('img', 'seq')
- grad_first: float32 [768], P('img')
- grad_second: float32 [768], P('img')
- grad_final: float32 [768], P('img')
- grad_probe: float32 [768], P('img')
- grad_pooler_query: float32 [768, 768], P('img', 'seq')
- grad_pooler_key: float32 [768, 768], P('img', 'seq')
- grad_pooler_value: float32 [768, 768], P('img', 'seq')
- grad_pooler_output: float32 [768, 768], P('img', 'seq')
- pair_loss: float32 [], replicated
- grad_temp: float32 [], replicated
- grad_bias: float32 [], replicated
Inputs may be any that keep to these rules, and one draw needn't show every extreme that they name: `positive_pairs`: row i has exactly caption_counts[i] ones, all in columns i*5 to i*5 + 4; every other entry is 0.
All inputs are finite; a program needn't handle non-finite values.
Results may differ from a plain program's by a relative error of at most 0.02.
The roundings to bfloat16 on the way count: a program that leaves them out, or rounds other values in their place, can miss the bound.
Values may be sent and summed in bfloat16 or wider, within the bound.
No kernel may reach another device: no remote copies, remote signals or barrier semaphores. Data moves between devices by JAX's collectives and lax.ppermute only.
A program may use at most 192 MiB of HBM per device.

v0:
```python
import functools
import math

import jax
import jax.numpy as jnp
from jax import lax
from jax.experimental import pallas as pl
from jax.experimental.pallas import tpu as pltpu
from jax.sharding import PartitionSpec as P

HEADS = 12
HEAD = 64
PAIR = 2 * HEAD
TOP = 16

norm_eps = 1e-06
highest = lax.Precision.HIGHEST
bf16 = jnp.bfloat16
f32 = jnp.float32


def layer_norm(values, gain_row):
    center = values - jnp.mean(values, axis=-1, keepdims=True)
    spread = jnp.mean(center * center, axis=-1, keepdims=True)
    inv_std = lax.rsqrt(spread + norm_eps)
    normed = center * inv_std
    return (normed * gain_row, normed, inv_std)


def norm_back(upstream, normed, inv_std, gain_row):
    scaled = upstream * gain_row
    gain_grad = jnp.sum(upstream * normed, axis=0)
    first_mean = jnp.mean(scaled, axis=-1, keepdims=True)
    second_mean = jnp.mean(scaled * normed, axis=-1, keepdims=True)
    return (inv_std * (scaled - first_mean - normed * second_mean), gain_grad)


def low_dot(left_side, right_side):
    return jnp.dot(left_side, right_side, preferred_element_type=f32)


def back_dot(left_side, right_side):
    return lax.dot_general(
        left_side, right_side, (((1,), (1,)), ((), ())), preferred_element_type=f32
    )


def gelu_tanh(values):
    return jax.nn.gelu(values, approximate=True)


def nn(left, right):
    return lax.dot_general(left, right, (((1,), (0,)), ((), ())), preferred_element_type=f32)


def nt(left, right):
    return lax.dot_general(left, right, (((1,), (1,)), ((), ())), preferred_element_type=f32)


def tn(left, right):
    return lax.dot_general(left, right, (((0,), (0,)), ((), ())), preferred_element_type=f32)


def thirds(value):
    high = value.astype(bf16)
    rest = value - high.astype(f32)
    middle = rest.astype(bf16)
    low = (rest - middle.astype(f32)).astype(bf16)
    return high, middle, low


def wide(product, value, right):
    stacked = product(jnp.concatenate(thirds(value), axis=0), right)
    return stacked[:TOP] + stacked[TOP : 2 * TOP] + stacked[2 * TOP :]


def wide_row(product, row, right):
    at = lax.broadcasted_iota(jnp.int32, (TOP, row.shape[1]), 0)
    high, middle, low = (part.astype(f32) for part in thirds(row))
    stacked = jnp.where(at == 0, high, jnp.where(at == 1, middle, jnp.where(at == 2, low, 0.0)))
    return jnp.sum(product(stacked.astype(bf16), right), axis=0, keepdims=True)


def head_rows(width):
    row = lax.broadcasted_iota(jnp.int32, (TOP, width), 0)
    lane = lax.broadcasted_iota(jnp.int32, (TOP, width), 1)
    return (lane // HEAD == row).astype(f32)


def probe_kernel(probe_ref, query_ref, key_ref, row_ref, key_probe_ref):
    row = wide_row(nn, probe_ref[...], query_ref[...])
    row_ref[...] = row
    key_probe_ref[...] = wide(nt, row * head_rows(row.shape[1]), key_ref[...])


def probe_call(probe, pool_query, pool_key):
    width = probe.shape[0]
    return pl.pallas_call(
        probe_kernel,
        out_shape=[
            jax.ShapeDtypeStruct((1, width), f32),
            jax.ShapeDtypeStruct((TOP, width), f32),
        ],
        cost_estimate=pl.CostEstimate(
            flops=128 * width * width, transcendentals=0, bytes_accessed=4 * width * width
        ),
        name="probe_rows",
    )(probe[None], pool_query, pool_key)


def pool_kernel(result_ref, gain_ref, key_probe_ref, low_ref, unit_ref, inv_ref, exp_ref, packed_ref):
    result = result_ref[...]
    width = result.shape[1]
    center = result - jnp.mean(result, axis=-1, keepdims=True)
    inv = lax.rsqrt(jnp.mean(center * center, axis=-1, keepdims=True) + norm_eps)
    unit = center * inv
    low = (unit * gain_ref[...]).astype(bf16)
    low_ref[...] = low
    unit_ref[...] = unit
    inv_ref[...] = inv
    scores = wide(nt, key_probe_ref[...], low) * 0.125
    top = jnp.max(scores, axis=-1, keepdims=True)
    exps = jnp.exp(scores - top)
    exp_ref[...] = exps
    packed_ref[:, :width] = wide(nn, exps, low)
    lane = lax.broadcasted_iota(jnp.int32, (TOP, 128), 1)
    total = jnp.sum(exps, axis=-1, keepdims=True)
    packed_ref[:, width:] = jnp.where(lane == 0, top, jnp.where(lane == 1, total, 0.0))


def pool_call(result, gain, key_probe):
    rows, width = result.shape
    return pl.pallas_call(
        pool_kernel,
        out_shape=[
            jax.ShapeDtypeStruct((rows, width), bf16),
            jax.ShapeDtypeStruct((rows, width), f32),
            jax.ShapeDtypeStruct((rows, 1), f32),
            jax.ShapeDtypeStruct((TOP, rows), f32),
            jax.ShapeDtypeStruct((TOP, width + 128), f32),
        ],
        cost_estimate=pl.CostEstimate(
            flops=256 * rows * width, transcendentals=TOP * rows, bytes_accessed=10 * rows * width
        ),
        name="pool_local",
    )(result, gain[None], key_probe)


def pool_back_kernel(
    images,
    seq_count,
    place_ref,
    count_ref,
    pairs_ref,
    temp_ref,
    bias_ref,
    own_ref,
    other_ref,
    exp_ref,
    low_ref,
    unit_ref,
    inv_ref,
    gain_ref,
    key_probe_ref,
    value_ref,
    output_ref,
    caps_ref,
    grad_ref,
    branch_ref,
    sums_ref,
    rank_ref,
):
    width = low_ref.shape[1]
    half = width // seq_count
    heads = head_rows(width)
    low = low_ref[...]
    value = value_ref[...]
    output = output_ref[...]
    own_top = own_ref[:, width : width + 1]
    other_top = other_ref[:, width : width + 1]
    top = jnp.maximum(own_top, other_top)
    own_factor = jnp.exp(own_top - top)
    other_factor = jnp.exp(other_top - top)
    total = (
        own_ref[:, width + 1 : width + 2] * own_factor
        + other_ref[:, width + 1 : width + 2] * other_factor
    )
    mix = (own_ref[:, :width] * own_factor + other_ref[:, :width] * other_factor) / total
    probs = exp_ref[...] * (own_factor / total)
    flat = jnp.sum(wide(nn, mix, value) * heads, axis=0, keepdims=True)
    pooled = wide_row(nn, flat, output)
    scale = lax.rsqrt(jnp.sum(pooled * pooled, axis=-1, keepdims=True) + norm_eps)
    embedding = pooled * scale

    caps = caps_ref[...]
    unit_caps = caps * lax.rsqrt(jnp.sum(caps * caps, axis=-1, keepdims=True) + norm_eps)
    similar = jnp.sum(unit_caps * embedding, axis=-1, keepdims=True)
    temper = jnp.exp(jnp.full((1, 1), temp_ref[0], f32))
    logits = temper * similar + bias_ref[0]
    slot = lax.broadcasted_iota(jnp.int32, similar.shape, 0)
    pair = jnp.zeros(similar.shape, jnp.int32)
    per_image = caps.shape[0] // images
    for j in range(per_image):
        pair = jnp.where(slot == j, pairs_ref[0, place_ref[0] * per_image + j], pair)
    positive = pair == 1
    sign = jnp.where(positive, 1.0, -1.0)
    weight = jnp.where(positive, 1.0 / jnp.full((1, 1), count_ref[0], jnp.int32).astype(f32), 1.0)
    signed = sign * logits
    decay = jnp.exp(-jnp.abs(signed))
    log_sigmoid = jnp.minimum(signed, 0.0) - jnp.log1p(decay)
    against = jnp.where(signed >= 0, decay, 1.0) / (1.0 + decay)
    row_loss = -jnp.sum(weight * log_sigmoid, axis=0, keepdims=True) / images
    logit_grad = -(weight / images) * sign * against
    temp_row = jnp.sum(logit_grad * temper * similar, axis=0, keepdims=True)
    bias_row = jnp.sum(logit_grad, axis=0, keepdims=True)
    embed_grad = temper * jnp.sum(logit_grad * unit_caps, axis=0, keepdims=True)
    pooled_grad = scale * (
        embed_grad - embedding * jnp.sum(embedding * embed_grad, axis=-1, keepdims=True)
    )

    head_grad = wide_row(nt, pooled_grad, output)
    value_probe = wide(nt, head_grad * heads, value)
    prob_grad = wide(nt, value_probe, low)
    center_term = jnp.sum(heads * (head_grad * flat), axis=-1, keepdims=True)
    score_grad = probs * (prob_grad - center_term) * 0.125
    key_mix_grad = wide(nn, score_grad, low)
    left = thirds(jnp.concatenate([score_grad, probs], axis=0))
    right = thirds(jnp.concatenate([key_probe_ref[...], value_probe], axis=0))
    order = ((0, 0), (0, 1), (1, 0), (0, 2), (1, 1), (2, 0))
    pool_grad = tn(
        jnp.concatenate([left[i] for i, _ in order], axis=0),
        jnp.concatenate([right[j] for _, j in order], axis=0),
    )

    unit = unit_ref[...]
    scaled = pool_grad * gain_ref[...]
    gain_grad = jnp.sum(pool_grad * unit, axis=0, keepdims=True)
    first_mean = jnp.mean(scaled, axis=-1, keepdims=True)
    second_mean = jnp.mean(scaled * unit, axis=-1, keepdims=True)
    grad = inv_ref[...] * (scaled - first_mean - unit * second_mean)
    grad_ref[...] = grad
    branch_ref[...] = grad.astype(bf16)

    row = lax.broadcasted_iota(jnp.int32, (TOP, width), 0)
    lane = lax.broadcasted_iota(jnp.int32, (1, width), 1)
    share = 1.0 / seq_count
    scalars = jnp.where(
        lane == 0,
        row_loss * share,
        jnp.where(lane == 1, temp_row * share, jnp.where(lane == 2, bias_row * share, 0.0)),
    )
    sums_ref[...] = jnp.where(
        row < HEADS,
        key_mix_grad,
        jnp.where(row == HEADS, gain_grad, jnp.where(row == HEADS + 1, scalars, 0.0)),
    )
    first = place_ref[1] == 0
    near = HEADS // 2
    my_mix = jnp.where(first, mix[:8], mix[near : near + 8])
    my_pair = jnp.concatenate(
        [
            jnp.where(first, pooled_grad[:, :half], pooled_grad[:, half:]),
            jnp.where(first, head_grad[:, :half], head_grad[:, half:]),
        ],
        axis=1,
    )
    row = row[:8]
    rank_ref[...] = jnp.where(row < near, my_mix, jnp.where(row == near, flat, my_pair))


def pool_back_call(
    place, counts, pairs, log_temp, pair_bias, own, other, exps, low, unit, inv, gain, key_probe,
    pool_value, pool_output, caps, images, seq_count,
):
    rows, width = low.shape
    smem = pl.BlockSpec(memory_space=pltpu.SMEM)
    vmem = pl.BlockSpec(memory_space=pltpu.VMEM)
    return pl.pallas_call(
        functools.partial(pool_back_kernel, images, seq_count),
        in_specs=[smem] * 5 + [vmem] * 11,
        out_specs=[vmem] * 4,
        out_shape=[
            jax.ShapeDtypeStruct((rows, width), f32),
            jax.ShapeDtypeStruct((rows, width), bf16),
            jax.ShapeDtypeStruct((TOP, width), f32),
            jax.ShapeDtypeStruct((8, width), f32),
        ],
        cost_estimate=pl.CostEstimate(
            flops=1024 * rows * width, transcendentals=TOP * rows, bytes_accessed=20 * rows * width
        ),
        name="pool_back",
    )(
        place, counts, pairs, log_temp[None], pair_bias[None], own, other, exps, low, unit, inv,
        gain[None], key_probe, pool_value, pool_output, caps,
    )


def attend_kernel(q_ref, ka_ref, kb_ref, va_ref, vb_ref, a_ref, lse_ref):
    q = q_ref[...]
    k = jnp.concatenate([ka_ref[...], kb_ref[...]], axis=0)
    v = jnp.concatenate([va_ref[...], vb_ref[...]], axis=0)
    lane = lax.broadcasted_iota(jnp.int32, (1, PAIR), 1)
    out = jnp.zeros(a_ref.shape, f32)
    for half in range(2):
        own = (lane < HEAD) if half == 0 else (lane >= HEAD)
        s = nt(jnp.where(own, q, 0), k) * 0.125
        top = jnp.max(s, axis=-1, keepdims=True)
        e = jnp.exp(s - top)
        total = jnp.sum(e, axis=-1, keepdims=True)
        p = (e * (1.0 / total)).astype(bf16)
        out = out + jnp.where(own, nn(p, v), 0.0)
        lse_ref[0, :, half : half + 1] = top + jnp.log(total)
    a_ref[...] = out.astype(bf16)


def attend(q, ka, kb, va, vb):
    rows, width = q.shape
    length = 2 * rows
    pairs = width // PAIR
    spec = pl.BlockSpec((rows, PAIR), lambda h: (0, h))
    return pl.pallas_call(
        attend_kernel,
        grid=(pairs,),
        in_specs=[spec] * 5,
        out_specs=[spec, pl.BlockSpec((1, rows, 2), lambda h: (h, 0, 0))],
        out_shape=[
            jax.ShapeDtypeStruct((rows, width), bf16),
            jax.ShapeDtypeStruct((pairs, rows, 2), f32),
        ],
        cost_estimate=pl.CostEstimate(
            flops=4 * rows * length * width,
            transcendentals=HEADS * rows * length,
            bytes_accessed=2 * (2 * rows + 2 * length) * width,
        ),
        name="attend",
    )(q, ka, kb, va, vb)


def attend_back_kernel(
    q_ref, ka_ref, kb_ref, va_ref, vb_ref, g_ref, lse_ref, dq_ref, dk_ref, dv_ref
):
    q = q_ref[...]
    k = jnp.concatenate([ka_ref[...], kb_ref[...]], axis=0)
    v = jnp.concatenate([va_ref[...], vb_ref[...]], axis=0)
    g = g_ref[...]
    lane = lax.broadcasted_iota(jnp.int32, (1, PAIR), 1)
    dq = jnp.zeros(dq_ref.shape, f32)
    dk = jnp.zeros(dk_ref.shape, f32)
    dv = jnp.zeros(dv_ref.shape, f32)
    for half in range(2):
        own = (lane < HEAD) if half == 0 else (lane >= HEAD)
        qh = jnp.where(own, q, 0)
        gh = jnp.where(own, g, 0)
        s = nt(qh, k) * 0.125
        p = jnp.exp(s - lse_ref[0, :, half : half + 1])
        dp = nt(gh, v)
        dv = dv + tn(p.astype(bf16), gh)
        row = jnp.sum(p * dp, axis=-1, keepdims=True)
        ds = (p * (dp - row)).astype(bf16)
        dq = dq + jnp.where(own, nn(ds, k), 0.0)
        dk = dk + tn(ds, qh)
    dq_ref[...] = (dq * 0.125).astype(bf16)
    dk_ref[...] = (dk * 0.125).astype(bf16)
    dv_ref[...] = dv.astype(bf16)


def attend_back(q, ka, kb, va, vb, g, lse):
    rows, width = q.shape
    length = 2 * rows
    pairs = width // PAIR
    row_spec = pl.BlockSpec((rows, PAIR), lambda h: (0, h))
    key_spec = pl.BlockSpec((length, PAIR), lambda h: (0, h))
    return pl.pallas_call(
        attend_back_kernel,
        grid=(pairs,),
        in_specs=[row_spec] * 6 + [pl.BlockSpec((1, rows, 2), lambda h: (h, 0, 0))],
        out_specs=[row_spec, key_spec, key_spec],
        out_shape=[
            jax.ShapeDtypeStruct((rows, width), bf16),
            jax.ShapeDtypeStruct((length, width), bf16),
            jax.ShapeDtypeStruct((length, width), bf16),
        ],
        cost_estimate=pl.CostEstimate(
            flops=10 * rows * length * width,
            transcendentals=HEADS * rows * length,
            bytes_accessed=2 * (3 * rows + 4 * length) * width,
        ),
        name="attend_back",
    )(q, ka, kb, va, vb, g, lse)


def store_halves(core, grad, block, send_refs, keep_refs):
    for j in range(grad.shape[0] // (2 * block)):
        near = grad[2 * j * block : (2 * j + 1) * block]
        far = grad[(2 * j + 1) * block : (2 * j + 2) * block]
        send_refs(j)[...] = jnp.where(core == 0, far, near).astype(bf16)
        keep_refs(j)[...] = jnp.where(core == 0, near, far).astype(bf16)


def wgrad_kernel(block, place_ref, left_ref, right_ref, send_ref, keep_ref):
    grad = tn(left_ref[...], right_ref[...])
    store_halves(
        place_ref[2], grad, block, lambda j: send_ref.at[0, j], lambda j: keep_ref.at[0, j]
    )


def wgrad(place, left, right, images):
    rows, depth = left.shape
    columns = right.shape[1] // 2
    block = depth // images
    chunk = math.lcm(2 * block, 128)
    pairs = chunk // (2 * block)
    out_spec = pl.BlockSpec((1, pairs, block, columns), lambda i, y: (y, i, 0, 0))
    out_shape = jax.ShapeDtypeStruct((2, images // 2, block, columns), bf16)
    return pl.pallas_call(
        functools.partial(wgrad_kernel, block),
        grid=(depth // chunk, 2),
        in_specs=[
            pl.BlockSpec(memory_space=pltpu.SMEM),
            pl.BlockSpec((rows, chunk), lambda i, y: (0, i)),
            pl.BlockSpec((rows, columns), lambda i, y: (0, y)),
        ],
        out_specs=[out_spec, out_spec],
        out_shape=[out_shape, out_shape],
        cost_estimate=pl.CostEstimate(
            flops=4 * rows * depth * columns,
            transcendentals=0,
            bytes_accessed=2 * rows * (depth + 2 * columns) + 4 * depth * columns,
        ),
        name="wgrad",
    )(place, left, right)


def wgrad_four_kernel(
    block, place_ref, na_ref, nb_ref, a_ref, dq_ref, dk_ref, dv_ref, dx_ref, send_ref, keep_ref
):
    na = na_ref[...]
    rows = na.shape[0]
    both = jnp.concatenate([na, nb_ref[...]], axis=0)
    grads = (
        tn(na, dq_ref[...]),
        tn(both, dk_ref[...]),
        tn(both, dv_ref[...]),
        tn(a_ref[...], dx_ref[...]),
    )
    for at, grad in enumerate(grads):
        store_halves(
            place_ref[2],
            grad,
            block,
            lambda j: send_ref.at[at // 2, 0, j, at % 2],
            lambda j: keep_ref.at[at // 2, 0, j, at % 2],
        )


def wgrad_four(place, na, nb, a, dq, dk, dv, dx, images):
    rows, depth = na.shape
    columns = dq.shape[1] // 2
    block = depth // images
    chunk = math.lcm(2 * block, 128)
    pairs = chunk // (2 * block)
    left = pl.BlockSpec((rows, chunk), lambda i, y: (0, i))
    right = pl.BlockSpec((rows, columns), lambda i, y: (0, y))
    right_all = pl.BlockSpec((2 * rows, columns), lambda i, y: (0, y))
    out_spec = pl.BlockSpec((2, 1, pairs, 2, block, columns), lambda i, y: (0, y, i, 0, 0, 0))
    out_shape = jax.ShapeDtypeStruct((2, 2, images // 2, 2, block, columns), bf16)
    return pl.pallas_call(
        functools.partial(wgrad_four_kernel, block),
        grid=(depth // chunk, 2),
        in_specs=[pl.BlockSpec(memory_space=pltpu.SMEM), left, left, left, right, right_all, right_all, right],
        out_specs=[out_spec, out_spec],
        out_shape=[out_shape, out_shape],
        cost_estimate=pl.CostEstimate(
            flops=24 * rows * depth * columns,
            transcendentals=0,
            bytes_accessed=2 * rows * (3 * depth + 12 * columns) + 16 * depth * columns,
        ),
        name="wgrad_four",
    )(place, na, nb, a, dq, dk, dv, dx)


def img_bits():
    return lax.axis_size("img").bit_length() - 1


def img_swap(value, mask):
    count = lax.axis_size("img")
    return lax.ppermute(value, "img", [(i, i ^ mask) for i in range(count)])


def seq_swap(value):
    return lax.ppermute(value, "seq", [(0, 1), (1, 0)])


def my_bit(bit):
    return (lax.axis_index("img") >> bit) & 1


def pick(value, index, axis):
    return lax.dynamic_index_in_dim(value, index, axis, keepdims=False)


def tie(*values):
    return lax.optimization_barrier(values)


def total_of(parts):
    total = parts[0].astype(f32)
    for part in parts[1:]:
        total = total + part.astype(f32)
    return total


def seq_send(parts, axis):
    mine = lax.axis_index("seq")
    send = total_of([pick(part, 1 - mine, axis) for part in parts]).astype(bf16)
    return send, [pick(part, mine, axis) for part in parts]


def img_send(parts, axis, bit):
    mine = my_bit(bit)
    cut = [
        part.reshape(*part.shape[:axis], part.shape[axis] // 2, 2, *part.shape[axis + 1 :])
        for part in parts
    ]
    send = total_of([pick(part, 1 - mine, axis + 1) for part in cut]).astype(bf16)
    return send, [pick(part, mine, axis + 1) for part in cut]


def finish(parts, axis, bit):
    while parts[0].shape[axis] > 1:
        send, parts = img_send(parts, axis, bit)
        parts = parts + [img_swap(send, 1 << bit)]
        bit += 1
    return jnp.squeeze(total_of(parts), axis)


def shards(
    tokens,
    w_query,
    w_key,
    w_value,
    w_output,
    w_up,
    w_down,
    first_gain,
    second_gain,
    final_gain,
    probe,
    pool_query,
    pool_key,
    pool_value,
    pool_output,
    captions,
    positive_pairs,
    caption_counts,
    log_temp,
    pair_bias,
):
    own_tokens = tokens[0]
    rows, width = own_tokens.shape
    images = lax.axis_size("img")
    seq_count = lax.axis_size("seq")
    bits = img_bits()
    me = lax.axis_index("img")
    seq_me = lax.axis_index("seq")
    half = width // seq_count
    caps = captions.shape[0]
    place = jnp.stack([me, seq_me, me & 1]).astype(jnp.int32)

    other_tokens = seq_swap(own_tokens)

    gathered = captions[None]

    def gather_more(gathered, bit):
        return jnp.concatenate([gathered, img_swap(gathered, 1 << bit)], axis=0)

    gathered = gather_more(gathered, 0)

    inputs = own_tokens.astype(f32)
    normed_one, unit_one, scale_one = layer_norm(inputs, first_gain)
    low_own = normed_one.astype(bf16)
    queries = low_dot(low_own, w_query).astype(bf16)
    keys_own = low_dot(low_own, w_key).astype(bf16)
    values_own = low_dot(low_own, w_value).astype(bf16)
    probe_query, key_probe = probe_call(probe, pool_query, pool_key)
    gathered = gather_more(gathered, 1)

    other_tokens, gathered, queries, keys_own, values_own, key_probe = tie(
        other_tokens, gathered, queries, keys_own, values_own, key_probe
    )
    low_other = layer_norm(other_tokens.astype(f32), first_gain)[0].astype(bf16)
    keys_other = low_dot(low_other, w_key).astype(bf16)
    values_other = low_dot(low_other, w_value).astype(bf16)
    gathered = gather_more(gathered, 2)
    attended_low, log_totals = attend(queries, keys_own, keys_other, values_own, values_other)
    attended_low, gathered = tie(attended_low, gathered)
    for bit in range(3, bits):
        gathered = gather_more(gathered, bit)
    residual = inputs + low_dot(attended_low, w_output)

    normed_two, unit_two, scale_two = layer_norm(residual, second_gain)
    second_low = normed_two.astype(bf16)
    upward = low_dot(second_low, w_up)
    activated, gelu_back = jax.vjp(gelu_tanh, upward)
    hidden_low = activated.astype(bf16)
    result = residual + low_dot(hidden_low, w_down)
    block_out = result.astype(bf16)[None]

    pool_low, unit_pool, inv_pool, exps, packed = pool_call(result, final_gain, key_probe)
    other_packed = seq_swap(packed)
    other_packed, gathered = tie(other_packed, gathered)
    result_grad, branch_grad, sums, rank = pool_back_call(
        place, caption_counts, positive_pairs, log_temp, pair_bias, packed, other_packed, exps,
        pool_low, unit_pool, inv_pool, final_gain, key_probe, pool_value, pool_output,
        gathered.reshape(images * caps, width), images, seq_count,
    )

    sums_other = seq_swap(sums)
    down_send, down_keep = wgrad(place, hidden_low, branch_grad, images)
    branch_grad, down_send = tie(branch_grad, down_send)
    down_core = img_swap(down_send, 1)
    hidden_grad = back_dot(branch_grad, w_down)
    up_grad_low = gelu_back(hidden_grad)[0].astype(bf16)

    up_grad_low, down_core, sums_other = tie(up_grad_low, down_core, sums_other)
    down_y, down_parts = seq_send([down_keep, down_core], 0)
    up_grad_low, down_y = tie(up_grad_low, down_y)
    down_parts = down_parts + [seq_swap(down_y)]
    sums = sums + sums_other

    def small_step(sums, rank, bit):
        both = img_swap(jnp.concatenate([sums, rank], axis=0), 1 << bit)
        return both

    small_in = small_step(sums, rank, 0)
    up_send, up_keep = wgrad(place, second_low, up_grad_low, images)
    up_grad_low, up_send = tie(up_grad_low, up_send)
    up_core = img_swap(up_send, 1)
    second_in_grad = back_dot(up_grad_low, w_up)
    residual_ln_grad, second_gain_grad = norm_back(second_in_grad, unit_two, scale_two, second_gain)
    residual_grad = result_grad + residual_ln_grad
    attn_branch = residual_grad.astype(bf16)

    attn_branch, up_core, small_in = tie(attn_branch, up_core, small_in)
    sums = sums + small_in[:TOP]
    rank = jnp.concatenate([rank, small_in[TOP:]], axis=0)
    up_x, up_parts = img_send([up_keep, up_core], 1, 1)
    attn_branch, up_x = tie(attn_branch, up_x)
    up_parts = up_parts + [img_swap(up_x, 2)]
    small_in = small_step(sums, rank, 1)

    attended_grad = back_dot(attn_branch, w_output).astype(bf16)
    query_grad, key_part, value_part = attend_back(
        queries, keys_own, keys_other, values_own, values_other, attended_grad, log_totals
    )
    other_in_grad = (
        back_dot(key_part[rows:], w_key) + back_dot(value_part[rows:], w_value)
    ).astype(bf16)
    other_in_grad, query_grad, key_part, value_part, small_in = tie(
        other_in_grad, query_grad, key_part, value_part, small_in
    )
    arrived_grad = seq_swap(other_in_grad)
    sums = sums + small_in[:TOP]
    rank = jnp.concatenate([rank, small_in[TOP:]], axis=0)
    small_in = small_step(sums, rank, 2)
    four_send, four_keep = wgrad_four(
        place, low_own, low_other, attended_low, query_grad, key_part, value_part, attn_branch, images
    )
    query_grad, four_send = tie(query_grad, four_send)
    four_core = img_swap(four_send, 1)
    own_in_grad = (
        back_dot(query_grad, w_query)
        + back_dot(key_part[:rows], w_key)
        + back_dot(value_part[:rows], w_value)
    )

    down_parts, own_in_grad, four_core = tie(tuple(down_parts), own_in_grad, four_core)
    down_x, down_parts = img_send(list(down_parts), 0, 1)
    down_parts = down_parts + [img_swap(down_x, 2)]
    early_parts = [four_keep[0], four_core[0]]
    late_parts = [four_keep[1], four_core[1]]
    early_send, early_parts = img_send(early_parts, 1, 1)
    late_send, late_parts = seq_send(late_parts, 0)
    early_parts = early_parts + [img_swap(early_send, 2)]
    late_parts = late_parts + [seq_swap(late_send)]

    first_in_grad = own_in_grad + arrived_grad.astype(f32)
    input_ln_grad, first_gain_grad = norm_back(first_in_grad, unit_one, scale_one, first_gain)
    input_grad = (residual_grad + input_ln_grad)[None]

    for bit in range(2, bits):
        sums = sums + small_in[:TOP]
        rank = jnp.concatenate([rank, small_in[TOP:]], axis=0)
        if bit + 1 < bits:
            small_in = small_step(sums, rank, bit + 1)

    up_y, up_parts = seq_send(up_parts, 0)
    up_parts = up_parts + [seq_swap(up_y)]
    down_grad = finish(down_parts, 0, 2)
    up_weight_grad = finish(up_parts, 0, 2)

    early_send, early_parts = seq_send(early_parts, 0)
    late_send, late_parts = img_send(late_parts, 0, 1)
    early_parts = early_parts + [seq_swap(early_send)]
    late_parts = late_parts + [img_swap(late_send, 2)]
    query_key = finish(early_parts, 0, 2)
    value_output = finish(late_parts, 0, 2)

    late = jnp.stack([second_gain_grad, first_gain_grad])
    late = late + seq_swap(late)
    for bit in range(bits):
        late = late + img_swap(late, 1 << bit)

    block = width // images

    def own_rows(vector):
        return lax.dynamic_slice_in_dim(vector, me * block, block)

    heads = head_rows(width)
    mix_total = sums[:HEADS]
    probe_query_grad = jnp.sum(
        jnp.dot(mix_total, pool_key.astype(f32), precision=highest) * heads[:HEADS], axis=0
    )
    query_pool_grad = own_rows(probe)[:, None] * lax.dynamic_slice_in_dim(
        probe_query_grad, seq_me * half, half
    )[None, :]
    own_query = lax.dynamic_slice_in_dim(pool_query, me * block, block, 0).astype(f32)
    probe_grad = jnp.dot(own_query, probe_query_grad, precision=highest)
    own_mix = lax.dynamic_slice_in_dim(mix_total, me * block, block, 1)
    my_query = lax.dynamic_slice_in_dim(
        probe_query * heads[:HEADS], seq_me * half, half, 1
    )
    key_pool_grad = lax.dot_general(
        own_mix, my_query, (((0,), (0,)), ((), ())), precision=highest
    )
    near = HEADS // 2
    factors = rank.reshape(images, 8, width)
    own_factors = lax.dynamic_slice_in_dim(factors, me * block, block, 2)
    out_pool_grad = lax.dot_general(
        own_factors[:, near], factors[:, near + 1, :half], (((0,), (0,)), ((), ())), precision=highest
    )
    spread = factors[:, near + 1 :, half:] * heads[None, :near, :half]
    value_pool_grad = lax.dot_general(
        own_factors[:, :near].reshape(images * near, block),
        spread.reshape(images * near, half),
        (((0,), (0,)), ((), ())),
        precision=highest,
    )
    return (
        block_out,
        input_grad,
        query_key[0],
        query_key[1],
        value_output[0],
        value_output[1],
        up_weight_grad,
        down_grad,
        own_rows(late[1]),
        own_rows(late[0]),
        own_rows(sums[HEADS]),
        probe_grad,
        query_pool_grad,
        key_pool_grad,
        value_pool_grad,
        out_pool_grad,
        sums[HEADS + 1, 0],
        sums[HEADS + 1, 1],
        sums[HEADS + 1, 2],
    )


def solution(mesh):
    return jax.shard_map(
        shards,
        mesh=mesh,
        in_specs=(
            P("img", "seq", None),
            P(),
            P(),
            P(),
            P(),
            P(),
            P(),
            P(),
            P(),
            P(),
            P(),
            P(),
            P(),
            P(),
            P(),
            P("img", None),
            P("img", None),
            P("img"),
            P(),
            P(),
        ),
        out_specs=(
            P("img", "seq", None),
            P("img", "seq", None),
            P("img", "seq"),
            P("img", "seq"),
            P("img", "seq"),
            P("img", "seq"),
            P("img", "seq"),
            P("img", "seq"),
            P("img"),
            P("img"),
            P("img"),
            P("img"),
            P("img", "seq"),
            P("img", "seq"),
            P("img", "seq"),
            P("img", "seq"),
            P(),
            P(),
            P(),
        ),
        check_vma=False,
    )
```

profile of v0, /device:TPU:0, one launch (start us, length us, event | category | flops | bytes accessed | tf_op | source)
XLA Modules:
  0.0 268.2 jit_solution(13516227378958604991)
XLA Ops:
  1.2 2.6 collective-permute-start
  16.6 3.0 %probe_rows.1 = (f32[1,768]{1,0:T(1,128)}, f32[16,768]{1,0:T(8,128)}) custom-call(f32[1,768]{1,0:T(1,128)} %broadcast_in_dim.15.probe_ref, bf16[768,768]{1,0:T(8,128)(2,1)} %query_ref.1, bf16[768,768]{1,0:T(8,128)(2,1)} %key_ref.1), custom_call_target="tpu_custom_call" | custom-call | flops 75497472 | bytes 2359296 | tf_op jit(solution)/shard_map/probe_rows/pallas_call | solution.py:98
  24.4 7.9 %attend.1 = (bf16[256,768]{1,0:T(8,128)(2,1)}, f32[6,256,2]{2,1,0:T(8,128)}) custom-call(bf16[256,768]{1,0:T(8,128)(2,1)} %convolution_convert_fusion.5.q_ref, bf16[256,768]{1,0:T(8,128)(2,1)} %convolution_convert_fusion.4.ka_ref, bf16[256,768]{1,0:T(8,128)(2,1)} %convolution_convert_fusion.2.kb_ref, bf16[256,768]{1,0:T(8,128)(2,1)} %convolution_convert_fusion.3.va_ref, ...), custom_call_target="tpu_custom_call" | custom-call | flops 402653184 | bytes 2359296 | tf_op jit(solution)/shard_map/attend/pallas_call | solution.py:321
  33.0 2.6 collective-permute-start.5
  39.1 3.6 %multiply_convert_fusion = (bf16[256,3072]{1,0:T(8,128)(2,1)S(1)}, f32[256,3072]{1,0:T(8,128)}) fusion(bf16[256,768]{1,0:T(8,128)(2,1)S(1)} %multiply_convert_fusion.1.left_ref, bf16[768,3072]{1,0:T(8,128)(2,1)S(1)} %copy-done.44), kind=kOutput, calls=%fused_computation.9 | convolution fusion | flops 1215037440 | bytes 9830400 | tf_op jit(solution)/shard_map/dot_general | solution.py:39
  43.9 2.3 convolution_add_fusion.4.result_ref
  46.2 2.6 pool_local.1
  51.1 2.1 collective-permute-done.4.other_ref
  55.0 5.7 %pool_back.1 = (f32[256,768]{1,0:T(8,128)}, bf16[256,768]{1,0:T(8,128)(2,1)}, f32[16,768]{1,0:T(8,128)}, f32[8,768]{1,0:T(8,128)}) custom-call(s32[3]{0:T(128)} %pad_add_fusion.place_ref, s32[1]{0:T(128)S(6)} %copy.74.count_ref, s32[1,80]{1,0:T(1,128)} %pairs_ref.1, f32[1]{0:T(128)} %bitcast.190.temp_ref, f32[1]{0:T(128)} %bitcast.191.bias_ref, ...), custom_call_target="tpu_custom_call" | custom-call | flops 201326592 | bytes 3932160 | tf_op jit(solution)/shard_map/pool_back/pallas_call | solution.py:278
  60.7 12.8 %wgrad.2 = (bf16[2,8,192,384]{3,2,1,0:T(8,128)(2,1)}, bf16[2,8,192,384]{3,2,1,0:T(8,128)(2,1)}) custom-call(s32[3]{0:T(128)} %pad_add_fusion.place_ref, bf16[256,3072]{1,0:T(8,128)(2,1)} %copy-done.47, bf16[256,768]{1,0:T(8,128)(2,1)} %get-tuple-element.97.right_ref), custom_call_target="tpu_custom_call" | custom-call | flops 1207959552 | bytes 6684672 | tf_op jit(solution)/shard_map/wgrad/pallas_call | solution.py:415
  74.7 7.4 %fusion.6.right_ref = bf16[256,3072]{1,0:T(8,128)(2,1)} fusion(f32[256,3072]{1,0:T(8,128)} %get-tuple-element.171, bf16[256,768]{1,0:T(8,128)(2,1)} %get-tuple-element.97.right_ref, bf16[3072,768]{1,0:T(8,128)(2,1)} %param.26), kind=kOutput, calls=%fused_computation.8 | convolution fusion | flops 1223688192 | bytes 9830400 | tf_op jit(solution)/shard_map/dot_general | solution.py:43
  82.1 2.6 fusion.8
  84.7 5.9 %wgrad.3 = (bf16[2,8,48,1536]{3,2,1,0:T(8,128)(2,1)}, bf16[2,8,48,1536]{3,2,1,0:T(8,128)(2,1)}) custom-call(s32[3]{0:T(128)} %pad_add_fusion.place_ref, bf16[256,768]{1,0:T(8,128)(2,1)} %copy-done.22, bf16[256,3072]{1,0:T(8,128)(2,1)} %fusion.6.right_ref), custom_call_target="tpu_custom_call" | custom-call | flops 1207959552 | bytes 6684672 | tf_op jit(solution)/shard_map/wgrad/pallas_call | solution.py:415
  96.0 2.5 dynamic-slice_bitcast_fusion.1
  101.3 4.0 %multiply_reduce_fusion = (f32[768]{0:T(1024)S(1)}, f32[256]{0:T(256)S(1)}, f32[256]{0:T(256)S(1)}, f32[256,768]{1,0:T(8,128)S(1)}) fusion(f32[256,768]{1,0:T(8,128)S(1)} %get-tuple-element.169, f32[256]{0:T(256)S(1)} %copy-done.39, f32[256]{0:T(256)S(1)} %copy-done.37, f32[768]{0:T(1024)S(1)} %copy-done.33, bf16[256,3072]{1,0:T(8,128)(2,1)S(1)} %copy-done.46, ...), kind=kOutput, calls=%fused_computation.60 | convolution fusion | flops 1209531136 | bytes 7874560 | tf_op jit(solution)/shard_map/dot_general | solution.py:43
  107.9 2.6 dynamic-slice_bitcast_fusion
  112.9 2.7 %fusion.9 = bf16[2,4,48,1536]{3,2,1,0:T(8,128)(2,1)} fusion(bf16[2,4,2,48,1536]{4,3,2,1,0:T(8,128)(2,1)} %bitcast.12, s32[]{:T(128)S(6)} %select_n.178, bf16[2,4,2,48,1536]{4,3,2,1,0:T(8,128)(2,1)S(1)} %bitcast.227), kind=kLoop, calls=%fused_computation.27 | loop fusion | flops 2359296 | bytes 3538948 | tf_op jit(solution)/shard_map/convert_element_type | solution.py:526
  116.8 10.2 %attend_back.1 = (bf16[256,768]{1,0:T(8,128)(2,1)}, bf16[512,768]{1,0:T(8,128)(2,1)}, bf16[512,768]{1,0:T(8,128)(2,1)}) custom-call(bf16[256,768]{1,0:T(8,128)(2,1)} %convolution_convert_fusion.5.q_ref, bf16[256,768]{1,0:T(8,128)(2,1)} %convolution_convert_fusion.4.ka_ref, bf16[256,768]{1,0:T(8,128)(2,1)} %convolution_convert_fusion.2.kb_ref, ...), custom_call_target="tpu_custom_call" | custom-call | flops 1006632960 | bytes 4325376 | tf_op jit(solution)/shard_map/attend_back/pallas_call | solution.py:373
  134.0 7.3 %wgrad_four.1 = (bf16[2,2,8,2,48,384]{5,4,3,2,1,0:T(8,128)(2,1)}, bf16[2,2,8,2,48,384]{5,4,3,2,1,0:T(8,128)(2,1)}) custom-call(s32[3]{0:T(128)} %pad_add_fusion.place_ref, bf16[256,768]{1,0:T(8,128)(2,1)} %copy-done.3, bf16[256,768]{1,0:T(8,128)(2,1)} %copy-done.9, bf16[256,768]{1,0:T(8,128)(2,1)} %get-tuple-element.84.a_ref, ...), custom_call_target="tpu_custom_call" | custom-call | flops 1811939328 | bytes 8257536 | tf_op jit(solution)/shard_map/wgrad_four/pallas_call | solution.py:467
  150.9 13.6 %collective-permute-done.35 = f32[80,768]{1,0:T(8,128)S(1)} collective-permute-done((f32[80,768]{1,0:T(8,128)S(1)}, f32[80,768]{1,0:T(8,128)S(1)}, u32[]{:S(2)}, u32[]{:S(2)}) %collective-permute-start.35) | collective-permute-done | bytes 245792 | tf_op jit(solution)/shard_map/ppermute | solution.py:488
  174.4 11.6 %collective-permute-done.23 = bf16[4,48,1536]{2,1,0:T(8,128)(2,1)S(1)} collective-permute-done((bf16[4,48,1536]{2,1,0:T(8,128)(2,1)S(1)}, bf16[4,48,1536]{2,1,0:T(8,128)(2,1)S(1)}, u32[]{:S(2)}, u32[]{:S(2)}) %collective-permute-start.23) | collective-permute-done | bytes 589856 | tf_op jit(solution)/shard_map/ppermute | solution.py:492
  187.3 6.7 %collective-permute-done.24 = bf16[2,48,1536]{2,1,0:T(8,128)(2,1)S(1)} collective-permute-done((bf16[2,48,1536]{2,1,0:T(8,128)(2,1)S(1)}, bf16[2,48,1536]{2,1,0:T(8,128)(2,1)S(1)}, u32[]{:S(2)}, u32[]{:S(2)}) %collective-permute-start.24) | collective-permute-done | bytes 294944 | tf_op jit(solution)/shard_map/ppermute | solution.py:488
  196.5 5.4 %collective-permute-done.25 = bf16[1,48,1536]{2,1,0:T(8,128)(2,1)S(1)} collective-permute-done((bf16[1,48,1536]{2,1,0:T(8,128)(2,1)S(1)}, bf16[1,48,1536]{2,1,0:T(8,128)(2,1)S(1)}, u32[]{:S(2)}, u32[]{:S(2)}) %collective-permute-start.25) | collective-permute-done | bytes 147488 | tf_op jit(solution)/shard_map/ppermute | solution.py:488
  208.1 2.2 fusion.25
  217.3 3.0 %collective-permute-done.32 = f32[2,768]{1,0:T(2,128)S(1)} collective-permute-done((f32[2,768]{1,0:T(2,128)S(1)}, f32[2,768]{1,0:T(2,128)S(1)}, u32[]{:S(2)}, u32[]{:S(2)}) %collective-permute-start.32) | collective-permute-done | bytes 6176 | tf_op jit(solution)/shard_map/ppermute | solution.py:488
  221.9 2.9 %collective-permute-done.33 = f32[2,768]{1,0:T(2,128)S(1)} collective-permute-done((f32[2,768]{1,0:T(2,128)S(1)}, f32[2,768]{1,0:T(2,128)S(1)}, u32[]{:S(2)}, u32[]{:S(2)}) %collective-permute-start.33) | collective-permute-done | bytes 6176 | tf_op jit(solution)/shard_map/ppermute | solution.py:488
  226.0 3.9 %collective-permute-done.14 = bf16[2,4,2,48,384]{4,3,2,1,0:T(8,128)(2,1)S(1)} collective-permute-done((bf16[2,4,2,48,384]{4,3,2,1,0:T(8,128)(2,1)S(1)}, bf16[2,4,2,48,384]{4,3,2,1,0:T(8,128)(2,1)S(1)}, u32[]{:S(2)}, u32[]{:S(2)}) %collective-permute-start.14) | collective-permute-done | bytes 589856 | tf_op jit(solution)/shard_map/ppermute | solution.py:488
  232.4 10.2 %collective-permute-done.26 = bf16[4,192,384]{2,1,0:T(8,128)(2,1)S(1)} collective-permute-done((bf16[4,192,384]{2,1,0:T(8,128)(2,1)S(1)}, bf16[4,192,384]{2,1,0:T(8,128)(2,1)S(1)}, u32[]{:S(2)}, u32[]{:S(2)}) %collective-permute-start.26) | collective-permute-done | bytes 589856 | tf_op jit(solution)/shard_map/ppermute | solution.py:488
  245.0 3.2 %collective-permute-done.19 = bf16[4,2,48,384]{3,2,1,0:T(8,128)(2,1)S(1)} collective-permute-done((bf16[4,2,48,384]{3,2,1,0:T(8,128)(2,1)S(1)}, bf16[4,2,48,384]{3,2,1,0:T(8,128)(2,1)S(1)}, u32[]{:S(2)}, u32[]{:S(2)}) %collective-permute-start.19) | collective-permute-done | bytes 294944 | tf_op jit(solution)/shard_map/ppermute | solution.py:488
  248.3 5.9 %collective-permute-done.27 = bf16[2,192,384]{2,1,0:T(8,128)(2,1)S(1)} collective-permute-done((bf16[2,192,384]{2,1,0:T(8,128)(2,1)S(1)}, bf16[2,192,384]{2,1,0:T(8,128)(2,1)S(1)}, u32[]{:S(2)}, u32[]{:S(2)}) %collective-permute-start.27) | collective-permute-done | bytes 294944 | tf_op jit(solution)/shard_map/ppermute | solution.py:488
  254.8 2.7 collective-permute-done.16
  260.7 5.2 %collective-permute-done.28 = bf16[1,192,384]{2,1,0:T(8,128)(2,1)S(1)} collective-permute-done((bf16[1,192,384]{2,1,0:T(8,128)(2,1)S(1)}, bf16[1,192,384]{2,1,0:T(8,128)(2,1)S(1)}, u32[]{:S(2)}, u32[]{:S(2)}) %collective-permute-start.28) | collective-permute-done | bytes 147488 | tf_op jit(solution)/shard_map/ppermute | solution.py:488
  (281 shorter events, 97.9 us)
Async XLA Ops:
  0.7 10.6 %collective-permute-start.1 = (f32[1,5,768]{2,1,0:T(8,128)}, f32[1,5,768]{2,1,0:T(8,128)S(1)}, u32[]{:S(2)}, u32[]{:S(2)}) collective-permute-start(f32[1,5,768]{2,1,0:T(8,128)} %bitcast.262), channel_id=1, source_target_pairs={{0,2},{2,0},{4,6},{6,4},{8,10},{10,8},{12,14},{14,12},{16,18},{18,... | collective-permute-start | bytes 46088 | tf_op jit(solution)/shard_map/ppermute | solution.py:488
  1.2 18.4 %collective-permute-start = (bf16[256,768]{1,0:T(8,128)(2,1)}, bf16[256,768]{1,0:T(8,128)(2,1)S(1)}, u32[]{:S(2)}, u32[]{:S(2)}) collective-permute-start(bf16[256,768]{1,0:T(8,128)(2,1)} %bitcast.192), channel_id=1, source_target_pairs={{0,1},{1,0},{2,3},{3,2},{4,5},{5,4},{6,7},{7,6},{8,9},{9,8},{10,11... | collective-permute-start | bytes 1179656 | tf_op jit(solution)/shard_map/ppermute | solution.py:492
  11.3 8.2 %collective-permute-start.2 = (f32[2,5,768]{2,1,0:T(8,128)S(1)}, f32[2,5,768]{2,1,0:T(8,128)S(1)}, u32[]{:S(2)}, u32[]{:S(2)}) collective-permute-start(f32[2,5,768]{2,1,0:T(8,128)S(1)} %pad_maximum_fusion.6), channel_id=1, source_target_pairs={{0,4},{2,6},{4,0},{6,2},{8,12},{10,14},{12,8},{14,10},{16,20},{18,... | collective-permute-start | bytes 92168 | tf_op jit(solution)/shard_map/ppermute | solution.py:488
  20.2 12.0 %collective-permute-start.3 = (f32[4,5,768]{2,1,0:T(8,128)S(1)}, f32[4,5,768]{2,1,0:T(8,128)S(1)}, u32[]{:S(2)}, u32[]{:S(2)}) collective-permute-start(f32[4,5,768]{2,1,0:T(8,128)S(1)} %pad_maximum_fusion.3), channel_id=1, source_target_pairs={{0,8},{2,10},{4,12},{6,14},{8,0},{10,2},{12,4},{14,6},{16,24},{18,... | collective-permute-start | bytes 184328 | tf_op jit(solution)/shard_map/ppermute | solution.py:488
  33.0 16.3 %collective-permute-start.5 = (f32[8,5,768]{2,1,0:T(8,128)}, f32[8,5,768]{2,1,0:T(8,128)}, u32[]{:S(2)}, u32[]{:S(2)}) collective-permute-start(f32[8,5,768]{2,1,0:T(8,128)} %pad_maximum_fusion.1), channel_id=1, source_target_pairs={{0,16},{2,18},{4,20},{6,22},{8,24},{10,26},{12,28},{14,30},{16,0},... | collective-permute-start | bytes 368648 | tf_op jit(solution)/shard_map/ppermute | solution.py:488
  73.6 8.5 %collective-permute-start.6 = (bf16[2,8,192,384]{3,2,1,0:T(8,128)(2,1)}, bf16[2,8,192,384]{3,2,1,0:T(8,128)(2,1)}, u32[]{:S(2)}, u32[]{:S(2)}) collective-permute-start(bf16[2,8,192,384]{3,2,1,0:T(8,128)(2,1)} %get-tuple-element.98), channel_id=1, source_target_pairs={{0,2},{2,0},{4,6},{6,4},{8,10},{10,8},{12,14},{14,12},{16,18},{18,... | collective-permute-start | bytes 7077896 | tf_op jit(solution)/shard_map/ppermute | solution.py:488
  74.2 7.9 %collective-permute-start.7 = (f32[16,768]{1,0:T(8,128)}, f32[16,768]{1,0:T(8,128)}, u32[]{:S(2)}, u32[]{:S(2)}) collective-permute-start(f32[16,768]{1,0:T(8,128)} %get-tuple-element.99), channel_id=1, source_target_pairs={{0,1},{1,0},{2,3},{3,2},{4,5},{5,4},{6,7},{7,6},{8,9},{9,8},{10,11... | collective-permute-start | bytes 147464 | tf_op jit(solution)/shard_map/ppermute | solution.py:492
  90.6 19.9 %collective-permute-start.9 = (bf16[2,8,48,1536]{3,2,1,0:T(8,128)(2,1)}, bf16[2,8,48,1536]{3,2,1,0:T(8,128)(2,1)}, u32[]{:S(2)}, u32[]{:S(2)}) collective-permute-start(bf16[2,8,48,1536]{3,2,1,0:T(8,128)(2,1)} %get-tuple-element.107), channel_id=1, source_target_pairs={{0,2},{2,0},{4,6},{6,4},{8,10},{10,8},{12,14},{14,12},{16,18},{18,... | collective-permute-start | bytes 7077896 | tf_op jit(solution)/shard_map/ppermute | solution.py:488
  99.4 11.1 %collective-permute-start.10 = (f32[24,768]{1,0:T(8,128)S(1)}, f32[24,768]{1,0:T(8,128)S(1)}, u32[]{:S(2)}, u32[]{:S(2)}) collective-permute-start(f32[24,768]{1,0:T(8,128)S(1)} %pad_maximum_fusion.5), channel_id=1, source_target_pairs={{0,2},{2,0},{4,6},{6,4},{8,10},{10,8},{12,14},{14,12},{16,18},{18,... | collective-permute-start | bytes 221192 | tf_op jit(solution)/shard_map/ppermute | solution.py:488
  99.8 102.9 %collective-permute-start.8 = (bf16[8,192,384]{2,1,0:T(8,128)(2,1)}, bf16[8,192,384]{2,1,0:T(8,128)(2,1)}, u32[]{:S(2)}, u32[]{:S(2)}) collective-permute-start(bf16[8,192,384]{2,1,0:T(8,128)(2,1)} %fusion.8), channel_id=1, source_target_pairs={{0,1},{1,0},{2,3},{3,2},{4,5},{5,4},{6,7},{7,6},{8,9},{9,8},{10,11... | collective-permute-start | bytes 3538952 | tf_op jit(solution)/shard_map/ppermute | solution.py:492
  111.2 20.3 %collective-permute-start.11 = (f32[32,768]{1,0:T(8,128)}, f32[32,768]{1,0:T(8,128)}, u32[]{:S(2)}, u32[]{:S(2)}) collective-permute-start(f32[32,768]{1,0:T(8,128)} %pad_maximum_fusion.4), channel_id=1, source_target_pairs={{0,4},{2,6},{4,0},{6,2},{8,12},{10,14},{12,8},{14,10},{16,20},{18,... | collective-permute-start | bytes 294920 | tf_op jit(solution)/shard_map/ppermute | solution.py:488
  128.7 40.7 %collective-permute-start.22 = (bf16[2,4,48,1536]{3,2,1,0:T(8,128)(2,1)}, bf16[2,4,48,1536]{3,2,1,0:T(8,128)(2,1)}, u32[]{:S(2)}, u32[]{:S(2)}) collective-permute-start(bf16[2,4,48,1536]{3,2,1,0:T(8,128)(2,1)} %fusion.9), channel_id=1, source_target_pairs={{0,4},{2,6},{4,0},{6,2},{8,12},{10,14},{12,8},{14,10},{16,20},{18,... | collective-permute-start | bytes 3538952 | tf_op jit(solution)/shard_map/ppermute | solution.py:488
  133.0 13.7 %collective-permute-start.34 = (f32[48,768]{1,0:T(8,128)}, f32[48,768]{1,0:T(8,128)}, u32[]{:S(2)}, u32[]{:S(2)}) collective-permute-start(f32[48,768]{1,0:T(8,128)} %pad_maximum_fusion.2), channel_id=1, source_target_pairs={{0,8},{2,10},{4,12},{6,14},{8,0},{10,2},{12,4},{14,6},{16,24},{18,... | collective-permute-start | bytes 442376 | tf_op jit(solution)/shard_map/ppermute | solution.py:488
  133.5 69.8 %collective-permute-start.13 = (bf16[256,768]{1,0:T(8,128)(2,1)}, bf16[256,768]{1,0:T(8,128)(2,1)}, u32[]{:S(2)}, u32[]{:S(2)}) collective-permute-start(bf16[256,768]{1,0:T(8,128)(2,1)} %fusion.7), channel_id=1, source_target_pairs={{0,1},{1,0},{2,3},{3,2},{4,5},{5,4},{6,7},{7,6},{8,9},{9,8},{10,11... | collective-permute-start | bytes 1179656 | tf_op jit(solution)/shard_map/ppermute | solution.py:492
  146.6 56.1 %collective-permute-start.12 = (bf16[2,2,8,2,48,384]{5,4,3,2,1,0:T(8,128)(2,1)S(1)}, bf16[2,2,8,2,48,384]{5,4,3,2,1,0:T(8,128)(2,1)S(1)}, u32[]{:S(2)}, u32[]{:S(2)}) collective-permute-start(bf16[2,2,8,2,48,384]{5,4,3,2,1,0:T(8,128)(2,1)S(1)} %copy-done.45), channel_id=1, source_target_pairs={{0,2},{2,0},{4,6},{6,4},{8,10},{10,8},{12,14},{14,12},{16,18},{18,... | collective-permute-start | bytes 7077896 | tf_op jit(solution)/shard_map/ppermute | solution.py:488
  150.0 14.6 %collective-permute-start.35 = (f32[80,768]{1,0:T(8,128)S(1)}, f32[80,768]{1,0:T(8,128)S(1)}, u32[]{:S(2)}, u32[]{:S(2)}) collective-permute-start(f32[80,768]{1,0:T(8,128)S(1)} %get-tuple-element.150), channel_id=1, source_target_pairs={{0,16},{2,18},{4,20},{6,22},{8,24},{10,26},{12,28},{14,30},{16,0},... | collective-permute-start | bytes 737288 | tf_op jit(solution)/shard_map/ppermute | solution.py:488
  171.1 14.9 %collective-permute-start.23 = (bf16[4,48,1536]{2,1,0:T(8,128)(2,1)S(1)}, bf16[4,48,1536]{2,1,0:T(8,128)(2,1)S(1)}, u32[]{:S(2)}, u32[]{:S(2)}) collective-permute-start(bf16[4,48,1536]{2,1,0:T(8,128)(2,1)S(1)} %fusion.10), channel_id=1, source_target_pairs={{0,1},{1,0},{2,3},{3,2},{4,5},{5,4},{6,7},{7,6},{8,9},{9,8},{10,11... | collective-permute-start | bytes 1769480 | tf_op jit(solution)/shard_map/ppermute | solution.py:492
  186.2 7.8 %collective-permute-start.24 = (bf16[2,48,1536]{2,1,0:T(8,128)(2,1)S(1)}, bf16[2,48,1536]{2,1,0:T(8,128)(2,1)S(1)}, u32[]{:S(2)}, u32[]{:S(2)}) collective-permute-start(bf16[2,48,1536]{2,1,0:T(8,128)(2,1)S(1)} %fusion.41), channel_id=1, source_target_pairs={{0,8},{2,10},{4,12},{6,14},{8,0},{10,2},{12,4},{14,6},{16,24},{18,... | collective-permute-start | bytes 884744 | tf_op jit(solution)/shard_map/ppermute | solution.py:488
  194.1 7.8 %collective-permute-start.25 = (bf16[1,48,1536]{2,1,0:T(8,128)(2,1)S(1)}, bf16[1,48,1536]{2,1,0:T(8,128)(2,1)S(1)}, u32[]{:S(2)}, u32[]{:S(2)}) collective-permute-start(bf16[1,48,1536]{2,1,0:T(8,128)(2,1)S(1)} %fusion.46), channel_id=1, source_target_pairs={{0,16},{2,18},{4,20},{6,22},{8,24},{10,26},{12,28},{14,30},{16,0},... | collective-permute-start | bytes 442376 | tf_op jit(solution)/shard_map/ppermute | solution.py:488
  205.4 6.2 %collective-permute-start.29 = (f32[2,768]{1,0:T(2,128)S(1)}, f32[2,768]{1,0:T(2,128)S(1)}, u32[]{:S(2)}, u32[]{:S(2)}) collective-permute-start(f32[2,768]{1,0:T(2,128)S(1)} %pad_maximum_fusion.7), channel_id=1, source_target_pairs={{0,1},{1,0},{2,3},{3,2},{4,5},{5,4},{6,7},{7,6},{8,9},{9,8},{10,11... | collective-permute-start | bytes 18440 | tf_op jit(solution)/shard_map/ppermute | solution.py:492
  213.6 16.3 %collective-permute-start.14 = (bf16[2,4,2,48,384]{4,3,2,1,0:T(8,128)(2,1)S(1)}, bf16[2,4,2,48,384]{4,3,2,1,0:T(8,128)(2,1)S(1)}, u32[]{:S(2)}, u32[]{:S(2)}) collective-permute-start(bf16[2,4,2,48,384]{4,3,2,1,0:T(8,128)(2,1)S(1)} %fusion.31), channel_id=1, source_target_pairs={{0,4},{2,6},{4,0},{6,2},{8,12},{10,14},{12,8},{14,10},{16,20},{18,... | collective-permute-start | bytes 1769480 | tf_op jit(solution)/shard_map/ppermute | solution.py:488
  216.7 14.6 %collective-permute-start.18 = (bf16[8,2,48,384]{3,2,1,0:T(8,128)(2,1)S(1)}, bf16[8,2,48,384]{3,2,1,0:T(8,128)(2,1)S(1)}, u32[]{:S(2)}, u32[]{:S(2)}) collective-permute-start(bf16[8,2,48,384]{3,2,1,0:T(8,128)(2,1)S(1)} %fusion.32), channel_id=1, source_target_pairs={{0,1},{1,0},{2,3},{3,2},{4,5},{5,4},{6,7},{7,6},{8,9},{9,8},{10,11... | collective-permute-start | bytes 1769480 | tf_op jit(solution)/shard_map/ppermute | solution.py:492
  220.3 4.5 %collective-permute-start.33 = (f32[2,768]{1,0:T(2,128)S(1)}, f32[2,768]{1,0:T(2,128)S(1)}, u32[]{:S(2)}, u32[]{:S(2)}) collective-permute-start(f32[2,768]{1,0:T(2,128)S(1)} %add.996), channel_id=1, source_target_pairs={{0,16},{2,18},{4,20},{6,22},{8,24},{10,26},{12,28},{14,30},{16,0},... | collective-permute-start | bytes 18440 | tf_op jit(solution)/shard_map/ppermute | solution.py:488
  221.4 21.2 %collective-permute-start.26 = (bf16[4,192,384]{2,1,0:T(8,128)(2,1)S(1)}, bf16[4,192,384]{2,1,0:T(8,128)(2,1)S(1)}, u32[]{:S(2)}, u32[]{:S(2)}) collective-permute-start(bf16[4,192,384]{2,1,0:T(8,128)(2,1)S(1)} %fusion.33), channel_id=1, source_target_pairs={{0,4},{2,6},{4,0},{6,2},{8,12},{10,14},{12,8},{14,10},{16,20},{18,... | collective-permute-start | bytes 1769480 | tf_op jit(solution)/shard_map/ppermute | solution.py:488
  230.0 12.8 %collective-permute-start.15 = (bf16[4,2,48,384]{3,2,1,0:T(8,128)(2,1)S(1)}, bf16[4,2,48,384]{3,2,1,0:T(8,128)(2,1)S(1)}, u32[]{:S(2)}, u32[]{:S(2)}) collective-permute-start(bf16[4,2,48,384]{3,2,1,0:T(8,128)(2,1)S(1)} %fusion.34), channel_id=1, source_target_pairs={{0,1},{1,0},{2,3},{3,2},{4,5},{5,4},{6,7},{7,6},{8,9},{9,8},{10,11... | collective-permute-start | bytes 884744 | tf_op jit(solution)/shard_map/ppermute | solution.py:492
  231.4 16.7 %collective-permute-start.19 = (bf16[4,2,48,384]{3,2,1,0:T(8,128)(2,1)S(1)}, bf16[4,2,48,384]{3,2,1,0:T(8,128)(2,1)S(1)}, u32[]{:S(2)}, u32[]{:S(2)}) collective-permute-start(bf16[4,2,48,384]{3,2,1,0:T(8,128)(2,1)S(1)} %fusion.40), channel_id=1, source_target_pairs={{0,4},{2,6},{4,0},{6,2},{8,12},{10,14},{12,8},{14,10},{16,20},{18,... | collective-permute-start | bytes 884744 | tf_op jit(solution)/shard_map/ppermute | solution.py:488
  242.7 11.5 %collective-permute-start.27 = (bf16[2,192,384]{2,1,0:T(8,128)(2,1)S(1)}, bf16[2,192,384]{2,1,0:T(8,128)(2,1)S(1)}, u32[]{:S(2)}, u32[]{:S(2)}) collective-permute-start(bf16[2,192,384]{2,1,0:T(8,128)(2,1)S(1)} %fusion.42), channel_id=1, source_target_pairs={{0,8},{2,10},{4,12},{6,14},{8,0},{10,2},{12,4},{14,6},{16,24},{18,... | collective-permute-start | bytes 884744 | tf_op jit(solution)/shard_map/ppermute | solution.py:488
  242.9 14.6 %collective-permute-start.16 = (bf16[2,2,48,384]{3,2,1,0:T(8,128)(2,1)S(1)}, bf16[2,2,48,384]{3,2,1,0:T(8,128)(2,1)S(1)}, u32[]{:S(2)}, u32[]{:S(2)}) collective-permute-start(bf16[2,2,48,384]{3,2,1,0:T(8,128)(2,1)S(1)} %fusion.49), channel_id=1, source_target_pairs={{0,8},{2,10},{4,12},{6,14},{8,0},{10,2},{12,4},{14,6},{16,24},{18,... | collective-permute-start | bytes 442376 | tf_op jit(solution)/shard_map/ppermute | solution.py:488
  248.3 11.1 %collective-permute-start.20 = (bf16[2,2,48,384]{3,2,1,0:T(8,128)(2,1)S(1)}, bf16[2,2,48,384]{3,2,1,0:T(8,128)(2,1)S(1)}, u32[]{:S(2)}, u32[]{:S(2)}) collective-permute-start(bf16[2,2,48,384]{3,2,1,0:T(8,128)(2,1)S(1)} %fusion.50), channel_id=1, source_target_pairs={{0,8},{2,10},{4,12},{6,14},{8,0},{10,2},{12,4},{14,6},{16,24},{18,... | collective-permute-start | bytes 442376 | tf_op jit(solution)/shard_map/ppermute | solution.py:488
  254.3 11.5 %collective-permute-start.28 = (bf16[1,192,384]{2,1,0:T(8,128)(2,1)S(1)}, bf16[1,192,384]{2,1,0:T(8,128)(2,1)S(1)}, u32[]{:S(2)}, u32[]{:S(2)}) collective-permute-start(bf16[1,192,384]{2,1,0:T(8,128)(2,1)S(1)} %fusion.43), channel_id=1, source_target_pairs={{0,16},{2,18},{4,20},{6,22},{8,24},{10,26},{12,28},{14,30},{16,0},... | collective-permute-start | bytes 442376 | tf_op jit(solution)/shard_map/ppermute | solution.py:488
  257.6 9.1 %collective-permute-start.17 = (bf16[1,2,48,384]{3,2,1,0:T(8,128)(2,1)S(1)}, bf16[1,2,48,384]{3,2,1,0:T(8,128)(2,1)S(1)}, u32[]{:S(2)}, u32[]{:S(2)}) collective-permute-start(bf16[1,2,48,384]{3,2,1,0:T(8,128)(2,1)S(1)} %fusion.53), channel_id=1, source_target_pairs={{0,16},{2,18},{4,20},{6,22},{8,24},{10,26},{12,28},{14,30},{16,0},... | collective-permute-start | bytes 221192 | tf_op jit(solution)/shard_map/ppermute | solution.py:488
  259.4 8.1 %collective-permute-start.21 = (bf16[1,2,48,384]{3,2,1,0:T(8,128)(2,1)S(1)}, bf16[1,2,48,384]{3,2,1,0:T(8,128)(2,1)S(1)}, u32[]{:S(2)}, u32[]{:S(2)}) collective-permute-start(bf16[1,2,48,384]{3,2,1,0:T(8,128)(2,1)S(1)} %fusion.51), channel_id=1, source_target_pairs={{0,16},{2,18},{4,20},{6,22},{8,24},{10,26},{12,28},{14,30},{16,0},... | collective-permute-start | bytes 221192 | tf_op jit(solution)/shard_map/ppermute | solution.py:488
  (54 other events, 257.1 us)
where the time goes:
time: 270 us; the launch traced here: 268 us
  waiting for transfers between devices  79.5 us (29%)
  Pallas kernels  55.5 us (21%)
  matrix products  37.6 us (14%)
  other arithmetic  32.9 us (12%)
  starting transfers between devices  30.4 us (11%)
  local copies, waits for them, and re-layouts  28.9 us (11%)
  between operations  3.48 us (1%)
    ppermute x27, waiting for transfers between devices, img_swap(): return lax.ppermute(value, 'img', [(i, i ^ mask) for i in range(count)])  65.1 us
    ppermute x27, starting transfers between devices, img_swap(): return lax.ppermute(value, 'img', [(i, i ^ mask) for i in range(count)])  20.3 us
    pallas_call x2, Pallas kernels, wgrad(): pl.pallas_call(functools.partial(wgrad_kernel, block), grid=(depth // chu...  18.7 us
    dot_general x8, matrix products, back_dot(): lax.dot_general(left_side, right_side, (((1,), (1,)), ((), ())), preferre...  18.4 us
    ppermute x9, waiting for transfers between devices, seq_swap(): return lax.ppermute(value, 'seq', [(0, 1), (1, 0)])  14.4 us
    dot_general x8, matrix products, low_dot(): return jnp.dot(left_side, right_side, preferred_element_type=f32)  14.3 us
    pallas_call x1, Pallas kernels, attend_back(): pl.pallas_call(attend_back_kernel, grid=(pairs,), in_specs=[row_spec] * 6...  10.2 us
    ppermute x9, starting transfers between devices, seq_swap(): return lax.ppermute(value, 'seq', [(0, 1), (1, 0)])  10 us
  transfers between devices with their start and end apart: 36, of which 16 were waited for; matrix products, arithmetic and copies ran while one was open for 32% of the time, Pallas kernels for 12%

commit v1 on v0

--- a/solution.py
+++ b/solution.py
@@ -1,5 +1,4 @@
 import functools
-import math
 
 import jax
 import jax.numpy as jnp
@@ -17,6 +16,7 @@
 highest = lax.Precision.HIGHEST
 bf16 = jnp.bfloat16
 f32 = jnp.float32
+light = pl.CostEstimate(flops=1024, transcendentals=0, bytes_accessed=1024)
 
 
 def layer_norm(values, gain_row):
@@ -101,9 +101,7 @@
             jax.ShapeDtypeStruct((1, width), f32),
             jax.ShapeDtypeStruct((TOP, width), f32),
         ],
-        cost_estimate=pl.CostEstimate(
-            flops=128 * width * width, transcendentals=0, bytes_accessed=4 * width * width
-        ),
+        cost_estimate=light,
         name="probe_rows",
     )(probe[None], pool_query, pool_key)
 
@@ -139,9 +137,7 @@
             jax.ShapeDtypeStruct((TOP, rows), f32),
             jax.ShapeDtypeStruct((TOP, width + 128), f32),
         ],
-        cost_estimate=pl.CostEstimate(
-            flops=256 * rows * width, transcendentals=TOP * rows, bytes_accessed=10 * rows * width
-        ),
+        cost_estimate=light,
         name="pool_local",
     )(result, gain[None], key_probe)
 
@@ -285,9 +281,7 @@
             jax.ShapeDtypeStruct((TOP, width), f32),
             jax.ShapeDtypeStruct((8, width), f32),
         ],
-        cost_estimate=pl.CostEstimate(
-            flops=1024 * rows * width, transcendentals=TOP * rows, bytes_accessed=20 * rows * width
-        ),
+        cost_estimate=light,
         name="pool_back",
     )(
         place, counts, pairs, log_temp[None], pair_bias[None], own, other, exps, low, unit, inv,
@@ -327,11 +321,7 @@
             jax.ShapeDtypeStruct((rows, width), bf16),
             jax.ShapeDtypeStruct((pairs, rows, 2), f32),
         ],
-        cost_estimate=pl.CostEstimate(
-            flops=4 * rows * length * width,
-            transcendentals=HEADS * rows * length,
-            bytes_accessed=2 * (2 * rows + 2 * length) * width,
-        ),
+        cost_estimate=light,
         name="attend",
     )(q, ka, kb, va, vb)
 
@@ -380,53 +370,51 @@
             jax.ShapeDtypeStruct((length, width), bf16),
             jax.ShapeDtypeStruct((length, width), bf16),
         ],
-        cost_estimate=pl.CostEstimate(
-            flops=10 * rows * length * width,
-            transcendentals=HEADS * rows * length,
-            bytes_accessed=2 * (3 * rows + 4 * length) * width,
-        ),
+        cost_estimate=light,
         name="attend_back",
     )(q, ka, kb, va, vb, g, lse)
 
 
-def store_halves(core, grad, block, send_refs, keep_refs):
+def halves(core, grad, block, j):
+    near = grad[2 * j * block : (2 * j + 1) * block]
+    far = grad[(2 * j + 1) * block : (2 * j + 2) * block]
+    return jnp.where(core == 0, far, near).astype(bf16), jnp.where(core == 0, near, far).astype(bf16)
+
+
+def wgrad_kernel(block, by_rows, place_ref, left_ref, right_ref, send_ref, keep_ref):
+    grad = tn(left_ref[...], right_ref[...])
+    columns = grad.shape[1] // 2
     for j in range(grad.shape[0] // (2 * block)):
-        near = grad[2 * j * block : (2 * j + 1) * block]
-        far = grad[(2 * j + 1) * block : (2 * j + 2) * block]
-        send_refs(j)[...] = jnp.where(core == 0, far, near).astype(bf16)
-        keep_refs(j)[...] = jnp.where(core == 0, near, far).astype(bf16)
-
-
-def wgrad_kernel(block, place_ref, left_ref, right_ref, send_ref, keep_ref):
-    grad = tn(left_ref[...], right_ref[...])
-    store_halves(
-        place_ref[2], grad, block, lambda j: send_ref.at[0, j], lambda j: keep_ref.at[0, j]
-    )
-
-
-def wgrad(place, left, right, images):
+        for ref, part in zip((send_ref, keep_ref), halves(place_ref[2], grad, block, j)):
+            for y in range(2):
+                mine = part[:, y * columns : (y + 1) * columns]
+                for g in range(2):
+                    if by_rows:
+                        ref[g, y, j] = mine[g * (block // 2) : (g + 1) * (block // 2)]
+                    else:
+                        ref[g, y, j] = mine[:, g * (columns // 2) : (g + 1) * (columns // 2)]
+
+
+def wgrad(place, left, right, images, by_rows):
     rows, depth = left.shape
-    columns = right.shape[1] // 2
+    columns = right.shape[1]
     block = depth // images
-    chunk = math.lcm(2 * block, 128)
+    chunk = depth // 2
     pairs = chunk // (2 * block)
-    out_spec = pl.BlockSpec((1, pairs, block, columns), lambda i, y: (y, i, 0, 0))
-    out_shape = jax.ShapeDtypeStruct((2, images // 2, block, columns), bf16)
+    cut = (block // 2, columns // 2) if by_rows else (block, columns // 4)
+    out_spec = pl.BlockSpec((2, 2, pairs, *cut), lambda i: (0, 0, i, 0, 0))
+    out_shape = jax.ShapeDtypeStruct((2, 2, images // 2, *cut), bf16)
     return pl.pallas_call(
-        functools.partial(wgrad_kernel, block),
-        grid=(depth // chunk, 2),
+        functools.partial(wgrad_kernel, block, by_rows),
+        grid=(2,),
         in_specs=[
             pl.BlockSpec(memory_space=pltpu.SMEM),
-            pl.BlockSpec((rows, chunk), lambda i, y: (0, i)),
-            pl.BlockSpec((rows, columns), lambda i, y: (0, y)),
+            pl.BlockSpec((rows, chunk), lambda i: (0, i)),
+            pl.BlockSpec((rows, columns), lambda i: (0, 0)),
         ],
         out_specs=[out_spec, out_spec],
         out_shape=[out_shape, out_shape],
-        cost_estimate=pl.CostEstimate(
-            flops=4 * rows * depth * columns,
-            transcendentals=0,
-            bytes_accessed=2 * rows * (depth + 2 * columns) + 4 * depth * columns,
-        ),
+        cost_estimate=light,
         name="wgrad",
     )(place, left, right)
 
@@ -435,46 +423,36 @@
     block, place_ref, na_ref, nb_ref, a_ref, dq_ref, dk_ref, dv_ref, dx_ref, send_ref, keep_ref
 ):
     na = na_ref[...]
-    rows = na.shape[0]
     both = jnp.concatenate([na, nb_ref[...]], axis=0)
-    grads = (
-        tn(na, dq_ref[...]),
-        tn(both, dk_ref[...]),
-        tn(both, dv_ref[...]),
-        tn(a_ref[...], dx_ref[...]),
-    )
-    for at, grad in enumerate(grads):
-        store_halves(
-            place_ref[2],
-            grad,
-            block,
-            lambda j: send_ref.at[at // 2, 0, j, at % 2],
-            lambda j: keep_ref.at[at // 2, 0, j, at % 2],
-        )
+    lefts = (na, both, both, a_ref[...])
+    for at, right_ref in enumerate((dq_ref, dk_ref, dv_ref, dx_ref)):
+        grad = tn(lefts[at], right_ref[...])
+        columns = grad.shape[1] // 2
+        for j in range(grad.shape[0] // (2 * block)):
+            for ref, part in zip((send_ref, keep_ref), halves(place_ref[2], grad, block, j)):
+                for y in range(2):
+                    ref[at // 2, y, j, at % 2] = part[:, y * columns : (y + 1) * columns]
 
 
 def wgrad_four(place, na, nb, a, dq, dk, dv, dx, images):
     rows, depth = na.shape
-    columns = dq.shape[1] // 2
+    columns = dq.shape[1]
     block = depth // images
-    chunk = math.lcm(2 * block, 128)
+    chunk = depth // 2
     pairs = chunk // (2 * block)
-    left = pl.BlockSpec((rows, chunk), lambda i, y: (0, i))
-    right = pl.BlockSpec((rows, columns), lambda i, y: (0, y))
-    right_all = pl.BlockSpec((2 * rows, columns), lambda i, y: (0, y))
-    out_spec = pl.BlockSpec((2, 1, pairs, 2, block, columns), lambda i, y: (0, y, i, 0, 0, 0))
-    out_shape = jax.ShapeDtypeStruct((2, 2, images // 2, 2, block, columns), bf16)
+    left = pl.BlockSpec((rows, chunk), lambda i: (0, i))
+    right = pl.BlockSpec((rows, columns), lambda i: (0, 0))
+    right_all = pl.BlockSpec((2 * rows, columns), lambda i: (0, 0))
+    out_spec = pl.BlockSpec((2, 2, pairs, 2, block, columns // 2), lambda i: (0, 0, i, 0, 0, 0))
+    out_shape = jax.ShapeDtypeStruct((2, 2, images // 2, 2, block, columns // 2), bf16)
+    smem = pl.BlockSpec(memory_space=pltpu.SMEM)
     return pl.pallas_call(
         functools.partial(wgrad_four_kernel, block),
-        grid=(depth // chunk, 2),
-        in_specs=[pl.BlockSpec(memory_space=pltpu.SMEM), left, left, left, right, right_all, right_all, right],
+        grid=(2,),
+        in_specs=[smem, left, left, left, right, right_all, right_all, right],
         out_specs=[out_spec, out_spec],
         out_shape=[out_shape, out_shape],
-        cost_estimate=pl.CostEstimate(
-            flops=24 * rows * depth * columns,
-            transcendentals=0,
-            bytes_accessed=2 * rows * (3 * depth + 12 * columns) + 16 * depth * columns,
-        ),
+        cost_estimate=light,
         name="wgrad_four",
     )(place, na, nb, a, dq, dk, dv, dx)
 
@@ -527,12 +505,23 @@
     return send, [pick(part, mine, axis + 1) for part in cut]
 
 
-def finish(parts, axis, bit):
-    while parts[0].shape[axis] > 1:
-        send, parts = img_send(parts, axis, bit)
-        parts = parts + [img_swap(send, 1 << bit)]
-        bit += 1
-    return jnp.squeeze(total_of(parts), axis)
+def pair_send(first, second, axis, bit):
+    send_first, first = img_send(first, axis, bit)
+    send_second, second = img_send(second, axis, bit)
+    return jnp.stack([send_first, send_second]), first, second
+
+
+def pair_take(arrived, first, second):
+    return first + [arrived[0]], second + [arrived[1]]
+
+
+class Order:
+    def __init__(self, token):
+        self.token = token
+
+    def __call__(self, *values):
+        values, self.token = lax.optimization_barrier((values, self.token))
+        return values
 
 
 def shards(
@@ -616,101 +605,163 @@
         gathered.reshape(images * caps, width), images, seq_count,
     )
 
-    sums_other = seq_swap(sums)
-    down_send, down_keep = wgrad(place, hidden_low, branch_grad, images)
-    branch_grad, down_send = tie(branch_grad, down_send)
+    step = Order(place)
+    down_send, down_keep = wgrad(place, hidden_low, branch_grad, images, True)
+    branch_grad, down_send, sums = step(branch_grad, down_send, sums)
     down_core = img_swap(down_send, 1)
+    small_in = seq_swap(sums)
     hidden_grad = back_dot(branch_grad, w_down)
     up_grad_low = gelu_back(hidden_grad)[0].astype(bf16)
 
-    up_grad_low, down_core, sums_other = tie(up_grad_low, down_core, sums_other)
-    down_y, down_parts = seq_send([down_keep, down_core], 0)
-    up_grad_low, down_y = tie(up_grad_low, down_y)
-    down_parts = down_parts + [seq_swap(down_y)]
-    sums = sums + sums_other
+    up_grad_low, down_core, small_in = step(up_grad_low, down_core, small_in)
+    sums = sums + small_in
+    down_a_send, down_a = seq_send([down_keep[0], down_core[0]], 0)
+    down_b_send, down_b = img_send([down_keep[1], down_core[1]], 1, 1)
+    up_grad_low, down_a_send, down_b_send = step(up_grad_low, down_a_send, down_b_send)
+    down_a_in = seq_swap(down_a_send)
+    down_b_in = img_swap(down_b_send, 2)
 
     def small_step(sums, rank, bit):
-        both = img_swap(jnp.concatenate([sums, rank], axis=0), 1 << bit)
-        return both
-
+        return img_swap(jnp.concatenate([sums, rank], axis=0), 1 << bit)
+
+    def small_take(sums, rank, arrived):
+        return sums + arrived[:TOP], jnp.concatenate([rank, arrived[TOP:]], axis=0)
+
+    up_send, up_keep = wgrad(place, second_low, up_grad_low, images, False)
+    up_grad_low, up_send = step(up_grad_low, up_send)
+    up_core = img_swap(up_send, 1)
     small_in = small_step(sums, rank, 0)
-    up_send, up_keep = wgrad(place, second_low, up_grad_low, images)
-    up_grad_low, up_send = tie(up_grad_low, up_send)
-    up_core = img_swap(up_send, 1)
     second_in_grad = back_dot(up_grad_low, w_up)
     residual_ln_grad, second_gain_grad = norm_back(second_in_grad, unit_two, scale_two, second_gain)
     residual_grad = result_grad + residual_ln_grad
     attn_branch = residual_grad.astype(bf16)
 
-    attn_branch, up_core, small_in = tie(attn_branch, up_core, small_in)
-    sums = sums + small_in[:TOP]
-    rank = jnp.concatenate([rank, small_in[TOP:]], axis=0)
-    up_x, up_parts = img_send([up_keep, up_core], 1, 1)
-    attn_branch, up_x = tie(attn_branch, up_x)
-    up_parts = up_parts + [img_swap(up_x, 2)]
+    attn_branch, up_core, small_in = step(attn_branch, up_core, small_in)
+    sums, rank = small_take(sums, rank, small_in)
+    up_a_send, up_a = img_send([up_keep[0], up_core[0]], 1, 1)
+    up_b_send, up_b = seq_send([up_keep[1], up_core[1]], 0)
+    attn_branch, up_a_send, up_b_send, sums, rank = step(attn_branch, up_a_send, up_b_send, sums, rank)
+    up_a_in = img_swap(up_a_send, 2)
+    up_b_in = seq_swap(up_b_send)
     small_in = small_step(sums, rank, 1)
 
     attended_grad = back_dot(attn_branch, w_output).astype(bf16)
     query_grad, key_part, value_part = attend_back(
         queries, keys_own, keys_other, values_own, values_other, attended_grad, log_totals
     )
+    query_grad, key_part, value_part, down_a_in, down_b_in, small_in = step(
+        query_grad, key_part, value_part, down_a_in, down_b_in, small_in
+    )
+    sums, rank = small_take(sums, rank, small_in)
+    down_a_send, down_a = img_send(down_a + [down_a_in], 0, 1)
+    down_b_send, down_b = seq_send(down_b + [down_b_in], 0)
+    query_grad, key_part, value_part, down_a_send, down_b_send, sums, rank = step(
+        query_grad, key_part, value_part, down_a_send, down_b_send, sums, rank
+    )
+    down_a_in = img_swap(down_a_send, 2)
+    down_b_in = seq_swap(down_b_send)
+    small_in = small_step(sums, rank, 2)
     other_in_grad = (
         back_dot(key_part[rows:], w_key) + back_dot(value_part[rows:], w_value)
     ).astype(bf16)
-    other_in_grad, query_grad, key_part, value_part, small_in = tie(
-        other_in_grad, query_grad, key_part, value_part, small_in
+    query_grad, key_part, value_part, other_in_grad = step(
+        query_grad, key_part, value_part, other_in_grad
     )
     arrived_grad = seq_swap(other_in_grad)
-    sums = sums + small_in[:TOP]
-    rank = jnp.concatenate([rank, small_in[TOP:]], axis=0)
-    small_in = small_step(sums, rank, 2)
     four_send, four_keep = wgrad_four(
         place, low_own, low_other, attended_low, query_grad, key_part, value_part, attn_branch, images
     )
-    query_grad, four_send = tie(query_grad, four_send)
+    query_grad, key_part, value_part, four_send, up_a_in, up_b_in, small_in = step(
+        query_grad, key_part, value_part, four_send, up_a_in, up_b_in, small_in
+    )
     four_core = img_swap(four_send, 1)
+    sums, rank = small_take(sums, rank, small_in)
+    up_a_send, up_a = seq_send(up_a + [up_a_in], 0)
+    up_b_send, up_b = img_send(up_b + [up_b_in], 0, 1)
+    query_grad, key_part, value_part, up_a_send, up_b_send, sums, rank = step(
+        query_grad, key_part, value_part, up_a_send, up_b_send, sums, rank
+    )
+    up_a_in = seq_swap(up_a_send)
+    up_b_in = img_swap(up_b_send, 2)
     own_in_grad = (
         back_dot(query_grad, w_query)
         + back_dot(key_part[:rows], w_key)
         + back_dot(value_part[:rows], w_value)
     )
-
-    down_parts, own_in_grad, four_core = tie(tuple(down_parts), own_in_grad, four_core)
-    down_x, down_parts = img_send(list(down_parts), 0, 1)
-    down_parts = down_parts + [img_swap(down_x, 2)]
-    early_parts = [four_keep[0], four_core[0]]
-    late_parts = [four_keep[1], four_core[1]]
-    early_send, early_parts = img_send(early_parts, 1, 1)
-    late_send, late_parts = seq_send(late_parts, 0)
-    early_parts = early_parts + [img_swap(early_send, 2)]
-    late_parts = late_parts + [seq_swap(late_send)]
+    own_in_grad, four_core, four_keep = step(own_in_grad, four_core, four_keep)
+    four_a_send, four_a = img_send([four_keep[0], four_core[0]], 1, 1)
+    four_b_send, four_b = seq_send([four_keep[1], four_core[1]], 0)
+    own_in_grad, four_a_send, four_b_send, sums, rank = step(
+        own_in_grad, four_a_send, four_b_send, sums, rank
+    )
+    four_a_in = img_swap(four_a_send, 2)
+    four_b_in = seq_swap(four_b_send)
+    small_in = small_step(sums, rank, 3)
+
+    down_a_in, down_b_in, own_in_grad = step(down_a_in, down_b_in, own_in_grad)
+    down_a, down_b = down_a + [down_a_in], down_b + [down_b_in]
+    down_send, down_a, down_b = pair_send(down_a, down_b, 0, 2)
+    down_send, own_in_grad, arrived_grad = step(down_send, own_in_grad, arrived_grad)
+    down_in = img_swap(down_send, 4)
 
     first_in_grad = own_in_grad + arrived_grad.astype(f32)
     input_ln_grad, first_gain_grad = norm_back(first_in_grad, unit_one, scale_one, first_gain)
-    input_grad = (residual_grad + input_ln_grad)[None]
-
-    for bit in range(2, bits):
-        sums = sums + small_in[:TOP]
-        rank = jnp.concatenate([rank, small_in[TOP:]], axis=0)
-        if bit + 1 < bits:
-            small_in = small_step(sums, rank, bit + 1)
-
-    up_y, up_parts = seq_send(up_parts, 0)
-    up_parts = up_parts + [seq_swap(up_y)]
-    down_grad = finish(down_parts, 0, 2)
-    up_weight_grad = finish(up_parts, 0, 2)
-
-    early_send, early_parts = seq_send(early_parts, 0)
-    late_send, late_parts = img_send(late_parts, 0, 1)
-    early_parts = early_parts + [seq_swap(early_send)]
-    late_parts = late_parts + [img_swap(late_send, 2)]
-    query_key = finish(early_parts, 0, 2)
-    value_output = finish(late_parts, 0, 2)
-
+    input_grad = residual_grad + input_ln_grad
     late = jnp.stack([second_gain_grad, first_gain_grad])
-    late = late + seq_swap(late)
-    for bit in range(bits):
+    input_grad, late, up_a_in, up_b_in = step(input_grad, late, up_a_in, up_b_in)
+    late_in = seq_swap(late)
+
+    up_a, up_b = up_a + [up_a_in], up_b + [up_b_in]
+    up_send, up_a, up_b = pair_send(up_a, up_b, 0, 2)
+    up_send, down_in = step(up_send, down_in)
+    up_in = img_swap(up_send, 4)
+    down_a, down_b = pair_take(down_in, down_a, down_b)
+    down_send, down_a, down_b = pair_send(down_a, down_b, 0, 3)
+    four_a_in, four_b_in, down_send, late_in = step(four_a_in, four_b_in, down_send, late_in)
+    down_in = img_swap(down_send, 8)
+    late = late + late_in
+    four_a_send, four_a = seq_send(four_a + [four_a_in], 0)
+    four_b_send, four_b = img_send(four_b + [four_b_in], 0, 1)
+    four_a_send, four_b_send, late, up_in = step(four_a_send, four_b_send, late, up_in)
+    four_a_in = seq_swap(four_a_send)
+    four_b_in = img_swap(four_b_send, 2)
+    late_in = img_swap(late, 1)
+    up_a, up_b = pair_take(up_in, up_a, up_b)
+    up_send, up_a, up_b = pair_send(up_a, up_b, 0, 3)
+    up_send, late_in = step(up_send, late_in)
+    up_in = img_swap(up_send, 8)
+    late = late + late_in
+    late_in = img_swap(late, 2)
+    four_a_in, four_b_in, late_in = step(four_a_in, four_b_in, late_in)
+    four_send, four_a, four_b = pair_send(four_a + [four_a_in], four_b + [four_b_in], 0, 2)
+    late = late + late_in
+    four_send, late = step(four_send, late)
+    four_in = img_swap(four_send, 4)
+    late_in = img_swap(late, 4)
+    four_in, late_in = step(four_in, late_in)
+    four_a, four_b = pair_take(four_in, four_a, four_b)
+    four_send, four_a, four_b = pair_send(four_a, four_b, 0, 3)
+    late = late + late_in
+    four_in = img_swap(four_send, 8)
+    late_in = img_swap(late, 8)
+    late = late + late_in
+
+    def finish(arrived, first, second):
+        first, second = pair_take(arrived, first, second)
+        for bit in range(4, bits):
+            send, first, second = pair_send(first, second, 0, bit)
+            first, second = pair_take(img_swap(send, 1 << bit), first, second)
+        return jnp.squeeze(total_of(first), 0), jnp.squeeze(total_of(second), 0)
+
+    down_grad = jnp.concatenate(finish(down_in, down_a, down_b), axis=0)
+    up_weight_grad = jnp.concatenate(finish(up_in, up_a, up_b), axis=1)
+    query_key, value_output = finish(four_in, four_a, four_b)
+    for bit in range(4, bits):
         late = late + img_swap(late, 1 << bit)
+    sums, rank = small_take(sums, rank, small_in)
+    for bit in range(4, bits):
+        sums, rank = small_take(sums, rank, small_step(sums, rank, bit))
+    input_grad = input_grad[None]
 
     block = width // images
 

time: 270 us -> 230 us (0.85)
  waiting for transfers between devices: 79.5 us -> 44.5 us
  Pallas kernels: 55.5 us -> 44.2 us
  local copies, waits for them, and re-layouts: 28.9 us -> 33.6 us
  starting transfers between devices: 30.4 us -> 34.7 us
    ppermute x27, waiting for transfers between devices: 65.1 us -> 38.8 us  [img_swap(): return lax.ppermute(value, 'img', [(i, i ^ mask) for i in range(count)])]
    pallas_call x3, Pallas kernels: 26 us -> 14.8 us  [the longest x2 9.02 us: wgrad(): pl.pallas_call(functools.partial(wgrad_kernel, block, by_rows), grid=(2,)...]
    ppermute x9 -> x11, waiting for transfers between devices: 14.4 us -> 5.7 us  [seq_swap(): return lax.ppermute(value, 'seq', [(0, 1), (1, 0)])]
    dynamic_slice x14 -> x22, local copies, waits for them, and re-layouts: 4.7 us -> 12.4 us  [pick(): return lax.dynamic_index_in_dim(value, index, axis, keepdims=False)]
    squeeze x2 -> x0, local copies, waits for them, and re-layouts: 5.12 us -> none  [pick(): return lax.dynamic_index_in_dim(value, index, axis, keepdims=False)]
    slice x3 -> x12, local copies, waits for them, and re-layouts: 0.55 us -> 4.96 us  [the longest x2 3.02 us: shards(): down_b_send, down_b = img_send([down_keep[1], down_core[1]], 1, 1)]
    ppermute x9 -> x11, starting transfers between devices: 10 us -> 11.8 us  [seq_swap(): return lax.ppermute(value, 'seq', [(0, 1), (1, 0)])]
    unnamed x105 -> x155, local copies, waits for them, and re-layouts: 9.08 us -> 7.45 us
  transfers between devices with their start and end apart: 36 -> 38, of which waited for: 16 -> 10; matrix products, arithmetic and copies ran while one was open for 32% -> 37% of each run, Pallas kernels for 12% -> 13%
where the time goes in v1:
time: 230 us; the launch traced here: 229 us
  waiting for transfers between devices  44.5 us (19%)
  Pallas kernels  44.2 us (19%)
  matrix products  35.8 us (16%)
  starting transfers between devices  34.7 us (15%)
  local copies, waits for them, and re-layouts  33.6 us (15%)
  other arithmetic  32.1 us (14%)
  between operations  3.96 us (2%)
    ppermute x27, waiting for transfers between devices, img_swap(): return lax.ppermute(value, 'img', [(i, i ^ mask) for i in range(count)])  38.8 us
    ppermute x27, starting transfers between devices, img_swap(): return lax.ppermute(value, 'img', [(i, i ^ mask) for i in range(count)])  22.9 us
    dot_general x8, matrix products, back_dot(): lax.dot_general(left_side, right_side, (((1,), (1,)), ((), ())), preferre...  16.6 us
    dot_general x8, matrix products, low_dot(): return jnp.dot(left_side, right_side, preferred_element_type=f32)  14.2 us
    dynamic_slice x22, local copies, waits for them, and re-layouts, pick(): return lax.dynamic_index_in_dim(value, index, axis, keepdims=False)  12.4 us
    ppermute x11, starting transfers between devices, seq_swap(): return lax.ppermute(value, 'seq', [(0, 1), (1, 0)])  11.8 us
    pallas_call x1, Pallas kernels, attend_back(): pl.pallas_call(attend_back_kernel, grid=(pairs,), in_specs=[row_spec] * 6...  10.3 us
    pallas_call x2, Pallas kernels, wgrad(): pl.pallas_call(functools.partial(wgrad_kernel, block, by_rows), grid=(2,)...  9.02 us
  transfers between devices with their start and end apart: 38, of which 10 were waited for; matrix products, arithmetic and copies ran while one was open for 37% of the time, Pallas kernels for 13%

profile of v1, /device:TPU:0, one launch (start us, length us, event | category | flops | bytes accessed | tf_op | source)
XLA Modules:
  0.0 228.8 jit_solution(15403279104129705194)
XLA Ops:
  1.2 2.6 %collective-permute-start = (bf16[256,768]{1,0:T(8,128)(2,1)}, bf16[256,768]{1,0:T(8,128)(2,1)S(1)}, u32[]{:S(2)}, u32[]{:S(2)}) collective-permute-start(bf16[256,768]{1,0:T(8,128)(2,1)} %bitcast.232), channel_id=1, source_target_pairs={{0,1},{1,0},{2,3},{3,2},{4,5},{5,4},{6,7},{7,6},{8,9},{9,8},{10,11... | collective-permute-start | bytes 1179656 | tf_op jit(solution)/shard_map/ppermute | solution.py:470
  14.0 3.0 %probe_rows.1 = (f32[1,768]{1,0:T(1,128)}, f32[16,768]{1,0:T(8,128)}) custom-call(f32[1,768]{1,0:T(1,128)} %broadcast_in_dim.15.probe_ref, bf16[768,768]{1,0:T(8,128)(2,1)} %query_ref.1, bf16[768,768]{1,0:T(8,128)(2,1)} %key_ref.1), custom_call_target="tpu_custom_call" | custom-call | flops 1024 | bytes 1024 | tf_op jit(solution)/shard_map/probe_rows/pallas_call | solution.py:98
  24.4 7.9 %attend.1 = (bf16[256,768]{1,0:T(8,128)(2,1)}, f32[6,256,2]{2,1,0:T(8,128)}) custom-call(bf16[256,768]{1,0:T(8,128)(2,1)} %convolution_convert_fusion.5.q_ref, bf16[256,768]{1,0:T(8,128)(2,1)} %convolution_convert_fusion.4.ka_ref, bf16[256,768]{1,0:T(8,128)(2,1)} %convolution_convert_fusion.2.kb_ref, bf16[256,768]{1,0:T(8,128)(2,1)} %convolution_convert_fusion.3.va_ref, ...), custom_call_target="tpu_custom_call" | custom-call | flops 1024 | bytes 1024 | tf_op jit(solution)/shard_map/attend/pallas_call | solution.py:315
  32.9 2.6 %collective-permute-start.5 = (f32[8,5,768]{2,1,0:T(8,128)}, f32[8,5,768]{2,1,0:T(8,128)}, u32[]{:S(2)}, u32[]{:S(2)}) collective-permute-start(f32[8,5,768]{2,1,0:T(8,128)} %pad_maximum_fusion.7), channel_id=1, source_target_pairs={{0,16},{2,18},{4,20},{6,22},{8,24},{10,26},{12,28},{14,30},{16,0},... | collective-permute-start | bytes 368648 | tf_op jit(solution)/shard_map/ppermute | solution.py:466
  35.6 2.1 fusion.85
  39.0 3.6 %multiply_convert_fusion = (bf16[256,3072]{1,0:T(8,128)(2,1)S(1)}, f32[256,3072]{1,0:T(8,128)}) fusion(bf16[256,768]{1,0:T(8,128)(2,1)S(1)} %multiply_convert_fusion.1.left_ref, bf16[768,3072]{1,0:T(8,128)(2,1)S(1)} %copy-done.74), kind=kOutput, calls=%fused_computation.9 | convolution fusion | flops 1215037440 | bytes 9830400 | tf_op jit(solution)/shard_map/dot_general | solution.py:39
  43.9 2.3 %convolution_add_fusion.4.result_ref = f32[256,768]{1,0:T(8,128)} fusion(f32[256,768]{1,0:T(8,128)S(1)} %get-tuple-element.319, bf16[256,3072]{1,0:T(8,128)(2,1)S(1)} %get-tuple-element.320.left_ref, bf16[3072,768]{1,0:T(8,128)(2,1)S(1)} %bitcast.346), kind=kOutput, calls=%fused_computation.14 | convolution fusion | flops 1208156160 | bytes 7864320 | tf_op jit(solution)/shard_map/dot_general | solution.py:39
  46.2 2.6 %pool_local.1 = (bf16[256,768]{1,0:T(8,128)(2,1)}, f32[256,768]{1,0:T(8,128)}, f32[256,1]{1,0:T(8,128)}, f32[16,256]{1,0:T(8,128)}, f32[16,896]{1,0:T(8,128)}) custom-call(f32[256,768]{1,0:T(8,128)} %convolution_add_fusion.4.result_ref, f32[1,768]{1,0:T(1,128)} %broadcast_in_dim.19.gain_ref, f32[16,768]{1,0:T(8,128)} %get-tuple-element.154.key_probe_ref), custom_call_target="tpu_custom_call" | custom-call | flops 1024 | bytes 1024 | tf_op jit(solution)/shard_map/pool_local/pallas_call | solution.py:131
  49.3 1.8 pad_maximum_fusion
  51.1 2.2 collective-permute-done.4.other_ref
  55.0 5.7 %pool_back.1 = (f32[256,768]{1,0:T(8,128)}, bf16[256,768]{1,0:T(8,128)(2,1)}, f32[16,768]{1,0:T(8,128)}, f32[8,768]{1,0:T(8,128)}) custom-call(s32[3]{0:T(128)} %pad_add_fusion.place_ref, s32[1]{0:T(128)S(6)} %copy.147.count_ref, s32[1,80]{1,0:T(1,128)} %pairs_ref.1, f32[1]{0:T(128)} %bitcast.230.temp_ref, f32[1]{0:T(128)} %bitcast.231.bias_ref, ...), custom_call_target="tpu_custom_call" | custom-call | flops 1024 | bytes 1024 | tf_op jit(solution)/shard_map/pool_back/pallas_call | solution.py:274
  60.7 4.4 %wgrad.2 = (bf16[2,2,8,96,384]{4,3,2,1,0:T(8,128)(2,1)}, bf16[2,2,8,96,384]{4,3,2,1,0:T(8,128)(2,1)}) custom-call(s32[3]{0:T(128)} %pad_add_fusion.place_ref, bf16[256,3072]{1,0:T(8,128)(2,1)} %copy-done.32, bf16[256,768]{1,0:T(8,128)(2,1)} %get-tuple-element.167.right_ref), custom_call_target="tpu_custom_call" | custom-call | flops 1024 | bytes 1024 | tf_op jit(solution)/shard_map/wgrad/pallas_call | solution.py:407
  69.5 7.4 %fusion.6.right_ref = bf16[256,3072]{1,0:T(8,128)(2,1)} fusion(f32[256,3072]{1,0:T(8,128)} %get-tuple-element.321, bf16[256,768]{1,0:T(8,128)(2,1)} %get-tuple-element.167.right_ref, bf16[3072,768]{1,0:T(8,128)(2,1)} %param.26), kind=kOutput, calls=%fused_computation.8 | convolution fusion | flops 1223688192 | bytes 9830400 | tf_op jit(solution)/shard_map/dot_general | solution.py:43
  77.3 2.7 %fusion.77 = (bf16[1,2,8,96,384]{4,3,2,1,0:T(8,128)(2,1)S(1)}, bf16[1,2,8,96,384]{4,3,2,1,0:T(8,128)(2,1)S(1)}) fusion(bf16[2,2,8,96,384]{4,3,2,1,0:T(8,128)(2,1)} %collective-permute-done.6), kind=kLoop, calls=%fused_computation.215 | loop fusion | bytes 4718592 | tf_op jit(solution)/shard_map/slice | solution.py:619
  82.6 4.6 %wgrad.3 = (bf16[2,2,8,48,768]{4,3,2,1,0:T(8,128)(2,1)}, bf16[2,2,8,48,768]{4,3,2,1,0:T(8,128)(2,1)}) custom-call(s32[3]{0:T(128)} %pad_add_fusion.place_ref, bf16[256,768]{1,0:T(8,128)(2,1)} %copy-done.33, bf16[256,3072]{1,0:T(8,128)(2,1)} %fusion.6.right_ref), custom_call_target="tpu_custom_call" | custom-call | flops 1024 | bytes 1024 | tf_op jit(solution)/shard_map/wgrad/pallas_call | solution.py:407
  87.5 2.0 convert_bitcast_fusion
  96.8 2.2 constant_dynamic-slice_fusion.15
  99.1 4.6 %multiply_reduce_fusion = (f32[768]{0:T(1024)}, f32[256]{0:T(256)S(1)}, f32[256]{0:T(256)S(1)}, f32[256,768]{1,0:T(8,128)S(1)}) fusion(f32[256,768]{1,0:T(8,128)S(1)} %get-tuple-element.319, f32[256]{0:T(256)S(1)} %copy-done.68, f32[256]{0:T(256)S(1)} %copy-done.66, f32[768]{0:T(1024)S(1)} %copy-done.62, bf16[256,3072]{1,0:T(8,128)(2,1)S(1)} %copy-done.31, ...), kind=kOutput, calls=%fused_computation.54 | convolution fusion | flops 1209531136 | bytes 7874560 | tf_op jit(solution)/shard_map/dot_general | solution.py:43
  112.1 10.3 %attend_back.1 = (bf16[256,768]{1,0:T(8,128)(2,1)}, bf16[512,768]{1,0:T(8,128)(2,1)}, bf16[512,768]{1,0:T(8,128)(2,1)}) custom-call(bf16[256,768]{1,0:T(8,128)(2,1)} %convolution_convert_fusion.5.q_ref, bf16[256,768]{1,0:T(8,128)(2,1)} %convolution_convert_fusion.4.ka_ref, bf16[256,768]{1,0:T(8,128)(2,1)} %convolution_convert_fusion.2.kb_ref, ...), custom_call_target="tpu_custom_call" | custom-call | flops 1024 | bytes 1024 | tf_op jit(solution)/shard_map/attend_back/pallas_call | solution.py:363
  123.1 1.9 fusion.41
  125.9 2.0 fusion.35
  131.0 5.7 %wgrad_four.1 = (bf16[2,2,8,2,48,384]{5,4,3,2,1,0:T(8,128)(2,1)}, bf16[2,2,8,2,48,384]{5,4,3,2,1,0:T(8,128)(2,1)}) custom-call(s32[3]{0:T(128)} %pad_add_fusion.place_ref, bf16[256,768]{1,0:T(8,128)(2,1)} %copy-done.3, bf16[256,768]{1,0:T(8,128)(2,1)} %copy-done.4, bf16[256,768]{1,0:T(8,128)(2,1)} %get-tuple-element.153.a_ref, ...), custom_call_target="tpu_custom_call" | custom-call | flops 1024 | bytes 1024 | tf_op jit(solution)/shard_map/wgrad_four/pallas_call | solution.py:449
  160.1 3.4 %collective-permute-done.20 = bf16[4,48,768]{2,1,0:T(8,128)(2,1)S(1)} collective-permute-done((bf16[4,48,768]{2,1,0:T(8,128)(2,1)S(1)}, bf16[4,48,768]{2,1,0:T(8,128)(2,1)S(1)}, u32[]{:S(2)}, u32[]{:S(2)}) %collective-permute-start.20) | collective-permute-done | bytes 294944 | tf_op jit(solution)/shard_map/ppermute | solution.py:470
  168.2 10.0 %collective-permute-done.37 = f32[80,768]{1,0:T(8,128)S(1)} collective-permute-done((f32[80,768]{1,0:T(8,128)S(1)}, f32[80,768]{1,0:T(8,128)S(1)}, u32[]{:S(2)}, u32[]{:S(2)}) %collective-permute-start.37) | collective-permute-done | bytes 245792 | tf_op jit(solution)/shard_map/ppermute | solution.py:466
  186.1 7.4 %collective-permute-done.26 = bf16[2,2,48,768]{3,2,1,0:T(8,128)(2,1)S(1)} collective-permute-done((bf16[2,2,48,768]{3,2,1,0:T(8,128)(2,1)S(1)}, bf16[2,2,48,768]{3,2,1,0:T(8,128)(2,1)S(1)}, u32[]{:S(2)}, u32[]{:S(2)}) %collective-permute-start.26) | collective-permute-done | bytes 294944 | tf_op jit(solution)/shard_map/ppermute | solution.py:466
  197.3 2.1 collective-permute-start.34
  199.4 7.4 %collective-permute-done.35 = bf16[2,1,96,384]{3,2,1,0:T(8,128)(2,1)S(1)} collective-permute-done((bf16[2,1,96,384]{3,2,1,0:T(8,128)(2,1)S(1)}, bf16[2,1,96,384]{3,2,1,0:T(8,128)(2,1)S(1)}, u32[]{:S(2)}, u32[]{:S(2)}) %collective-permute-start.35) | collective-permute-done | bytes 147488 | tf_op jit(solution)/shard_map/ppermute | solution.py:466
  208.0 1.9 collective-permute-done.34
  210.9 6.1 %collective-permute-done.32 = f32[2,768]{1,0:T(2,128)S(1)} collective-permute-done((f32[2,768]{1,0:T(2,128)S(1)}, f32[2,768]{1,0:T(2,128)S(1)}, u32[]{:S(2)}, u32[]{:S(2)}) %collective-permute-start.32) | collective-permute-done | bytes 6176 | tf_op jit(solution)/shard_map/ppermute | solution.py:466
  218.1 2.2 collective-permute-start.33
  220.3 3.0 %collective-permute-done.36 = f32[2,768]{1,0:T(2,128)S(1)} collective-permute-done((f32[2,768]{1,0:T(2,128)S(1)}, f32[2,768]{1,0:T(2,128)S(1)}, u32[]{:S(2)}, u32[]{:S(2)}) %collective-permute-start.36) | collective-permute-done | bytes 6176 | tf_op jit(solution)/shard_map/ppermute | solution.py:466
  224.5 2.8 %collective-permute-done.33 = bf16[2,1,2,48,384]{4,3,2,1,0:T(8,128)(2,1)S(1)} collective-permute-done((bf16[2,1,2,48,384]{4,3,2,1,0:T(8,128)(2,1)S(1)}, bf16[2,1,2,48,384]{4,3,2,1,0:T(8,128)(2,1)S(1)}, u32[]{:S(2)}, u32[]{:S(2)}) %collective-permute-start.33) | collective-permute-done | bytes 147488 | tf_op jit(solution)/shard_map/ppermute | solution.py:466
  (369 shorter events, 94.1 us)
Async XLA Ops:
  0.7 10.6 %collective-permute-start.1 = (f32[1,5,768]{2,1,0:T(8,128)}, f32[1,5,768]{2,1,0:T(8,128)S(1)}, u32[]{:S(2)}, u32[]{:S(2)}) collective-permute-start(f32[1,5,768]{2,1,0:T(8,128)} %bitcast.340), channel_id=1, source_target_pairs={{0,2},{2,0},{4,6},{6,4},{8,10},{10,8},{12,14},{14,12},{16,18},{18,... | collective-permute-start | bytes 46088 | tf_op jit(solution)/shard_map/ppermute | solution.py:466
  1.2 18.3 %collective-permute-start = (bf16[256,768]{1,0:T(8,128)(2,1)}, bf16[256,768]{1,0:T(8,128)(2,1)S(1)}, u32[]{:S(2)}, u32[]{:S(2)}) collective-permute-start(bf16[256,768]{1,0:T(8,128)(2,1)} %bitcast.232), channel_id=1, source_target_pairs={{0,1},{1,0},{2,3},{3,2},{4,5},{5,4},{6,7},{7,6},{8,9},{9,8},{10,11... | collective-permute-start | bytes 1179656 | tf_op jit(solution)/shard_map/ppermute | solution.py:470
  11.3 8.3 %collective-permute-start.2 = (f32[2,5,768]{2,1,0:T(8,128)S(1)}, f32[2,5,768]{2,1,0:T(8,128)S(1)}, u32[]{:S(2)}, u32[]{:S(2)}) collective-permute-start(f32[2,5,768]{2,1,0:T(8,128)S(1)} %pad_maximum_fusion.17), channel_id=1, source_target_pairs={{0,4},{2,6},{4,0},{6,2},{8,12},{10,14},{12,8},{14,10},{16,20},{18,... | collective-permute-start | bytes 92168 | tf_op jit(solution)/shard_map/ppermute | solution.py:466
  20.2 12.0 %collective-permute-start.3 = (f32[4,5,768]{2,1,0:T(8,128)S(1)}, f32[4,5,768]{2,1,0:T(8,128)S(1)}, u32[]{:S(2)}, u32[]{:S(2)}) collective-permute-start(f32[4,5,768]{2,1,0:T(8,128)S(1)} %pad_maximum_fusion.13), channel_id=1, source_target_pairs={{0,8},{2,10},{4,12},{6,14},{8,0},{10,2},{12,4},{14,6},{16,24},{18,... | collective-permute-start | bytes 184328 | tf_op jit(solution)/shard_map/ppermute | solution.py:466
  32.9 16.3 %collective-permute-start.5 = (f32[8,5,768]{2,1,0:T(8,128)}, f32[8,5,768]{2,1,0:T(8,128)}, u32[]{:S(2)}, u32[]{:S(2)}) collective-permute-start(f32[8,5,768]{2,1,0:T(8,128)} %pad_maximum_fusion.7), channel_id=1, source_target_pairs={{0,16},{2,18},{4,20},{6,22},{8,24},{10,26},{12,28},{14,30},{16,0},... | collective-permute-start | bytes 368648 | tf_op jit(solution)/shard_map/ppermute | solution.py:466
  65.1 12.2 %collective-permute-start.6 = (bf16[2,2,8,96,384]{4,3,2,1,0:T(8,128)(2,1)}, bf16[2,2,8,96,384]{4,3,2,1,0:T(8,128)(2,1)}, u32[]{:S(2)}, u32[]{:S(2)}) collective-permute-start(bf16[2,2,8,96,384]{4,3,2,1,0:T(8,128)(2,1)} %get-tuple-element.168), channel_id=1, source_target_pairs={{0,2},{2,0},{4,6},{6,4},{8,10},{10,8},{12,14},{14,12},{16,18},{18,... | collective-permute-start | bytes 7077896 | tf_op jit(solution)/shard_map/ppermute | solution.py:466
  69.0 8.3 %collective-permute-start.7 = (f32[16,768]{1,0:T(8,128)}, f32[16,768]{1,0:T(8,128)S(1)}, u32[]{:S(2)}, u32[]{:S(2)}) collective-permute-start(f32[16,768]{1,0:T(8,128)} %get-tuple-element.169), channel_id=1, source_target_pairs={{0,1},{1,0},{2,3},{3,2},{4,5},{5,4},{6,7},{7,6},{8,9},{9,8},{10,11... | collective-permute-start | bytes 147464 | tf_op jit(solution)/shard_map/ppermute | solution.py:470
  87.2 18.5 %collective-permute-start.8 = (bf16[2,2,8,48,768]{4,3,2,1,0:T(8,128)(2,1)}, bf16[2,2,8,48,768]{4,3,2,1,0:T(8,128)(2,1)S(1)}, u32[]{:S(2)}, u32[]{:S(2)}) collective-permute-start(bf16[2,2,8,48,768]{4,3,2,1,0:T(8,128)(2,1)} %get-tuple-element.179), channel_id=1, source_target_pairs={{0,2},{2,0},{4,6},{6,4},{8,10},{10,8},{12,14},{14,12},{16,18},{18,... | collective-permute-start | bytes 7077896 | tf_op jit(solution)/shard_map/ppermute | solution.py:466
  90.4 15.4 %collective-permute-start.9 = (f32[24,768]{1,0:T(8,128)S(1)}, f32[24,768]{1,0:T(8,128)S(1)}, u32[]{:S(2)}, u32[]{:S(2)}) collective-permute-start(f32[24,768]{1,0:T(8,128)S(1)} %pad_maximum_fusion.16), channel_id=1, source_target_pairs={{0,2},{2,0},{4,6},{6,4},{8,10},{10,8},{12,14},{14,12},{16,18},{18,... | collective-permute-start | bytes 221192 | tf_op jit(solution)/shard_map/ppermute | solution.py:466
  90.7 31.7 %collective-permute-start.11 = (bf16[2,4,96,384]{3,2,1,0:T(8,128)(2,1)}, bf16[2,4,96,384]{3,2,1,0:T(8,128)(2,1)}, u32[]{:S(2)}, u32[]{:S(2)}) collective-permute-start(bf16[2,4,96,384]{3,2,1,0:T(8,128)(2,1)} %fusion.28), channel_id=1, source_target_pairs={{0,4},{2,6},{4,0},{6,2},{8,12},{10,14},{12,8},{14,10},{16,20},{18,... | collective-permute-start | bytes 1769480 | tf_op jit(solution)/shard_map/ppermute | solution.py:466
  91.2 31.2 %collective-permute-start.10 = (bf16[8,96,384]{2,1,0:T(8,128)(2,1)}, bf16[8,96,384]{2,1,0:T(8,128)(2,1)}, u32[]{:S(2)}, u32[]{:S(2)}) collective-permute-start(bf16[8,96,384]{2,1,0:T(8,128)(2,1)} %fusion.27), channel_id=1, source_target_pairs={{0,1},{1,0},{2,3},{3,2},{4,5},{5,4},{6,7},{7,6},{8,9},{9,8},{10,11... | collective-permute-start | bytes 1769480 | tf_op jit(solution)/shard_map/ppermute | solution.py:470
  108.2 14.2 %collective-permute-start.12 = (f32[32,768]{1,0:T(8,128)S(1)}, f32[32,768]{1,0:T(8,128)S(1)}, u32[]{:S(2)}, u32[]{:S(2)}) collective-permute-start(f32[32,768]{1,0:T(8,128)S(1)} %pad_maximum_fusion.14), channel_id=1, source_target_pairs={{0,4},{2,6},{4,0},{6,2},{8,12},{10,14},{12,8},{14,10},{16,20},{18,... | collective-permute-start | bytes 294920 | tf_op jit(solution)/shard_map/ppermute | solution.py:466
  111.0 25.7 %collective-permute-start.16 = (bf16[8,48,768]{2,1,0:T(8,128)(2,1)}, bf16[8,48,768]{2,1,0:T(8,128)(2,1)}, u32[]{:S(2)}, u32[]{:S(2)}) collective-permute-start(bf16[8,48,768]{2,1,0:T(8,128)(2,1)} %fusion.30), channel_id=1, source_target_pairs={{0,1},{1,0},{2,3},{3,2},{4,5},{5,4},{6,7},{7,6},{8,9},{9,8},{10,11... | collective-permute-start | bytes 1769480 | tf_op jit(solution)/shard_map/ppermute | solution.py:470
  111.5 25.2 %collective-permute-start.15 = (bf16[2,4,48,768]{3,2,1,0:T(8,128)(2,1)}, bf16[2,4,48,768]{3,2,1,0:T(8,128)(2,1)}, u32[]{:S(2)}, u32[]{:S(2)}) collective-permute-start(bf16[2,4,48,768]{3,2,1,0:T(8,128)(2,1)} %fusion.29), channel_id=1, source_target_pairs={{0,4},{2,6},{4,0},{6,2},{8,12},{10,14},{12,8},{14,10},{16,20},{18,... | collective-permute-start | bytes 1769480 | tf_op jit(solution)/shard_map/ppermute | solution.py:466
  136.7 17.5 %collective-permute-start.18 = (bf16[2,2,8,2,48,384]{5,4,3,2,1,0:T(8,128)(2,1)}, bf16[2,2,8,2,48,384]{5,4,3,2,1,0:T(8,128)(2,1)S(1)}, u32[]{:S(2)}, u32[]{:S(2)}) collective-permute-start(bf16[2,2,8,2,48,384]{5,4,3,2,1,0:T(8,128)(2,1)} %get-tuple-element.228), channel_id=1, source_target_pairs={{0,2},{2,0},{4,6},{6,4},{8,10},{10,8},{12,14},{14,12},{16,18},{18,... | collective-permute-start | bytes 7077896 | tf_op jit(solution)/shard_map/ppermute | solution.py:466
  138.1 18.4 %collective-permute-start.13 = (bf16[4,96,384]{2,1,0:T(8,128)(2,1)S(1)}, bf16[4,96,384]{2,1,0:T(8,128)(2,1)S(1)}, u32[]{:S(2)}, u32[]{:S(2)}) collective-permute-start(bf16[4,96,384]{2,1,0:T(8,128)(2,1)S(1)} %copy-done.53), channel_id=1, source_target_pairs={{0,4},{2,6},{4,0},{6,2},{8,12},{10,14},{12,8},{14,10},{16,20},{18,... | collective-permute-start | bytes 884744 | tf_op jit(solution)/shard_map/ppermute | solution.py:466
  139.7 16.9 %collective-permute-start.14 = (bf16[4,96,384]{2,1,0:T(8,128)(2,1)S(1)}, bf16[4,96,384]{2,1,0:T(8,128)(2,1)S(1)}, u32[]{:S(2)}, u32[]{:S(2)}) collective-permute-start(bf16[4,96,384]{2,1,0:T(8,128)(2,1)S(1)} %copy-done.52), channel_id=1, source_target_pairs={{0,1},{1,0},{2,3},{3,2},{4,5},{5,4},{6,7},{7,6},{8,9},{9,8},{10,11... | collective-permute-start | bytes 884744 | tf_op jit(solution)/shard_map/ppermute | solution.py:470
  141.2 16.8 %collective-permute-start.19 = (bf16[256,768]{1,0:T(8,128)(2,1)S(1)}, bf16[256,768]{1,0:T(8,128)(2,1)S(1)}, u32[]{:S(2)}, u32[]{:S(2)}) collective-permute-start(bf16[256,768]{1,0:T(8,128)(2,1)S(1)} %copy-done.49), channel_id=1, source_target_pairs={{0,1},{1,0},{2,3},{3,2},{4,5},{5,4},{6,7},{7,6},{8,9},{9,8},{10,11... | collective-permute-start | bytes 1179656 | tf_op jit(solution)/shard_map/ppermute | solution.py:470
  148.0 15.5 %collective-permute-start.20 = (bf16[4,48,768]{2,1,0:T(8,128)(2,1)S(1)}, bf16[4,48,768]{2,1,0:T(8,128)(2,1)S(1)}, u32[]{:S(2)}, u32[]{:S(2)}) collective-permute-start(bf16[4,48,768]{2,1,0:T(8,128)(2,1)S(1)} %fusion.34), channel_id=1, source_target_pairs={{0,1},{1,0},{2,3},{3,2},{4,5},{5,4},{6,7},{7,6},{8,9},{9,8},{10,11... | collective-permute-start | bytes 884744 | tf_op jit(solution)/shard_map/ppermute | solution.py:470
  154.3 9.2 %collective-permute-start.21 = (bf16[4,48,768]{2,1,0:T(8,128)(2,1)S(1)}, bf16[4,48,768]{2,1,0:T(8,128)(2,1)S(1)}, u32[]{:S(2)}, u32[]{:S(2)}) collective-permute-start(bf16[4,48,768]{2,1,0:T(8,128)(2,1)S(1)} %fusion.42), channel_id=1, source_target_pairs={{0,4},{2,6},{4,0},{6,2},{8,12},{10,14},{12,8},{14,10},{16,20},{18,... | collective-permute-start | bytes 884744 | tf_op jit(solution)/shard_map/ppermute | solution.py:466
  163.5 22.2 %collective-permute-start.25 = (f32[2,768]{1,0:T(2,128)S(1)}, f32[2,768]{1,0:T(2,128)S(1)}, u32[]{:S(2)}, u32[]{:S(2)}) collective-permute-start(f32[2,768]{1,0:T(2,128)S(1)} %pad_maximum_fusion.19), channel_id=1, source_target_pairs={{0,1},{1,0},{2,3},{3,2},{4,5},{5,4},{6,7},{7,6},{8,9},{9,8},{10,11... | collective-permute-start | bytes 18440 | tf_op jit(solution)/shard_map/ppermute | solution.py:470
  165.0 13.2 %collective-permute-start.37 = (f32[80,768]{1,0:T(8,128)S(1)}, f32[80,768]{1,0:T(8,128)S(1)}, u32[]{:S(2)}, u32[]{:S(2)}) collective-permute-start(f32[80,768]{1,0:T(8,128)S(1)} %pad_maximum_fusion.6), channel_id=1, source_target_pairs={{0,16},{2,18},{4,20},{6,22},{8,24},{10,26},{12,28},{14,30},{16,0},... | collective-permute-start | bytes 737288 | tf_op jit(solution)/shard_map/ppermute | solution.py:466
  165.4 20.1 %collective-permute-start.24 = (bf16[2,2,96,384]{3,2,1,0:T(8,128)(2,1)S(1)}, bf16[2,2,96,384]{3,2,1,0:T(8,128)(2,1)S(1)}, u32[]{:S(2)}, u32[]{:S(2)}) collective-permute-start(bf16[2,2,96,384]{3,2,1,0:T(8,128)(2,1)S(1)} %pad_maximum_fusion.1), channel_id=1, source_target_pairs={{0,8},{2,10},{4,12},{6,14},{8,0},{10,2},{12,4},{14,6},{16,24},{18,... | collective-permute-start | bytes 884744 | tf_op jit(solution)/shard_map/ppermute | solution.py:466
  166.8 18.9 %collective-permute-start.22 = (bf16[2,4,2,48,384]{4,3,2,1,0:T(8,128)(2,1)S(1)}, bf16[2,4,2,48,384]{4,3,2,1,0:T(8,128)(2,1)S(1)}, u32[]{:S(2)}, u32[]{:S(2)}) collective-permute-start(bf16[2,4,2,48,384]{4,3,2,1,0:T(8,128)(2,1)S(1)} %fusion.31), channel_id=1, source_target_pairs={{0,4},{2,6},{4,0},{6,2},{8,12},{10,14},{12,8},{14,10},{16,20},{18,... | collective-permute-start | bytes 1769480 | tf_op jit(solution)/shard_map/ppermute | solution.py:466
  167.4 18.4 %collective-permute-start.23 = (bf16[8,2,48,384]{3,2,1,0:T(8,128)(2,1)S(1)}, bf16[8,2,48,384]{3,2,1,0:T(8,128)(2,1)S(1)}, u32[]{:S(2)}, u32[]{:S(2)}) collective-permute-start(bf16[8,2,48,384]{3,2,1,0:T(8,128)(2,1)S(1)} %fusion.32), channel_id=1, source_target_pairs={{0,1},{1,0},{2,3},{3,2},{4,5},{5,4},{6,7},{7,6},{8,9},{9,8},{10,11... | collective-permute-start | bytes 1769480 | tf_op jit(solution)/shard_map/ppermute | solution.py:470
  193.6 13.2 %collective-permute-start.35 = (bf16[2,1,96,384]{3,2,1,0:T(8,128)(2,1)S(1)}, bf16[2,1,96,384]{3,2,1,0:T(8,128)(2,1)S(1)}, u32[]{:S(2)}, u32[]{:S(2)}) collective-permute-start(bf16[2,1,96,384]{3,2,1,0:T(8,128)(2,1)S(1)} %pad_maximum_fusion.10), channel_id=1, source_target_pairs={{0,16},{2,18},{4,20},{6,22},{8,24},{10,26},{12,28},{14,30},{16,0},... | collective-permute-start | bytes 442376 | tf_op jit(solution)/shard_map/ppermute | solution.py:466
  194.5 13.2 %collective-permute-start.27 = (bf16[4,2,48,384]{3,2,1,0:T(8,128)(2,1)S(1)}, bf16[4,2,48,384]{3,2,1,0:T(8,128)(2,1)S(1)}, u32[]{:S(2)}, u32[]{:S(2)}) collective-permute-start(bf16[4,2,48,384]{3,2,1,0:T(8,128)(2,1)S(1)} %fusion.33), channel_id=1, source_target_pairs={{0,1},{1,0},{2,3},{3,2},{4,5},{5,4},{6,7},{7,6},{8,9},{9,8},{10,11... | collective-permute-start | bytes 884744 | tf_op jit(solution)/shard_map/ppermute | solution.py:470
  195.1 12.5 %collective-permute-start.28 = (bf16[4,2,48,384]{3,2,1,0:T(8,128)(2,1)S(1)}, bf16[4,2,48,384]{3,2,1,0:T(8,128)(2,1)S(1)}, u32[]{:S(2)}, u32[]{:S(2)}) collective-permute-start(bf16[4,2,48,384]{3,2,1,0:T(8,128)(2,1)S(1)} %fusion.43), channel_id=1, source_target_pairs={{0,4},{2,6},{4,0},{6,2},{8,12},{10,14},{12,8},{14,10},{16,20},{18,... | collective-permute-start | bytes 884744 | tf_op jit(solution)/shard_map/ppermute | solution.py:466
  195.7 12.0 %collective-permute-start.30 = (f32[2,768]{1,0:T(2,128)S(1)}, f32[2,768]{1,0:T(2,128)S(1)}, u32[]{:S(2)}, u32[]{:S(2)}) collective-permute-start(f32[2,768]{1,0:T(2,128)S(1)} %add.1348), channel_id=1, source_target_pairs={{0,4},{2,6},{4,0},{6,2},{8,12},{10,14},{12,8},{14,10},{16,20},{18,... | collective-permute-start | bytes 18440 | tf_op jit(solution)/shard_map/ppermute | solution.py:466
  197.3 12.7 %collective-permute-start.34 = (bf16[2,1,48,768]{3,2,1,0:T(8,128)(2,1)S(1)}, bf16[2,1,48,768]{3,2,1,0:T(8,128)(2,1)S(1)}, u32[]{:S(2)}, u32[]{:S(2)}) collective-permute-start(bf16[2,1,48,768]{3,2,1,0:T(8,128)(2,1)S(1)} %pad_maximum_fusion.11), channel_id=1, source_target_pairs={{0,16},{2,18},{4,20},{6,22},{8,24},{10,26},{12,28},{14,30},{16,0},... | collective-permute-start | bytes 442376 | tf_op jit(solution)/shard_map/ppermute | solution.py:466
  207.9 9.1 %collective-permute-start.31 = (bf16[2,2,2,48,384]{4,3,2,1,0:T(8,128)(2,1)S(1)}, bf16[2,2,2,48,384]{4,3,2,1,0:T(8,128)(2,1)S(1)}, u32[]{:S(2)}, u32[]{:S(2)}) collective-permute-start(bf16[2,2,2,48,384]{4,3,2,1,0:T(8,128)(2,1)S(1)} %pad_maximum_fusion.3), channel_id=1, source_target_pairs={{0,8},{2,10},{4,12},{6,14},{8,0},{10,2},{12,4},{14,6},{16,24},{18,... | collective-permute-start | bytes 884744 | tf_op jit(solution)/shard_map/ppermute | solution.py:466
  218.1 9.2 %collective-permute-start.33 = (bf16[2,1,2,48,384]{4,3,2,1,0:T(8,128)(2,1)S(1)}, bf16[2,1,2,48,384]{4,3,2,1,0:T(8,128)(2,1)S(1)}, u32[]{:S(2)}, u32[]{:S(2)}) collective-permute-start(bf16[2,1,2,48,384]{4,3,2,1,0:T(8,128)(2,1)S(1)} %pad_maximum_fusion.12), channel_id=1, source_target_pairs={{0,16},{2,18},{4,20},{6,22},{8,24},{10,26},{12,28},{14,30},{16,0},... | collective-permute-start | bytes 442376 | tf_op jit(solution)/shard_map/ppermute | solution.py:466
  (83 other events, 316.6 us)

commit v2 on v1

--- a/solution.py
+++ b/solution.py
@@ -1,4 +1,5 @@
 import functools
+import math
 
 import jax
 import jax.numpy as jnp
@@ -27,22 +28,8 @@
     return (normed * gain_row, normed, inv_std)
 
 
-def norm_back(upstream, normed, inv_std, gain_row):
-    scaled = upstream * gain_row
-    gain_grad = jnp.sum(upstream * normed, axis=0)
-    first_mean = jnp.mean(scaled, axis=-1, keepdims=True)
-    second_mean = jnp.mean(scaled * normed, axis=-1, keepdims=True)
-    return (inv_std * (scaled - first_mean - normed * second_mean), gain_grad)
-
-
 def low_dot(left_side, right_side):
     return jnp.dot(left_side, right_side, preferred_element_type=f32)
-
-
-def back_dot(left_side, right_side):
-    return lax.dot_general(
-        left_side, right_side, (((1,), (1,)), ((), ())), preferred_element_type=f32
-    )
 
 
 def gelu_tanh(values):
@@ -163,8 +150,7 @@
     caps_ref,
     grad_ref,
     branch_ref,
-    sums_ref,
-    rank_ref,
+    message_ref,
 ):
     width = low_ref.shape[1]
     half = width // seq_count
@@ -245,7 +231,7 @@
         row_loss * share,
         jnp.where(lane == 1, temp_row * share, jnp.where(lane == 2, bias_row * share, 0.0)),
     )
-    sums_ref[...] = jnp.where(
+    message_ref[:TOP] = jnp.where(
         row < HEADS,
         key_mix_grad,
         jnp.where(row == HEADS, gain_grad, jnp.where(row == HEADS + 1, scalars, 0.0)),
@@ -261,7 +247,7 @@
         axis=1,
     )
     row = row[:8]
-    rank_ref[...] = jnp.where(row < near, my_mix, jnp.where(row == near, flat, my_pair))
+    message_ref[TOP:] = jnp.where(row < near, my_mix, jnp.where(row == near, flat, my_pair))
 
 
 def pool_back_call(
@@ -274,12 +260,11 @@
     return pl.pallas_call(
         functools.partial(pool_back_kernel, images, seq_count),
         in_specs=[smem] * 5 + [vmem] * 11,
-        out_specs=[vmem] * 4,
+        out_specs=[vmem] * 3,
         out_shape=[
             jax.ShapeDtypeStruct((rows, width), f32),
             jax.ShapeDtypeStruct((rows, width), bf16),
-            jax.ShapeDtypeStruct((TOP, width), f32),
-            jax.ShapeDtypeStruct((8, width), f32),
+            jax.ShapeDtypeStruct((TOP + 8, width), f32),
         ],
         cost_estimate=light,
         name="pool_back",
@@ -381,7 +366,7 @@
     return jnp.where(core == 0, far, near).astype(bf16), jnp.where(core == 0, near, far).astype(bf16)
 
 
-def wgrad_kernel(block, by_rows, place_ref, left_ref, right_ref, send_ref, keep_ref):
+def wgrad_kernel(block, place_ref, left_ref, right_ref, send_ref, keep_ref):
     grad = tn(left_ref[...], right_ref[...])
     columns = grad.shape[1] // 2
     for j in range(grad.shape[0] // (2 * block)):
@@ -389,23 +374,20 @@
             for y in range(2):
                 mine = part[:, y * columns : (y + 1) * columns]
                 for g in range(2):
-                    if by_rows:
-                        ref[g, y, j] = mine[g * (block // 2) : (g + 1) * (block // 2)]
-                    else:
-                        ref[g, y, j] = mine[:, g * (columns // 2) : (g + 1) * (columns // 2)]
-
-
-def wgrad(place, left, right, images, by_rows):
+                    ref[g, y, j] = mine[g * (block // 2) : (g + 1) * (block // 2)]
+
+
+def wgrad(place, left, right, images):
     rows, depth = left.shape
     columns = right.shape[1]
     block = depth // images
     chunk = depth // 2
     pairs = chunk // (2 * block)
-    cut = (block // 2, columns // 2) if by_rows else (block, columns // 4)
+    cut = (block // 2, columns // 2)
     out_spec = pl.BlockSpec((2, 2, pairs, *cut), lambda i: (0, 0, i, 0, 0))
     out_shape = jax.ShapeDtypeStruct((2, 2, images // 2, *cut), bf16)
     return pl.pallas_call(
-        functools.partial(wgrad_kernel, block, by_rows),
+        functools.partial(wgrad_kernel, block),
         grid=(2,),
         in_specs=[
             pl.BlockSpec(memory_space=pltpu.SMEM),
@@ -470,49 +452,341 @@
     return lax.ppermute(value, "seq", [(0, 1), (1, 0)])
 
 
-def my_bit(bit):
-    return (lax.axis_index("img") >> bit) & 1
-
-
-def pick(value, index, axis):
-    return lax.dynamic_index_in_dim(value, index, axis, keepdims=False)
-
-
 def tie(*values):
     return lax.optimization_barrier(values)
 
 
-def total_of(parts):
-    total = parts[0].astype(f32)
-    for part in parts[1:]:
-        total = total + part.astype(f32)
-    return total
-
-
-def seq_send(parts, axis):
-    mine = lax.axis_index("seq")
-    send = total_of([pick(part, 1 - mine, axis) for part in parts]).astype(bf16)
-    return send, [pick(part, mine, axis) for part in parts]
-
-
-def img_send(parts, axis, bit):
-    mine = my_bit(bit)
-    cut = [
-        part.reshape(*part.shape[:axis], part.shape[axis] // 2, 2, *part.shape[axis + 1 :])
-        for part in parts
-    ]
-    send = total_of([pick(part, 1 - mine, axis + 1) for part in cut]).astype(bf16)
-    return send, [pick(part, mine, axis + 1) for part in cut]
-
-
-def pair_send(first, second, axis, bit):
-    send_first, first = img_send(first, axis, bit)
-    send_second, second = img_send(second, axis, bit)
-    return jnp.stack([send_first, send_second]), first, second
-
-
-def pair_take(arrived, first, second):
-    return first + [arrived[0]], second + [arrived[1]]
+def at(index):
+    return lambda p: index
+
+
+def my_seq(p):
+    return p[1]
+
+
+def other_seq(p):
+    return 1 - p[1]
+
+
+def my_x(p):
+    return p[3]
+
+
+def other_x(p):
+    return 1 - p[3]
+
+
+def z_from(bit, count):
+    return lambda p: (p[4] >> bit) & ((1 << count) - 1)
+
+
+def z_other(bit):
+    return lambda p: 1 - ((p[4] >> bit) & 1)
+
+
+def fold_kernel(plan, place_ref, *refs):
+    count = sum(sum(slots) for slots, _ in plan)
+    inputs = iter(refs[:count])
+    for (slots, join), out in zip(plan, refs[count:]):
+        start = 0
+        for slot, parts in enumerate(slots):
+            total = next(inputs)[...].astype(f32)
+            for _ in range(parts - 1):
+                total = total + next(inputs)[...].astype(f32)
+            total = total.astype(out.dtype)
+            if join is None:
+                out[...] = total
+            elif join == "stack":
+                out[slot] = total
+            elif join == "rows":
+                out[start : start + total.shape[0]] = total
+                start += total.shape[0]
+            else:
+                out[:, start : start + total.shape[1]] = total
+                start += total.shape[1]
+
+
+def fold(place, outputs, dtype):
+    arrays, specs, plan, shapes = [], [], [], []
+    for slots, join in outputs:
+        counts = []
+        for parts in slots:
+            counts.append(len(parts))
+            for array, picks in parts:
+                picks = picks + (None,) * (array.ndim - len(picks))
+                shape = tuple(d for d, choose in zip(array.shape, picks) if choose is None)
+                block = tuple(d if choose is None else None for d, choose in zip(array.shape, picks))
+                arrays.append(array)
+                specs.append(
+                    pl.BlockSpec(
+                        block,
+                        lambda i, p, picks=picks: tuple(0 if c is None else c(p) for c in picks),
+                    )
+                )
+        if join == "stack":
+            shape = (len(slots), *shape)
+        elif join == "rows":
+            shape = (len(slots) * shape[0], *shape[1:])
+        elif join == "columns":
+            shape = (shape[0], len(slots) * shape[1])
+        plan.append((tuple(counts), join))
+        shapes.append(shape)
+    return pl.pallas_call(
+        functools.partial(fold_kernel, tuple(plan)),
+        grid_spec=pltpu.PrefetchScalarGridSpec(
+            num_scalar_prefetch=1,
+            grid=(1,),
+            in_specs=specs,
+            out_specs=[pl.BlockSpec(t, lambda i, p, t=t: (0,) * len(t)) for t in shapes],
+        ),
+        out_shape=[jax.ShapeDtypeStruct(t, dtype) for t in shapes],
+        cost_estimate=light,
+        name="fold",
+    )(place, *arrays)
+
+
+class Staged:
+    def __init__(self, group, seq_first, keep, core):
+        self.group, self.seq_first = group, seq_first
+        self.level = [keep, core]
+        self.rest = keep.shape[3:]
+        self.quarter = keep.shape[2] // 2
+        self.first = self.second = None
+        self.arrived = []
+
+    def cut(self, array, *lead):
+        return array.reshape(*lead, *self.rest)
+
+    def stage_one(self):
+        q, g = self.quarter, at(self.group)
+        if self.seq_first:
+            return [(a, (g, other_seq, None)) for a in self.level]
+        return [(self.cut(a, 2, 2, q, 2), (g, None, None, other_x)) for a in self.level]
+
+    def stage_two(self):
+        q, g = self.quarter, at(self.group)
+        if self.seq_first:
+            parts = [(self.cut(a, 2, 2, q, 2), (g, my_seq, None, other_x)) for a in self.level]
+            return parts + [(self.cut(self.first, q, 2), (None, other_x))]
+        parts = [(self.cut(a, 2, 2, q, 2), (g, other_seq, None, my_x)) for a in self.level]
+        return parts + [(self.first, (other_seq, None))]
+
+    def z_parts(self, split, choose):
+        g = at(self.group)
+        parts = [(self.cut(a, 2, 2, *split, 2), (g, my_seq, *choose, my_x)) for a in self.level]
+        if self.seq_first:
+            parts.append((self.cut(self.first, *split, 2), (*choose, my_x)))
+        else:
+            parts.append((self.cut(self.first, 2, *split), (my_seq, *choose)))
+        parts.append((self.cut(self.second, *split), choose))
+        return parts
+
+    def stage_z(self, k):
+        high = self.quarter >> (k + 1)
+        parts = self.z_parts((high, 2, 1 << k), (None, z_other(k), z_from(0, k)))
+        for j, array in enumerate(self.arrived):
+            view = self.cut(array, 2, high, 2, 1 << (k - j - 1))
+            parts.append((view, (at(self.group), None, z_other(k), z_from(j + 1, k - j - 1))))
+        return parts
+
+    def whole(self, *more):
+        bits = self.quarter.bit_length() - 1
+        more = tuple(at(m) for m in more)
+        parts = self.z_parts((self.quarter,), (z_from(0, bits),))
+        for j, array in enumerate(self.arrived):
+            parts.append((array, (at(self.group), z_from(j + 1, bits - j - 1))))
+        return [(array, picks + more) for array, picks in parts]
+
+
+def merge_kernel(gather, own_ref, other_ref, out_ref):
+    out_ref[:TOP] = own_ref[:TOP] + other_ref[:TOP]
+    rows = own_ref.shape[0]
+    out_ref[TOP:rows] = own_ref[TOP:]
+    if gather:
+        out_ref[rows:] = other_ref[TOP:]
+
+
+def merge(own, other, gather):
+    rows, width = own.shape
+    if gather:
+        rows = 2 * rows - TOP
+    return pl.pallas_call(
+        functools.partial(merge_kernel, gather),
+        out_shape=jax.ShapeDtypeStruct((rows, width), f32),
+        cost_estimate=light,
+        name="merge",
+    )(own, other)
+
+
+def gelu_back_kernel(grad_ref, down_ref, up_ref, out_ref):
+    hidden_grad = nt(grad_ref[...], down_ref[...])
+    u = up_ref[...]
+    factor = math.sqrt(2.0 / math.pi)
+    square = u * u
+    t = jnp.tanh(factor * (u + 0.044715 * (square * u)))
+    slope = 0.5 * (1.0 + t) + 0.5 * u * (1.0 - t * t) * (
+        factor * (1.0 + (3.0 * 0.044715) * square)
+    )
+    out_ref[...] = (hidden_grad * slope).astype(bf16)
+
+
+def gelu_back_call(grad, w_down, upward):
+    rows, width = grad.shape
+    depth = upward.shape[1]
+    chunk = depth // 4
+    return pl.pallas_call(
+        gelu_back_kernel,
+        grid=(4,),
+        in_specs=[
+            pl.BlockSpec((rows, width), lambda c: (0, 0)),
+            pl.BlockSpec((chunk, width), lambda c: (c, 0)),
+            pl.BlockSpec((rows, chunk), lambda c: (0, c)),
+        ],
+        out_specs=pl.BlockSpec((rows, chunk), lambda c: (0, c)),
+        out_shape=jax.ShapeDtypeStruct((rows, depth), bf16),
+        cost_estimate=light,
+        name="gelu_back",
+    )(grad, w_down, upward)
+
+
+def norm_back_rows(grad, unit, inv, gain):
+    scaled = grad * gain
+    first_mean = jnp.mean(scaled, axis=-1, keepdims=True)
+    second_mean = jnp.mean(scaled * unit, axis=-1, keepdims=True)
+    gain_grad = jnp.sum(grad * unit, axis=0, keepdims=True)
+    return inv * (scaled - first_mean - unit * second_mean), gain_grad
+
+
+def up_back_kernel(
+    block, place_ref, low_ref, du_ref, up_ref, unit_ref, inv_ref, gain_ref, above_ref, wo_ref,
+    send_ref, keep_ref, grad_ref, branch_ref, heads_ref, gain_grad_ref, acc_ref,
+):
+    c = pl.program_id(0)
+    du = du_ref[...]
+    grad = tn(low_ref[...], du)
+    for j in range(grad.shape[0] // (2 * block)):
+        send, keep = halves(place_ref[2], grad, block, j)
+        send_ref[0, 0, j] = send
+        keep_ref[0, 0, j] = keep
+    back = nt(du, up_ref[...])
+
+    @pl.when(c == 0)
+    def _():
+        acc_ref[...] = back
+
+    @pl.when(c > 0)
+    def _():
+        acc_ref[...] += back
+
+    @pl.when(c == pl.num_programs(0) - 1)
+    def _():
+        through, gain_grad = norm_back_rows(
+            acc_ref[...], unit_ref[...], inv_ref[...], gain_ref[...]
+        )
+        total = above_ref[...] + through
+        gain_grad_ref[...] = gain_grad
+        grad_ref[...] = total
+        branch = total.astype(bf16)
+        branch_ref[...] = branch
+        heads_ref[...] = nt(branch, wo_ref[...]).astype(bf16)
+
+
+def up_back_call(place, low, du, w_up, unit, inv, gain, above, w_output, images):
+    rows, width = low.shape
+    depth = du.shape[1]
+    chunk = depth // 4
+    block = width // images
+    whole = lambda *shape: pl.BlockSpec(shape, lambda c: (0,) * len(shape))
+    half_spec = pl.BlockSpec(
+        (1, 1, images // 2, block, chunk), lambda c: (c % 2, c // 2, 0, 0, 0)
+    )
+    half_shape = jax.ShapeDtypeStruct((2, 2, images // 2, block, chunk), bf16)
+    return pl.pallas_call(
+        functools.partial(up_back_kernel, block),
+        grid=(4,),
+        in_specs=[
+            pl.BlockSpec(memory_space=pltpu.SMEM),
+            whole(rows, width),
+            pl.BlockSpec((rows, chunk), lambda c: (0, c)),
+            pl.BlockSpec((width, chunk), lambda c: (0, c)),
+            whole(rows, width),
+            whole(rows, 1),
+            whole(1, width),
+            whole(rows, width),
+            whole(width, width),
+        ],
+        out_specs=[
+            half_spec,
+            half_spec,
+            whole(rows, width),
+            whole(rows, width),
+            whole(rows, width),
+            whole(1, width),
+        ],
+        out_shape=[
+            half_shape,
+            half_shape,
+            jax.ShapeDtypeStruct((rows, width), f32),
+            jax.ShapeDtypeStruct((rows, width), bf16),
+            jax.ShapeDtypeStruct((rows, width), bf16),
+            jax.ShapeDtypeStruct((1, width), f32),
+        ],
+        scratch_shapes=[pltpu.VMEM((rows, width), f32)],
+        cost_estimate=light,
+        name="up_back",
+    )(place, low, du, w_up, unit, inv, gain[None], above, w_output)
+
+
+def other_in_kernel(dk_ref, dv_ref, wk_ref, wv_ref, out_ref):
+    out_ref[...] = (nt(dk_ref[...], wk_ref[...]) + nt(dv_ref[...], wv_ref[...])).astype(bf16)
+
+
+def other_in_call(dk, dv, w_key, w_value):
+    rows, width = dk.shape[0] // 2, dk.shape[1]
+    far = pl.BlockSpec((rows, width), lambda i: (1, 0))
+    whole = pl.BlockSpec((width, width), lambda i: (0, 0))
+    return pl.pallas_call(
+        other_in_kernel,
+        grid=(1,),
+        in_specs=[far, far, whole, whole],
+        out_specs=pl.BlockSpec((rows, width), lambda i: (0, 0)),
+        out_shape=jax.ShapeDtypeStruct((rows, width), bf16),
+        cost_estimate=light,
+        name="other_in",
+    )(dk, dv, w_key, w_value)
+
+
+def own_in_kernel(
+    dq_ref, dk_ref, dv_ref, wq_ref, wk_ref, wv_ref, arrived_ref, unit_ref, inv_ref, gain_ref,
+    above_ref, second_ref, out_ref, gains_ref,
+):
+    grad = nt(dq_ref[...], wq_ref[...]) + nt(dk_ref[...], wk_ref[...])
+    grad = grad + nt(dv_ref[...], wv_ref[...]) + arrived_ref[...].astype(f32)
+    through, gain_grad = norm_back_rows(grad, unit_ref[...], inv_ref[...], gain_ref[...])
+    out_ref[...] = above_ref[...] + through
+    row = lax.broadcasted_iota(jnp.int32, gains_ref.shape, 0)
+    gains_ref[...] = jnp.where(row == 0, second_ref[...], jnp.where(row == 1, gain_grad, 0.0))
+
+
+def own_in_call(dq, dk, dv, w_query, w_key, w_value, arrived, unit, inv, gain, above, second):
+    rows, width = dq.shape
+    near = pl.BlockSpec((rows, width), lambda i: (0, 0))
+    whole = pl.BlockSpec((width, width), lambda i: (0, 0))
+    row = pl.BlockSpec((1, width), lambda i: (0, 0))
+    return pl.pallas_call(
+        own_in_kernel,
+        grid=(1,),
+        in_specs=[near] * 3
+        + [whole] * 3
+        + [near, near, pl.BlockSpec((rows, 1), lambda i: (0, 0)), row, near, row],
+        out_specs=[near, pl.BlockSpec((8, width), lambda i: (0, 0))],
+        out_shape=[
+            jax.ShapeDtypeStruct((rows, width), f32),
+            jax.ShapeDtypeStruct((8, width), f32),
+        ],
+        cost_estimate=light,
+        name="own_in",
+    )(dq, dk, dv, w_query, w_key, w_value, arrived, unit, inv, gain[None], above, second)
 
 
 class Order:
@@ -555,7 +829,7 @@
     seq_me = lax.axis_index("seq")
     half = width // seq_count
     caps = captions.shape[0]
-    place = jnp.stack([me, seq_me, me & 1]).astype(jnp.int32)
+    place = jnp.stack([me, seq_me, me & 1, (me >> 1) & 1, me >> 2]).astype(jnp.int32)
 
     other_tokens = seq_swap(own_tokens)
 
@@ -591,79 +865,58 @@
     normed_two, unit_two, scale_two = layer_norm(residual, second_gain)
     second_low = normed_two.astype(bf16)
     upward = low_dot(second_low, w_up)
-    activated, gelu_back = jax.vjp(gelu_tanh, upward)
-    hidden_low = activated.astype(bf16)
+    hidden_low = gelu_tanh(upward).astype(bf16)
     result = residual + low_dot(hidden_low, w_down)
     block_out = result.astype(bf16)[None]
 
     pool_low, unit_pool, inv_pool, exps, packed = pool_call(result, final_gain, key_probe)
     other_packed = seq_swap(packed)
     other_packed, gathered = tie(other_packed, gathered)
-    result_grad, branch_grad, sums, rank = pool_back_call(
+    result_grad, branch_grad, message = pool_back_call(
         place, caption_counts, positive_pairs, log_temp, pair_bias, packed, other_packed, exps,
         pool_low, unit_pool, inv_pool, final_gain, key_probe, pool_value, pool_output,
         gathered.reshape(images * caps, width), images, seq_count,
     )
 
     step = Order(place)
-    down_send, down_keep = wgrad(place, hidden_low, branch_grad, images, True)
-    branch_grad, down_send, sums = step(branch_grad, down_send, sums)
+    down_send, down_keep = wgrad(place, hidden_low, branch_grad, images)
+    branch_grad, down_send, message = step(branch_grad, down_send, message)
     down_core = img_swap(down_send, 1)
-    small_in = seq_swap(sums)
-    hidden_grad = back_dot(branch_grad, w_down)
-    up_grad_low = gelu_back(hidden_grad)[0].astype(bf16)
-
-    up_grad_low, down_core, small_in = step(up_grad_low, down_core, small_in)
-    sums = sums + small_in
-    down_a_send, down_a = seq_send([down_keep[0], down_core[0]], 0)
-    down_b_send, down_b = img_send([down_keep[1], down_core[1]], 1, 1)
-    up_grad_low, down_a_send, down_b_send = step(up_grad_low, down_a_send, down_b_send)
-    down_a_in = seq_swap(down_a_send)
-    down_b_in = img_swap(down_b_send, 2)
-
-    def small_step(sums, rank, bit):
-        return img_swap(jnp.concatenate([sums, rank], axis=0), 1 << bit)
-
-    def small_take(sums, rank, arrived):
-        return sums + arrived[:TOP], jnp.concatenate([rank, arrived[TOP:]], axis=0)
-
-    up_send, up_keep = wgrad(place, second_low, up_grad_low, images, False)
-    up_grad_low, up_send = step(up_grad_low, up_send)
+    message_in = seq_swap(message)
+    up_grad_low = gelu_back_call(branch_grad, w_down, upward)
+
+    up_grad_low, down_core, message_in = step(up_grad_low, down_core, message_in)
+    down_a = Staged(0, True, down_keep, down_core)
+    down_b = Staged(1, False, down_keep, down_core)
+    down_sends = fold(place, [([down_a.stage_one()], None), ([down_b.stage_one()], None)], bf16)
+    message = merge(message, message_in, False)
+    up_grad_low, down_sends, message = step(up_grad_low, down_sends, message)
+    down_a.first = seq_swap(down_sends[0])
+    down_b.first = img_swap(down_sends[1], 2)
+    message_in = img_swap(message, 1)
+
+    up_send, up_keep, residual_grad, attn_branch, attended_grad, second_gain_grad = up_back_call(
+        place, second_low, up_grad_low, w_up, unit_two, scale_two, second_gain, result_grad,
+        w_output, images,
+    )
+    attended_grad, up_send, message_in = step(attended_grad, up_send, message_in)
     up_core = img_swap(up_send, 1)
-    small_in = small_step(sums, rank, 0)
-    second_in_grad = back_dot(up_grad_low, w_up)
-    residual_ln_grad, second_gain_grad = norm_back(second_in_grad, unit_two, scale_two, second_gain)
-    residual_grad = result_grad + residual_ln_grad
-    attn_branch = residual_grad.astype(bf16)
-
-    attn_branch, up_core, small_in = step(attn_branch, up_core, small_in)
-    sums, rank = small_take(sums, rank, small_in)
-    up_a_send, up_a = img_send([up_keep[0], up_core[0]], 1, 1)
-    up_b_send, up_b = seq_send([up_keep[1], up_core[1]], 0)
-    attn_branch, up_a_send, up_b_send, sums, rank = step(attn_branch, up_a_send, up_b_send, sums, rank)
-    up_a_in = img_swap(up_a_send, 2)
-    up_b_in = seq_swap(up_b_send)
-    small_in = small_step(sums, rank, 1)
-
-    attended_grad = back_dot(attn_branch, w_output).astype(bf16)
+    message = merge(message, message_in, True)
+
     query_grad, key_part, value_part = attend_back(
         queries, keys_own, keys_other, values_own, values_other, attended_grad, log_totals
     )
-    query_grad, key_part, value_part, down_a_in, down_b_in, small_in = step(
-        query_grad, key_part, value_part, down_a_in, down_b_in, small_in
-    )
-    sums, rank = small_take(sums, rank, small_in)
-    down_a_send, down_a = img_send(down_a + [down_a_in], 0, 1)
-    down_b_send, down_b = seq_send(down_b + [down_b_in], 0)
-    query_grad, key_part, value_part, down_a_send, down_b_send, sums, rank = step(
-        query_grad, key_part, value_part, down_a_send, down_b_send, sums, rank
-    )
-    down_a_in = img_swap(down_a_send, 2)
-    down_b_in = seq_swap(down_b_send)
-    small_in = small_step(sums, rank, 2)
-    other_in_grad = (
-        back_dot(key_part[rows:], w_key) + back_dot(value_part[rows:], w_value)
-    ).astype(bf16)
+    query_grad, key_part, value_part, up_core, message = step(
+        query_grad, key_part, value_part, up_core, message
+    )
+    up_a = Staged(0, False, up_keep, up_core)
+    up_b = Staged(1, True, up_keep, up_core)
+    up_sends = fold(place, [([up_a.stage_one()], None), ([up_b.stage_one()], None)], bf16)
+    query_grad, key_part, value_part, up_sends = step(query_grad, key_part, value_part, up_sends)
+    up_a.first = img_swap(up_sends[0], 2)
+    up_b.first = seq_swap(up_sends[1])
+    message_in = img_swap(message, 2)
+    other_in_grad = other_in_call(key_part, value_part, w_key, w_value)
     query_grad, key_part, value_part, other_in_grad = step(
         query_grad, key_part, value_part, other_in_grad
     )
@@ -671,96 +924,114 @@
     four_send, four_keep = wgrad_four(
         place, low_own, low_other, attended_low, query_grad, key_part, value_part, attn_branch, images
     )
-    query_grad, key_part, value_part, four_send, up_a_in, up_b_in, small_in = step(
-        query_grad, key_part, value_part, four_send, up_a_in, up_b_in, small_in
-    )
+    four_send, down_a.first, down_b.first = step(four_send, down_a.first, down_b.first)
     four_core = img_swap(four_send, 1)
-    sums, rank = small_take(sums, rank, small_in)
-    up_a_send, up_a = seq_send(up_a + [up_a_in], 0)
-    up_b_send, up_b = img_send(up_b + [up_b_in], 0, 1)
-    query_grad, key_part, value_part, up_a_send, up_b_send, sums, rank = step(
-        query_grad, key_part, value_part, up_a_send, up_b_send, sums, rank
-    )
-    up_a_in = seq_swap(up_a_send)
-    up_b_in = img_swap(up_b_send, 2)
-    own_in_grad = (
-        back_dot(query_grad, w_query)
-        + back_dot(key_part[:rows], w_key)
-        + back_dot(value_part[:rows], w_value)
-    )
-    own_in_grad, four_core, four_keep = step(own_in_grad, four_core, four_keep)
-    four_a_send, four_a = img_send([four_keep[0], four_core[0]], 1, 1)
-    four_b_send, four_b = seq_send([four_keep[1], four_core[1]], 0)
-    own_in_grad, four_a_send, four_b_send, sums, rank = step(
-        own_in_grad, four_a_send, four_b_send, sums, rank
-    )
-    four_a_in = img_swap(four_a_send, 2)
-    four_b_in = seq_swap(four_b_send)
-    small_in = small_step(sums, rank, 3)
-
-    down_a_in, down_b_in, own_in_grad = step(down_a_in, down_b_in, own_in_grad)
-    down_a, down_b = down_a + [down_a_in], down_b + [down_b_in]
-    down_send, down_a, down_b = pair_send(down_a, down_b, 0, 2)
-    down_send, own_in_grad, arrived_grad = step(down_send, own_in_grad, arrived_grad)
+    down_sends = fold(place, [([down_a.stage_two()], None), ([down_b.stage_two()], None)], bf16)
+    down_sends, message_in = step(down_sends, message_in)
+    down_a.second = img_swap(down_sends[0], 2)
+    down_b.second = seq_swap(down_sends[1])
+    message = merge(message, message_in, True)
+
+    four_core, four_keep, message = step(four_core, four_keep, message)
+    four_a = Staged(0, False, four_keep, four_core)
+    four_b = Staged(1, True, four_keep, four_core)
+    four_sends = fold(place, [([four_a.stage_one()], None), ([four_b.stage_one()], None)], bf16)
+    four_sends, query_grad = step(four_sends, query_grad)
+    four_a.first = img_swap(four_sends[0], 2)
+    four_b.first = seq_swap(four_sends[1])
+    message_in = img_swap(message, 4)
+
+    up_a.first, up_b.first = step(up_a.first, up_b.first)
+    up_sends = fold(place, [([up_a.stage_two()], None), ([up_b.stage_two()], None)], bf16)
+    up_sends, arrived_grad, query_grad = step(up_sends, arrived_grad, query_grad)
+    up_a.second = seq_swap(up_sends[0])
+    up_b.second = img_swap(up_sends[1], 2)
+    input_grad, gains = own_in_call(
+        query_grad, key_part, value_part, w_query, w_key, w_value, arrived_grad, unit_one,
+        scale_one, first_gain, residual_grad, second_gain_grad,
+    )
+    input_grad, gains, down_a.second, down_b.second = step(
+        input_grad, gains, down_a.second, down_b.second
+    )
+    gains_in = seq_swap(gains)
+
+    def z_send(first, second, k):
+        return fold(place, [([first.stage_z(k), second.stage_z(k)], "stack")], bf16)[0]
+
+    def z_take(first, second, arrived):
+        first.arrived.append(arrived)
+        second.arrived.append(arrived)
+
+    down_send = z_send(down_a, down_b, 0)
+    down_send, message_in = step(down_send, message_in)
     down_in = img_swap(down_send, 4)
-
-    first_in_grad = own_in_grad + arrived_grad.astype(f32)
-    input_ln_grad, first_gain_grad = norm_back(first_in_grad, unit_one, scale_one, first_gain)
-    input_grad = residual_grad + input_ln_grad
-    late = jnp.stack([second_gain_grad, first_gain_grad])
-    input_grad, late, up_a_in, up_b_in = step(input_grad, late, up_a_in, up_b_in)
-    late_in = seq_swap(late)
-
-    up_a, up_b = up_a + [up_a_in], up_b + [up_b_in]
-    up_send, up_a, up_b = pair_send(up_a, up_b, 0, 2)
+    message = merge(message, message_in, True)
+    four_a.first, four_b.first, message = step(four_a.first, four_b.first, message)
+    four_sends = fold(place, [([four_a.stage_two()], None), ([four_b.stage_two()], None)], bf16)
+    four_sends, gains_in = step(four_sends, gains_in)
+    four_a.second = seq_swap(four_sends[0])
+    four_b.second = img_swap(four_sends[1], 2)
+    gains = gains + gains_in
+    message_in = img_swap(message, 8)
+
+    gains, up_a.second, up_b.second = step(gains, up_a.second, up_b.second)
+    up_send = z_send(up_a, up_b, 0)
     up_send, down_in = step(up_send, down_in)
     up_in = img_swap(up_send, 4)
-    down_a, down_b = pair_take(down_in, down_a, down_b)
-    down_send, down_a, down_b = pair_send(down_a, down_b, 0, 3)
-    four_a_in, four_b_in, down_send, late_in = step(four_a_in, four_b_in, down_send, late_in)
+    gains_in = img_swap(gains, 1)
+    z_take(down_a, down_b, down_in)
+    down_send = z_send(down_a, down_b, 1)
+    down_send, gains_in = step(down_send, gains_in)
     down_in = img_swap(down_send, 8)
-    late = late + late_in
-    four_a_send, four_a = seq_send(four_a + [four_a_in], 0)
-    four_b_send, four_b = img_send(four_b + [four_b_in], 0, 1)
-    four_a_send, four_b_send, late, up_in = step(four_a_send, four_b_send, late, up_in)
-    four_a_in = seq_swap(four_a_send)
-    four_b_in = img_swap(four_b_send, 2)
-    late_in = img_swap(late, 1)
-    up_a, up_b = pair_take(up_in, up_a, up_b)
-    up_send, up_a, up_b = pair_send(up_a, up_b, 0, 3)
-    up_send, late_in = step(up_send, late_in)
+    gains = gains + gains_in
+    four_a.second, four_b.second, gains = step(four_a.second, four_b.second, gains)
+    four_send = z_send(four_a, four_b, 0)
+    four_send, up_in = step(four_send, up_in)
+    four_in = img_swap(four_send, 4)
+    gains_in = img_swap(gains, 2)
+    z_take(up_a, up_b, up_in)
+    up_send = z_send(up_a, up_b, 1)
+    up_send, gains_in, message_in = step(up_send, gains_in, message_in)
     up_in = img_swap(up_send, 8)
-    late = late + late_in
-    late_in = img_swap(late, 2)
-    four_a_in, four_b_in, late_in = step(four_a_in, four_b_in, late_in)
-    four_send, four_a, four_b = pair_send(four_a + [four_a_in], four_b + [four_b_in], 0, 2)
-    late = late + late_in
-    four_send, late = step(four_send, late)
-    four_in = img_swap(four_send, 4)
-    late_in = img_swap(late, 4)
-    four_in, late_in = step(four_in, late_in)
-    four_a, four_b = pair_take(four_in, four_a, four_b)
-    four_send, four_a, four_b = pair_send(four_a, four_b, 0, 3)
-    late = late + late_in
+    gains = gains + gains_in
+    message = merge(message, message_in, True)
+    four_in, gains, message = step(four_in, gains, message)
+    z_take(four_a, four_b, four_in)
+    four_send = z_send(four_a, four_b, 1)
+    (four_send,) = step(four_send)
     four_in = img_swap(four_send, 8)
-    late_in = img_swap(late, 8)
-    late = late + late_in
-
-    def finish(arrived, first, second):
-        first, second = pair_take(arrived, first, second)
+    gains_in = img_swap(gains, 4)
+    down_in, up_in, gains_in = step(down_in, up_in, gains_in)
+    gains = gains + gains_in
+    gains_in = img_swap(gains, 8)
+
+    def rest(first, second, arrived):
+        z_take(first, second, arrived)
         for bit in range(4, bits):
-            send, first, second = pair_send(first, second, 0, bit)
-            first, second = pair_take(img_swap(send, 1 << bit), first, second)
-        return jnp.squeeze(total_of(first), 0), jnp.squeeze(total_of(second), 0)
-
-    down_grad = jnp.concatenate(finish(down_in, down_a, down_b), axis=0)
-    up_weight_grad = jnp.concatenate(finish(up_in, up_a, up_b), axis=1)
-    query_key, value_output = finish(four_in, four_a, four_b)
+            z_take(first, second, img_swap(z_send(first, second, bit - 2), 1 << bit))
+
+    rest(down_a, down_b, down_in)
+    rest(up_a, up_b, up_in)
+    down_grad, up_weight_grad = fold(
+        place,
+        [
+            ([down_a.whole(), down_b.whole()], "rows"),
+            ([up_a.whole(), up_b.whole()], "columns"),
+        ],
+        f32,
+    )
     for bit in range(4, bits):
-        late = late + img_swap(late, 1 << bit)
-    sums, rank = small_take(sums, rank, small_in)
+        message = merge(message, img_swap(message, 1 << bit), True)
+    sums, rank = message[:TOP], message[TOP:]
+    rest(four_a, four_b, four_in)
+    gains = gains + gains_in
     for bit in range(4, bits):
-        sums, rank = small_take(sums, rank, small_step(sums, rank, bit))
+        gains = gains + img_swap(gains, 1 << bit)
+    query_weight_grad, key_weight_grad, value_weight_grad, output_grad = fold(
+        place,
+        [([group.whole(m)], None) for group in (four_a, four_b) for m in range(2)],
+        f32,
+    )
     input_grad = input_grad[None]
 
     block = width // images
@@ -801,14 +1072,14 @@
     return (
         block_out,
         input_grad,
-        query_key[0],
-        query_key[1],
-        value_output[0],
-        value_output[1],
+        query_weight_grad,
+        key_weight_grad,
+        value_weight_grad,
+        output_grad,
         up_weight_grad,
         down_grad,
-        own_rows(late[1]),
-        own_rows(late[0]),
+        own_rows(gains[1]),
+        own_rows(gains[0]),
         own_rows(sums[HEADS]),
         probe_grad,
         query_pool_grad,

time: 230 us -> 235 us (1.022)
  Pallas kernels: 44.2 us -> 115 us
  other arithmetic: 32.1 us -> 8.19 us
  local copies, waits for them, and re-layouts: 33.6 us -> 15.7 us
  matrix products: 35.8 us -> 19.8 us
  waiting for transfers between devices: 44.5 us -> 35.9 us
    pallas_call x2 -> x24, Pallas kernels: 9.02 us -> 79.9 us  [the longest x14 42.4 us: fold(): pl.pallas_call(functools.partial(fold_kernel, tuple(plan)), grid_spec=plt...]
    dot_general x8 -> x0, matrix products: 16.6 us -> none  [back_dot(): lax.dot_general(left_side, right_side, (((1,), (1,)), ((), ())), preferre...]
    convert_element_type x20 -> x0, other arithmetic: 14 us -> none  [the longest x6 5.81 us: seq_send(): send = total_of([pick(part, 1 - mine, axis) for part in parts]).astype(bf16)]
    dynamic_slice x22 -> x0, local copies, waits for them, and re-layouts: 12.4 us -> none  [pick(): return lax.dynamic_index_in_dim(value, index, axis, keepdims=False)]
    ppermute x27, waiting for transfers between devices: 38.8 us -> 30.8 us  [img_swap(): return lax.ppermute(value, 'img', [(i, i ^ mask) for i in range(count)])]
    slice x13 -> x3, local copies, waits for them, and re-layouts: 4.96 us -> 0.01 us  [the longest x1 0.01 us: shards(): gains[0]]
    add x19 -> x5, other arithmetic: 3.8 us -> 0.03 us  [shards(): gains = gains + gains_in]
    concatenate x4, other arithmetic: 2.53 us -> 0.08 us  [gather_more(): return jnp.concatenate([gathered, img_swap(gathered, 1 << bit)], axis=0)]
  transfers between devices with their start and end apart: 38 -> 38, of which waited for: 10 -> 6; matrix products, arithmetic and copies ran while one was open for 37% -> 13% of each run, Pallas kernels for 13% -> 42%
where the time goes in v2:
time: 235 us; the launch traced here: 234 us
  Pallas kernels  115 us (49%)
  waiting for transfers between devices  35.9 us (15%)
  starting transfers between devices  35.3 us (15%)
  matrix products  19.8 us (8%)
  local copies, waits for them, and re-layouts  15.7 us (7%)
  other arithmetic  8.19 us (3%)
  between operations  3.32 us (1%)
    pallas_call x14, Pallas kernels, fold(): pl.pallas_call(functools.partial(fold_kernel, tuple(plan)), grid_spec=plt...  42.4 us
    ppermute x27, waiting for transfers between devices, img_swap(): return lax.ppermute(value, 'img', [(i, i ^ mask) for i in range(count)])  30.8 us
    ppermute x27, starting transfers between devices, img_swap(): return lax.ppermute(value, 'img', [(i, i ^ mask) for i in range(count)])  23 us
    dot_general x8, matrix products, low_dot(): return jnp.dot(left_side, right_side, preferred_element_type=f32)  13.9 us
    ppermute x11, starting transfers between devices, seq_swap(): return lax.ppermute(value, 'seq', [(0, 1), (1, 0)])  12.3 us
    pallas_call x1, Pallas kernels, attend_back(): pl.pallas_call(attend_back_kernel, grid=(pairs,), in_specs=[row_spec] * 6...  10.3 us
    pallas_call x1, Pallas kernels, up_back_call(): pl.pallas_call(functools.partial(up_back_kernel, block), grid=(4,), in_sp...  9.44 us
    pallas_call x5, Pallas kernels, merge(): pl.pallas_call(functools.partial(merge_kernel, gather), out_shape=jax.Sha...  8.47 us
  transfers between devices with their start and end apart: 38, of which 6 were waited for; matrix products, arithmetic and copies ran while one was open for 13% of the time, Pallas kernels for 42%

profile of v2, /device:TPU:0, one launch (start us, length us, event | category | flops | bytes accessed | tf_op | source)
XLA Modules:
  0.0 233.5 jit_solution(5487099320128548001)
XLA Ops:
  0.7 3.1 %collective-permute-start = (bf16[256,768]{1,0:T(8,128)(2,1)}, bf16[256,768]{1,0:T(8,128)(2,1)S(1)}, u32[]{:S(2)}, u32[]{:S(2)}) collective-permute-start(bf16[256,768]{1,0:T(8,128)(2,1)} %bitcast.220), channel_id=1, source_target_pairs={{0,1},{1,0},{2,3},{3,2},{4,5},{5,4},{6,7},{7,6},{8,9},{9,8},{10,11... | collective-permute-start | bytes 1179656 | tf_op jit(solution)/shard_map/ppermute | solution.py:452
  14.3 3.0 %probe_rows.1 = (f32[1,768]{1,0:T(1,128)}, f32[16,768]{1,0:T(8,128)}) custom-call(f32[1,768]{1,0:T(1,128)} %broadcast_in_dim.19.probe_ref, bf16[768,768]{1,0:T(8,128)(2,1)} %query_ref.1, bf16[768,768]{1,0:T(8,128)(2,1)} %key_ref.1), custom_call_target="tpu_custom_call" | custom-call | flops 1024 | bytes 1024 | tf_op jit(solution)/shard_map/probe_rows/pallas_call | solution.py:85
  25.2 8.2 %attend.1 = (bf16[256,768]{1,0:T(8,128)(2,1)}, f32[6,256,2]{2,1,0:T(8,128)}) custom-call(bf16[256,768]{1,0:T(8,128)(2,1)} %convolution_convert_fusion.4.q_ref, bf16[256,768]{1,0:T(8,128)(2,1)} %convolution_convert_fusion.3.ka_ref, bf16[256,768]{1,0:T(8,128)(2,1)} %convolution_convert_fusion.1.kb_ref, bf16[256,768]{1,0:T(8,128)(2,1)} %convolution_convert_fusion.2.va_ref, ...), custom_call_target="tpu_custom_call" | custom-call | flops 1024 | bytes 1024 | tf_op jit(solution)/shard_map/attend/pallas_call | solution.py:300
  35.4 2.7 %collective-permute-start.5 = (f32[8,5,768]{2,1,0:T(8,128)S(1)}, f32[8,5,768]{2,1,0:T(8,128)S(1)}, u32[]{:S(2)}, u32[]{:S(2)}) collective-permute-start(f32[8,5,768]{2,1,0:T(8,128)S(1)} %pad_maximum_fusion.1), channel_id=1, source_target_pairs={{0,16},{2,18},{4,20},{6,22},{8,24},{10,26},{12,28},{14,30},{16,0},... | collective-permute-start | bytes 368648 | tf_op jit(solution)/shard_map/ppermute | solution.py:448
  39.2 3.6 %fusion.7 = (bf16[256,3072]{1,0:T(8,128)(2,1)S(1)}, f32[256,3072]{1,0:T(8,128)}) fusion(bf16[256,768]{1,0:T(8,128)(2,1)S(1)} %get-tuple-element.307.low_ref, bf16[768,3072]{1,0:T(8,128)(2,1)S(1)} %copy-done.14), kind=kOutput, calls=%fused_computation.8 | convolution fusion | flops 1215037440 | bytes 9830400 | tf_op jit(solution)/shard_map/dot_general | solution.py:32
  48.3 3.8 %collective-permute-done.4.other_ref = f32[16,896]{1,0:T(8,128)S(1)} collective-permute-done((f32[16,896]{1,0:T(8,128)}, f32[16,896]{1,0:T(8,128)S(1)}, u32[]{:S(2)}, u32[]{:S(2)}) %collective-permute-start.4) | collective-permute-done | bytes 57376 | tf_op jit(solution)/shard_map/ppermute | solution.py:452
  52.9 5.7 %pool_back.1 = (f32[256,768]{1,0:T(8,128)}, bf16[256,768]{1,0:T(8,128)(2,1)}, f32[24,768]{1,0:T(8,128)}) custom-call(s32[5]{0:T(128)} %stack.23.place_ref, s32[1]{0:T(128)S(6)} %copy.92.count_ref, s32[1,80]{1,0:T(1,128)} %pairs_ref.1, f32[1]{0:T(128)} %bitcast.145.temp_ref, f32[1]{0:T(128)} %bitcast.146.bias_ref, f32[16,896]{1,0:T(8,128)} %get-tuple-element.172.own_ref, ...), custom_call_target="tpu_custom_call" | custom-call | flops 1024 | bytes 1024 | tf_op jit(solution)/shard_map/pool_back/pallas_call | solution.py:260
  58.6 4.4 %wgrad.1 = (bf16[2,2,8,96,384]{4,3,2,1,0:T(8,128)(2,1)}, bf16[2,2,8,96,384]{4,3,2,1,0:T(8,128)(2,1)}) custom-call(s32[5]{0:T(128)} %stack.23.place_ref, bf16[256,3072]{1,0:T(8,128)(2,1)} %copy-done.29, bf16[256,768]{1,0:T(8,128)(2,1)} %get-tuple-element.183.right_ref.grad_ref), custom_call_target="tpu_custom_call" | custom-call | flops 1024 | bytes 1024 | tf_op jit(solution)/shard_map/wgrad/pallas_call | solution.py:389
  63.6 6.6 %gelu_back.1.du_ref = bf16[256,3072]{1,0:T(8,128)(2,1)} custom-call(bf16[256,768]{1,0:T(8,128)(2,1)} %get-tuple-element.183.right_ref.grad_ref, bf16[3072,768]{1,0:T(8,128)(2,1)} %down_ref.1, f32[256,3072]{1,0:T(8,128)} %get-tuple-element.321.up_ref), custom_call_target="tpu_custom_call" | custom-call | flops 1024 | bytes 1024 | tf_op jit(solution)/shard_map/gelu_back/pallas_call | solution.py:637
  72.5 3.6 %fold.14 = (bf16[8,96,384]{2,1,0:T(8,128)(2,1)}, bf16[2,4,96,384]{3,2,1,0:T(8,128)(2,1)}) custom-call(s32[5]{0:T(128)} %stack.23.place_ref, bf16[2,2,8,96,384]{4,3,2,1,0:T(8,128)(2,1)} %get-tuple-element.188.refs_0_, bf16[2,2,8,96,384]{4,3,2,1,0:T(8,128)(2,1)} %copy-done.1, bf16[2,2,4,2,96,384]{5,4,3,2,1,0:T(8,128)(2,1)} %bitcast.169, ...), custom_call_target="tpu_custom_call" | custom-call | flops 1024 | bytes 1024 | tf_op jit(solution)/shard_map/fold/pallas_call | solution.py:534
  77.7 9.4 %up_back.1 = (bf16[2,2,8,48,768]{4,3,2,1,0:T(8,128)(2,1)}, bf16[2,2,8,48,768]{4,3,2,1,0:T(8,128)(2,1)}, f32[256,768]{1,0:T(8,128)}, bf16[256,768]{1,0:T(8,128)(2...) custom-call(s32[5]{0:T(128)} %stack.23.place_ref, bf16[256,768]{1,0:T(8,128)(2,1)} %copy-done.28, ...), custom_call_target="tpu_custom_call" | custom-call | flops 1024 | bytes 1024 | tf_op jit(solution)/shard_map/up_back/pallas_call | solution.py:704
  91.7 10.3 %attend_back.1 = (bf16[256,768]{1,0:T(8,128)(2,1)}, bf16[512,768]{1,0:T(8,128)(2,1)}, bf16[512,768]{1,0:T(8,128)(2,1)}) custom-call(bf16[256,768]{1,0:T(8,128)(2,1)} %convolution_convert_fusion.4.q_ref, bf16[256,768]{1,0:T(8,128)(2,1)} %convolution_convert_fusion.3.ka_ref, bf16[256,768]{1,0:T(8,128)(2,1)} %convolution_convert_fusion.1.kb_ref, ...), custom_call_target="tpu_custom_call" | custom-call | flops 1024 | bytes 1024 | tf_op jit(solution)/shard_map/attend_back/pallas_call | solution.py:348
  103.5 3.4 %fold.15 = (bf16[2,4,48,768]{3,2,1,0:T(8,128)(2,1)}, bf16[8,48,768]{2,1,0:T(8,128)(2,1)}) custom-call(s32[5]{0:T(128)} %stack.23.place_ref, bf16[2,2,4,2,48,768]{5,4,3,2,1,0:T(8,128)(2,1)} %bitcast.187, bf16[2,2,4,2,48,768]{5,4,3,2,1,0:T(8,128)(2,1)} %bitcast.196, bf16[2,2,8,48,768]{4,3,2,1,0:T(8,128)(2,1)} %get-tuple-element.196.refs_2_, ...), custom_call_target="tpu_custom_call" | custom-call | flops 1024 | bytes 1024 | tf_op jit(solution)/shard_map/fold/pallas_call | solution.py:534
  106.9 3.4 %other_in.1 = bf16[256,768]{1,0:T(8,128)(2,1)} custom-call(bf16[512,768]{1,0:T(8,128)(2,1)} %get-tuple-element.223.dk_ref, bf16[512,768]{1,0:T(8,128)(2,1)} %get-tuple-element.224.dv_ref, bf16[768,768]{1,0:T(8,128)(2,1)} %wk_ref.3, bf16[768,768]{1,0:T(8,128)(2,1)} %wv_ref.3), custom_call_target="tpu_custom_call" | custom-call | flops 1024 | bytes 1024 | tf_op jit(solution)/shard_map/other_in/pallas_call | solution.py:748
  110.4 5.7 %wgrad_four.1 = (bf16[2,2,8,2,48,384]{5,4,3,2,1,0:T(8,128)(2,1)}, bf16[2,2,8,2,48,384]{5,4,3,2,1,0:T(8,128)(2,1)}) custom-call(s32[5]{0:T(128)} %stack.23.place_ref, bf16[256,768]{1,0:T(8,128)(2,1)} %copy-done.8, bf16[256,768]{1,0:T(8,128)(2,1)} %copy-done.12, bf16[256,768]{1,0:T(8,128)(2,1)} %get-tuple-element.170.a_ref, ...), custom_call_target="tpu_custom_call" | custom-call | flops 1024 | bytes 1024 | tf_op jit(solution)/shard_map/wgrad_four/pallas_call | solution.py:431
  120.3 3.0 %fold.16 = (bf16[4,96,384]{2,1,0:T(8,128)(2,1)}, bf16[4,96,384]{2,1,0:T(8,128)(2,1)}) custom-call(s32[5]{0:T(128)} %stack.23.place_ref, bf16[2,2,4,2,96,384]{5,4,3,2,1,0:T(8,128)(2,1)} %bitcast.170, bf16[2,2,4,2,96,384]{5,4,3,2,1,0:T(8,128)(2,1)} %bitcast.179, bf16[4,2,96,384]{3,2,1,0:T(8,128)(2,1)} %bitcast.214, bf16[2,2,4,2,96,384]{5,4,3,2,1,0:T(8,128)(2,1)} %bitcast.171, ...), custom_call_target="tpu_custom_call" | custom-call | flops 1024 | bytes 1024 | tf_op jit(solution)/shard_map/fold/pallas_call | solution.py:534
  123.3 11.0 %collective-permute-done.15.other_ref = f32[32,768]{1,0:T(8,128)} collective-permute-done((f32[32,768]{1,0:T(8,128)}, f32[32,768]{1,0:T(8,128)}, u32[]{:S(2)}, u32[]{:S(2)}) %collective-permute-start.15) | collective-permute-done | bytes 98336 | tf_op jit(solution)/shard_map/ppermute | solution.py:448
  137.4 3.6 %fold.17 = (bf16[2,4,2,48,384]{4,3,2,1,0:T(8,128)(2,1)}, bf16[8,2,48,384]{3,2,1,0:T(8,128)(2,1)}) custom-call(s32[5]{0:T(128)} %stack.23.place_ref, bf16[2,2,4,2,2,48,384]{6,5,4,3,2,1,0:T(8,128)(2,1)} %bitcast.147, bf16[2,2,4,2,2,48,384]{6,5,4,3,2,1,0:T(8,128)(2,1)} %bitcast.158, bf16[2,2,8,2,48,384]{5,4,3,2,1,0:T(8,128)(2,1)} %get-tuple-element.240.refs_2_, ...), custom_call_target="tpu_custom_call" | custom-call | flops 1024 | bytes 1024 | tf_op jit(solution)/shard_map/fold/pallas_call | solution.py:534
  146.8 3.0 %fold.18 = (bf16[4,48,768]{2,1,0:T(8,128)(2,1)}, bf16[4,48,768]{2,1,0:T(8,128)(2,1)}) custom-call(s32[5]{0:T(128)} %stack.23.place_ref, bf16[2,2,4,2,48,768]{5,4,3,2,1,0:T(8,128)(2,1)} %bitcast.188, bf16[2,2,4,2,48,768]{5,4,3,2,1,0:T(8,128)(2,1)} %bitcast.197, bf16[2,4,48,768]{3,2,1,0:T(8,128)(2,1)} %collective-permute-done.10.refs_2_.refs_14_, ...), custom_call_target="tpu_custom_call" | custom-call | flops 1024 | bytes 1024 | tf_op jit(solution)/shard_map/fold/pallas_call | solution.py:534
  149.8 5.2 %own_in.1 = (f32[256,768]{1,0:T(8,128)}, f32[8,768]{1,0:T(8,128)}) custom-call(bf16[256,768]{1,0:T(8,128)(2,1)} %get-tuple-element.252.dq_ref, bf16[512,768]{1,0:T(8,128)(2,1)} %get-tuple-element.223.dk_ref, bf16[512,768]{1,0:T(8,128)(2,1)} %get-tuple-element.224.dv_ref, bf16[768,768]{1,0:T(8,128)(2,1)} %wq_ref.1, bf16[768,768]{1,0:T(8,128)(2,1)} %wk_ref.3, ...), custom_call_target="tpu_custom_call" | custom-call | flops 1024 | bytes 1024 | tf_op jit(solution)/shard_map/own_in/pallas_call | solution.py:776
  155.0 7.2 %collective-permute-done.17.refs_3_ = bf16[4,96,384]{2,1,0:T(8,128)(2,1)S(1)} collective-permute-done((bf16[4,96,384]{2,1,0:T(8,128)(2,1)}, bf16[4,96,384]{2,1,0:T(8,128)(2,1)S(1)}, u32[]{:S(2)}, u32[]{:S(2)}) %collective-permute-start.17) | collective-permute-done | bytes 294944 | tf_op jit(solution)/shard_map/ppermute | solution.py:448
  164.5 3.0 %fold.19 = bf16[2,2,96,384]{3,2,1,0:T(8,128)(2,1)} custom-call(s32[5]{0:T(128)} %stack.23.place_ref, bf16[2,2,2,2,1,2,96,384]{7,6,5,4,3,2,1,0:T(8,128)(2,1)} %bitcast.172, bf16[2,2,2,2,1,2,96,384]{7,6,5,4,3,2,1,0:T(8,128)(2,1)} %bitcast.181, bf16[2,2,1,2,96,384]{5,4,3,2,1,0:T(8,128)(2,1)} %bitcast.215, bf16[2,2,1,96,384]{4,3,2,1,0:T(8,128)(2,1)} %bitcast.231, ...), custom_call_target="tpu_custom_call" | custom-call | flops 1024 | bytes 1024 | tf_op jit(solution)/shard_map/fold/pallas_call | solution.py:534
  172.2 3.1 %fold.20 = (bf16[4,2,48,384]{3,2,1,0:T(8,128)(2,1)}, bf16[4,2,48,384]{3,2,1,0:T(8,128)(2,1)}) custom-call(s32[5]{0:T(128)} %stack.23.place_ref, bf16[2,2,4,2,2,48,384]{6,5,4,3,2,1,0:T(8,128)(2,1)} %bitcast.148, bf16[2,2,4,2,2,48,384]{6,5,4,3,2,1,0:T(8,128)(2,1)} %bitcast.159, bf16[2,4,2,48,384]{4,3,2,1,0:T(8,128)(2,1)} %copy-done.5, ...), custom_call_target="tpu_custom_call" | custom-call | flops 1024 | bytes 1024 | tf_op jit(solution)/shard_map/fold/pallas_call | solution.py:534
  178.2 2.9 %fold.21 = bf16[2,2,48,768]{3,2,1,0:T(8,128)(2,1)} custom-call(s32[5]{0:T(128)} %stack.23.place_ref, bf16[2,2,2,2,1,2,48,768]{7,6,5,4,3,2,1,0:T(8,128)(2,1)} %bitcast.190, bf16[2,2,2,2,1,2,48,768]{7,6,5,4,3,2,1,0:T(8,128)(2,1)} %bitcast.199, bf16[2,2,2,1,48,768]{5,4,3,2,1,0:T(8,128)(2,1)} %bitcast.38.refs_2_, bf16[2,2,1,48,768]{4,3,2,1,0:T(8,128)(2,1)} %bitcast.235, ...), custom_call_target="tpu_custom_call" | custom-call | flops 1024 | bytes 1024 | tf_op jit(solution)/shard_map/fold/pallas_call | solution.py:534
  182.7 2.6 %fold.22 = bf16[2,1,96,384]{3,2,1,0:T(8,128)(2,1)} custom-call(s32[5]{0:T(128)} %stack.23.place_ref, bf16[2,2,1,2,2,2,96,384]{7,6,5,4,3,2,1,0:T(8,128)(2,1)} %bitcast.174, bf16[2,2,1,2,2,2,96,384]{7,6,5,4,3,2,1,0:T(8,128)(2,1)} %bitcast.183, bf16[1,2,2,2,96,384]{5,4,3,2,1,0:T(8,128)(2,1)} %bitcast.216, bf16[1,2,2,96,384]{4,3,2,1,0:T(8,128)(2,1)} %bitcast.232, ...), custom_call_target="tpu_custom_call" | custom-call | flops 1024 | bytes 1024 | tf_op jit(solution)/shard_map/fold/pallas_call | solution.py:534
  186.2 3.0 %fold.23 = bf16[2,2,2,48,384]{4,3,2,1,0:T(8,128)(2,1)} custom-call(s32[5]{0:T(128)} %stack.23.place_ref, bf16[2,2,2,2,1,2,2,48,384]{8,7,6,5,4,3,2,1,0:T(8,128)(2,1)} %bitcast.150, bf16[2,2,2,2,1,2,2,48,384]{8,7,6,5,4,3,2,1,0:T(8,128)(2,1)} %bitcast.161, bf16[2,2,2,1,2,48,384]{6,5,4,3,2,1,0:T(8,128)(2,1)} %bitcast.205, ...), custom_call_target="tpu_custom_call" | custom-call | flops 1024 | bytes 1024 | tf_op jit(solution)/shard_map/fold/pallas_call | solution.py:534
  191.8 2.6 %collective-permute-start.34 = (bf16[2,1,96,384]{3,2,1,0:T(8,128)(2,1)S(1)}, bf16[2,1,96,384]{3,2,1,0:T(8,128)(2,1)S(1)}, u32[]{:S(2)}, u32[]{:S(2)}) collective-permute-start(bf16[2,1,96,384]{3,2,1,0:T(8,128)(2,1)S(1)} %copy-done.37), channel_id=1, source_target_pairs={{0,16},{2,18},{4,20},{6,22},{8,24},{10,26},{12,28},{14,30},{16,0},... | collective-permute-start | bytes 442376 | tf_op jit(solution)/shard_map/ppermute | solution.py:448
  194.4 2.8 %fold.24 = bf16[2,1,48,768]{3,2,1,0:T(8,128)(2,1)} custom-call(s32[5]{0:T(128)} %stack.23.place_ref, bf16[2,2,1,2,2,2,48,768]{7,6,5,4,3,2,1,0:T(8,128)(2,1)} %bitcast.192, bf16[2,2,1,2,2,2,48,768]{7,6,5,4,3,2,1,0:T(8,128)(2,1)} %bitcast.201, bf16[2,1,2,2,48,768]{5,4,3,2,1,0:T(8,128)(2,1)} %bitcast.62.refs_2_, bf16[1,2,2,48,768]{4,3,2,1,0:T(8,128)(2,1)} %bitcast.236, ...), custom_call_target="tpu_custom_call" | custom-call | flops 1024 | bytes 1024 | tf_op jit(solution)/shard_map/fold/pallas_call | solution.py:534
  197.2 11.2 %collective-permute-done.32.other_ref = f32[80,768]{1,0:T(8,128)S(1)} collective-permute-done((f32[80,768]{1,0:T(8,128)S(1)}, f32[80,768]{1,0:T(8,128)S(1)}, u32[]{:S(2)}, u32[]{:S(2)}) %collective-permute-start.32) | collective-permute-done | bytes 245792 | tf_op jit(solution)/shard_map/ppermute | solution.py:448
  218.7 2.6 %fold.25 = bf16[2,1,2,48,384]{4,3,2,1,0:T(8,128)(2,1)} custom-call(s32[5]{0:T(128)} %stack.23.place_ref, bf16[2,2,1,2,2,2,2,48,384]{8,7,6,5,4,3,2,1,0:T(8,128)(2,1)} %bitcast.152, bf16[2,2,1,2,2,2,2,48,384]{8,7,6,5,4,3,2,1,0:T(8,128)(2,1)} %bitcast.163, bf16[2,1,2,2,2,48,384]{6,5,4,3,2,1,0:T(8,128)(2,1)} %bitcast.206, ...), custom_call_target="tpu_custom_call" | custom-call | flops 1024 | bytes 1024 | tf_op jit(solution)/shard_map/fold/pallas_call | solution.py:534
  221.4 2.8 %collective-permute-start.33 = (bf16[2,1,2,48,384]{4,3,2,1,0:T(8,128)(2,1)}, bf16[2,1,2,48,384]{4,3,2,1,0:T(8,128)(2,1)S(1)}, u32[]{:S(2)}, u32[]{:S(2)}) collective-permute-start(bf16[2,1,2,48,384]{4,3,2,1,0:T(8,128)(2,1)} %fold.25), channel_id=1, source_target_pairs={{0,16},{2,18},{4,20},{6,22},{8,24},{10,26},{12,28},{14,30},{16,0},... | collective-permute-start | bytes 442376 | tf_op jit(solution)/shard_map/ppermute | solution.py:448
  225.1 3.1 %fold.27 = (f32[192,384]{1,0:T(8,128)}, f32[48,1536]{1,0:T(8,128)}) custom-call(s32[5]{0:T(128)} %stack.23.place_ref, bf16[2,2,4,2,96,384]{5,4,3,2,1,0:T(8,128)(2,1)} %bitcast.176, bf16[2,2,4,2,96,384]{5,4,3,2,1,0:T(8,128)(2,1)} %bitcast.185, bf16[4,2,96,384]{3,2,1,0:T(8,128)(2,1)} %bitcast.217, bf16[4,96,384]{2,1,0:T(8,128)(2,1)} %copy-done.22, ...), custom_call_target="tpu_custom_call" | custom-call | flops 1024 | bytes 1024 | tf_op jit(solution)/shard_map/fold/pallas_call | solution.py:534
  (248 shorter events, 80.5 us)
Async XLA Ops:
  0.7 19.8 %collective-permute-start = (bf16[256,768]{1,0:T(8,128)(2,1)}, bf16[256,768]{1,0:T(8,128)(2,1)S(1)}, u32[]{:S(2)}, u32[]{:S(2)}) collective-permute-start(bf16[256,768]{1,0:T(8,128)(2,1)} %bitcast.220), channel_id=1, source_target_pairs={{0,1},{1,0},{2,3},{3,2},{4,5},{5,4},{6,7},{7,6},{8,9},{9,8},{10,11... | collective-permute-start | bytes 1179656 | tf_op jit(solution)/shard_map/ppermute | solution.py:452
  10.9 9.6 %collective-permute-start.2 = (f32[2,5,768]{2,1,0:T(8,128)S(1)}, f32[2,5,768]{2,1,0:T(8,128)S(1)}, u32[]{:S(2)}, u32[]{:S(2)}) collective-permute-start(f32[2,5,768]{2,1,0:T(8,128)S(1)} %pad_maximum_fusion.3), channel_id=1, source_target_pairs={{0,4},{2,6},{4,0},{6,2},{8,12},{10,14},{12,8},{14,10},{16,20},{18,... | collective-permute-start | bytes 92168 | tf_op jit(solution)/shard_map/ppermute | solution.py:448
  22.4 11.0 %collective-permute-start.3 = (f32[4,5,768]{2,1,0:T(8,128)S(1)}, f32[4,5,768]{2,1,0:T(8,128)S(1)}, u32[]{:S(2)}, u32[]{:S(2)}) collective-permute-start(f32[4,5,768]{2,1,0:T(8,128)S(1)} %pad_maximum_fusion.2), channel_id=1, source_target_pairs={{0,8},{2,10},{4,12},{6,14},{8,0},{10,2},{12,4},{14,6},{16,24},{18,... | collective-permute-start | bytes 184328 | tf_op jit(solution)/shard_map/ppermute | solution.py:448
  35.4 12.8 %collective-permute-start.5 = (f32[8,5,768]{2,1,0:T(8,128)S(1)}, f32[8,5,768]{2,1,0:T(8,128)S(1)}, u32[]{:S(2)}, u32[]{:S(2)}) collective-permute-start(f32[8,5,768]{2,1,0:T(8,128)S(1)} %pad_maximum_fusion.1), channel_id=1, source_target_pairs={{0,16},{2,18},{4,20},{6,22},{8,24},{10,26},{12,28},{14,30},{16,0},... | collective-permute-start | bytes 368648 | tf_op jit(solution)/shard_map/ppermute | solution.py:448
  76.1 11.0 %collective-permute-start.8 = (f32[24,768]{1,0:T(8,128)S(1)}, f32[24,768]{1,0:T(8,128)S(1)}, u32[]{:S(2)}, u32[]{:S(2)}) collective-permute-start(f32[24,768]{1,0:T(8,128)S(1)} %copy-done.34), channel_id=1, source_target_pairs={{0,2},{2,0},{4,6},{6,4},{8,10},{10,8},{12,14},{14,12},{16,18},{18,... | collective-permute-start | bytes 221192 | tf_op jit(solution)/shard_map/ppermute | solution.py:448
  87.7 14.3 %collective-permute-start.9 = (bf16[2,2,8,48,768]{4,3,2,1,0:T(8,128)(2,1)}, bf16[2,2,8,48,768]{4,3,2,1,0:T(8,128)(2,1)S(1)}, u32[]{:S(2)}, u32[]{:S(2)}) collective-permute-start(bf16[2,2,8,48,768]{4,3,2,1,0:T(8,128)(2,1)} %get-tuple-element.206), channel_id=1, source_target_pairs={{0,2},{2,0},{4,6},{6,4},{8,10},{10,8},{12,14},{14,12},{16,18},{18,... | collective-permute-start | bytes 7077896 | tf_op jit(solution)/shard_map/ppermute | solution.py:448
  88.1 27.9 %collective-permute-start.12 = (bf16[8,96,384]{2,1,0:T(8,128)(2,1)}, bf16[8,96,384]{2,1,0:T(8,128)(2,1)S(1)}, u32[]{:S(2)}, u32[]{:S(2)}) collective-permute-start(bf16[8,96,384]{2,1,0:T(8,128)(2,1)} %get-tuple-element.227), channel_id=1, source_target_pairs={{0,1},{1,0},{2,3},{3,2},{4,5},{5,4},{6,7},{7,6},{8,9},{9,8},{10,11... | collective-permute-start | bytes 1769480 | tf_op jit(solution)/shard_map/ppermute | solution.py:452
  89.6 26.4 %collective-permute-start.13 = (bf16[2,4,96,384]{3,2,1,0:T(8,128)(2,1)}, bf16[2,4,96,384]{3,2,1,0:T(8,128)(2,1)S(1)}, u32[]{:S(2)}, u32[]{:S(2)}) collective-permute-start(bf16[2,4,96,384]{3,2,1,0:T(8,128)(2,1)} %get-tuple-element.228), channel_id=1, source_target_pairs={{0,4},{2,6},{4,0},{6,2},{8,12},{10,14},{12,8},{14,10},{16,20},{18,... | collective-permute-start | bytes 1769480 | tf_op jit(solution)/shard_map/ppermute | solution.py:448
  116.1 19.9 %collective-permute-start.14 = (bf16[2,2,8,2,48,384]{5,4,3,2,1,0:T(8,128)(2,1)}, bf16[2,2,8,2,48,384]{5,4,3,2,1,0:T(8,128)(2,1)S(1)}, u32[]{:S(2)}, u32[]{:S(2)}) collective-permute-start(bf16[2,2,8,2,48,384]{5,4,3,2,1,0:T(8,128)(2,1)} %get-tuple-element.230), channel_id=1, source_target_pairs={{0,2},{2,0},{4,6},{6,4},{8,10},{10,8},{12,14},{14,12},{16,18},{18,... | collective-permute-start | bytes 7077896 | tf_op jit(solution)/shard_map/ppermute | solution.py:448
  116.2 27.3 %collective-permute-start.10 = (bf16[2,4,48,768]{3,2,1,0:T(8,128)(2,1)}, bf16[2,4,48,768]{3,2,1,0:T(8,128)(2,1)}, u32[]{:S(2)}, u32[]{:S(2)}) collective-permute-start(bf16[2,4,48,768]{3,2,1,0:T(8,128)(2,1)} %get-tuple-element.216), channel_id=1, source_target_pairs={{0,4},{2,6},{4,0},{6,2},{8,12},{10,14},{12,8},{14,10},{16,20},{18,... | collective-permute-start | bytes 1769480 | tf_op jit(solution)/shard_map/ppermute | solution.py:448
  117.7 27.3 %collective-permute-start.11 = (bf16[8,48,768]{2,1,0:T(8,128)(2,1)}, bf16[8,48,768]{2,1,0:T(8,128)(2,1)}, u32[]{:S(2)}, u32[]{:S(2)}) collective-permute-start(bf16[8,48,768]{2,1,0:T(8,128)(2,1)} %get-tuple-element.217), channel_id=1, source_target_pairs={{0,1},{1,0},{2,3},{3,2},{4,5},{5,4},{6,7},{7,6},{8,9},{9,8},{10,11... | collective-permute-start | bytes 1769480 | tf_op jit(solution)/shard_map/ppermute | solution.py:452
  118.2 24.7 %collective-permute-start.16 = (bf16[256,768]{1,0:T(8,128)(2,1)}, bf16[256,768]{1,0:T(8,128)(2,1)}, u32[]{:S(2)}, u32[]{:S(2)}) collective-permute-start(bf16[256,768]{1,0:T(8,128)(2,1)} %other_in.1), channel_id=1, source_target_pairs={{0,1},{1,0},{2,3},{3,2},{4,5},{5,4},{6,7},{7,6},{8,9},{9,8},{10,11... | collective-permute-start | bytes 1179656 | tf_op jit(solution)/shard_map/ppermute | solution.py:452
  119.7 14.6 %collective-permute-start.15 = (f32[32,768]{1,0:T(8,128)}, f32[32,768]{1,0:T(8,128)}, u32[]{:S(2)}, u32[]{:S(2)}) collective-permute-start(f32[32,768]{1,0:T(8,128)} %merge.6.own_ref), channel_id=1, source_target_pairs={{0,4},{2,6},{4,0},{6,2},{8,12},{10,14},{12,8},{14,10},{16,20},{18,... | collective-permute-start | bytes 294920 | tf_op jit(solution)/shard_map/ppermute | solution.py:448
  140.9 27.1 %collective-permute-start.19 = (bf16[2,4,2,48,384]{4,3,2,1,0:T(8,128)(2,1)}, bf16[2,4,2,48,384]{4,3,2,1,0:T(8,128)(2,1)S(1)}, u32[]{:S(2)}, u32[]{:S(2)}) collective-permute-start(bf16[2,4,2,48,384]{4,3,2,1,0:T(8,128)(2,1)} %get-tuple-element.261), channel_id=1, source_target_pairs={{0,4},{2,6},{4,0},{6,2},{8,12},{10,14},{12,8},{14,10},{16,20},{18,... | collective-permute-start | bytes 1769480 | tf_op jit(solution)/shard_map/ppermute | solution.py:448
  142.4 28.9 %collective-permute-start.20 = (bf16[8,2,48,384]{3,2,1,0:T(8,128)(2,1)}, bf16[8,2,48,384]{3,2,1,0:T(8,128)(2,1)S(1)}, u32[]{:S(2)}, u32[]{:S(2)}) collective-permute-start(bf16[8,2,48,384]{3,2,1,0:T(8,128)(2,1)} %get-tuple-element.262), channel_id=1, source_target_pairs={{0,1},{1,0},{2,3},{3,2},{4,5},{5,4},{6,7},{7,6},{8,9},{9,8},{10,11... | collective-permute-start | bytes 1769480 | tf_op jit(solution)/shard_map/ppermute | solution.py:452
  142.9 19.3 %collective-permute-start.17 = (bf16[4,96,384]{2,1,0:T(8,128)(2,1)}, bf16[4,96,384]{2,1,0:T(8,128)(2,1)S(1)}, u32[]{:S(2)}, u32[]{:S(2)}) collective-permute-start(bf16[4,96,384]{2,1,0:T(8,128)(2,1)} %get-tuple-element.258), channel_id=1, source_target_pairs={{0,4},{2,6},{4,0},{6,2},{8,12},{10,14},{12,8},{14,10},{16,20},{18,... | collective-permute-start | bytes 884744 | tf_op jit(solution)/shard_map/ppermute | solution.py:448
  143.5 20.0 %collective-permute-start.18 = (bf16[4,96,384]{2,1,0:T(8,128)(2,1)S(1)}, bf16[4,96,384]{2,1,0:T(8,128)(2,1)S(1)}, u32[]{:S(2)}, u32[]{:S(2)}) collective-permute-start(bf16[4,96,384]{2,1,0:T(8,128)(2,1)S(1)} %copy-done.50), channel_id=1, source_target_pairs={{0,1},{1,0},{2,3},{3,2},{4,5},{5,4},{6,7},{7,6},{8,9},{9,8},{10,11... | collective-permute-start | bytes 884744 | tf_op jit(solution)/shard_map/ppermute | solution.py:452
  145.0 22.6 %collective-permute-start.21 = (f32[48,768]{1,0:T(8,128)S(1)}, f32[48,768]{1,0:T(8,128)S(1)}, u32[]{:S(2)}, u32[]{:S(2)}) collective-permute-start(f32[48,768]{1,0:T(8,128)S(1)} %copy-done.31), channel_id=1, source_target_pairs={{0,8},{2,10},{4,12},{6,14},{8,0},{10,2},{12,4},{14,6},{16,24},{18,... | collective-permute-start | bytes 442376 | tf_op jit(solution)/shard_map/ppermute | solution.py:448
  163.5 13.9 %collective-permute-start.25 = (bf16[4,48,768]{2,1,0:T(8,128)(2,1)}, bf16[4,48,768]{2,1,0:T(8,128)(2,1)S(1)}, u32[]{:S(2)}, u32[]{:S(2)}) collective-permute-start(bf16[4,48,768]{2,1,0:T(8,128)(2,1)} %get-tuple-element.275), channel_id=1, source_target_pairs={{0,1},{1,0},{2,3},{3,2},{4,5},{5,4},{6,7},{7,6},{8,9},{9,8},{10,11... | collective-permute-start | bytes 884744 | tf_op jit(solution)/shard_map/ppermute | solution.py:452
  164.0 13.4 %collective-permute-start.26 = (bf16[4,48,768]{2,1,0:T(8,128)(2,1)}, bf16[4,48,768]{2,1,0:T(8,128)(2,1)S(1)}, u32[]{:S(2)}, u32[]{:S(2)}) collective-permute-start(bf16[4,48,768]{2,1,0:T(8,128)(2,1)} %get-tuple-element.276), channel_id=1, source_target_pairs={{0,4},{2,6},{4,0},{6,2},{8,12},{10,14},{12,8},{14,10},{16,20},{18,... | collective-permute-start | bytes 884744 | tf_op jit(solution)/shard_map/ppermute | solution.py:448
  167.6 13.5 %collective-permute-start.27 = (bf16[2,2,96,384]{3,2,1,0:T(8,128)(2,1)}, bf16[2,2,96,384]{3,2,1,0:T(8,128)(2,1)S(1)}, u32[]{:S(2)}, u32[]{:S(2)}) collective-permute-start(bf16[2,2,96,384]{3,2,1,0:T(8,128)(2,1)} %fold.19), channel_id=1, source_target_pairs={{0,8},{2,10},{4,12},{6,14},{8,0},{10,2},{12,4},{14,6},{16,24},{18,... | collective-permute-start | bytes 884744 | tf_op jit(solution)/shard_map/ppermute | solution.py:448
  168.1 7.2 %collective-permute-start.22 = (f32[8,768]{1,0:T(8,128)S(1)}, f32[8,768]{1,0:T(8,128)S(1)}, u32[]{:S(2)}, u32[]{:S(2)}) collective-permute-start(f32[8,768]{1,0:T(8,128)S(1)} %copy-done.44), channel_id=1, source_target_pairs={{0,1},{1,0},{2,3},{3,2},{4,5},{5,4},{6,7},{7,6},{8,9},{9,8},{10,11... | collective-permute-start | bytes 73736 | tf_op jit(solution)/shard_map/ppermute | solution.py:452
  175.3 10.1 %collective-permute-start.23 = (bf16[4,2,48,384]{3,2,1,0:T(8,128)(2,1)}, bf16[4,2,48,384]{3,2,1,0:T(8,128)(2,1)S(1)}, u32[]{:S(2)}, u32[]{:S(2)}) collective-permute-start(bf16[4,2,48,384]{3,2,1,0:T(8,128)(2,1)} %get-tuple-element.272), channel_id=1, source_target_pairs={{0,1},{1,0},{2,3},{3,2},{4,5},{5,4},{6,7},{7,6},{8,9},{9,8},{10,11... | collective-permute-start | bytes 884744 | tf_op jit(solution)/shard_map/ppermute | solution.py:452
  175.8 9.6 %collective-permute-start.24 = (bf16[4,2,48,384]{3,2,1,0:T(8,128)(2,1)}, bf16[4,2,48,384]{3,2,1,0:T(8,128)(2,1)S(1)}, u32[]{:S(2)}, u32[]{:S(2)}) collective-permute-start(bf16[4,2,48,384]{3,2,1,0:T(8,128)(2,1)} %get-tuple-element.273), channel_id=1, source_target_pairs={{0,4},{2,6},{4,0},{6,2},{8,12},{10,14},{12,8},{14,10},{16,20},{18,... | collective-permute-start | bytes 884744 | tf_op jit(solution)/shard_map/ppermute | solution.py:448
  181.1 8.2 %collective-permute-start.29 = (bf16[2,2,48,768]{3,2,1,0:T(8,128)(2,1)}, bf16[2,2,48,768]{3,2,1,0:T(8,128)(2,1)S(1)}, u32[]{:S(2)}, u32[]{:S(2)}) collective-permute-start(bf16[2,2,48,768]{3,2,1,0:T(8,128)(2,1)} %fold.21), channel_id=1, source_target_pairs={{0,8},{2,10},{4,12},{6,14},{8,0},{10,2},{12,4},{14,6},{16,24},{18,... | collective-permute-start | bytes 884744 | tf_op jit(solution)/shard_map/ppermute | solution.py:448
  189.3 21.8 %collective-permute-start.30 = (bf16[2,2,2,48,384]{4,3,2,1,0:T(8,128)(2,1)}, bf16[2,2,2,48,384]{4,3,2,1,0:T(8,128)(2,1)S(1)}, u32[]{:S(2)}, u32[]{:S(2)}) collective-permute-start(bf16[2,2,2,48,384]{4,3,2,1,0:T(8,128)(2,1)} %fold.23), channel_id=1, source_target_pairs={{0,8},{2,10},{4,12},{6,14},{8,0},{10,2},{12,4},{14,6},{16,24},{18,... | collective-permute-start | bytes 884744 | tf_op jit(solution)/shard_map/ppermute | solution.py:448
  190.2 18.2 %collective-permute-start.32 = (f32[80,768]{1,0:T(8,128)S(1)}, f32[80,768]{1,0:T(8,128)S(1)}, u32[]{:S(2)}, u32[]{:S(2)}) collective-permute-start(f32[80,768]{1,0:T(8,128)S(1)} %copy-done.30), channel_id=1, source_target_pairs={{0,16},{2,18},{4,20},{6,22},{8,24},{10,26},{12,28},{14,30},{16,0},... | collective-permute-start | bytes 737288 | tf_op jit(solution)/shard_map/ppermute | solution.py:448
  190.5 17.9 %collective-permute-start.31 = (f32[8,768]{1,0:T(8,128)S(1)}, f32[8,768]{1,0:T(8,128)S(1)}, u32[]{:S(2)}, u32[]{:S(2)}) collective-permute-start(f32[8,768]{1,0:T(8,128)S(1)} %add.88), channel_id=1, source_target_pairs={{0,4},{2,6},{4,0},{6,2},{8,12},{10,14},{12,8},{14,10},{16,20},{18,... | collective-permute-start | bytes 73736 | tf_op jit(solution)/shard_map/ppermute | solution.py:448
  191.8 32.4 %collective-permute-start.34 = (bf16[2,1,96,384]{3,2,1,0:T(8,128)(2,1)S(1)}, bf16[2,1,96,384]{3,2,1,0:T(8,128)(2,1)S(1)}, u32[]{:S(2)}, u32[]{:S(2)}) collective-permute-start(bf16[2,1,96,384]{3,2,1,0:T(8,128)(2,1)S(1)} %copy-done.37), channel_id=1, source_target_pairs={{0,16},{2,18},{4,20},{6,22},{8,24},{10,26},{12,28},{14,30},{16,0},... | collective-permute-start | bytes 442376 | tf_op jit(solution)/shard_map/ppermute | solution.py:448
  210.9 13.3 %collective-permute-start.35 = (bf16[2,1,48,768]{3,2,1,0:T(8,128)(2,1)}, bf16[2,1,48,768]{3,2,1,0:T(8,128)(2,1)S(1)}, u32[]{:S(2)}, u32[]{:S(2)}) collective-permute-start(bf16[2,1,48,768]{3,2,1,0:T(8,128)(2,1)} %fold.24), channel_id=1, source_target_pairs={{0,16},{2,18},{4,20},{6,22},{8,24},{10,26},{12,28},{14,30},{16,0},... | collective-permute-start | bytes 442376 | tf_op jit(solution)/shard_map/ppermute | solution.py:448
  212.9 11.4 %collective-permute-start.36 = (f32[8,768]{1,0:T(8,128)S(1)}, f32[8,768]{1,0:T(8,128)S(1)}, u32[]{:S(2)}, u32[]{:S(2)}) collective-permute-start(f32[8,768]{1,0:T(8,128)S(1)} %add.89), channel_id=1, source_target_pairs={{0,8},{2,10},{4,12},{6,14},{8,0},{10,2},{12,4},{14,6},{16,24},{18,... | collective-permute-start | bytes 73736 | tf_op jit(solution)/shard_map/ppermute | solution.py:448
  221.4 8.8 %collective-permute-start.33 = (bf16[2,1,2,48,384]{4,3,2,1,0:T(8,128)(2,1)}, bf16[2,1,2,48,384]{4,3,2,1,0:T(8,128)(2,1)S(1)}, u32[]{:S(2)}, u32[]{:S(2)}) collective-permute-start(bf16[2,1,2,48,384]{4,3,2,1,0:T(8,128)(2,1)} %fold.25), channel_id=1, source_target_pairs={{0,16},{2,18},{4,20},{6,22},{8,24},{10,26},{12,28},{14,30},{16,0},... | collective-permute-start | bytes 442376 | tf_op jit(solution)/shard_map/ppermute | solution.py:448
  (60 other events, 233.0 us)

commit v3 on v2

--- a/solution.py
+++ b/solution.py
@@ -363,18 +363,19 @@
 def halves(core, grad, block, j):
     near = grad[2 * j * block : (2 * j + 1) * block]
     far = grad[(2 * j + 1) * block : (2 * j + 2) * block]
-    return jnp.where(core == 0, far, near).astype(bf16), jnp.where(core == 0, near, far).astype(bf16)
+    return jnp.where(core == 0, far, near), jnp.where(core == 0, near, far)
 
 
 def wgrad_kernel(block, place_ref, left_ref, right_ref, send_ref, keep_ref):
     grad = tn(left_ref[...], right_ref[...])
     columns = grad.shape[1] // 2
+    low = block // 2
     for j in range(grad.shape[0] // (2 * block)):
         for ref, part in zip((send_ref, keep_ref), halves(place_ref[2], grad, block, j)):
             for y in range(2):
                 mine = part[:, y * columns : (y + 1) * columns]
                 for g in range(2):
-                    ref[g, y, j] = mine[g * (block // 2) : (g + 1) * (block // 2)]
+                    ref[g, y, j] = mine[g * low : (g + 1) * low].astype(bf16)
 
 
 def wgrad(place, left, right, images):
@@ -401,42 +402,45 @@
     )(place, left, right)
 
 
-def wgrad_four_kernel(
-    block, place_ref, na_ref, nb_ref, a_ref, dq_ref, dk_ref, dv_ref, dx_ref, send_ref, keep_ref
+def wgrad_three_kernel(
+    block, place_ref, na_ref, nb_ref, dq_ref, dk_ref, dv_ref, send_ref, keep_ref
 ):
     na = na_ref[...]
     both = jnp.concatenate([na, nb_ref[...]], axis=0)
-    lefts = (na, both, both, a_ref[...])
-    for at, right_ref in enumerate((dq_ref, dk_ref, dv_ref, dx_ref)):
-        grad = tn(lefts[at], right_ref[...])
+    low = block // 2
+    for m, (left, right_ref) in enumerate(((na, dq_ref), (both, dk_ref), (both, dv_ref))):
+        grad = tn(left, right_ref[...])
         columns = grad.shape[1] // 2
         for j in range(grad.shape[0] // (2 * block)):
             for ref, part in zip((send_ref, keep_ref), halves(place_ref[2], grad, block, j)):
                 for y in range(2):
-                    ref[at // 2, y, j, at % 2] = part[:, y * columns : (y + 1) * columns]
-
-
-def wgrad_four(place, na, nb, a, dq, dk, dv, dx, images):
+                    mine = part[:, y * columns : (y + 1) * columns]
+                    for g in range(2):
+                        ref[g, y, j, m] = mine[g * low : (g + 1) * low].astype(bf16)
+
+
+def wgrad_three(place, na, nb, dq, dk, dv, images):
     rows, depth = na.shape
     columns = dq.shape[1]
     block = depth // images
     chunk = depth // 2
     pairs = chunk // (2 * block)
+    cut = (3, block // 2, columns // 2)
     left = pl.BlockSpec((rows, chunk), lambda i: (0, i))
     right = pl.BlockSpec((rows, columns), lambda i: (0, 0))
     right_all = pl.BlockSpec((2 * rows, columns), lambda i: (0, 0))
-    out_spec = pl.BlockSpec((2, 2, pairs, 2, block, columns // 2), lambda i: (0, 0, i, 0, 0, 0))
-    out_shape = jax.ShapeDtypeStruct((2, 2, images // 2, 2, block, columns // 2), bf16)
+    out_spec = pl.BlockSpec((2, 2, pairs, *cut), lambda i: (0, 0, i, 0, 0, 0))
+    out_shape = jax.ShapeDtypeStruct((2, 2, images // 2, *cut), bf16)
     smem = pl.BlockSpec(memory_space=pltpu.SMEM)
     return pl.pallas_call(
-        functools.partial(wgrad_four_kernel, block),
+        functools.partial(wgrad_three_kernel, block),
         grid=(2,),
-        in_specs=[smem, left, left, left, right, right_all, right_all, right],
+        in_specs=[smem, left, left, right, right_all, right_all],
         out_specs=[out_spec, out_spec],
         out_shape=[out_shape, out_shape],
         cost_estimate=light,
-        name="wgrad_four",
-    )(place, na, nb, a, dq, dk, dv, dx)
+        name="wgrad_three",
+    )(place, na, nb, dq, dk, dv)
 
 
 def img_bits():
@@ -484,10 +488,13 @@
     return lambda p: 1 - ((p[4] >> bit) & 1)
 
 
-def fold_kernel(plan, place_ref, *refs):
+def fold_kernel(plan, gathers, place_ref, *refs):
     count = sum(sum(slots) for slots, _ in plan)
-    inputs = iter(refs[:count])
-    for (slots, join), out in zip(plan, refs[count:]):
+    inputs = iter(refs[: count + 2 * len(gathers)])
+    outs = iter(refs[count + 2 * len(gathers) :])
+    for slots, join in plan:
+        out = next(outs)
+        extra = next(outs) if join == "wide" else None
         start = 0
         for slot, parts in enumerate(slots):
             total = next(inputs)[...].astype(f32)
@@ -499,15 +506,35 @@
             elif join == "stack":
                 out[slot] = total
             elif join == "rows":
-                out[start : start + total.shape[0]] = total
-                start += total.shape[0]
+                axis = total.ndim - 2
+                size = total.shape[axis]
+                if axis:
+                    for m in range(total.shape[0]):
+                        out[m, start : start + size] = total[m]
+                else:
+                    out[start : start + size] = total
+                start += size
             else:
-                out[:, start : start + total.shape[1]] = total
-                start += total.shape[1]
-
-
-def fold(place, outputs, dtype):
-    arrays, specs, plan, shapes = [], [], [], []
+                size, half = total.shape[0], extra.shape[1]
+                chunk = (total.shape[1] - half) // 2
+                for piece in range(2):
+                    out[piece * size : (piece + 1) * size, slot * chunk : (slot + 1) * chunk] = (
+                        total[:, piece * chunk : (piece + 1) * chunk]
+                    )
+                extra[slot * size : (slot + 1) * size] = total[:, 2 * chunk :]
+    for gather in gathers:
+        own, other, out = next(inputs), next(inputs), next(outs)
+        rows = own.shape[0]
+        sums = min(TOP, rows)
+        out[:sums] = own[:sums] + other[:sums]
+        if rows > sums:
+            out[sums:rows] = own[sums:]
+        if gather:
+            out[rows:] = other[sums:]
+
+
+def fold(place, outputs, dtype, notes=()):
+    arrays, specs, plan, shapes, gathers = [], [], [], [], []
     for slots, join in outputs:
         counts = []
         for parts in slots:
@@ -523,23 +550,32 @@
                         lambda i, p, picks=picks: tuple(0 if c is None else c(p) for c in picks),
                     )
                 )
+        plan.append((tuple(counts), join))
         if join == "stack":
             shape = (len(slots), *shape)
         elif join == "rows":
-            shape = (len(slots) * shape[0], *shape[1:])
-        elif join == "columns":
-            shape = (shape[0], len(slots) * shape[1])
-        plan.append((tuple(counts), join))
-        shapes.append(shape)
+            shape = (*shape[:-2], len(slots) * shape[-2], shape[-1])
+        elif join == "wide":
+            size, total = shape
+            shapes.append(((2 * size, 2 * ((total - total // 5) // 2)), dtype))
+            shape = (2 * size, total // 5)
+        shapes.append((shape, dtype))
+    whole = lambda t: pl.BlockSpec(t, lambda i, p: (0,) * len(t))
+    for own, other, gather in notes:
+        rows, width = own.shape
+        arrays += [own, other]
+        specs += [whole(own.shape), whole(other.shape)]
+        gathers.append(gather)
+        shapes.append(((2 * rows - TOP if gather else rows, width), f32))
     return pl.pallas_call(
-        functools.partial(fold_kernel, tuple(plan)),
+        functools.partial(fold_kernel, tuple(plan), tuple(gathers)),
         grid_spec=pltpu.PrefetchScalarGridSpec(
             num_scalar_prefetch=1,
             grid=(1,),
             in_specs=specs,
-            out_specs=[pl.BlockSpec(t, lambda i, p, t=t: (0,) * len(t)) for t in shapes],
+            out_specs=[whole(t) for t, _ in shapes],
         ),
-        out_shape=[jax.ShapeDtypeStruct(t, dtype) for t in shapes],
+        out_shape=[jax.ShapeDtypeStruct(t, d) for t, d in shapes],
         cost_estimate=light,
         name="fold",
     )(place, *arrays)
@@ -581,41 +617,44 @@
         parts.append((self.cut(self.second, *split), choose))
         return parts
 
+    def stage_near(self, d):
+        return self.z_parts((self.quarter // 4, 4), (None, lambda p: (p[4] & 3) ^ d))
+
     def stage_z(self, k):
         high = self.quarter >> (k + 1)
         parts = self.z_parts((high, 2, 1 << k), (None, z_other(k), z_from(0, k)))
-        for j, array in enumerate(self.arrived):
-            view = self.cut(array, 2, high, 2, 1 << (k - j - 1))
-            parts.append((view, (at(self.group), None, z_other(k), z_from(j + 1, k - j - 1))))
+        for array, done in self.arrived:
+            view = self.cut(array, 2, high, 2, 1 << (k - done))
+            parts.append((view, (at(self.group), None, z_other(k), z_from(done, k - done))))
         return parts
 
     def whole(self, *more):
         bits = self.quarter.bit_length() - 1
         more = tuple(at(m) for m in more)
         parts = self.z_parts((self.quarter,), (z_from(0, bits),))
-        for j, array in enumerate(self.arrived):
-            parts.append((array, (at(self.group), z_from(j + 1, bits - j - 1))))
+        for array, done in self.arrived:
+            parts.append((array, (at(self.group), z_from(done, bits - done))))
         return [(array, picks + more) for array, picks in parts]
 
 
-def merge_kernel(gather, own_ref, other_ref, out_ref):
-    out_ref[:TOP] = own_ref[:TOP] + other_ref[:TOP]
-    rows = own_ref.shape[0]
-    out_ref[TOP:rows] = own_ref[TOP:]
-    if gather:
-        out_ref[rows:] = other_ref[TOP:]
-
-
-def merge(own, other, gather):
-    rows, width = own.shape
-    if gather:
-        rows = 2 * rows - TOP
-    return pl.pallas_call(
-        functools.partial(merge_kernel, gather),
-        out_shape=jax.ShapeDtypeStruct((rows, width), f32),
-        cost_estimate=light,
-        name="merge",
-    )(own, other)
+def near_sends(first, second):
+    return [([first.stage_near(d), second.stage_near(d)], "stack") for d in (1, 2, 3)]
+
+
+def near_swap(sends):
+    return [img_swap(send, 4 * d) for d, send in zip((1, 2, 3), sends)]
+
+
+def take(place, first, second, arrived):
+    for array in arrived:
+        for group in (first, second):
+            group.arrived.append((array, 2))
+    for bit in range(4, img_bits()):
+        k = bit - 2
+        (send,) = fold(place, [([first.stage_z(k), second.stage_z(k)], "stack")], bf16)
+        array = img_swap(send, 1 << bit)
+        for group in (first, second):
+            group.arrived.append((array, k + 1))
 
 
 def gelu_back_kernel(grad_ref, down_ref, up_ref, out_ref):
@@ -659,26 +698,28 @@
 
 def up_back_kernel(
     block, place_ref, low_ref, du_ref, up_ref, unit_ref, inv_ref, gain_ref, above_ref, wo_ref,
-    send_ref, keep_ref, grad_ref, branch_ref, heads_ref, gain_grad_ref, acc_ref,
+    a_ref, send_ref, keep_ref, grad_ref, heads_ref, gain_grad_ref, acc_ref, out_ref,
 ):
     c = pl.program_id(0)
+    steps = pl.num_programs(0) // 2
     du = du_ref[...]
-    grad = tn(low_ref[...], du)
-    for j in range(grad.shape[0] // (2 * block)):
-        send, keep = halves(place_ref[2], grad, block, j)
-        send_ref[0, 0, j] = send
-        keep_ref[0, 0, j] = keep
-    back = nt(du, up_ref[...])
-
-    @pl.when(c == 0)
+    chunk = du.shape[1]
+    half = out_ref.shape[2]
+    size = block // 2
+
+    @pl.when(c < steps)
     def _():
-        acc_ref[...] = back
-
-    @pl.when(c > 0)
-    def _():
-        acc_ref[...] += back
-
-    @pl.when(c == pl.num_programs(0) - 1)
+        back = nt(du, up_ref[...])
+
+        @pl.when(c == 0)
+        def _():
+            acc_ref[...] = back
+
+        @pl.when(c > 0)
+        def _():
+            acc_ref[...] += back
+
+    @pl.when(c == steps - 1)
     def _():
         through, gain_grad = norm_back_rows(
             acc_ref[...], unit_ref[...], inv_ref[...], gain_ref[...]
@@ -687,40 +728,64 @@
         gain_grad_ref[...] = gain_grad
         grad_ref[...] = total
         branch = total.astype(bf16)
-        branch_ref[...] = branch
         heads_ref[...] = nt(branch, wo_ref[...]).astype(bf16)
-
-
-def up_back_call(place, low, du, w_up, unit, inv, gain, above, w_output, images):
+        out_grad = tn(a_ref[...], branch)
+        for y in range(2):
+            out_ref[y] = out_grad[:, y * half : (y + 1) * half]
+
+    @pl.when(c >= steps)
+    def _():
+        grad = tn(low_ref[...], du)
+        out_grad = out_ref[(c - steps) // 2]
+        first = (c - steps) % 2 == 0
+        for j in range(grad.shape[0] // (2 * block)):
+            for ref, part, more in zip(
+                (send_ref, keep_ref),
+                halves(place_ref[2], grad, block, j),
+                halves(place_ref[2], out_grad, block, j),
+            ):
+                for piece in range(2):
+                    ref[0, 0, j, :, piece * chunk : (piece + 1) * chunk] = part[
+                        piece * size : (piece + 1) * size
+                    ].astype(bf16)
+                ref[0, 0, j, :, 2 * chunk :] = jnp.where(first, more[:size], more[size:]).astype(bf16)
+
+
+def up_back_call(place, low, du, w_up, unit, inv, gain, above, w_output, attended, images):
     rows, width = low.shape
     depth = du.shape[1]
-    chunk = depth // 4
+    steps = 4
+    chunk = depth // steps
     block = width // images
+    wide = 2 * chunk + width // 2
     whole = lambda *shape: pl.BlockSpec(shape, lambda c: (0,) * len(shape))
-    half_spec = pl.BlockSpec(
-        (1, 1, images // 2, block, chunk), lambda c: (c % 2, c // 2, 0, 0, 0)
-    )
-    half_shape = jax.ShapeDtypeStruct((2, 2, images // 2, block, chunk), bf16)
+
+    def half_index(c):
+        k = jnp.maximum(c - steps, 0)
+        return (k % 2, k // 2, 0, 0, 0)
+
+    half_spec = pl.BlockSpec((1, 1, images // 2, block // 2, wide), half_index)
+    half_shape = jax.ShapeDtypeStruct((2, 2, images // 2, block // 2, wide), bf16)
     return pl.pallas_call(
         functools.partial(up_back_kernel, block),
-        grid=(4,),
+        grid=(2 * steps,),
         in_specs=[
             pl.BlockSpec(memory_space=pltpu.SMEM),
             whole(rows, width),
-            pl.BlockSpec((rows, chunk), lambda c: (0, c)),
-            pl.BlockSpec((width, chunk), lambda c: (0, c)),
+            pl.BlockSpec((rows, chunk), lambda c: (0, c % steps)),
+            pl.BlockSpec((width, chunk), lambda c: (0, jnp.minimum(c, steps - 1))),
             whole(rows, width),
             whole(rows, 1),
             whole(1, width),
             whole(rows, width),
             whole(width, width),
+            whole(rows, width),
         ],
         out_specs=[
             half_spec,
             half_spec,
             whole(rows, width),
             whole(rows, width),
-            whole(rows, width),
             whole(1, width),
         ],
         out_shape=[
@@ -728,65 +793,59 @@
             half_shape,
             jax.ShapeDtypeStruct((rows, width), f32),
             jax.ShapeDtypeStruct((rows, width), bf16),
-            jax.ShapeDtypeStruct((rows, width), bf16),
             jax.ShapeDtypeStruct((1, width), f32),
         ],
-        scratch_shapes=[pltpu.VMEM((rows, width), f32)],
+        scratch_shapes=[
+            pltpu.VMEM((rows, width), f32),
+            pltpu.VMEM((2, width, width // 2), f32),
+        ],
         cost_estimate=light,
         name="up_back",
-    )(place, low, du, w_up, unit, inv, gain[None], above, w_output)
-
-
-def other_in_kernel(dk_ref, dv_ref, wk_ref, wv_ref, out_ref):
-    out_ref[...] = (nt(dk_ref[...], wk_ref[...]) + nt(dv_ref[...], wv_ref[...])).astype(bf16)
-
-
-def other_in_call(dk, dv, w_key, w_value):
-    rows, width = dk.shape[0] // 2, dk.shape[1]
-    far = pl.BlockSpec((rows, width), lambda i: (1, 0))
-    whole = pl.BlockSpec((width, width), lambda i: (0, 0))
+    )(place, low, du, w_up, unit, inv, gain[None], above, w_output, attended)
+
+
+def parts_in_kernel(
+    dq_ref, dk_ref, dv_ref, wq_ref, wk_ref, wv_ref, unit_ref, other_unit_ref, second_ref,
+    own_ref, other_ref, gains_ref,
+):
+    rows = dq_ref.shape[0]
+    both = nt(dk_ref[...], wk_ref[...]) + nt(dv_ref[...], wv_ref[...])
+    own = nt(dq_ref[...], wq_ref[...]) + both[:rows]
+    other = both[rows:]
+    own_ref[...] = own
+    other_ref[...] = other.astype(bf16)
+    first = jnp.sum(own * unit_ref[...] + other * other_unit_ref[...], axis=0, keepdims=True)
+    row = lax.broadcasted_iota(jnp.int32, gains_ref.shape, 0)
+    gains_ref[...] = jnp.where(row == 0, second_ref[...], jnp.where(row == 1, first, 0.0))
+
+
+def parts_in_call(dq, dk, dv, w_query, w_key, w_value, unit, other_unit, second):
+    rows, width = dq.shape
     return pl.pallas_call(
-        other_in_kernel,
-        grid=(1,),
-        in_specs=[far, far, whole, whole],
-        out_specs=pl.BlockSpec((rows, width), lambda i: (0, 0)),
-        out_shape=jax.ShapeDtypeStruct((rows, width), bf16),
+        parts_in_kernel,
+        out_shape=[
+            jax.ShapeDtypeStruct((rows, width), f32),
+            jax.ShapeDtypeStruct((rows, width), bf16),
+            jax.ShapeDtypeStruct((8, width), f32),
+        ],
         cost_estimate=light,
-        name="other_in",
-    )(dk, dv, w_key, w_value)
-
-
-def own_in_kernel(
-    dq_ref, dk_ref, dv_ref, wq_ref, wk_ref, wv_ref, arrived_ref, unit_ref, inv_ref, gain_ref,
-    above_ref, second_ref, out_ref, gains_ref,
-):
-    grad = nt(dq_ref[...], wq_ref[...]) + nt(dk_ref[...], wk_ref[...])
-    grad = grad + nt(dv_ref[...], wv_ref[...]) + arrived_ref[...].astype(f32)
-    through, gain_grad = norm_back_rows(grad, unit_ref[...], inv_ref[...], gain_ref[...])
+        name="parts_in",
+    )(dq, dk, dv, w_query, w_key, w_value, unit, other_unit, second)
+
+
+def own_in_kernel(own_ref, arrived_ref, unit_ref, inv_ref, gain_ref, above_ref, out_ref):
+    grad = own_ref[...] + arrived_ref[...].astype(f32)
+    through, _ = norm_back_rows(grad, unit_ref[...], inv_ref[...], gain_ref[...])
     out_ref[...] = above_ref[...] + through
-    row = lax.broadcasted_iota(jnp.int32, gains_ref.shape, 0)
-    gains_ref[...] = jnp.where(row == 0, second_ref[...], jnp.where(row == 1, gain_grad, 0.0))
-
-
-def own_in_call(dq, dk, dv, w_query, w_key, w_value, arrived, unit, inv, gain, above, second):
-    rows, width = dq.shape
-    near = pl.BlockSpec((rows, width), lambda i: (0, 0))
-    whole = pl.BlockSpec((width, width), lambda i: (0, 0))
-    row = pl.BlockSpec((1, width), lambda i: (0, 0))
+
+
+def own_in_call(own, arrived, unit, inv, gain, above):
     return pl.pallas_call(
         own_in_kernel,
-        grid=(1,),
-        in_specs=[near] * 3
-        + [whole] * 3
-        + [near, near, pl.BlockSpec((rows, 1), lambda i: (0, 0)), row, near, row],
-        out_specs=[near, pl.BlockSpec((8, width), lambda i: (0, 0))],
-        out_shape=[
-            jax.ShapeDtypeStruct((rows, width), f32),
-            jax.ShapeDtypeStruct((8, width), f32),
-        ],
+        out_shape=jax.ShapeDtypeStruct(own.shape, f32),
         cost_estimate=light,
         name="own_in",
-    )(dq, dk, dv, w_query, w_key, w_value, arrived, unit, inv, gain[None], above, second)
+    )(own, arrived, unit, inv, gain[None], above)
 
 
 class Order:
@@ -852,7 +911,8 @@
     other_tokens, gathered, queries, keys_own, values_own, key_probe = tie(
         other_tokens, gathered, queries, keys_own, values_own, key_probe
     )
-    low_other = layer_norm(other_tokens.astype(f32), first_gain)[0].astype(bf16)
+    normed_other, unit_other, _ = layer_norm(other_tokens.astype(f32), first_gain)
+    low_other = normed_other.astype(bf16)
     keys_other = low_dot(low_other, w_key).astype(bf16)
     values_other = low_dot(low_other, w_value).astype(bf16)
     gathered = gather_more(gathered, 2)
@@ -879,159 +939,138 @@
     )
 
     step = Order(place)
+    message_in = seq_swap(message)
     down_send, down_keep = wgrad(place, hidden_low, branch_grad, images)
-    branch_grad, down_send, message = step(branch_grad, down_send, message)
+    down_send, down_keep, branch_grad, message_in = step(
+        down_send, down_keep, branch_grad, message_in
+    )
     down_core = img_swap(down_send, 1)
-    message_in = seq_swap(message)
     up_grad_low = gelu_back_call(branch_grad, w_down, upward)
-
-    up_grad_low, down_core, message_in = step(up_grad_low, down_core, message_in)
+    up_grad_low, down_core = step(up_grad_low, down_core)
     down_a = Staged(0, True, down_keep, down_core)
     down_b = Staged(1, False, down_keep, down_core)
-    down_sends = fold(place, [([down_a.stage_one()], None), ([down_b.stage_one()], None)], bf16)
-    message = merge(message, message_in, False)
-    up_grad_low, down_sends, message = step(up_grad_low, down_sends, message)
-    down_a.first = seq_swap(down_sends[0])
-    down_b.first = img_swap(down_sends[1], 2)
+
+    def first_stage(first, second, notes=()):
+        return fold(place, [([first.stage_one()], None), ([second.stage_one()], None)], bf16, notes)
+
+    def second_stage(first, second, notes=()):
+        return fold(place, [([first.stage_two()], None), ([second.stage_two()], None)], bf16, notes)
+
+    send_a, send_b, message = first_stage(down_a, down_b, [(message, message_in, False)])
+    up_grad_low, send_a, send_b, message = step(up_grad_low, send_a, send_b, message)
+    down_a.first = seq_swap(send_a)
+    down_b.first = img_swap(send_b, 2)
     message_in = img_swap(message, 1)
-
-    up_send, up_keep, residual_grad, attn_branch, attended_grad, second_gain_grad = up_back_call(
+    up_send, up_keep, residual_grad, attended_grad, second_gain_grad = up_back_call(
         place, second_low, up_grad_low, w_up, unit_two, scale_two, second_gain, result_grad,
-        w_output, images,
-    )
-    attended_grad, up_send, message_in = step(attended_grad, up_send, message_in)
+        w_output, attended_low, images,
+    )
+    attended_grad, up_send, down_a.first, down_b.first, message_in = step(
+        attended_grad, up_send, down_a.first, down_b.first, message_in
+    )
     up_core = img_swap(up_send, 1)
-    message = merge(message, message_in, True)
+    send_a, send_b, message = second_stage(down_a, down_b, [(message, message_in, True)])
+    attended_grad, send_a, send_b, message = step(attended_grad, send_a, send_b, message)
+    down_a.second = img_swap(send_a, 2)
+    down_b.second = seq_swap(send_b)
+    message_in = img_swap(message, 2)
 
     query_grad, key_part, value_part = attend_back(
         queries, keys_own, keys_other, values_own, values_other, attended_grad, log_totals
     )
-    query_grad, key_part, value_part, up_core, message = step(
-        query_grad, key_part, value_part, up_core, message
+    query_grad, key_part, value_part, up_core, down_a.second, down_b.second, message_in = step(
+        query_grad, key_part, value_part, up_core, down_a.second, down_b.second, message_in
     )
     up_a = Staged(0, False, up_keep, up_core)
     up_b = Staged(1, True, up_keep, up_core)
-    up_sends = fold(place, [([up_a.stage_one()], None), ([up_b.stage_one()], None)], bf16)
-    query_grad, key_part, value_part, up_sends = step(query_grad, key_part, value_part, up_sends)
-    up_a.first = img_swap(up_sends[0], 2)
-    up_b.first = seq_swap(up_sends[1])
-    message_in = img_swap(message, 2)
-    other_in_grad = other_in_call(key_part, value_part, w_key, w_value)
-    query_grad, key_part, value_part, other_in_grad = step(
-        query_grad, key_part, value_part, other_in_grad
-    )
-    arrived_grad = seq_swap(other_in_grad)
-    four_send, four_keep = wgrad_four(
-        place, low_own, low_other, attended_low, query_grad, key_part, value_part, attn_branch, images
-    )
-    four_send, down_a.first, down_b.first = step(four_send, down_a.first, down_b.first)
-    four_core = img_swap(four_send, 1)
-    down_sends = fold(place, [([down_a.stage_two()], None), ([down_b.stage_two()], None)], bf16)
-    down_sends, message_in = step(down_sends, message_in)
-    down_a.second = img_swap(down_sends[0], 2)
-    down_b.second = seq_swap(down_sends[1])
-    message = merge(message, message_in, True)
-
-    four_core, four_keep, message = step(four_core, four_keep, message)
-    four_a = Staged(0, False, four_keep, four_core)
-    four_b = Staged(1, True, four_keep, four_core)
-    four_sends = fold(place, [([four_a.stage_one()], None), ([four_b.stage_one()], None)], bf16)
-    four_sends, query_grad = step(four_sends, query_grad)
-    four_a.first = img_swap(four_sends[0], 2)
-    four_b.first = seq_swap(four_sends[1])
+    send_a, send_b, message = first_stage(up_a, up_b, [(message, message_in, True)])
+    query_grad, key_part, value_part, send_a, send_b, message = step(
+        query_grad, key_part, value_part, send_a, send_b, message
+    )
+    up_a.first = img_swap(send_a, 2)
+    up_b.first = seq_swap(send_b)
     message_in = img_swap(message, 4)
-
-    up_a.first, up_b.first = step(up_a.first, up_b.first)
-    up_sends = fold(place, [([up_a.stage_two()], None), ([up_b.stage_two()], None)], bf16)
-    up_sends, arrived_grad, query_grad = step(up_sends, arrived_grad, query_grad)
-    up_a.second = seq_swap(up_sends[0])
-    up_b.second = img_swap(up_sends[1], 2)
-    input_grad, gains = own_in_call(
-        query_grad, key_part, value_part, w_query, w_key, w_value, arrived_grad, unit_one,
-        scale_one, first_gain, residual_grad, second_gain_grad,
-    )
-    input_grad, gains, down_a.second, down_b.second = step(
-        input_grad, gains, down_a.second, down_b.second
-    )
+    three_send, three_keep = wgrad_three(
+        place, low_own, low_other, query_grad, key_part, value_part, images
+    )
+    three_send, query_grad, key_part, value_part, message_in = step(
+        three_send, query_grad, key_part, value_part, message_in
+    )
+    three_core = img_swap(three_send, 1)
+    *down_sends, message = fold(
+        place, near_sends(down_a, down_b), bf16, [(message, message_in, True)]
+    )
+    query_grad, *down_sends, message = step(query_grad, *down_sends, message)
+    message_in = img_swap(message, 8)
+    own_part, other_part, gains = parts_in_call(
+        query_grad, key_part, value_part, w_query, w_key, w_value, unit_one, unit_other,
+        second_gain_grad,
+    )
+    other_part, gains, three_core = step(other_part, gains, three_core)
+    down_in = near_swap(down_sends)
+    gains_in = img_swap(gains, 1)
+    three_a = Staged(0, False, three_keep, three_core)
+    three_b = Staged(1, True, three_keep, three_core)
+    send_a, send_b = first_stage(three_a, three_b)
+    send_a, send_b, up_a.first, up_b.first, gains_in = step(
+        send_a, send_b, up_a.first, up_b.first, gains_in
+    )
+    three_a.first = img_swap(send_a, 2)
+    three_b.first = seq_swap(send_b)
+    send_a, send_b, gains = second_stage(up_a, up_b, [(gains, gains_in, False)])
+    send_a, send_b, gains, other_part = step(send_a, send_b, gains, other_part)
+    gains_in = img_swap(gains, 2)
+    up_a.second = seq_swap(send_a)
+    up_b.second = img_swap(send_b, 2)
+    arrived_part = seq_swap(other_part)
+
+    message_in, gains, *down_in = step(message_in, gains, *down_in)
+    take(place, down_a, down_b, down_in)
+    down_grad, message = fold(
+        place, [([down_a.whole(), down_b.whole()], "rows")], f32, [(message, message_in, True)]
+    )
+    for bit in range(4, bits):
+        (message,) = fold(place, [], f32, [(message, img_swap(message, 1 << bit), True)])
+    sums, rank = message[:TOP], message[TOP:]
+    down_grad, three_a.first, three_b.first, gains_in = step(
+        down_grad, three_a.first, three_b.first, gains_in
+    )
+    send_a, send_b, gains = second_stage(three_a, three_b, [(gains, gains_in, False)])
+    send_a, send_b, gains = step(send_a, send_b, gains)
+    three_a.second = seq_swap(send_a)
+    three_b.second = img_swap(send_b, 2)
     gains_in = seq_swap(gains)
-
-    def z_send(first, second, k):
-        return fold(place, [([first.stage_z(k), second.stage_z(k)], "stack")], bf16)[0]
-
-    def z_take(first, second, arrived):
-        first.arrived.append(arrived)
-        second.arrived.append(arrived)
-
-    down_send = z_send(down_a, down_b, 0)
-    down_send, message_in = step(down_send, message_in)
-    down_in = img_swap(down_send, 4)
-    message = merge(message, message_in, True)
-    four_a.first, four_b.first, message = step(four_a.first, four_b.first, message)
-    four_sends = fold(place, [([four_a.stage_two()], None), ([four_b.stage_two()], None)], bf16)
-    four_sends, gains_in = step(four_sends, gains_in)
-    four_a.second = seq_swap(four_sends[0])
-    four_b.second = img_swap(four_sends[1], 2)
-    gains = gains + gains_in
-    message_in = img_swap(message, 8)
-
     gains, up_a.second, up_b.second = step(gains, up_a.second, up_b.second)
-    up_send = z_send(up_a, up_b, 0)
-    up_send, down_in = step(up_send, down_in)
-    up_in = img_swap(up_send, 4)
-    gains_in = img_swap(gains, 1)
-    z_take(down_a, down_b, down_in)
-    down_send = z_send(down_a, down_b, 1)
-    down_send, gains_in = step(down_send, gains_in)
-    down_in = img_swap(down_send, 8)
-    gains = gains + gains_in
-    four_a.second, four_b.second, gains = step(four_a.second, four_b.second, gains)
-    four_send = z_send(four_a, four_b, 0)
-    four_send, up_in = step(four_send, up_in)
-    four_in = img_swap(four_send, 4)
-    gains_in = img_swap(gains, 2)
-    z_take(up_a, up_b, up_in)
-    up_send = z_send(up_a, up_b, 1)
-    up_send, gains_in, message_in = step(up_send, gains_in, message_in)
-    up_in = img_swap(up_send, 8)
-    gains = gains + gains_in
-    message = merge(message, message_in, True)
-    four_in, gains, message = step(four_in, gains, message)
-    z_take(four_a, four_b, four_in)
-    four_send = z_send(four_a, four_b, 1)
-    (four_send,) = step(four_send)
-    four_in = img_swap(four_send, 8)
+    up_sends = fold(place, near_sends(up_a, up_b), bf16)
+    up_sends = step(*up_sends)
+    up_in = near_swap(up_sends)
+    arrived_part, gains = step(arrived_part, gains)
+    input_grad = own_in_call(
+        own_part, arrived_part, unit_one, scale_one, first_gain, residual_grad
+    )
+    input_grad, gains_in, three_a.second, three_b.second = step(
+        input_grad, gains_in, three_a.second, three_b.second
+    )
+    *three_sends, gains = fold(
+        place, near_sends(three_a, three_b), bf16, [(gains, gains_in, False)]
+    )
+    *three_sends, gains = step(*three_sends, gains)
+    three_in = near_swap(three_sends)
     gains_in = img_swap(gains, 4)
-    down_in, up_in, gains_in = step(down_in, up_in, gains_in)
+    up_in = step(*up_in)
+    take(place, up_a, up_b, up_in)
+    up_weight_grad, output_grad = fold(place, [([up_a.whole(), up_b.whole()], "wide")], f32)
+    up_weight_grad, output_grad, gains_in = step(up_weight_grad, output_grad, gains_in)
     gains = gains + gains_in
     gains_in = img_swap(gains, 8)
-
-    def rest(first, second, arrived):
-        z_take(first, second, arrived)
-        for bit in range(4, bits):
-            z_take(first, second, img_swap(z_send(first, second, bit - 2), 1 << bit))
-
-    rest(down_a, down_b, down_in)
-    rest(up_a, up_b, up_in)
-    down_grad, up_weight_grad = fold(
-        place,
-        [
-            ([down_a.whole(), down_b.whole()], "rows"),
-            ([up_a.whole(), up_b.whole()], "columns"),
-        ],
-        f32,
-    )
-    for bit in range(4, bits):
-        message = merge(message, img_swap(message, 1 << bit), True)
-    sums, rank = message[:TOP], message[TOP:]
-    rest(four_a, four_b, four_in)
+    three_in = step(*three_in)
+    take(place, three_a, three_b, three_in)
+    query_weight_grad, key_weight_grad, value_weight_grad = fold(
+        place, [([three_a.whole(m), three_b.whole(m)], "rows") for m in range(3)], f32
+    )
     gains = gains + gains_in
     for bit in range(4, bits):
         gains = gains + img_swap(gains, 1 << bit)
-    query_weight_grad, key_weight_grad, value_weight_grad, output_grad = fold(
-        place,
-        [([group.whole(m)], None) for group in (four_a, four_b) for m in range(2)],
-        f32,
-    )
     input_grad = input_grad[None]
 
     block = width // images

time: 235 us -> 237 us (level)
  Pallas kernels: 115 us -> 104 us
  starting transfers between devices: 35.3 us -> 45.7 us
  local copies, waits for them, and re-layouts: 15.7 us -> 19 us
  waiting for transfers between devices: 35.9 us -> 32.6 us
    ppermute x27 -> x30, waiting for transfers between devices: 30.8 us -> 18.7 us  [img_swap(): return lax.ppermute(value, 'img', [(i, i ^ mask) for i in range(count)])]
    pallas_call x23 -> x16, Pallas kernels: 74.6 us -> 63.5 us  [the longest x12 37.5 us: fold(): pl.pallas_call(functools.partial(fold_kernel, tuple(plan), tuple(gathers)...]
    ppermute x27 -> x30, starting transfers between devices: 23 us -> 33.5 us  [img_swap(): return lax.ppermute(value, 'img', [(i, i ^ mask) for i in range(count)])]
    ppermute x11, waiting for transfers between devices: 5.07 us -> 14 us  [seq_swap(): return lax.ppermute(value, 'seq', [(0, 1), (1, 0)])]
    unnamed x107 -> x119, local copies, waits for them, and re-layouts: 8.09 us -> 10.2 us
  transfers between devices with their start and end apart: 38 -> 41, of which waited for: 6 -> 12; matrix products, arithmetic and copies ran while one was open for 13% -> 14% of each run, Pallas kernels for 42% -> 38%
where the time goes in v3:
time: 237 us; the launch traced here: 235 us
  Pallas kernels  104 us (44%)
  starting transfers between devices  45.7 us (19%)
  waiting for transfers between devices  32.6 us (14%)
  matrix products  19.7 us (8%)
  local copies, waits for them, and re-layouts  19 us (8%)
  other arithmetic  10.5 us (4%)
  between operations  3.39 us (1%)
    pallas_call x12, Pallas kernels, fold(): pl.pallas_call(functools.partial(fold_kernel, tuple(plan), tuple(gathers)...  37.5 us
    ppermute x30, starting transfers between devices, img_swap(): return lax.ppermute(value, 'img', [(i, i ^ mask) for i in range(count)])  33.5 us
    ppermute x30, waiting for transfers between devices, img_swap(): return lax.ppermute(value, 'img', [(i, i ^ mask) for i in range(count)])  18.7 us
    ppermute x11, waiting for transfers between devices, seq_swap(): return lax.ppermute(value, 'seq', [(0, 1), (1, 0)])  14 us
    dot_general x8, matrix products, low_dot(): return jnp.dot(left_side, right_side, preferred_element_type=f32)  13.8 us
    pallas_call x1, Pallas kernels, up_back_call(): pl.pallas_call(functools.partial(up_back_kernel, block), grid=(2 * steps,...  12.4 us
    ppermute x11, starting transfers between devices, seq_swap(): return lax.ppermute(value, 'seq', [(0, 1), (1, 0)])  12.2 us
    pallas_call x1, Pallas kernels, attend_back(): pl.pallas_call(attend_back_kernel, grid=(pairs,), in_specs=[row_spec] * 6...  10.3 us
  transfers between devices with their start and end apart: 41, of which 12 were waited for; matrix products, arithmetic and copies ran while one was open for 14% of the time, Pallas kernels for 38%

profile of v3, /device:TPU:0, one launch (start us, length us, event | category | flops | bytes accessed | tf_op | source)
XLA Modules:
  0.0 235.0 jit_solution(12595098516704552227)
XLA Ops:
  0.7 3.1 %collective-permute-start = (bf16[256,768]{1,0:T(8,128)(2,1)}, bf16[256,768]{1,0:T(8,128)(2,1)S(1)}, u32[]{:S(2)}, u32[]{:S(2)}) collective-permute-start(bf16[256,768]{1,0:T(8,128)(2,1)} %bitcast.211), channel_id=1, source_target_pairs={{0,1},{1,0},{2,3},{3,2},{4,5},{5,4},{6,7},{7,6},{8,9},{9,8},{10,11... | collective-permute-start | bytes 1179656 | tf_op jit(solution)/shard_map/ppermute | solution.py:456
  14.3 3.0 %probe_rows.1 = (f32[1,768]{1,0:T(1,128)}, f32[16,768]{1,0:T(8,128)}) custom-call(f32[1,768]{1,0:T(1,128)} %broadcast_in_dim.19.probe_ref, bf16[768,768]{1,0:T(8,128)(2,1)} %query_ref.1, bf16[768,768]{1,0:T(8,128)(2,1)} %key_ref.1), custom_call_target="tpu_custom_call" | custom-call | flops 1024 | bytes 1024 | tf_op jit(solution)/shard_map/probe_rows/pallas_call | solution.py:85
  26.0 8.1 %attend.1 = (bf16[256,768]{1,0:T(8,128)(2,1)}, f32[6,256,2]{2,1,0:T(8,128)}) custom-call(bf16[256,768]{1,0:T(8,128)(2,1)} %convolution_convert_fusion.4.q_ref, bf16[256,768]{1,0:T(8,128)(2,1)} %convolution_convert_fusion.3.ka_ref, bf16[256,768]{1,0:T(8,128)(2,1)} %convolution_convert_fusion.1.kb_ref, bf16[256,768]{1,0:T(8,128)(2,1)} %convolution_convert_fusion.2.va_ref, ...), custom_call_target="tpu_custom_call" | custom-call | flops 1024 | bytes 1024 | tf_op jit(solution)/shard_map/attend/pallas_call | solution.py:300
  36.2 2.7 %collective-permute-start.5 = (f32[8,5,768]{2,1,0:T(8,128)S(1)}, f32[8,5,768]{2,1,0:T(8,128)S(1)}, u32[]{:S(2)}, u32[]{:S(2)}) collective-permute-start(f32[8,5,768]{2,1,0:T(8,128)S(1)} %pad_maximum_fusion.1), channel_id=1, source_target_pairs={{0,16},{2,18},{4,20},{6,22},{8,24},{10,26},{12,28},{14,30},{16,0},... | collective-permute-start | bytes 368648 | tf_op jit(solution)/shard_map/ppermute | solution.py:452
  39.9 3.6 %fusion.7 = (bf16[256,3072]{1,0:T(8,128)(2,1)S(1)}, f32[256,3072]{1,0:T(8,128)}) fusion(bf16[256,768]{1,0:T(8,128)(2,1)S(1)} %get-tuple-element.341.low_ref, bf16[768,3072]{1,0:T(8,128)(2,1)S(1)} %copy-done.20), kind=kOutput, calls=%fused_computation.8 | convolution fusion | flops 1215037440 | bytes 9830400 | tf_op jit(solution)/shard_map/dot_general | solution.py:32
  49.0 3.8 %collective-permute-done.4.other_ref = f32[16,896]{1,0:T(8,128)S(1)} collective-permute-done((f32[16,896]{1,0:T(8,128)}, f32[16,896]{1,0:T(8,128)S(1)}, u32[]{:S(2)}, u32[]{:S(2)}) %collective-permute-start.4) | collective-permute-done | bytes 57376 | tf_op jit(solution)/shard_map/ppermute | solution.py:456
  53.6 5.7 %pool_back.1 = (f32[256,768]{1,0:T(8,128)}, bf16[256,768]{1,0:T(8,128)(2,1)}, f32[24,768]{1,0:T(8,128)}) custom-call(s32[5]{0:T(128)} %stack.23.place_ref, s32[1]{0:T(128)S(6)} %copy.74.count_ref, s32[1,80]{1,0:T(1,128)} %pairs_ref.1, f32[1]{0:T(128)} %bitcast.103.temp_ref, f32[1]{0:T(128)} %bitcast.104.bias_ref, f32[16,896]{1,0:T(8,128)} %get-tuple-element.189.own_ref, ...), custom_call_target="tpu_custom_call" | custom-call | flops 1024 | bytes 1024 | tf_op jit(solution)/shard_map/pool_back/pallas_call | solution.py:260
  59.8 4.4 %wgrad.1 = (bf16[2,2,8,96,384]{4,3,2,1,0:T(8,128)(2,1)}, bf16[2,2,8,96,384]{4,3,2,1,0:T(8,128)(2,1)}) custom-call(s32[5]{0:T(128)} %stack.23.place_ref, bf16[256,3072]{1,0:T(8,128)(2,1)} %copy-done.28, bf16[256,768]{1,0:T(8,128)(2,1)} %get-tuple-element.201.right_ref.grad_ref), custom_call_target="tpu_custom_call" | custom-call | flops 1024 | bytes 1024 | tf_op jit(solution)/shard_map/wgrad/pallas_call | solution.py:390
  64.3 6.6 %gelu_back.1.du_ref = bf16[256,3072]{1,0:T(8,128)(2,1)} custom-call(bf16[256,768]{1,0:T(8,128)(2,1)} %get-tuple-element.201.right_ref.grad_ref, bf16[3072,768]{1,0:T(8,128)(2,1)} %down_ref.1, f32[256,3072]{1,0:T(8,128)} %get-tuple-element.357.up_ref), custom_call_target="tpu_custom_call" | custom-call | flops 1024 | bytes 1024 | tf_op jit(solution)/shard_map/gelu_back/pallas_call | solution.py:676
  72.3 3.4 %fold.12 = (bf16[8,96,384]{2,1,0:T(8,128)(2,1)}, bf16[2,4,96,384]{3,2,1,0:T(8,128)(2,1)}, f32[24,768]{1,0:T(8,128)}) custom-call(s32[5]{0:T(128)} %stack.23.place_ref, bf16[2,2,8,96,384]{4,3,2,1,0:T(8,128)(2,1)} %get-tuple-element.205.refs_0_, bf16[2,2,8,96,384]{4,3,2,1,0:T(8,128)(2,1)} %copy-done.2, bf16[2,2,4,2,96,384]{5,4,3,2,1,0:T(8,128)(2,1)} %bitcast.157, ...), custom_call_target="tpu_custom_call" | custom-call | flops 1024 | bytes 1024 | tf_op jit(solution)/shard_map/fold/pallas_call | solution.py:570
  79.2 12.4 %up_back.1 = (bf16[2,2,8,24,1920]{4,3,2,1,0:T(8,128)(2,1)}, bf16[2,2,8,24,1920]{4,3,2,1,0:T(8,128)(2,1)}, f32[256,768]{1,0:T(8,128)}, bf16[256,768]{1,0:T(8,128)(2,1)}, f32[1,768]{1,0:T(1,128)}) custom-call(s32[5]{0:T(128)} %stack.23.place_ref, bf16[256,768]{1,0:T(8,128)(2,1)} %copy-done.27, bf16[256,3072]{1,0:T(8,128)(2,1)} %gelu_back.1.du_ref, ...), custom_call_target="tpu_custom_call" | custom-call | flops 1024 | bytes 1024 | tf_op jit(solution)/shard_map/up_back/pallas_call | solution.py:769
  93.7 3.1 %fold.13 = (bf16[4,96,384]{2,1,0:T(8,128)(2,1)}, bf16[4,96,384]{2,1,0:T(8,128)(2,1)}, f32[32,768]{1,0:T(8,128)}) custom-call(s32[5]{0:T(128)} %stack.23.place_ref, bf16[2,2,4,2,96,384]{5,4,3,2,1,0:T(8,128)(2,1)} %bitcast.158, bf16[2,2,4,2,96,384]{5,4,3,2,1,0:T(8,128)(2,1)} %bitcast.169, bf16[4,2,96,384]{3,2,1,0:T(8,128)(2,1)} %bitcast.197, ...), custom_call_target="tpu_custom_call" | custom-call | flops 1024 | bytes 1024 | tf_op jit(solution)/shard_map/fold/pallas_call | solution.py:570
  99.3 10.3 %attend_back.1 = (bf16[256,768]{1,0:T(8,128)(2,1)}, bf16[512,768]{1,0:T(8,128)(2,1)}, bf16[512,768]{1,0:T(8,128)(2,1)}) custom-call(bf16[256,768]{1,0:T(8,128)(2,1)} %convolution_convert_fusion.4.q_ref, bf16[256,768]{1,0:T(8,128)(2,1)} %convolution_convert_fusion.3.ka_ref, bf16[256,768]{1,0:T(8,128)(2,1)} %convolution_convert_fusion.1.kb_ref, ...), custom_call_target="tpu_custom_call" | custom-call | flops 1024 | bytes 1024 | tf_op jit(solution)/shard_map/attend_back/pallas_call | solution.py:348
  111.3 3.8 %fold.14 = (bf16[2,4,24,1920]{3,2,1,0:T(8,128)(2,1)}, bf16[8,24,1920]{2,1,0:T(8,128)(2,1)}, f32[48,768]{1,0:T(8,128)}) custom-call(s32[5]{0:T(128)} %stack.23.place_ref, bf16[2,2,4,2,24,1920]{5,4,3,2,1,0:T(8,128)(2,1)} %bitcast.135, bf16[2,2,4,2,24,1920]{5,4,3,2,1,0:T(8,128)(2,1)} %bitcast.146, bf16[2,2,8,24,1920]{4,3,2,1,0:T(8,128)(2,1)} %get-tuple-element.241.refs_2_, ...), custom_call_target="tpu_custom_call" | custom-call | flops 1024 | bytes 1024 | tf_op jit(solution)/shard_map/fold/pallas_call | solution.py:570
  115.7 5.0 %wgrad_three.1 = (bf16[2,2,8,3,24,384]{5,4,3,2,1,0:T(8,128)(2,1)}, bf16[2,2,8,3,24,384]{5,4,3,2,1,0:T(8,128)(2,1)}) custom-call(s32[5]{0:T(128)} %stack.23.place_ref, bf16[256,768]{1,0:T(8,128)(2,1)} %copy-done.11, bf16[256,768]{1,0:T(8,128)(2,1)} %copy-done.15, bf16[256,768]{1,0:T(8,128)(2,1)} %get-tuple-element.263.dq_ref, ...), custom_call_target="tpu_custom_call" | custom-call | flops 1024 | bytes 1024 | tf_op jit(solution)/shard_map/wgrad_three/pallas_call | solution.py:435
  125.7 3.3 %fold.15 = (bf16[2,1,96,384]{3,2,1,0:T(8,128)(2,1)}, bf16[2,1,96,384]{3,2,1,0:T(8,128)(2,1)}, bf16[2,1,96,384]{3,2,1,0:T(8,128)(2,1)}, f32[80,768]{1,0:T(8,128)}) custom-call(s32[5]{0:T(128)} %stack.23.place_ref, bf16[2,2,1,4,2,96,384]{6,5,4,3,2,1,0:T(8,128)(2,1)} %bitcast.160, bf16[2,2,1,4,2,96,384]{6,5,4,3,2,1,0:T(8,128)(2,1)} %bitcast.171, ...), custom_call_target="tpu_custom_call" | custom-call | flops 1024 | bytes 1024 | tf_op jit(solution)/shard_map/fold/pallas_call | solution.py:570
  131.0 5.7 %parts_in.1 = (f32[256,768]{1,0:T(8,128)}, bf16[256,768]{1,0:T(8,128)(2,1)}, f32[8,768]{1,0:T(8,128)}) custom-call(bf16[256,768]{1,0:T(8,128)(2,1)} %get-tuple-element.263.dq_ref, bf16[512,768]{1,0:T(8,128)(2,1)} %get-tuple-element.264.dk_ref, bf16[512,768]{1,0:T(8,128)(2,1)} %get-tuple-element.265.dv_ref, bf16[768,768]{1,0:T(8,128)(2,1)} %wq_ref.1, ...), custom_call_target="tpu_custom_call" | custom-call | flops 1024 | bytes 1024 | tf_op jit(solution)/shard_map/parts_in/pallas_call | solution.py:824
  136.7 2.7 %collective-permute-start.23 = (bf16[2,1,96,384]{3,2,1,0:T(8,128)(2,1)}, bf16[2,1,96,384]{3,2,1,0:T(8,128)(2,1)S(1)}, u32[]{:S(2)}, u32[]{:S(2)}) collective-permute-start(bf16[2,1,96,384]{3,2,1,0:T(8,128)(2,1)} %get-tuple-element.289), channel_id=1, source_target_pairs={{0,16},{2,18},{4,20},{6,22},{8,24},{10,26},{12,28},{14,30},{16,0},... | collective-permute-start | bytes 442376 | tf_op jit(solution)/shard_map/ppermute | solution.py:452
  143.4 3.1 %fold.16 = (bf16[2,4,3,24,384]{4,3,2,1,0:T(8,128)(2,1)}, bf16[8,3,24,384]{3,2,1,0:T(8,128)(2,1)}) custom-call(s32[5]{0:T(128)} %stack.23.place_ref, bf16[2,2,4,2,3,24,384]{6,5,4,3,2,1,0:T(8,128)(2,1)} %bitcast.105, bf16[2,2,4,2,3,24,384]{6,5,4,3,2,1,0:T(8,128)(2,1)} %bitcast.120, bf16[2,2,8,3,24,384]{5,4,3,2,1,0:T(8,128)(2,1)} %get-tuple-element.268.refs_2_, ...), custom_call_target="tpu_custom_call" | custom-call | flops 1024 | bytes 1024 | tf_op jit(solution)/shard_map/fold/pallas_call | solution.py:570
  146.5 3.3 %fold.17 = (bf16[4,24,1920]{2,1,0:T(8,128)(2,1)}, bf16[4,24,1920]{2,1,0:T(8,128)(2,1)}, f32[8,768]{1,0:T(8,128)}) custom-call(s32[5]{0:T(128)} %stack.23.place_ref, bf16[2,2,4,2,24,1920]{5,4,3,2,1,0:T(8,128)(2,1)} %bitcast.136, bf16[2,2,4,2,24,1920]{5,4,3,2,1,0:T(8,128)(2,1)} %bitcast.147, bf16[2,4,24,1920]{3,2,1,0:T(8,128)(2,1)} %copy-done.5, ...), custom_call_target="tpu_custom_call" | custom-call | flops 1024 | bytes 1024 | tf_op jit(solution)/shard_map/fold/pallas_call | solution.py:570
  150.5 3.2 %collective-permute-done.23.refs_5_.refs_12_ = bf16[2,1,96,384]{3,2,1,0:T(8,128)(2,1)S(1)} collective-permute-done((bf16[2,1,96,384]{3,2,1,0:T(8,128)(2,1)}, bf16[2,1,96,384]{3,2,1,0:T(8,128)(2,1)S(1)}, u32[]{:S(2)}, u32[]{:S(2)}) %collective-permute-start.23) | collective-permute-done | bytes 147488 | tf_op jit(solution)/shard_map/ppermute | solution.py:452
  154.4 3.1 %fold.18 = (f32[192,384]{1,0:T(8,128)}, f32[144,768]{1,0:T(8,128)}) custom-call(s32[5]{0:T(128)} %stack.23.place_ref, bf16[2,2,4,2,96,384]{5,4,3,2,1,0:T(8,128)(2,1)} %bitcast.166, bf16[2,2,4,2,96,384]{5,4,3,2,1,0:T(8,128)(2,1)} %bitcast.177, bf16[4,2,96,384]{3,2,1,0:T(8,128)(2,1)} %bitcast.201, bf16[4,96,384]{2,1,0:T(8,128)(2,1)} %copy-done.22, ...), custom_call_target="tpu_custom_call" | custom-call | flops 1024 | bytes 1024 | tf_op jit(solution)/shard_map/fold/pallas_call | solution.py:570
  167.5 6.0 %collective-permute-done.25.refs_2_.refs_16_.refs_30_ = bf16[2,4,3,24,384]{4,3,2,1,0:T(8,128)(2,1)S(1)} collective-permute-done((bf16[2,4,3,24,384]{4,3,2,1,0:T(8,128)(2,1)S(1)}, bf16[2,4,3,24,384]{4,3,2,1,0:T(8,128)(2,1)S(1)}, u32[]{:S(2)}, u32[]{:S(2)}) %collective-permute-start.25) | collective-permute-done | bytes 442400 | tf_op jit(solution)/shard_map/ppermute | solution.py:452
  173.5 8.2 %collective-permute-done.26 = bf16[8,3,24,384]{3,2,1,0:T(8,128)(2,1)S(1)} collective-permute-done((bf16[8,3,24,384]{3,2,1,0:T(8,128)(2,1)S(1)}, bf16[8,3,24,384]{3,2,1,0:T(8,128)(2,1)S(1)}, u32[]{:S(2)}, u32[]{:S(2)}) %collective-permute-start.26) | collective-permute-done | bytes 442400 | tf_op jit(solution)/shard_map/ppermute | solution.py:456
  182.4 2.9 %fold.19 = (bf16[4,3,24,384]{3,2,1,0:T(8,128)(2,1)}, bf16[4,3,24,384]{3,2,1,0:T(8,128)(2,1)}, f32[8,768]{1,0:T(8,128)}) custom-call(s32[5]{0:T(128)} %stack.23.place_ref, bf16[2,2,4,2,3,24,384]{6,5,4,3,2,1,0:T(8,128)(2,1)} %bitcast.106, bf16[2,2,4,2,3,24,384]{6,5,4,3,2,1,0:T(8,128)(2,1)} %bitcast.121, bf16[2,4,3,24,384]{4,3,2,1,0:T(8,128)(2,1)} %copy-done.3, ...), custom_call_target="tpu_custom_call" | custom-call | flops 1024 | bytes 1024 | tf_op jit(solution)/shard_map/fold/pallas_call | solution.py:570
  192.4 3.3 %fold.22 = (bf16[2,1,24,1920]{3,2,1,0:T(8,128)(2,1)}, bf16[2,1,24,1920]{3,2,1,0:T(8,128)(2,1)}, bf16[2,1,24,1920]{3,2,1,0:T(8,128)(2,1)}) custom-call(s32[5]{0:T(128)} %stack.23.place_ref, bf16[2,2,1,4,2,24,1920]{6,5,4,3,2,1,0:T(8,128)(2,1)} %bitcast.138, bf16[2,2,1,4,2,24,1920]{6,5,4,3,2,1,0:T(8,128)(2,1)} %bitcast.149, ...), custom_call_target="tpu_custom_call" | custom-call | flops 1024 | bytes 1024 | tf_op jit(solution)/shard_map/fold/pallas_call | solution.py:570
  202.1 3.1 %own_in.1 = f32[256,768]{1,0:T(8,128)} custom-call(f32[256,768]{1,0:T(8,128)} %get-tuple-element.267.own_ref, bf16[256,768]{1,0:T(8,128)(2,1)} %copy-done.35, f32[256,768]{1,0:T(8,128)} %get-tuple-element.348.unit_ref, f32[256,1]{1,0:T(8,128)} %copy.53.inv_ref, f32[1,768]{1,0:T(1,128)} %broadcast_in_dim.47.gain_ref, f32[256,768]{1,0:T(8,128)} %get-tuple-element.307.above_ref), custom_call_target="tpu_custom_call" | custom-call | flops 1024 | bytes 1024 | tf_op jit(solution)/shard_map/own_in/pallas_call | solution.py:843
  206.0 2.8 %fold.20 = (bf16[2,1,3,24,384]{4,3,2,1,0:T(8,128)(2,1)}, bf16[2,1,3,24,384]{4,3,2,1,0:T(8,128)(2,1)}, bf16[2,1,3,24,384]{4,3,2,1,0:T(8,128)(2,1)}, f32[8,768]{1,0:T(8,128)}) custom-call(s32[5]{0:T(128)} %stack.23.place_ref, bf16[2,2,1,4,2,3,24,384]{7,6,5,4,3,2,1,0:T(8,128)(2,1)} %bitcast.108, bf16[2,2,1,4,2,3,24,384]{7,6,5,4,3,2,1,0:T(8,128)(2,1)} %bitcast.123, ...), custom_call_target="tpu_custom_call" | custom-call | flops 1024 | bytes 1024 | tf_op jit(solution)/shard_map/fold/pallas_call | solution.py:570
  212.9 2.9 %fold.23 = (f32[48,1536]{1,0:T(8,128)}, f32[48,384]{1,0:T(8,128)}) custom-call(s32[5]{0:T(128)} %stack.23.place_ref, bf16[2,2,4,2,24,1920]{5,4,3,2,1,0:T(8,128)(2,1)} %bitcast.144, bf16[2,2,4,2,24,1920]{5,4,3,2,1,0:T(8,128)(2,1)} %bitcast.155, bf16[2,4,24,1920]{3,2,1,0:T(8,128)(2,1)} %copy-done.5, bf16[4,24,1920]{2,1,0:T(8,128)(2,1)} %copy-done.16, ...), custom_call_target="tpu_custom_call" | custom-call | flops 1024 | bytes 1024 | tf_op jit(solution)/shard_map/fold/pallas_call | solution.py:570
  215.8 3.4 %collective-permute-start.40 = (f32[8,768]{1,0:T(8,128)S(1)}, f32[8,768]{1,0:T(8,128)S(1)}, u32[]{:S(2)}, u32[]{:S(2)}) collective-permute-start(f32[8,768]{1,0:T(8,128)S(1)} %add.78), channel_id=1, source_target_pairs={{0,16},{2,18},{4,20},{6,22},{8,24},{10,26},{12,28},{14,30},{16,0},... | collective-permute-start | bytes 73736 | tf_op jit(solution)/shard_map/ppermute | solution.py:452
  221.3 2.9 %collective-permute-start.35 = (bf16[2,1,3,24,384]{4,3,2,1,0:T(8,128)(2,1)S(1)}, bf16[2,1,3,24,384]{4,3,2,1,0:T(8,128)(2,1)S(1)}, u32[]{:S(2)}, u32[]{:S(2)}) collective-permute-start(bf16[2,1,3,24,384]{4,3,2,1,0:T(8,128)(2,1)S(1)} %copy-done.54), channel_id=1, source_target_pairs={{0,24},{2,26},{4,28},{6,30},{8,16},{10,18},{12,20},{14,22},{16,8},... | collective-permute-start | bytes 331784 | tf_op jit(solution)/shard_map/ppermute | solution.py:452
  225.4 5.7 %collective-permute-done.34.refs_5_.refs_12_.refs_19_.refs_26_.refs_33_.refs_40_ = bf16[2,1,3,24,384]{4,3,2,1,0:T(8,128)(2,1)S(1)} collective-permute-done((bf16[2,1,3,24,384]{4,3,2,1,0:T(8,128)(2,1)S(1)}, bf16[2,1,3,24,384]{4,3,2,1,0:T(8,128)(2,1)S(1)}, u32[]{:S(2)}, u32[]{:S(2)}) %collective-permute-start.34) | collective-permute-done | bytes 110624 | tf_op jit(solution)/shard_map/ppermute | solution.py:452
  (255 shorter events, 87.4 us)
Async XLA Ops:
  0.7 19.8 %collective-permute-start = (bf16[256,768]{1,0:T(8,128)(2,1)}, bf16[256,768]{1,0:T(8,128)(2,1)S(1)}, u32[]{:S(2)}, u32[]{:S(2)}) collective-permute-start(bf16[256,768]{1,0:T(8,128)(2,1)} %bitcast.211), channel_id=1, source_target_pairs={{0,1},{1,0},{2,3},{3,2},{4,5},{5,4},{6,7},{7,6},{8,9},{9,8},{10,11... | collective-permute-start | bytes 1179656 | tf_op jit(solution)/shard_map/ppermute | solution.py:456
  10.9 9.5 %collective-permute-start.2 = (f32[2,5,768]{2,1,0:T(8,128)S(1)}, f32[2,5,768]{2,1,0:T(8,128)S(1)}, u32[]{:S(2)}, u32[]{:S(2)}) collective-permute-start(f32[2,5,768]{2,1,0:T(8,128)S(1)} %pad_maximum_fusion.3), channel_id=1, source_target_pairs={{0,4},{2,6},{4,0},{6,2},{8,12},{10,14},{12,8},{14,10},{16,20},{18,... | collective-permute-start | bytes 92168 | tf_op jit(solution)/shard_map/ppermute | solution.py:452
  23.2 10.9 %collective-permute-start.3 = (f32[4,5,768]{2,1,0:T(8,128)S(1)}, f32[4,5,768]{2,1,0:T(8,128)S(1)}, u32[]{:S(2)}, u32[]{:S(2)}) collective-permute-start(f32[4,5,768]{2,1,0:T(8,128)S(1)} %pad_maximum_fusion.2), channel_id=1, source_target_pairs={{0,8},{2,10},{4,12},{6,14},{8,0},{10,2},{12,4},{14,6},{16,24},{18,... | collective-permute-start | bytes 184328 | tf_op jit(solution)/shard_map/ppermute | solution.py:452
  36.2 12.8 %collective-permute-start.5 = (f32[8,5,768]{2,1,0:T(8,128)S(1)}, f32[8,5,768]{2,1,0:T(8,128)S(1)}, u32[]{:S(2)}, u32[]{:S(2)}) collective-permute-start(f32[8,5,768]{2,1,0:T(8,128)S(1)} %pad_maximum_fusion.1), channel_id=1, source_target_pairs={{0,16},{2,18},{4,20},{6,22},{8,24},{10,26},{12,28},{14,30},{16,0},... | collective-permute-start | bytes 368648 | tf_op jit(solution)/shard_map/ppermute | solution.py:452
  75.7 15.9 %collective-permute-start.8 = (bf16[8,96,384]{2,1,0:T(8,128)(2,1)}, bf16[8,96,384]{2,1,0:T(8,128)(2,1)S(1)}, u32[]{:S(2)}, u32[]{:S(2)}) collective-permute-start(bf16[8,96,384]{2,1,0:T(8,128)(2,1)} %get-tuple-element.216), channel_id=1, source_target_pairs={{0,1},{1,0},{2,3},{3,2},{4,5},{5,4},{6,7},{7,6},{8,9},{9,8},{10,11... | collective-permute-start | bytes 1769480 | tf_op jit(solution)/shard_map/ppermute | solution.py:456
  77.2 15.6 %collective-permute-start.9 = (bf16[2,4,96,384]{3,2,1,0:T(8,128)(2,1)}, bf16[2,4,96,384]{3,2,1,0:T(8,128)(2,1)S(1)}, u32[]{:S(2)}, u32[]{:S(2)}) collective-permute-start(bf16[2,4,96,384]{3,2,1,0:T(8,128)(2,1)} %get-tuple-element.217), channel_id=1, source_target_pairs={{0,4},{2,6},{4,0},{6,2},{8,12},{10,14},{12,8},{14,10},{16,20},{18,... | collective-permute-start | bytes 1769480 | tf_op jit(solution)/shard_map/ppermute | solution.py:452
  77.8 13.8 %collective-permute-start.10 = (f32[24,768]{1,0:T(8,128)}, f32[24,768]{1,0:T(8,128)S(1)}, u32[]{:S(2)}, u32[]{:S(2)}) collective-permute-start(f32[24,768]{1,0:T(8,128)} %get-tuple-element.218.refs_6_), channel_id=1, source_target_pairs={{0,2},{2,0},{4,6},{6,4},{8,10},{10,8},{12,14},{14,12},{16,18},{18,... | collective-permute-start | bytes 221192 | tf_op jit(solution)/shard_map/ppermute | solution.py:452
  93.7 15.9 %collective-permute-start.11 = (bf16[2,2,8,24,1920]{4,3,2,1,0:T(8,128)(2,1)}, bf16[2,2,8,24,1920]{4,3,2,1,0:T(8,128)(2,1)S(1)}, u32[]{:S(2)}, u32[]{:S(2)}) collective-permute-start(bf16[2,2,8,24,1920]{4,3,2,1,0:T(8,128)(2,1)} %get-tuple-element.233), channel_id=1, source_target_pairs={{0,2},{2,0},{4,6},{6,4},{8,10},{10,8},{12,14},{14,12},{16,18},{18,... | collective-permute-start | bytes 8847368 | tf_op jit(solution)/shard_map/ppermute | solution.py:452
  96.8 12.8 %collective-permute-start.12 = (bf16[4,96,384]{2,1,0:T(8,128)(2,1)}, bf16[4,96,384]{2,1,0:T(8,128)(2,1)S(1)}, u32[]{:S(2)}, u32[]{:S(2)}) collective-permute-start(bf16[4,96,384]{2,1,0:T(8,128)(2,1)} %get-tuple-element.234), channel_id=1, source_target_pairs={{0,4},{2,6},{4,0},{6,2},{8,12},{10,14},{12,8},{14,10},{16,20},{18,... | collective-permute-start | bytes 884744 | tf_op jit(solution)/shard_map/ppermute | solution.py:452
  97.5 12.1 %collective-permute-start.13 = (bf16[4,96,384]{2,1,0:T(8,128)(2,1)}, bf16[4,96,384]{2,1,0:T(8,128)(2,1)S(1)}, u32[]{:S(2)}, u32[]{:S(2)}) collective-permute-start(bf16[4,96,384]{2,1,0:T(8,128)(2,1)} %get-tuple-element.235), channel_id=1, source_target_pairs={{0,1},{1,0},{2,3},{3,2},{4,5},{5,4},{6,7},{7,6},{8,9},{9,8},{10,11... | collective-permute-start | bytes 884744 | tf_op jit(solution)/shard_map/ppermute | solution.py:456
  98.0 11.6 %collective-permute-start.14 = (f32[32,768]{1,0:T(8,128)}, f32[32,768]{1,0:T(8,128)}, u32[]{:S(2)}, u32[]{:S(2)}) collective-permute-start(f32[32,768]{1,0:T(8,128)} %get-tuple-element.236.refs_4_), channel_id=1, source_target_pairs={{0,4},{2,6},{4,0},{6,2},{8,12},{10,14},{12,8},{14,10},{16,20},{18,... | collective-permute-start | bytes 294920 | tf_op jit(solution)/shard_map/ppermute | solution.py:452
  120.8 15.8 %collective-permute-start.16 = (bf16[2,2,8,3,24,384]{5,4,3,2,1,0:T(8,128)(2,1)}, bf16[2,2,8,3,24,384]{5,4,3,2,1,0:T(8,128)(2,1)S(1)}, u32[]{:S(2)}, u32[]{:S(2)}) collective-permute-start(bf16[2,2,8,3,24,384]{5,4,3,2,1,0:T(8,128)(2,1)} %get-tuple-element.271), channel_id=1, source_target_pairs={{0,2},{2,0},{4,6},{6,4},{8,10},{10,8},{12,14},{14,12},{16,18},{18,... | collective-permute-start | bytes 5308424 | tf_op jit(solution)/shard_map/ppermute | solution.py:452
  120.9 19.1 %collective-permute-start.17 = (bf16[2,4,24,1920]{3,2,1,0:T(8,128)(2,1)}, bf16[2,4,24,1920]{3,2,1,0:T(8,128)(2,1)S(1)}, u32[]{:S(2)}, u32[]{:S(2)}) collective-permute-start(bf16[2,4,24,1920]{3,2,1,0:T(8,128)(2,1)} %get-tuple-element.275), channel_id=1, source_target_pairs={{0,4},{2,6},{4,0},{6,2},{8,12},{10,14},{12,8},{14,10},{16,20},{18,... | collective-permute-start | bytes 2211848 | tf_op jit(solution)/shard_map/ppermute | solution.py:452
  121.5 19.7 %collective-permute-start.18 = (bf16[8,24,1920]{2,1,0:T(8,128)(2,1)}, bf16[8,24,1920]{2,1,0:T(8,128)(2,1)S(1)}, u32[]{:S(2)}, u32[]{:S(2)}) collective-permute-start(bf16[8,24,1920]{2,1,0:T(8,128)(2,1)} %get-tuple-element.276), channel_id=1, source_target_pairs={{0,1},{1,0},{2,3},{3,2},{4,5},{5,4},{6,7},{7,6},{8,9},{9,8},{10,11... | collective-permute-start | bytes 2211848 | tf_op jit(solution)/shard_map/ppermute | solution.py:456
  129.0 24.7 %collective-permute-start.21 = (f32[80,768]{1,0:T(8,128)}, f32[80,768]{1,0:T(8,128)}, u32[]{:S(2)}, u32[]{:S(2)}) collective-permute-start(f32[80,768]{1,0:T(8,128)} %get-tuple-element.286.refs_14_), channel_id=1, source_target_pairs={{0,16},{2,18},{4,20},{6,22},{8,24},{10,26},{12,28},{14,30},{16,0},... | collective-permute-start | bytes 737288 | tf_op jit(solution)/shard_map/ppermute | solution.py:452
  129.4 21.1 %collective-permute-start.22 = (bf16[2,1,96,384]{3,2,1,0:T(8,128)(2,1)}, bf16[2,1,96,384]{3,2,1,0:T(8,128)(2,1)S(1)}, u32[]{:S(2)}, u32[]{:S(2)}) collective-permute-start(bf16[2,1,96,384]{3,2,1,0:T(8,128)(2,1)} %get-tuple-element.288), channel_id=1, source_target_pairs={{0,8},{2,10},{4,12},{6,14},{8,0},{10,2},{12,4},{14,6},{16,24},{18,... | collective-permute-start | bytes 442376 | tf_op jit(solution)/shard_map/ppermute | solution.py:452
  136.7 17.1 %collective-permute-start.23 = (bf16[2,1,96,384]{3,2,1,0:T(8,128)(2,1)}, bf16[2,1,96,384]{3,2,1,0:T(8,128)(2,1)S(1)}, u32[]{:S(2)}, u32[]{:S(2)}) collective-permute-start(bf16[2,1,96,384]{3,2,1,0:T(8,128)(2,1)} %get-tuple-element.289), channel_id=1, source_target_pairs={{0,16},{2,18},{4,20},{6,22},{8,24},{10,26},{12,28},{14,30},{16,0},... | collective-permute-start | bytes 442376 | tf_op jit(solution)/shard_map/ppermute | solution.py:452
  140.0 13.8 %collective-permute-start.24 = (bf16[2,1,96,384]{3,2,1,0:T(8,128)(2,1)}, bf16[2,1,96,384]{3,2,1,0:T(8,128)(2,1)}, u32[]{:S(2)}, u32[]{:S(2)}) collective-permute-start(bf16[2,1,96,384]{3,2,1,0:T(8,128)(2,1)} %get-tuple-element.290), channel_id=1, source_target_pairs={{0,24},{2,26},{4,28},{6,30},{8,16},{10,18},{12,20},{14,22},{16,8},... | collective-permute-start | bytes 442376 | tf_op jit(solution)/shard_map/ppermute | solution.py:452
  149.7 16.0 %collective-permute-start.27 = (f32[8,768]{1,0:T(8,128)}, f32[8,768]{1,0:T(8,128)S(1)}, u32[]{:S(2)}, u32[]{:S(2)}) collective-permute-start(f32[8,768]{1,0:T(8,128)} %get-tuple-element.300.refs_6_), channel_id=1, source_target_pairs={{0,4},{2,6},{4,0},{6,2},{8,12},{10,14},{12,8},{14,10},{16,20},{18,... | collective-permute-start | bytes 73736 | tf_op jit(solution)/shard_map/ppermute | solution.py:452
  159.9 38.2 %collective-permute-start.20 = (bf16[256,768]{1,0:T(8,128)(2,1)}, bf16[256,768]{1,0:T(8,128)(2,1)S(1)}, u32[]{:S(2)}, u32[]{:S(2)}) collective-permute-start(bf16[256,768]{1,0:T(8,128)(2,1)} %get-tuple-element.285), channel_id=1, source_target_pairs={{0,1},{1,0},{2,3},{3,2},{4,5},{5,4},{6,7},{7,6},{8,9},{9,8},{10,11... | collective-permute-start | bytes 1179656 | tf_op jit(solution)/shard_map/ppermute | solution.py:456
  160.5 13.0 %collective-permute-start.25 = (bf16[2,4,3,24,384]{4,3,2,1,0:T(8,128)(2,1)S(1)}, bf16[2,4,3,24,384]{4,3,2,1,0:T(8,128)(2,1)S(1)}, u32[]{:S(2)}, u32[]{:S(2)}) collective-permute-start(bf16[2,4,3,24,384]{4,3,2,1,0:T(8,128)(2,1)S(1)} %copy-done.53), channel_id=1, source_target_pairs={{0,4},{2,6},{4,0},{6,2},{8,12},{10,14},{12,8},{14,10},{16,20},{18,... | collective-permute-start | bytes 1327112 | tf_op jit(solution)/shard_map/ppermute | solution.py:452
  161.8 19.8 %collective-permute-start.26 = (bf16[8,3,24,384]{3,2,1,0:T(8,128)(2,1)S(1)}, bf16[8,3,24,384]{3,2,1,0:T(8,128)(2,1)S(1)}, u32[]{:S(2)}, u32[]{:S(2)}) collective-permute-start(bf16[8,3,24,384]{3,2,1,0:T(8,128)(2,1)S(1)} %copy-done.52), channel_id=1, source_target_pairs={{0,1},{1,0},{2,3},{3,2},{4,5},{5,4},{6,7},{7,6},{8,9},{9,8},{10,11... | collective-permute-start | bytes 1327112 | tf_op jit(solution)/shard_map/ppermute | solution.py:456
  163.4 25.9 %collective-permute-start.28 = (bf16[4,24,1920]{2,1,0:T(8,128)(2,1)}, bf16[4,24,1920]{2,1,0:T(8,128)(2,1)S(1)}, u32[]{:S(2)}, u32[]{:S(2)}) collective-permute-start(bf16[4,24,1920]{2,1,0:T(8,128)(2,1)} %get-tuple-element.303), channel_id=1, source_target_pairs={{0,1},{1,0},{2,3},{3,2},{4,5},{5,4},{6,7},{7,6},{8,9},{9,8},{10,11... | collective-permute-start | bytes 1105928 | tf_op jit(solution)/shard_map/ppermute | solution.py:456
  165.8 25.9 %collective-permute-start.29 = (bf16[4,24,1920]{2,1,0:T(8,128)(2,1)}, bf16[4,24,1920]{2,1,0:T(8,128)(2,1)S(1)}, u32[]{:S(2)}, u32[]{:S(2)}) collective-permute-start(bf16[4,24,1920]{2,1,0:T(8,128)(2,1)} %get-tuple-element.304), channel_id=1, source_target_pairs={{0,4},{2,6},{4,0},{6,2},{8,12},{10,14},{12,8},{14,10},{16,20},{18,... | collective-permute-start | bytes 1105928 | tf_op jit(solution)/shard_map/ppermute | solution.py:452
  185.4 12.7 %collective-permute-start.30 = (f32[8,768]{1,0:T(8,128)}, f32[8,768]{1,0:T(8,128)S(1)}, u32[]{:S(2)}, u32[]{:S(2)}) collective-permute-start(f32[8,768]{1,0:T(8,128)} %get-tuple-element.313.refs_24_), channel_id=1, source_target_pairs={{0,1},{1,0},{2,3},{3,2},{4,5},{5,4},{6,7},{7,6},{8,9},{9,8},{10,11... | collective-permute-start | bytes 73736 | tf_op jit(solution)/shard_map/ppermute | solution.py:456
  185.8 19.4 %collective-permute-start.31 = (bf16[4,3,24,384]{3,2,1,0:T(8,128)(2,1)}, bf16[4,3,24,384]{3,2,1,0:T(8,128)(2,1)S(1)}, u32[]{:S(2)}, u32[]{:S(2)}) collective-permute-start(bf16[4,3,24,384]{3,2,1,0:T(8,128)(2,1)} %get-tuple-element.308), channel_id=1, source_target_pairs={{0,1},{1,0},{2,3},{3,2},{4,5},{5,4},{6,7},{7,6},{8,9},{9,8},{10,11... | collective-permute-start | bytes 663560 | tf_op jit(solution)/shard_map/ppermute | solution.py:456
  189.3 16.0 %collective-permute-start.32 = (bf16[4,3,24,384]{3,2,1,0:T(8,128)(2,1)}, bf16[4,3,24,384]{3,2,1,0:T(8,128)(2,1)S(1)}, u32[]{:S(2)}, u32[]{:S(2)}) collective-permute-start(bf16[4,3,24,384]{3,2,1,0:T(8,128)(2,1)} %get-tuple-element.309), channel_id=1, source_target_pairs={{0,4},{2,6},{4,0},{6,2},{8,12},{10,14},{12,8},{14,10},{16,20},{18,... | collective-permute-start | bytes 663560 | tf_op jit(solution)/shard_map/ppermute | solution.py:452
  195.7 14.9 %collective-permute-start.36 = (bf16[2,1,24,1920]{3,2,1,0:T(8,128)(2,1)}, bf16[2,1,24,1920]{3,2,1,0:T(8,128)(2,1)S(1)}, u32[]{:S(2)}, u32[]{:S(2)}) collective-permute-start(bf16[2,1,24,1920]{3,2,1,0:T(8,128)(2,1)} %get-tuple-element.326), channel_id=1, source_target_pairs={{0,8},{2,10},{4,12},{6,14},{8,0},{10,2},{12,4},{14,6},{16,24},{18,... | collective-permute-start | bytes 552968 | tf_op jit(solution)/shard_map/ppermute | solution.py:452
  198.1 13.5 %collective-permute-start.37 = (bf16[2,1,24,1920]{3,2,1,0:T(8,128)(2,1)}, bf16[2,1,24,1920]{3,2,1,0:T(8,128)(2,1)S(1)}, u32[]{:S(2)}, u32[]{:S(2)}) collective-permute-start(bf16[2,1,24,1920]{3,2,1,0:T(8,128)(2,1)} %get-tuple-element.327), channel_id=1, source_target_pairs={{0,16},{2,18},{4,20},{6,22},{8,24},{10,26},{12,28},{14,30},{16,0},... | collective-permute-start | bytes 552968 | tf_op jit(solution)/shard_map/ppermute | solution.py:452
  198.1 13.5 %collective-permute-start.38 = (bf16[2,1,24,1920]{3,2,1,0:T(8,128)(2,1)}, bf16[2,1,24,1920]{3,2,1,0:T(8,128)(2,1)S(1)}, u32[]{:S(2)}, u32[]{:S(2)}) collective-permute-start(bf16[2,1,24,1920]{3,2,1,0:T(8,128)(2,1)} %get-tuple-element.328), channel_id=1, source_target_pairs={{0,24},{2,26},{4,28},{6,30},{8,16},{10,18},{12,20},{14,22},{16,8},... | collective-permute-start | bytes 552968 | tf_op jit(solution)/shard_map/ppermute | solution.py:452
  219.8 11.3 %collective-permute-start.34 = (bf16[2,1,3,24,384]{4,3,2,1,0:T(8,128)(2,1)S(1)}, bf16[2,1,3,24,384]{4,3,2,1,0:T(8,128)(2,1)S(1)}, u32[]{:S(2)}, u32[]{:S(2)}) collective-permute-start(bf16[2,1,3,24,384]{4,3,2,1,0:T(8,128)(2,1)S(1)} %copy-done.55), channel_id=1, source_target_pairs={{0,16},{2,18},{4,20},{6,22},{8,24},{10,26},{12,28},{14,30},{16,0},... | collective-permute-start | bytes 331784 | tf_op jit(solution)/shard_map/ppermute | solution.py:452
  221.3 9.8 %collective-permute-start.35 = (bf16[2,1,3,24,384]{4,3,2,1,0:T(8,128)(2,1)S(1)}, bf16[2,1,3,24,384]{4,3,2,1,0:T(8,128)(2,1)S(1)}, u32[]{:S(2)}, u32[]{:S(2)}) collective-permute-start(bf16[2,1,3,24,384]{4,3,2,1,0:T(8,128)(2,1)S(1)} %copy-done.54), channel_id=1, source_target_pairs={{0,24},{2,26},{4,28},{6,30},{8,16},{10,18},{12,20},{14,22},{16,8},... | collective-permute-start | bytes 331784 | tf_op jit(solution)/shard_map/ppermute | solution.py:452
  (68 other events, 317.4 us)

commit v4 on v3

--- a/solution.py
+++ b/solution.py
@@ -274,6 +274,76 @@
     )
 
 
+def exact(contract, left, right):
+    return lax.dot_general(
+        left, right, (contract, ((), ())), precision=highest, preferred_element_type=f32
+    )
+
+
+def pool_weights_kernel(
+    images, place_ref, rows_ref, probe_ref, probe_query_ref, query_ref, key_ref, *out_refs
+):
+    query_out, key_out, value_out, output_out, probe_out, final_out = out_refs
+    width = rows_ref.shape[1]
+    block = width // images
+    half = width // 2
+    near = HEADS // 2
+    heads = head_rows(width)
+    first = place_ref[1] == 0
+
+    def mine(value):
+        return jnp.where(first, value[:, :half], value[:, half:])
+
+    pick = lax.broadcasted_iota(jnp.int32, (block, width), 1) == (
+        lax.broadcasted_iota(jnp.int32, (block, width), 0) + place_ref[0] * block
+    )
+    pick = pick.astype(f32)
+    rows = exact(((1,), (1,)), pick, rows_ref[...])
+    probe_query_grad = jnp.sum(wide(nn, rows_ref[:TOP], key_ref[...]) * heads, axis=0, keepdims=True)
+    own_probe = jnp.sum(pick * probe_ref[...], axis=1, keepdims=True)
+    query_out[...] = own_probe * mine(probe_query_grad)
+    probe_out[...] = jnp.sum(query_ref[...].astype(f32) * probe_query_grad, axis=1, keepdims=True)
+    final_out[...] = rows[:, HEADS : HEADS + 1]
+    key_out[...] = exact(((1,), (0,)), rows[:, :TOP], mine(probe_query_ref[...] * heads))
+    row = lax.broadcasted_iota(jnp.int32, (8, half), 0)
+    lane = lax.broadcasted_iota(jnp.int32, (8, half), 1)
+    own_heads = (lane // HEAD == row).astype(f32)
+    value_rights, output_rights = [], []
+    for i in range(images):
+        factor = rows_ref[TOP + 8 * i : TOP + 8 * i + 8]
+        pair = factor[near + 1 : near + 2]
+        value_rights.append(pair[:, half:] * own_heads)
+        output_rights.append(jnp.where(row == near, pair[:, :half], 0.0))
+    left = rows[:, TOP:]
+    value_out[...] = exact(((1,), (0,)), left, jnp.concatenate(value_rights, axis=0))
+    output_out[...] = exact(((1,), (0,)), left, jnp.concatenate(output_rights, axis=0))
+
+
+def pool_weights_call(place, rows, probe, probe_query, pool_query, pool_key, images):
+    width = rows.shape[1]
+    block = width // images
+    whole = lambda *shape: pl.BlockSpec(shape, lambda i, p: (0,) * len(shape))
+    grads = [(block, width // 2)] * 4 + [(block, 1)] * 2
+    return pl.pallas_call(
+        functools.partial(pool_weights_kernel, images),
+        grid_spec=pltpu.PrefetchScalarGridSpec(
+            num_scalar_prefetch=1,
+            grid=(1,),
+            in_specs=[
+                whole(*rows.shape),
+                whole(1, width),
+                whole(1, width),
+                whole(block, width),
+                whole(width, width),
+            ],
+            out_specs=[whole(*t) for t in grads],
+        ),
+        out_shape=[jax.ShapeDtypeStruct(t, f32) for t in grads],
+        cost_estimate=light,
+        name="pool_weights",
+    )(place, rows, probe, probe_query, pool_query, pool_key)
+
+
 def attend_kernel(q_ref, ka_ref, kb_ref, va_ref, vb_ref, a_ref, lse_ref):
     q = q_ref[...]
     k = jnp.concatenate([ka_ref[...], kb_ref[...]], axis=0)
@@ -490,8 +560,9 @@
 
 def fold_kernel(plan, gathers, place_ref, *refs):
     count = sum(sum(slots) for slots, _ in plan)
-    inputs = iter(refs[: count + 2 * len(gathers)])
-    outs = iter(refs[count + 2 * len(gathers) :])
+    count += 2 * len(gathers)
+    inputs = iter(refs[:count])
+    outs = iter(refs[count:])
     for slots, join in plan:
         out = next(outs)
         extra = next(outs) if join == "wide" else None
@@ -564,7 +635,7 @@
     for own, other, gather in notes:
         rows, width = own.shape
         arrays += [own, other]
-        specs += [whole(own.shape), whole(other.shape)]
+        specs += [whole(own.shape)] * 2
         gathers.append(gather)
         shapes.append(((2 * rows - TOP if gather else rows, width), f32))
     return pl.pallas_call(
@@ -645,16 +716,20 @@
     return [img_swap(send, 4 * d) for d, send in zip((1, 2, 3), sends)]
 
 
-def take(place, first, second, arrived):
+def far_send(first, second, k):
+    return [([first.stage_z(k), second.stage_z(k)], "stack")]
+
+
+def take(first, second, arrived, done):
     for array in arrived:
         for group in (first, second):
-            group.arrived.append((array, 2))
+            group.arrived.append((array, done))
+
+
+def finish(place, first, second):
     for bit in range(4, img_bits()):
-        k = bit - 2
-        (send,) = fold(place, [([first.stage_z(k), second.stage_z(k)], "stack")], bf16)
-        array = img_swap(send, 1 << bit)
-        for group in (first, second):
-            group.arrived.append((array, k + 1))
+        (send,) = fold(place, far_send(first, second, bit - 2), bf16)
+        take(first, second, [img_swap(send, 1 << bit)], bit - 1)
 
 
 def gelu_back_kernel(grad_ref, down_ref, up_ref, out_ref):
@@ -692,13 +767,12 @@
     scaled = grad * gain
     first_mean = jnp.mean(scaled, axis=-1, keepdims=True)
     second_mean = jnp.mean(scaled * unit, axis=-1, keepdims=True)
-    gain_grad = jnp.sum(grad * unit, axis=0, keepdims=True)
-    return inv * (scaled - first_mean - unit * second_mean), gain_grad
+    return inv * (scaled - first_mean - unit * second_mean)
 
 
 def up_back_kernel(
     block, place_ref, low_ref, du_ref, up_ref, unit_ref, inv_ref, gain_ref, above_ref, wo_ref,
-    a_ref, send_ref, keep_ref, grad_ref, heads_ref, gain_grad_ref, acc_ref, out_ref,
+    a_ref, send_ref, keep_ref, grad_ref, heads_ref, acc_ref, out_ref,
 ):
     c = pl.program_id(0)
     steps = pl.num_programs(0) // 2
@@ -721,11 +795,9 @@
 
     @pl.when(c == steps - 1)
     def _():
-        through, gain_grad = norm_back_rows(
+        total = above_ref[...] + norm_back_rows(
             acc_ref[...], unit_ref[...], inv_ref[...], gain_ref[...]
         )
-        total = above_ref[...] + through
-        gain_grad_ref[...] = gain_grad
         grad_ref[...] = total
         branch = total.astype(bf16)
         heads_ref[...] = nt(branch, wo_ref[...]).astype(bf16)
@@ -786,14 +858,12 @@
             half_spec,
             whole(rows, width),
             whole(rows, width),
-            whole(1, width),
         ],
         out_shape=[
             half_shape,
             half_shape,
             jax.ShapeDtypeStruct((rows, width), f32),
             jax.ShapeDtypeStruct((rows, width), bf16),
-            jax.ShapeDtypeStruct((1, width), f32),
         ],
         scratch_shapes=[
             pltpu.VMEM((rows, width), f32),
@@ -801,41 +871,32 @@
         ],
         cost_estimate=light,
         name="up_back",
-    )(place, low, du, w_up, unit, inv, gain[None], above, w_output, attended)
-
-
-def parts_in_kernel(
-    dq_ref, dk_ref, dv_ref, wq_ref, wk_ref, wv_ref, unit_ref, other_unit_ref, second_ref,
-    own_ref, other_ref, gains_ref,
-):
+    )(place, low, du, w_up, unit, inv, gain, above, w_output, attended)
+
+
+def parts_in_kernel(dq_ref, dk_ref, dv_ref, wq_ref, wk_ref, wv_ref, own_ref, other_ref):
     rows = dq_ref.shape[0]
     both = nt(dk_ref[...], wk_ref[...]) + nt(dv_ref[...], wv_ref[...])
-    own = nt(dq_ref[...], wq_ref[...]) + both[:rows]
-    other = both[rows:]
-    own_ref[...] = own
-    other_ref[...] = other.astype(bf16)
-    first = jnp.sum(own * unit_ref[...] + other * other_unit_ref[...], axis=0, keepdims=True)
-    row = lax.broadcasted_iota(jnp.int32, gains_ref.shape, 0)
-    gains_ref[...] = jnp.where(row == 0, second_ref[...], jnp.where(row == 1, first, 0.0))
-
-
-def parts_in_call(dq, dk, dv, w_query, w_key, w_value, unit, other_unit, second):
+    own_ref[...] = nt(dq_ref[...], wq_ref[...]) + both[:rows]
+    other_ref[...] = both[rows:].astype(bf16)
+
+
+def parts_in_call(dq, dk, dv, w_query, w_key, w_value):
     rows, width = dq.shape
     return pl.pallas_call(
         parts_in_kernel,
         out_shape=[
             jax.ShapeDtypeStruct((rows, width), f32),
             jax.ShapeDtypeStruct((rows, width), bf16),
-            jax.ShapeDtypeStruct((8, width), f32),
         ],
         cost_estimate=light,
         name="parts_in",
-    )(dq, dk, dv, w_query, w_key, w_value, unit, other_unit, second)
+    )(dq, dk, dv, w_query, w_key, w_value)
 
 
 def own_in_kernel(own_ref, arrived_ref, unit_ref, inv_ref, gain_ref, above_ref, out_ref):
     grad = own_ref[...] + arrived_ref[...].astype(f32)
-    through, _ = norm_back_rows(grad, unit_ref[...], inv_ref[...], gain_ref[...])
+    through = norm_back_rows(grad, unit_ref[...], inv_ref[...], gain_ref[...])
     out_ref[...] = above_ref[...] + through
 
 
@@ -845,7 +906,7 @@
         out_shape=jax.ShapeDtypeStruct(own.shape, f32),
         cost_estimate=light,
         name="own_in",
-    )(own, arrived, unit, inv, gain[None], above)
+    )(own, arrived, unit, inv, gain, above)
 
 
 class Order:
@@ -890,6 +951,10 @@
     caps = captions.shape[0]
     place = jnp.stack([me, seq_me, me & 1, (me >> 1) & 1, me >> 2]).astype(jnp.int32)
 
+    own_query = lax.dynamic_slice_in_dim(pool_query, me * (width // images), width // images, 0)
+    first_row, second_row = first_gain[None], second_gain[None]
+    place, own_query, first_row, second_row = tie(place, own_query, first_row, second_row)
+
     other_tokens = seq_swap(own_tokens)
 
     gathered = captions[None]
@@ -911,8 +976,7 @@
     other_tokens, gathered, queries, keys_own, values_own, key_probe = tie(
         other_tokens, gathered, queries, keys_own, values_own, key_probe
     )
-    normed_other, unit_other, _ = layer_norm(other_tokens.astype(f32), first_gain)
-    low_other = normed_other.astype(bf16)
+    low_other = layer_norm(other_tokens.astype(f32), first_gain)[0].astype(bf16)
     keys_other = low_dot(low_other, w_key).astype(bf16)
     values_other = low_dot(low_other, w_value).astype(bf16)
     gathered = gather_more(gathered, 2)
@@ -950,26 +1014,30 @@
     down_a = Staged(0, True, down_keep, down_core)
     down_b = Staged(1, False, down_keep, down_core)
 
-    def first_stage(first, second, notes=()):
-        return fold(place, [([first.stage_one()], None), ([second.stage_one()], None)], bf16, notes)
-
-    def second_stage(first, second, notes=()):
-        return fold(place, [([first.stage_two()], None), ([second.stage_two()], None)], bf16, notes)
-
-    send_a, send_b, message = first_stage(down_a, down_b, [(message, message_in, False)])
+    def first_stage(first, second):
+        return [([first.stage_one()], None), ([second.stage_one()], None)]
+
+    def second_stage(first, second):
+        return [([first.stage_two()], None), ([second.stage_two()], None)]
+
+    send_a, send_b, message = fold(
+        place, first_stage(down_a, down_b), bf16, [(message, message_in, False)]
+    )
     up_grad_low, send_a, send_b, message = step(up_grad_low, send_a, send_b, message)
     down_a.first = seq_swap(send_a)
     down_b.first = img_swap(send_b, 2)
     message_in = img_swap(message, 1)
-    up_send, up_keep, residual_grad, attended_grad, second_gain_grad = up_back_call(
-        place, second_low, up_grad_low, w_up, unit_two, scale_two, second_gain, result_grad,
+    up_send, up_keep, residual_grad, attended_grad = up_back_call(
+        place, second_low, up_grad_low, w_up, unit_two, scale_two, second_row, result_grad,
         w_output, attended_low, images,
     )
-    attended_grad, up_send, down_a.first, down_b.first, message_in = step(
-        attended_grad, up_send, down_a.first, down_b.first, message_in
+    attended_grad, up_send, message_in, down_a.first, down_b.first = step(
+        attended_grad, up_send, message_in, down_a.first, down_b.first
     )
     up_core = img_swap(up_send, 1)
-    send_a, send_b, message = second_stage(down_a, down_b, [(message, message_in, True)])
+    send_a, send_b, message = fold(
+        place, second_stage(down_a, down_b), bf16, [(message, message_in, True)]
+    )
     attended_grad, send_a, send_b, message = step(attended_grad, send_a, send_b, message)
     down_a.second = img_swap(send_a, 2)
     down_b.second = seq_swap(send_b)
@@ -978,156 +1046,148 @@
     query_grad, key_part, value_part = attend_back(
         queries, keys_own, keys_other, values_own, values_other, attended_grad, log_totals
     )
-    query_grad, key_part, value_part, up_core, down_a.second, down_b.second, message_in = step(
-        query_grad, key_part, value_part, up_core, down_a.second, down_b.second, message_in
+    query_grad, key_part, value_part, up_core, message_in, down_a.second, down_b.second = step(
+        query_grad, key_part, value_part, up_core, message_in, down_a.second, down_b.second
     )
     up_a = Staged(0, False, up_keep, up_core)
     up_b = Staged(1, True, up_keep, up_core)
-    send_a, send_b, message = first_stage(up_a, up_b, [(message, message_in, True)])
-    query_grad, key_part, value_part, send_a, send_b, message = step(
-        query_grad, key_part, value_part, send_a, send_b, message
-    )
+    three_send, three_keep = wgrad_three(
+        place, low_own, low_other, query_grad, key_part, value_part, images
+    )
+    send_a, send_b, down_send, message = fold(
+        place,
+        first_stage(up_a, up_b) + far_send(down_a, down_b, 0),
+        bf16,
+        [(message, message_in, True)],
+    )
+    three_send, three_keep, query_grad, send_a, send_b, down_send, message = step(
+        three_send, three_keep, query_grad, send_a, send_b, down_send, message
+    )
+
+    three_core = img_swap(three_send, 1)
     up_a.first = img_swap(send_a, 2)
     up_b.first = seq_swap(send_b)
+    down_in = img_swap(down_send, 4)
     message_in = img_swap(message, 4)
-    three_send, three_keep = wgrad_three(
-        place, low_own, low_other, query_grad, key_part, value_part, images
-    )
-    three_send, query_grad, key_part, value_part, message_in = step(
-        three_send, query_grad, key_part, value_part, message_in
-    )
-    three_core = img_swap(three_send, 1)
-    *down_sends, message = fold(
-        place, near_sends(down_a, down_b), bf16, [(message, message_in, True)]
-    )
-    query_grad, *down_sends, message = step(query_grad, *down_sends, message)
-    message_in = img_swap(message, 8)
-    own_part, other_part, gains = parts_in_call(
-        query_grad, key_part, value_part, w_query, w_key, w_value, unit_one, unit_other,
-        second_gain_grad,
-    )
-    other_part, gains, three_core = step(other_part, gains, three_core)
-    down_in = near_swap(down_sends)
-    gains_in = img_swap(gains, 1)
+    own_part, other_part = parts_in_call(
+        query_grad, key_part, value_part, w_query, w_key, w_value
+    )
+    own_part, other_part, three_core, up_a.first, up_b.first, down_in, message_in = step(
+        own_part, other_part, three_core, up_a.first, up_b.first, down_in, message_in
+    )
+    take(down_a, down_b, [down_in], 1)
     three_a = Staged(0, False, three_keep, three_core)
     three_b = Staged(1, True, three_keep, three_core)
-    send_a, send_b = first_stage(three_a, three_b)
-    send_a, send_b, up_a.first, up_b.first, gains_in = step(
-        send_a, send_b, up_a.first, up_b.first, gains_in
-    )
+    send_a, send_b, send_c, send_d, message = fold(
+        place,
+        first_stage(three_a, three_b) + second_stage(up_a, up_b),
+        bf16,
+        [(message, message_in, True)],
+    )
+    send_a, send_b, send_c, send_d, message, other_part = step(
+        send_a, send_b, send_c, send_d, message, other_part
+    )
+
     three_a.first = img_swap(send_a, 2)
     three_b.first = seq_swap(send_b)
-    send_a, send_b, gains = second_stage(up_a, up_b, [(gains, gains_in, False)])
-    send_a, send_b, gains, other_part = step(send_a, send_b, gains, other_part)
-    gains_in = img_swap(gains, 2)
-    up_a.second = seq_swap(send_a)
-    up_b.second = img_swap(send_b, 2)
+    up_a.second = seq_swap(send_c)
+    up_b.second = img_swap(send_d, 2)
+    message_in = img_swap(message, 8)
+    (down_send,) = fold(place, far_send(down_a, down_b, 1), bf16)
+    down_send, message_in, three_a.first, three_b.first, up_a.second, up_b.second = step(
+        down_send, message_in, three_a.first, three_b.first, up_a.second, up_b.second
+    )
+    send_a, send_b, up_send, message = fold(
+        place,
+        second_stage(three_a, three_b) + far_send(up_a, up_b, 0),
+        bf16,
+        [(message, message_in, True)],
+    )
+    other_part, send_a, send_b, up_send, down_send, message = step(
+        other_part, send_a, send_b, up_send, down_send, message
+    )
+
+    three_a.second = seq_swap(send_a)
+    three_b.second = img_swap(send_b, 2)
+    up_in = img_swap(up_send, 4)
+    down_in = img_swap(down_send, 8)
     arrived_part = seq_swap(other_part)
-
-    message_in, gains, *down_in = step(message_in, gains, *down_in)
-    take(place, down_a, down_b, down_in)
-    down_grad, message = fold(
-        place, [([down_a.whole(), down_b.whole()], "rows")], f32, [(message, message_in, True)]
-    )
     for bit in range(4, bits):
         (message,) = fold(place, [], f32, [(message, img_swap(message, 1 << bit), True)])
-    sums, rank = message[:TOP], message[TOP:]
-    down_grad, three_a.first, three_b.first, gains_in = step(
-        down_grad, three_a.first, three_b.first, gains_in
-    )
-    send_a, send_b, gains = second_stage(three_a, three_b, [(gains, gains_in, False)])
-    send_a, send_b, gains = step(send_a, send_b, gains)
-    three_a.second = seq_swap(send_a)
-    three_b.second = img_swap(send_b, 2)
-    gains_in = seq_swap(gains)
-    gains, up_a.second, up_b.second = step(gains, up_a.second, up_b.second)
-    up_sends = fold(place, near_sends(up_a, up_b), bf16)
-    up_sends = step(*up_sends)
-    up_in = near_swap(up_sends)
-    arrived_part, gains = step(arrived_part, gains)
+    pool_grads = pool_weights_call(
+        place, message, probe[None], probe_query, own_query, pool_key, images
+    )
+    pool_grads, three_a.second, three_b.second, arrived_part, up_in, down_in = step(
+        pool_grads, three_a.second, three_b.second, arrived_part, up_in, down_in
+    )
+    take(up_a, up_b, [up_in], 1)
+    take(down_a, down_b, [down_in], 2)
+    *three_sends, up_send = fold(
+        place, near_sends(three_a, three_b) + far_send(up_a, up_b, 1), bf16
+    )
+    up_send, *three_sends = step(up_send, *three_sends)
+
+    three_in = near_swap(three_sends)
+    up_in = img_swap(up_send, 8)
+    finish(place, down_a, down_b)
+    (down_grad,) = fold(place, [([down_a.whole(), down_b.whole()], "rows")], f32)
     input_grad = own_in_call(
-        own_part, arrived_part, unit_one, scale_one, first_gain, residual_grad
-    )
-    input_grad, gains_in, three_a.second, three_b.second = step(
-        input_grad, gains_in, three_a.second, three_b.second
-    )
-    *three_sends, gains = fold(
-        place, near_sends(three_a, three_b), bf16, [(gains, gains_in, False)]
-    )
-    *three_sends, gains = step(*three_sends, gains)
-    three_in = near_swap(three_sends)
-    gains_in = img_swap(gains, 4)
-    up_in = step(*up_in)
-    take(place, up_a, up_b, up_in)
-    up_weight_grad, output_grad = fold(place, [([up_a.whole(), up_b.whole()], "wide")], f32)
-    up_weight_grad, output_grad, gains_in = step(up_weight_grad, output_grad, gains_in)
-    gains = gains + gains_in
-    gains_in = img_swap(gains, 8)
-    three_in = step(*three_in)
-    take(place, three_a, three_b, three_in)
-    query_weight_grad, key_weight_grad, value_weight_grad = fold(
-        place, [([three_a.whole(m), three_b.whole(m)], "rows") for m in range(3)], f32
-    )
-    gains = gains + gains_in
-    for bit in range(4, bits):
-        gains = gains + img_swap(gains, 1 << bit)
-    input_grad = input_grad[None]
+        own_part, arrived_part, unit_one, scale_one, first_row, residual_grad
+    )
+    input_grad, down_grad, up_in, *three_in = step(input_grad, down_grad, up_in, *three_in)
+    take(up_a, up_b, [up_in], 2)
+    take(three_a, three_b, three_in, 2)
+    finish(place, up_a, up_b)
+    finish(place, three_a, three_b)
+    up_weight_grad, output_grad, query_weight_grad, key_weight_grad, value_weight_grad = fold(
+        place,
+        [([up_a.whole(), up_b.whole()], "wide")]
+        + [([three_a.whole(m), three_b.whole(m)], "rows") for m in range(3)],
+        f32,
+    )
 
     block = width // images
+
+    def own_product(weight, grad):
+        columns = grad.shape[1]
+        own = lax.dynamic_slice(weight, (me * block, seq_me * columns), (block, columns))
+        return jnp.sum(own.astype(f32) * grad, axis=1)
 
     def own_rows(vector):
         return lax.dynamic_slice_in_dim(vector, me * block, block)
 
-    heads = head_rows(width)
-    mix_total = sums[:HEADS]
-    probe_query_grad = jnp.sum(
-        jnp.dot(mix_total, pool_key.astype(f32), precision=highest) * heads[:HEADS], axis=0
-    )
-    query_pool_grad = own_rows(probe)[:, None] * lax.dynamic_slice_in_dim(
-        probe_query_grad, seq_me * half, half
-    )[None, :]
-    own_query = lax.dynamic_slice_in_dim(pool_query, me * block, block, 0).astype(f32)
-    probe_grad = jnp.dot(own_query, probe_query_grad, precision=highest)
-    own_mix = lax.dynamic_slice_in_dim(mix_total, me * block, block, 1)
-    my_query = lax.dynamic_slice_in_dim(
-        probe_query * heads[:HEADS], seq_me * half, half, 1
-    )
-    key_pool_grad = lax.dot_general(
-        own_mix, my_query, (((0,), (0,)), ((), ())), precision=highest
-    )
-    near = HEADS // 2
-    factors = rank.reshape(images, 8, width)
-    own_factors = lax.dynamic_slice_in_dim(factors, me * block, block, 2)
-    out_pool_grad = lax.dot_general(
-        own_factors[:, near], factors[:, near + 1, :half], (((0,), (0,)), ((), ())), precision=highest
-    )
-    spread = factors[:, near + 1 :, half:] * heads[None, :near, :half]
-    value_pool_grad = lax.dot_general(
-        own_factors[:, :near].reshape(images * near, block),
-        spread.reshape(images * near, half),
-        (((0,), (0,)), ((), ())),
-        precision=highest,
+    gains = jnp.stack(
+        [
+            own_product(w_query, query_weight_grad)
+            + own_product(w_key, key_weight_grad)
+            + own_product(w_value, value_weight_grad),
+            own_product(w_up, up_weight_grad),
+        ]
+    )
+    gains = (gains + seq_swap(gains)) / jnp.stack([own_rows(first_gain), own_rows(second_gain)])
+    query_pool_grad, key_pool_grad, value_pool_grad, out_pool_grad, probe_grad, final_grad = (
+        pool_grads
     )
     return (
         block_out,
-        input_grad,
+        input_grad[None],
         query_weight_grad,
         key_weight_grad,
         value_weight_grad,
         output_grad,
         up_weight_grad,
         down_grad,
-        own_rows(gains[1]),
-        own_rows(gains[0]),
-        own_rows(sums[HEADS]),
-        probe_grad,
+        gains[0],
+        gains[1],
+        final_grad[:, 0],
+        probe_grad[:, 0],
         query_pool_grad,
         key_pool_grad,
         value_pool_grad,
         out_pool_grad,
-        sums[HEADS + 1, 0],
-        sums[HEADS + 1, 1],
-        sums[HEADS + 1, 2],
+        message[HEADS + 1, 0],
+        message[HEADS + 1, 1],
+        message[HEADS + 1, 2],
     )
 
 

time: 237 us -> 223 us (0.941)
  starting transfers between devices: 45.7 us -> 32.9 us
  waiting for transfers between devices: 32.6 us -> 42.3 us
  matrix products: 19.7 us -> 13.8 us
  local copies, waits for them, and re-layouts: 19 us -> 15.3 us
    ppermute x30 -> x24, starting transfers between devices: 33.5 us -> 20.1 us  [img_swap(): return lax.ppermute(value, 'img', [(i, i ^ mask) for i in range(count)])]
    ppermute x30 -> x24, waiting for transfers between devices: 18.7 us -> 30.7 us  [img_swap(): return lax.ppermute(value, 'img', [(i, i ^ mask) for i in range(count)])]
    pallas_call x12 -> x9, Pallas kernels: 37.5 us -> 31 us  [fold(): pl.pallas_call(functools.partial(fold_kernel, tuple(plan), tuple(gathers)...]
    dot_general x5 -> x0, matrix products: 5.85 us -> none  [the longest x1 1.57 us: shards(): probe_grad = jnp.dot(own_query, probe_query_grad, precision=highest)]
    pallas_call x0 -> x1, Pallas kernels: none -> 4.17 us  [pool_weights_call(): pl.pallas_call(functools.partial(pool_weights_kernel, images), grid_spec=...]
    unnamed x119 -> x98, local copies, waits for them, and re-layouts: 10.2 us -> 6.52 us
    reduce_sum x0 -> x3, other arithmetic: none -> 3.22 us  [own_product(): return jnp.sum(own.astype(f32) * grad, axis=1)]
    ppermute x11, waiting for transfers between devices: 14 us -> 11.6 us  [seq_swap(): return lax.ppermute(value, 'seq', [(0, 1), (1, 0)])]
  transfers between devices with their start and end apart: 41 -> 35, of which waited for: 12 -> 12; matrix products, arithmetic and copies ran while one was open for 14% -> 13% of each run, Pallas kernels for 38% -> 31%
where the time goes in v4:
time: 223 us; the launch traced here: 222 us
  Pallas kernels  103 us (46%)
  waiting for transfers between devices  42.3 us (19%)
  starting transfers between devices  32.9 us (15%)
  local copies, waits for them, and re-layouts  15.3 us (7%)
  matrix products  13.8 us (6%)
  other arithmetic  11.9 us (5%)
  between operations  3.06 us (1%)
    pallas_call x9, Pallas kernels, fold(): pl.pallas_call(functools.partial(fold_kernel, tuple(plan), tuple(gathers)...  31 us
    ppermute x24, waiting for transfers between devices, img_swap(): return lax.ppermute(value, 'img', [(i, i ^ mask) for i in range(count)])  30.7 us
    ppermute x24, starting transfers between devices, img_swap(): return lax.ppermute(value, 'img', [(i, i ^ mask) for i in range(count)])  20.1 us
    dot_general x8, matrix products, low_dot(): return jnp.dot(left_side, right_side, preferred_element_type=f32)  13.8 us
    ppermute x11, starting transfers between devices, seq_swap(): return lax.ppermute(value, 'seq', [(0, 1), (1, 0)])  12.8 us
    pallas_call x1, Pallas kernels, up_back_call(): pl.pallas_call(functools.partial(up_back_kernel, block), grid=(2 * steps,...  12.4 us
    ppermute x11, waiting for transfers between devices, seq_swap(): return lax.ppermute(value, 'seq', [(0, 1), (1, 0)])  11.6 us
    pallas_call x1, Pallas kernels, attend_back(): pl.pallas_call(attend_back_kernel, grid=(pairs,), in_specs=[row_spec] * 6...  10.3 us
  transfers between devices with their start and end apart: 35, of which 12 were waited for; matrix products, arithmetic and copies ran while one was open for 13% of the time, Pallas kernels for 31%

profile of v4, /device:TPU:0, one launch (start us, length us, event | category | flops | bytes accessed | tf_op | source)
XLA Modules:
  0.0 222.1 jit_solution(10127481009148304512)
XLA Ops:
  1.2 2.6 %collective-permute-start = (bf16[256,768]{1,0:T(8,128)(2,1)}, bf16[256,768]{1,0:T(8,128)(2,1)S(1)}, u32[]{:S(2)}, u32[]{:S(2)}) collective-permute-start(bf16[256,768]{1,0:T(8,128)(2,1)} %bitcast.213), channel_id=1, source_target_pairs={{0,1},{1,0},{2,3},{3,2},{4,5},{5,4},{6,7},{7,6},{8,9},{9,8},{10,11... | collective-permute-start | bytes 1179656 | tf_op jit(solution)/shard_map/ppermute | solution.py:526
  15.9 3.0 %probe_rows.1 = (f32[1,768]{1,0:T(1,128)}, f32[16,768]{1,0:T(8,128)}) custom-call(f32[1,768]{1,0:T(1,128)} %broadcast_in_dim.19.probe_ref, bf16[768,768]{1,0:T(8,128)(2,1)} %query_ref.1, bf16[768,768]{1,0:T(8,128)(2,1)} %key_ref.3), custom_call_target="tpu_custom_call" | custom-call | flops 1024 | bytes 1024 | tf_op jit(solution)/shard_map/probe_rows/pallas_call | solution.py:85
  27.9 8.1 %attend.1 = (bf16[256,768]{1,0:T(8,128)(2,1)}, f32[6,256,2]{2,1,0:T(8,128)}) custom-call(bf16[256,768]{1,0:T(8,128)(2,1)} %convolution_convert_fusion.4.q_ref, bf16[256,768]{1,0:T(8,128)(2,1)} %convolution_convert_fusion.3.ka_ref, bf16[256,768]{1,0:T(8,128)(2,1)} %convolution_convert_fusion.1.kb_ref, bf16[256,768]{1,0:T(8,128)(2,1)} %convolution_convert_fusion.2.va_ref, ...), custom_call_target="tpu_custom_call" | custom-call | flops 1024 | bytes 1024 | tf_op jit(solution)/shard_map/attend/pallas_call | solution.py:370
  36.1 2.7 %collective-permute-start.5 = (f32[8,5,768]{2,1,0:T(8,128)S(1)}, f32[8,5,768]{2,1,0:T(8,128)S(1)}, u32[]{:S(2)}, u32[]{:S(2)}) collective-permute-start(f32[8,5,768]{2,1,0:T(8,128)S(1)} %pad_maximum_fusion.1), channel_id=1, source_target_pairs={{0,16},{2,18},{4,20},{6,22},{8,24},{10,26},{12,28},{14,30},{16,0},... | collective-permute-start | bytes 368648 | tf_op jit(solution)/shard_map/ppermute | solution.py:522
  41.8 3.6 %fusion.7 = (bf16[256,3072]{1,0:T(8,128)(2,1)S(1)}, f32[256,3072]{1,0:T(8,128)}) fusion(bf16[256,768]{1,0:T(8,128)(2,1)S(1)} %get-tuple-element.323.low_ref, bf16[768,3072]{1,0:T(8,128)(2,1)S(1)} %copy-done.17), kind=kOutput, calls=%fused_computation.8 | convolution fusion | flops 1215037440 | bytes 9830400 | tf_op jit(solution)/shard_map/dot_general | solution.py:32
  50.9 3.8 %collective-permute-done.4.other_ref = f32[16,896]{1,0:T(8,128)S(1)} collective-permute-done((f32[16,896]{1,0:T(8,128)}, f32[16,896]{1,0:T(8,128)S(1)}, u32[]{:S(2)}, u32[]{:S(2)}) %collective-permute-start.4) | collective-permute-done | bytes 57376 | tf_op jit(solution)/shard_map/ppermute | solution.py:526
  55.5 5.7 %pool_back.1 = (f32[256,768]{1,0:T(8,128)}, bf16[256,768]{1,0:T(8,128)(2,1)}, f32[24,768]{1,0:T(8,128)}) custom-call(s32[5]{0:T(128)} %stack.39.place_ref, s32[1]{0:T(128)S(6)} %copy.71.count_ref, s32[1,80]{1,0:T(1,128)} %pairs_ref.1, f32[1]{0:T(128)} %bitcast.117.temp_ref, f32[1]{0:T(128)} %bitcast.118.bias_ref, f32[16,896]{1,0:T(8,128)} %get-tuple-element.181.own_ref, ...), custom_call_target="tpu_custom_call" | custom-call | flops 1024 | bytes 1024 | tf_op jit(solution)/shard_map/pool_back/pallas_call | solution.py:260
  61.7 4.4 %wgrad.1 = (bf16[2,2,8,96,384]{4,3,2,1,0:T(8,128)(2,1)}, bf16[2,2,8,96,384]{4,3,2,1,0:T(8,128)(2,1)}) custom-call(s32[5]{0:T(128)} %stack.39.place_ref, bf16[256,3072]{1,0:T(8,128)(2,1)} %copy-done.30, bf16[256,768]{1,0:T(8,128)(2,1)} %get-tuple-element.193.right_ref.grad_ref), custom_call_target="tpu_custom_call" | custom-call | flops 1024 | bytes 1024 | tf_op jit(solution)/shard_map/wgrad/pallas_call | solution.py:460
  66.2 6.7 %gelu_back.1.du_ref = bf16[256,3072]{1,0:T(8,128)(2,1)} custom-call(bf16[256,768]{1,0:T(8,128)(2,1)} %get-tuple-element.193.right_ref.grad_ref, bf16[3072,768]{1,0:T(8,128)(2,1)} %down_ref.1, f32[256,3072]{1,0:T(8,128)} %get-tuple-element.335.up_ref), custom_call_target="tpu_custom_call" | custom-call | flops 1024 | bytes 1024 | tf_op jit(solution)/shard_map/gelu_back/pallas_call | solution.py:751
  74.2 3.5 %fold.9 = (bf16[8,96,384]{2,1,0:T(8,128)(2,1)}, bf16[2,4,96,384]{3,2,1,0:T(8,128)(2,1)}, f32[24,768]{1,0:T(8,128)}) custom-call(s32[5]{0:T(128)} %stack.39.place_ref, bf16[2,2,8,96,384]{4,3,2,1,0:T(8,128)(2,1)} %get-tuple-element.196.refs_0_, bf16[2,2,8,96,384]{4,3,2,1,0:T(8,128)(2,1)} %copy-done.2, bf16[2,2,4,2,96,384]{5,4,3,2,1,0:T(8,128)(2,1)} %bitcast.167, ...), custom_call_target="tpu_custom_call" | custom-call | flops 1024 | bytes 1024 | tf_op jit(solution)/shard_map/fold/pallas_call | solution.py:641
  80.5 12.4 %up_back.1 = (bf16[2,2,8,24,1920]{4,3,2,1,0:T(8,128)(2,1)}, bf16[2,2,8,24,1920]{4,3,2,1,0:T(8,128)(2,1)}, f32[256,768]{1,0:T(8,128)}, bf16[256,768]{1,0:T(8,128)(2,1)}) custom-call(s32[5]{0:T(128)} %stack.39.place_ref, bf16[256,768]{1,0:T(8,128)(2,1)} %copy-done.29, bf16[256,3072]{1,0:T(8,128)(2,1)} %gelu_back.1.du_ref, bf16[768,3072]{1,0:T(8,128)(2,1)} %up_ref.1, ...), custom_call_target="tpu_custom_call" | custom-call | flops 1024 | bytes 1024 | tf_op jit(solution)/shard_map/up_back/pallas_call | solution.py:841
  95.7 3.1 %fold.10 = (bf16[4,96,384]{2,1,0:T(8,128)(2,1)}, bf16[4,96,384]{2,1,0:T(8,128)(2,1)}, f32[32,768]{1,0:T(8,128)}) custom-call(s32[5]{0:T(128)} %stack.39.place_ref, bf16[2,2,4,2,96,384]{5,4,3,2,1,0:T(8,128)(2,1)} %bitcast.168, bf16[2,2,4,2,96,384]{5,4,3,2,1,0:T(8,128)(2,1)} %bitcast.177, bf16[4,2,96,384]{3,2,1,0:T(8,128)(2,1)} %bitcast.201, ...), custom_call_target="tpu_custom_call" | custom-call | flops 1024 | bytes 1024 | tf_op jit(solution)/shard_map/fold/pallas_call | solution.py:641
  101.3 10.3 %attend_back.1 = (bf16[256,768]{1,0:T(8,128)(2,1)}, bf16[512,768]{1,0:T(8,128)(2,1)}, bf16[512,768]{1,0:T(8,128)(2,1)}) custom-call(bf16[256,768]{1,0:T(8,128)(2,1)} %convolution_convert_fusion.4.q_ref, bf16[256,768]{1,0:T(8,128)(2,1)} %convolution_convert_fusion.3.ka_ref, bf16[256,768]{1,0:T(8,128)(2,1)} %convolution_convert_fusion.1.kb_ref, ...), custom_call_target="tpu_custom_call" | custom-call | flops 1024 | bytes 1024 | tf_op jit(solution)/shard_map/attend_back/pallas_call | solution.py:418
  111.7 6.3 %wgrad_three.1 = (bf16[2,2,8,3,24,384]{5,4,3,2,1,0:T(8,128)(2,1)}, bf16[2,2,8,3,24,384]{5,4,3,2,1,0:T(8,128)(2,1)}) custom-call(s32[5]{0:T(128)} %stack.39.place_ref, bf16[256,768]{1,0:T(8,128)(2,1)} %copy-done.9, bf16[256,768]{1,0:T(8,128)(2,1)} %copy-done.15, bf16[256,768]{1,0:T(8,128)(2,1)} %get-tuple-element.240.dq_ref, ...), custom_call_target="tpu_custom_call" | custom-call | flops 1024 | bytes 1024 | tf_op jit(solution)/shard_map/wgrad_three/pallas_call | solution.py:505
  117.9 4.3 %fold.11 = (bf16[2,4,24,1920]{3,2,1,0:T(8,128)(2,1)}, bf16[8,24,1920]{2,1,0:T(8,128)(2,1)}, bf16[2,2,96,384]{3,2,1,0:T(8,128)(2,1)}, f32[48,768]{1,0:T(8,128)}) custom-call(s32[5]{0:T(128)} %stack.39.place_ref, bf16[2,2,4,2,24,1920]{5,4,3,2,1,0:T(8,128)(2,1)} %bitcast.149, bf16[2,2,4,2,24,1920]{5,4,3,2,1,0:T(8,128)(2,1)} %bitcast.158, ...), custom_call_target="tpu_custom_call" | custom-call | flops 1024 | bytes 1024 | tf_op jit(solution)/shard_map/fold/pallas_call | solution.py:641
  126.4 5.2 %parts_in.1 = (f32[256,768]{1,0:T(8,128)}, bf16[256,768]{1,0:T(8,128)(2,1)}) custom-call(bf16[256,768]{1,0:T(8,128)(2,1)} %get-tuple-element.240.dq_ref, bf16[512,768]{1,0:T(8,128)(2,1)} %get-tuple-element.227.dk_ref, bf16[512,768]{1,0:T(8,128)(2,1)} %get-tuple-element.228.dv_ref, bf16[768,768]{1,0:T(8,128)(2,1)} %wq_ref.1, bf16[768,768]{1,0:T(8,128)(2,1)} %wk_ref.1, ...), custom_call_target="tpu_custom_call" | custom-call | flops 1024 | bytes 1024 | tf_op jit(solution)/shard_map/parts_in/pallas_call | solution.py:886
  131.6 5.0 %collective-permute-done.19.refs_11_ = f32[48,768]{1,0:T(8,128)} collective-permute-done((f32[48,768]{1,0:T(8,128)}, f32[48,768]{1,0:T(8,128)}, u32[]{:S(2)}, u32[]{:S(2)}) %collective-permute-start.19) | collective-permute-done | bytes 147488 | tf_op jit(solution)/shard_map/ppermute | solution.py:522
  136.6 4.8 %collective-permute-done.16.refs_6_.refs_2_ = bf16[2,4,24,1920]{3,2,1,0:T(8,128)(2,1)S(1)} collective-permute-done((bf16[2,4,24,1920]{3,2,1,0:T(8,128)(2,1)}, bf16[2,4,24,1920]{3,2,1,0:T(8,128)(2,1)S(1)}, u32[]{:S(2)}, u32[]{:S(2)}) %collective-permute-start.16) | collective-permute-done | bytes 737312 | tf_op jit(solution)/shard_map/ppermute | solution.py:522
  143.0 4.2 %fold.12 = (bf16[2,4,3,24,384]{4,3,2,1,0:T(8,128)(2,1)}, bf16[8,3,24,384]{3,2,1,0:T(8,128)(2,1)}, bf16[4,24,1920]{2,1,0:T(8,128)(2,1)}, bf16[4,24,1920]{2,1,0:T(8,128)(2,1)}, f32[80,768]{1,0:T(8,128)}) custom-call(s32[5]{0:T(128)} %stack.39.place_ref, bf16[2,2,4,2,3,24,384]{6,5,4,3,2,1,0:T(8,128)(2,1)} %bitcast.119, ...), custom_call_target="tpu_custom_call" | custom-call | flops 1024 | bytes 1024 | tf_op jit(solution)/shard_map/fold/pallas_call | solution.py:641
  151.7 2.6 %fold.13 = bf16[2,1,96,384]{3,2,1,0:T(8,128)(2,1)} custom-call(s32[5]{0:T(128)} %stack.39.place_ref, bf16[2,2,1,2,2,2,96,384]{7,6,5,4,3,2,1,0:T(8,128)(2,1)} %bitcast.172, bf16[2,2,1,2,2,2,96,384]{7,6,5,4,3,2,1,0:T(8,128)(2,1)} %bitcast.181, bf16[1,2,2,2,96,384]{5,4,3,2,1,0:T(8,128)(2,1)} %bitcast.203, bf16[1,2,2,96,384]{4,3,2,1,0:T(8,128)(2,1)} %bitcast.225, ...), custom_call_target="tpu_custom_call" | custom-call | flops 1024 | bytes 1024 | tf_op jit(solution)/shard_map/fold/pallas_call | solution.py:641
  154.3 9.6 %collective-permute-done.20.refs_15_ = f32[80,768]{1,0:T(8,128)S(1)} collective-permute-done((f32[80,768]{1,0:T(8,128)}, f32[80,768]{1,0:T(8,128)S(1)}, u32[]{:S(2)}, u32[]{:S(2)}) %collective-permute-start.20) | collective-permute-done | bytes 245792 | tf_op jit(solution)/shard_map/ppermute | solution.py:522
  163.9 4.1 %collective-permute-done.23.refs_3_ = bf16[4,24,1920]{2,1,0:T(8,128)(2,1)S(1)} collective-permute-done((bf16[4,24,1920]{2,1,0:T(8,128)(2,1)}, bf16[4,24,1920]{2,1,0:T(8,128)(2,1)S(1)}, u32[]{:S(2)}, u32[]{:S(2)}) %collective-permute-start.23) | collective-permute-done | bytes 368672 | tf_op jit(solution)/shard_map/ppermute | solution.py:526
  169.2 4.1 %fold.14 = (bf16[4,3,24,384]{3,2,1,0:T(8,128)(2,1)}, bf16[4,3,24,384]{3,2,1,0:T(8,128)(2,1)}, bf16[2,2,24,1920]{3,2,1,0:T(8,128)(2,1)}, f32[144,768]{1,0:T(8,128)}) custom-call(s32[5]{0:T(128)} %stack.39.place_ref, bf16[2,2,4,2,3,24,384]{6,5,4,3,2,1,0:T(8,128)(2,1)} %bitcast.120, bf16[2,2,4,2,3,24,384]{6,5,4,3,2,1,0:T(8,128)(2,1)} %bitcast.135, ...), custom_call_target="tpu_custom_call" | custom-call | flops 1024 | bytes 1024 | tf_op jit(solution)/shard_map/fold/pallas_call | solution.py:641
  177.8 4.2 %pool_weights.1 = (f32[48,384]{1,0:T(8,128)}, f32[48,384]{1,0:T(8,128)}, f32[48,384]{1,0:T(8,128)}, f32[48,384]{1,0:T(8,128)}, f32[48,1]{1,0:T(8,128)}, /*index=5*/f32[48,1]{1,0:T(8,128)}) custom-call(s32[5]{0:T(128)} %stack.39.place_ref, f32[144,768]{1,0:T(8,128)} %get-tuple-element.277.rows_ref, f32[1,768]{1,0:T(1,128)} %broadcast_in_dim.19.probe_ref, ...), custom_call_target="tpu_custom_call" | custom-call | flops 1024 | bytes 1024 | tf_op jit(solution)/shard_map/pool_weights/pallas_call | solution.py:327
  184.5 2.7 %collective-permute-done.25.refs_15_.refs_29_.refs_43_ = bf16[4,3,24,384]{3,2,1,0:T(8,128)(2,1)S(1)} collective-permute-done((bf16[4,3,24,384]{3,2,1,0:T(8,128)(2,1)}, bf16[4,3,24,384]{3,2,1,0:T(8,128)(2,1)S(1)}, u32[]{:S(2)}, u32[]{:S(2)}) %collective-permute-start.25) | collective-permute-done | bytes 221216 | tf_op jit(solution)/shard_map/ppermute | solution.py:526
  188.1 3.5 %fold.16 = (bf16[2,1,3,24,384]{4,3,2,1,0:T(8,128)(2,1)}, bf16[2,1,3,24,384]{4,3,2,1,0:T(8,128)(2,1)}, bf16[2,1,3,24,384]{4,3,2,1,0:T(8,128)(2,1)}, bf16[2,1,24,1920]{3,2,1,0:T(8,128)(2,1)}) custom-call(s32[5]{0:T(128)} %stack.39.place_ref, bf16[2,2,1,4,2,3,24,384]{7,6,5,4,3,2,1,0:T(8,128)(2,1)} %bitcast.122, ...), custom_call_target="tpu_custom_call" | custom-call | flops 1024 | bytes 1024 | tf_op jit(solution)/shard_map/fold/pallas_call | solution.py:641
  192.5 3.6 %collective-permute-start.33 = (bf16[2,1,3,24,384]{4,3,2,1,0:T(8,128)(2,1)}, bf16[2,1,3,24,384]{4,3,2,1,0:T(8,128)(2,1)S(1)}, u32[]{:S(2)}, u32[]{:S(2)}) collective-permute-start(bf16[2,1,3,24,384]{4,3,2,1,0:T(8,128)(2,1)} %get-tuple-element.305), channel_id=1, source_target_pairs={{0,24},{2,26},{4,28},{6,30},{8,16},{10,18},{12,20},{14,22},{16,8},... | collective-permute-start | bytes 331784 | tf_op jit(solution)/shard_map/ppermute | solution.py:522
  196.9 2.7 %fold.15 = f32[192,384]{1,0:T(8,128)} custom-call(s32[5]{0:T(128)} %stack.39.place_ref, bf16[2,2,4,2,96,384]{5,4,3,2,1,0:T(8,128)(2,1)} %bitcast.174, bf16[2,2,4,2,96,384]{5,4,3,2,1,0:T(8,128)(2,1)} %bitcast.183, bf16[4,2,96,384]{3,2,1,0:T(8,128)(2,1)} %bitcast.204, bf16[4,96,384]{2,1,0:T(8,128)(2,1)} %copy-done.27, bf16[2,2,96,384]{3,2,1,0:T(8,128)(2,1)} %copy-done.19, ...), custom_call_target="tpu_custom_call" | custom-call | flops 1024 | bytes 1024 | tf_op jit(solution)/shard_map/fold/pallas_call | solution.py:641
  199.6 3.1 %own_in.1 = f32[256,768]{1,0:T(8,128)} custom-call(f32[256,768]{1,0:T(8,128)} %get-tuple-element.248.own_ref, bf16[256,768]{1,0:T(8,128)(2,1)} %copy-done.33, f32[256,768]{1,0:T(8,128)} %get-tuple-element.328.unit_ref, f32[256,1]{1,0:T(8,128)} %copy.64.inv_ref, f32[1,768]{1,0:T(1,128)} %broadcast_in_dim.41.gain_ref, f32[256,768]{1,0:T(8,128)} %get-tuple-element.293.above_ref), custom_call_target="tpu_custom_call" | custom-call | flops 1024 | bytes 1024 | tf_op jit(solution)/shard_map/own_in/pallas_call | solution.py:904
  202.7 2.9 %collective-permute-done.32.refs_17_.refs_24_.refs_31_.refs_38_.refs_45_.refs_52_ = bf16[2,1,3,24,384]{4,3,2,1,0:T(8,128)(2,1)S(1)} collective-permute-done((bf16[2,1,3,24,384]{4,3,2,1,0:T(8,128)(2,1)}, bf16[2,1,3,24,384]{4,3,2,1,0:T(8,128)(2,1)S(1)}, u32[]{:S(2)}, u32[]{:S(2)}) %collective-permute-start.32) | collective-permute-done | bytes 110624 | tf_op jit(solution)/shard_map/ppermute | solution.py:522
  205.6 4.7 %collective-permute-done.30.refs_5_.refs_11_ = bf16[2,1,24,1920]{3,2,1,0:T(8,128)(2,1)S(1)} collective-permute-done((bf16[2,1,24,1920]{3,2,1,0:T(8,128)(2,1)}, bf16[2,1,24,1920]{3,2,1,0:T(8,128)(2,1)S(1)}, u32[]{:S(2)}, u32[]{:S(2)}) %collective-permute-start.30) | collective-permute-done | bytes 184352 | tf_op jit(solution)/shard_map/ppermute | solution.py:522
  211.0 3.1 %fold.17 = (f32[48,1536]{1,0:T(8,128)}, f32[48,384]{1,0:T(8,128)}, f32[48,384]{1,0:T(8,128)}, f32[48,384]{1,0:T(8,128)}, f32[48,384]{1,0:T(8,128)}) custom-call(s32[5]{0:T(128)} %stack.39.place_ref, bf16[2,2,4,2,24,1920]{5,4,3,2,1,0:T(8,128)(2,1)} %bitcast.156, bf16[2,2,4,2,24,1920]{5,4,3,2,1,0:T(8,128)(2,1)} %bitcast.165, ...), custom_call_target="tpu_custom_call" | custom-call | flops 1024 | bytes 1024 | tf_op jit(solution)/shard_map/fold/pallas_call | solution.py:641
  (205 shorter events, 68.8 us)
Async XLA Ops:
  0.7 11.5 %collective-permute-start.1 = (f32[1,5,768]{2,1,0:T(8,128)}, f32[1,5,768]{2,1,0:T(8,128)S(1)}, u32[]{:S(2)}, u32[]{:S(2)}) collective-permute-start(f32[1,5,768]{2,1,0:T(8,128)} %bitcast.229), channel_id=1, source_target_pairs={{0,2},{2,0},{4,6},{6,4},{8,10},{10,8},{12,14},{14,12},{16,18},{18,... | collective-permute-start | bytes 46088 | tf_op jit(solution)/shard_map/ppermute | solution.py:522
  1.2 22.0 %collective-permute-start = (bf16[256,768]{1,0:T(8,128)(2,1)}, bf16[256,768]{1,0:T(8,128)(2,1)S(1)}, u32[]{:S(2)}, u32[]{:S(2)}) collective-permute-start(bf16[256,768]{1,0:T(8,128)(2,1)} %bitcast.213), channel_id=1, source_target_pairs={{0,1},{1,0},{2,3},{3,2},{4,5},{5,4},{6,7},{7,6},{8,9},{9,8},{10,11... | collective-permute-start | bytes 1179656 | tf_op jit(solution)/shard_map/ppermute | solution.py:526
  12.2 10.9 %collective-permute-start.2 = (f32[2,5,768]{2,1,0:T(8,128)S(1)}, f32[2,5,768]{2,1,0:T(8,128)S(1)}, u32[]{:S(2)}, u32[]{:S(2)}) collective-permute-start(f32[2,5,768]{2,1,0:T(8,128)S(1)} %pad_maximum_fusion.3), channel_id=1, source_target_pairs={{0,4},{2,6},{4,0},{6,2},{8,12},{10,14},{12,8},{14,10},{16,20},{18,... | collective-permute-start | bytes 92168 | tf_op jit(solution)/shard_map/ppermute | solution.py:522
  23.8 12.2 %collective-permute-start.3 = (f32[4,5,768]{2,1,0:T(8,128)S(1)}, f32[4,5,768]{2,1,0:T(8,128)S(1)}, u32[]{:S(2)}, u32[]{:S(2)}) collective-permute-start(f32[4,5,768]{2,1,0:T(8,128)S(1)} %pad_maximum_fusion.2), channel_id=1, source_target_pairs={{0,8},{2,10},{4,12},{6,14},{8,0},{10,2},{12,4},{14,6},{16,24},{18,... | collective-permute-start | bytes 184328 | tf_op jit(solution)/shard_map/ppermute | solution.py:522
  36.1 14.8 %collective-permute-start.5 = (f32[8,5,768]{2,1,0:T(8,128)S(1)}, f32[8,5,768]{2,1,0:T(8,128)S(1)}, u32[]{:S(2)}, u32[]{:S(2)}) collective-permute-start(f32[8,5,768]{2,1,0:T(8,128)S(1)} %pad_maximum_fusion.1), channel_id=1, source_target_pairs={{0,16},{2,18},{4,20},{6,22},{8,24},{10,26},{12,28},{14,30},{16,0},... | collective-permute-start | bytes 368648 | tf_op jit(solution)/shard_map/ppermute | solution.py:522
  66.1 6.7 %collective-permute-start.7 = (bf16[2,2,8,96,384]{4,3,2,1,0:T(8,128)(2,1)}, bf16[2,2,8,96,384]{4,3,2,1,0:T(8,128)(2,1)S(1)}, u32[]{:S(2)}, u32[]{:S(2)}) collective-permute-start(bf16[2,2,8,96,384]{4,3,2,1,0:T(8,128)(2,1)} %get-tuple-element.194), channel_id=1, source_target_pairs={{0,2},{2,0},{4,6},{6,4},{8,10},{10,8},{12,14},{14,12},{16,18},{18,... | collective-permute-start | bytes 7077896 | tf_op jit(solution)/shard_map/ppermute | solution.py:522
  77.7 15.9 %collective-permute-start.9 = (bf16[8,96,384]{2,1,0:T(8,128)(2,1)}, bf16[8,96,384]{2,1,0:T(8,128)(2,1)S(1)}, u32[]{:S(2)}, u32[]{:S(2)}) collective-permute-start(bf16[8,96,384]{2,1,0:T(8,128)(2,1)} %get-tuple-element.208), channel_id=1, source_target_pairs={{0,1},{1,0},{2,3},{3,2},{4,5},{5,4},{6,7},{7,6},{8,9},{9,8},{10,11... | collective-permute-start | bytes 1769480 | tf_op jit(solution)/shard_map/ppermute | solution.py:526
  79.2 15.6 %collective-permute-start.10 = (bf16[2,4,96,384]{3,2,1,0:T(8,128)(2,1)}, bf16[2,4,96,384]{3,2,1,0:T(8,128)(2,1)S(1)}, u32[]{:S(2)}, u32[]{:S(2)}) collective-permute-start(bf16[2,4,96,384]{3,2,1,0:T(8,128)(2,1)} %get-tuple-element.209), channel_id=1, source_target_pairs={{0,4},{2,6},{4,0},{6,2},{8,12},{10,14},{12,8},{14,10},{16,20},{18,... | collective-permute-start | bytes 1769480 | tf_op jit(solution)/shard_map/ppermute | solution.py:522
  79.7 13.2 %collective-permute-start.8 = (f32[24,768]{1,0:T(8,128)}, f32[24,768]{1,0:T(8,128)S(1)}, u32[]{:S(2)}, u32[]{:S(2)}) collective-permute-start(f32[24,768]{1,0:T(8,128)} %get-tuple-element.207.refs_6_), channel_id=1, source_target_pairs={{0,2},{2,0},{4,6},{6,4},{8,10},{10,8},{12,14},{14,12},{16,18},{18,... | collective-permute-start | bytes 221192 | tf_op jit(solution)/shard_map/ppermute | solution.py:522
  95.7 15.9 %collective-permute-start.11 = (bf16[2,2,8,24,1920]{4,3,2,1,0:T(8,128)(2,1)}, bf16[2,2,8,24,1920]{4,3,2,1,0:T(8,128)(2,1)S(1)}, u32[]{:S(2)}, u32[]{:S(2)}) collective-permute-start(bf16[2,2,8,24,1920]{4,3,2,1,0:T(8,128)(2,1)} %get-tuple-element.222), channel_id=1, source_target_pairs={{0,2},{2,0},{4,6},{6,4},{8,10},{10,8},{12,14},{14,12},{16,18},{18,... | collective-permute-start | bytes 8847368 | tf_op jit(solution)/shard_map/ppermute | solution.py:522
  98.8 12.8 %collective-permute-start.13 = (bf16[4,96,384]{2,1,0:T(8,128)(2,1)}, bf16[4,96,384]{2,1,0:T(8,128)(2,1)S(1)}, u32[]{:S(2)}, u32[]{:S(2)}) collective-permute-start(bf16[4,96,384]{2,1,0:T(8,128)(2,1)} %get-tuple-element.224), channel_id=1, source_target_pairs={{0,4},{2,6},{4,0},{6,2},{8,12},{10,14},{12,8},{14,10},{16,20},{18,... | collective-permute-start | bytes 884744 | tf_op jit(solution)/shard_map/ppermute | solution.py:522
  99.3 12.3 %collective-permute-start.14 = (bf16[4,96,384]{2,1,0:T(8,128)(2,1)}, bf16[4,96,384]{2,1,0:T(8,128)(2,1)S(1)}, u32[]{:S(2)}, u32[]{:S(2)}) collective-permute-start(bf16[4,96,384]{2,1,0:T(8,128)(2,1)} %get-tuple-element.225), channel_id=1, source_target_pairs={{0,1},{1,0},{2,3},{3,2},{4,5},{5,4},{6,7},{7,6},{8,9},{9,8},{10,11... | collective-permute-start | bytes 884744 | tf_op jit(solution)/shard_map/ppermute | solution.py:526
  99.8 11.8 %collective-permute-start.12 = (f32[32,768]{1,0:T(8,128)}, f32[32,768]{1,0:T(8,128)}, u32[]{:S(2)}, u32[]{:S(2)}) collective-permute-start(f32[32,768]{1,0:T(8,128)} %get-tuple-element.223.refs_12_), channel_id=1, source_target_pairs={{0,4},{2,6},{4,0},{6,2},{8,12},{10,14},{12,8},{14,10},{16,20},{18,... | collective-permute-start | bytes 294920 | tf_op jit(solution)/shard_map/ppermute | solution.py:522
  122.2 19.3 %collective-permute-start.15 = (bf16[2,2,8,3,24,384]{5,4,3,2,1,0:T(8,128)(2,1)}, bf16[2,2,8,3,24,384]{5,4,3,2,1,0:T(8,128)(2,1)S(1)}, u32[]{:S(2)}, u32[]{:S(2)}) collective-permute-start(bf16[2,2,8,3,24,384]{5,4,3,2,1,0:T(8,128)(2,1)} %get-tuple-element.243), channel_id=1, source_target_pairs={{0,2},{2,0},{4,6},{6,4},{8,10},{10,8},{12,14},{14,12},{16,18},{18,... | collective-permute-start | bytes 5308424 | tf_op jit(solution)/shard_map/ppermute | solution.py:522
  122.3 19.1 %collective-permute-start.16 = (bf16[2,4,24,1920]{3,2,1,0:T(8,128)(2,1)}, bf16[2,4,24,1920]{3,2,1,0:T(8,128)(2,1)S(1)}, u32[]{:S(2)}, u32[]{:S(2)}) collective-permute-start(bf16[2,4,24,1920]{3,2,1,0:T(8,128)(2,1)} %get-tuple-element.244), channel_id=1, source_target_pairs={{0,4},{2,6},{4,0},{6,2},{8,12},{10,14},{12,8},{14,10},{16,20},{18,... | collective-permute-start | bytes 2211848 | tf_op jit(solution)/shard_map/ppermute | solution.py:522
  122.8 18.8 %collective-permute-start.17 = (bf16[8,24,1920]{2,1,0:T(8,128)(2,1)}, bf16[8,24,1920]{2,1,0:T(8,128)(2,1)S(1)}, u32[]{:S(2)}, u32[]{:S(2)}) collective-permute-start(bf16[8,24,1920]{2,1,0:T(8,128)(2,1)} %get-tuple-element.245), channel_id=1, source_target_pairs={{0,1},{1,0},{2,3},{3,2},{4,5},{5,4},{6,7},{7,6},{8,9},{9,8},{10,11... | collective-permute-start | bytes 2211848 | tf_op jit(solution)/shard_map/ppermute | solution.py:526
  124.3 12.3 %collective-permute-start.18 = (bf16[2,2,96,384]{3,2,1,0:T(8,128)(2,1)}, bf16[2,2,96,384]{3,2,1,0:T(8,128)(2,1)S(1)}, u32[]{:S(2)}, u32[]{:S(2)}) collective-permute-start(bf16[2,2,96,384]{3,2,1,0:T(8,128)(2,1)} %get-tuple-element.246), channel_id=1, source_target_pairs={{0,8},{2,10},{4,12},{6,14},{8,0},{10,2},{12,4},{14,6},{16,24},{18,... | collective-permute-start | bytes 884744 | tf_op jit(solution)/shard_map/ppermute | solution.py:522
  124.8 11.8 %collective-permute-start.19 = (f32[48,768]{1,0:T(8,128)}, f32[48,768]{1,0:T(8,128)}, u32[]{:S(2)}, u32[]{:S(2)}) collective-permute-start(f32[48,768]{1,0:T(8,128)} %get-tuple-element.247.refs_10_), channel_id=1, source_target_pairs={{0,8},{2,10},{4,12},{6,14},{8,0},{10,2},{12,4},{14,6},{16,24},{18,... | collective-permute-start | bytes 442376 | tf_op jit(solution)/shard_map/ppermute | solution.py:522
  147.2 20.8 %collective-permute-start.21 = (bf16[2,4,3,24,384]{4,3,2,1,0:T(8,128)(2,1)}, bf16[2,4,3,24,384]{4,3,2,1,0:T(8,128)(2,1)S(1)}, u32[]{:S(2)}, u32[]{:S(2)}) collective-permute-start(bf16[2,4,3,24,384]{4,3,2,1,0:T(8,128)(2,1)} %get-tuple-element.263), channel_id=1, source_target_pairs={{0,4},{2,6},{4,0},{6,2},{8,12},{10,14},{12,8},{14,10},{16,20},{18,... | collective-permute-start | bytes 1327112 | tf_op jit(solution)/shard_map/ppermute | solution.py:522
  148.8 19.2 %collective-permute-start.22 = (bf16[8,3,24,384]{3,2,1,0:T(8,128)(2,1)}, bf16[8,3,24,384]{3,2,1,0:T(8,128)(2,1)S(1)}, u32[]{:S(2)}, u32[]{:S(2)}) collective-permute-start(bf16[8,3,24,384]{3,2,1,0:T(8,128)(2,1)} %get-tuple-element.264), channel_id=1, source_target_pairs={{0,1},{1,0},{2,3},{3,2},{4,5},{5,4},{6,7},{7,6},{8,9},{9,8},{10,11... | collective-permute-start | bytes 1327112 | tf_op jit(solution)/shard_map/ppermute | solution.py:526
  150.3 17.7 %collective-permute-start.23 = (bf16[4,24,1920]{2,1,0:T(8,128)(2,1)}, bf16[4,24,1920]{2,1,0:T(8,128)(2,1)S(1)}, u32[]{:S(2)}, u32[]{:S(2)}) collective-permute-start(bf16[4,24,1920]{2,1,0:T(8,128)(2,1)} %get-tuple-element.265), channel_id=1, source_target_pairs={{0,1},{1,0},{2,3},{3,2},{4,5},{5,4},{6,7},{7,6},{8,9},{9,8},{10,11... | collective-permute-start | bytes 1105928 | tf_op jit(solution)/shard_map/ppermute | solution.py:526
  150.8 17.2 %collective-permute-start.24 = (bf16[4,24,1920]{2,1,0:T(8,128)(2,1)}, bf16[4,24,1920]{2,1,0:T(8,128)(2,1)S(1)}, u32[]{:S(2)}, u32[]{:S(2)}) collective-permute-start(bf16[4,24,1920]{2,1,0:T(8,128)(2,1)} %get-tuple-element.266), channel_id=1, source_target_pairs={{0,4},{2,6},{4,0},{6,2},{8,12},{10,14},{12,8},{14,10},{16,20},{18,... | collective-permute-start | bytes 1105928 | tf_op jit(solution)/shard_map/ppermute | solution.py:522
  151.4 12.5 %collective-permute-start.20 = (f32[80,768]{1,0:T(8,128)}, f32[80,768]{1,0:T(8,128)S(1)}, u32[]{:S(2)}, u32[]{:S(2)}) collective-permute-start(f32[80,768]{1,0:T(8,128)} %get-tuple-element.262.refs_14_), channel_id=1, source_target_pairs={{0,16},{2,18},{4,20},{6,22},{8,24},{10,26},{12,28},{14,30},{16,0},... | collective-permute-start | bytes 737288 | tf_op jit(solution)/shard_map/ppermute | solution.py:522
  173.2 14.0 %collective-permute-start.27 = (bf16[256,768]{1,0:T(8,128)(2,1)S(1)}, bf16[256,768]{1,0:T(8,128)(2,1)S(1)}, u32[]{:S(2)}, u32[]{:S(2)}) collective-permute-start(bf16[256,768]{1,0:T(8,128)(2,1)S(1)} %copy-done.46), channel_id=1, source_target_pairs={{0,1},{1,0},{2,3},{3,2},{4,5},{5,4},{6,7},{7,6},{8,9},{9,8},{10,11... | collective-permute-start | bytes 1179656 | tf_op jit(solution)/shard_map/ppermute | solution.py:526
  174.8 12.4 %collective-permute-start.28 = (bf16[2,2,24,1920]{3,2,1,0:T(8,128)(2,1)}, bf16[2,2,24,1920]{3,2,1,0:T(8,128)(2,1)S(1)}, u32[]{:S(2)}, u32[]{:S(2)}) collective-permute-start(bf16[2,2,24,1920]{3,2,1,0:T(8,128)(2,1)} %get-tuple-element.289), channel_id=1, source_target_pairs={{0,8},{2,10},{4,12},{6,14},{8,0},{10,2},{12,4},{14,6},{16,24},{18,... | collective-permute-start | bytes 1105928 | tf_op jit(solution)/shard_map/ppermute | solution.py:522
  175.2 12.0 %collective-permute-start.25 = (bf16[4,3,24,384]{3,2,1,0:T(8,128)(2,1)}, bf16[4,3,24,384]{3,2,1,0:T(8,128)(2,1)S(1)}, u32[]{:S(2)}, u32[]{:S(2)}) collective-permute-start(bf16[4,3,24,384]{3,2,1,0:T(8,128)(2,1)} %get-tuple-element.286), channel_id=1, source_target_pairs={{0,1},{1,0},{2,3},{3,2},{4,5},{5,4},{6,7},{7,6},{8,9},{9,8},{10,11... | collective-permute-start | bytes 663560 | tf_op jit(solution)/shard_map/ppermute | solution.py:526
  175.8 11.5 %collective-permute-start.26 = (bf16[4,3,24,384]{3,2,1,0:T(8,128)(2,1)}, bf16[4,3,24,384]{3,2,1,0:T(8,128)(2,1)S(1)}, u32[]{:S(2)}, u32[]{:S(2)}) collective-permute-start(bf16[4,3,24,384]{3,2,1,0:T(8,128)(2,1)} %get-tuple-element.287), channel_id=1, source_target_pairs={{0,4},{2,6},{4,0},{6,2},{8,12},{10,14},{12,8},{14,10},{16,20},{18,... | collective-permute-start | bytes 663560 | tf_op jit(solution)/shard_map/ppermute | solution.py:522
  176.6 7.9 %collective-permute-start.29 = (bf16[2,1,96,384]{3,2,1,0:T(8,128)(2,1)S(1)}, bf16[2,1,96,384]{3,2,1,0:T(8,128)(2,1)S(1)}, u32[]{:S(2)}, u32[]{:S(2)}) collective-permute-start(bf16[2,1,96,384]{3,2,1,0:T(8,128)(2,1)S(1)} %copy-done.35), channel_id=1, source_target_pairs={{0,16},{2,18},{4,20},{6,22},{8,24},{10,26},{12,28},{14,30},{16,0},... | collective-permute-start | bytes 442376 | tf_op jit(solution)/shard_map/ppermute | solution.py:522
  191.6 11.1 %collective-permute-start.31 = (bf16[2,1,3,24,384]{4,3,2,1,0:T(8,128)(2,1)}, bf16[2,1,3,24,384]{4,3,2,1,0:T(8,128)(2,1)S(1)}, u32[]{:S(2)}, u32[]{:S(2)}) collective-permute-start(bf16[2,1,3,24,384]{4,3,2,1,0:T(8,128)(2,1)} %get-tuple-element.303), channel_id=1, source_target_pairs={{0,8},{2,10},{4,12},{6,14},{8,0},{10,2},{12,4},{14,6},{16,24},{18,... | collective-permute-start | bytes 331784 | tf_op jit(solution)/shard_map/ppermute | solution.py:522
  192.1 13.5 %collective-permute-start.32 = (bf16[2,1,3,24,384]{4,3,2,1,0:T(8,128)(2,1)}, bf16[2,1,3,24,384]{4,3,2,1,0:T(8,128)(2,1)S(1)}, u32[]{:S(2)}, u32[]{:S(2)}) collective-permute-start(bf16[2,1,3,24,384]{4,3,2,1,0:T(8,128)(2,1)} %get-tuple-element.304), channel_id=1, source_target_pairs={{0,16},{2,18},{4,20},{6,22},{8,24},{10,26},{12,28},{14,30},{16,0},... | collective-permute-start | bytes 331784 | tf_op jit(solution)/shard_map/ppermute | solution.py:522
  192.5 13.1 %collective-permute-start.33 = (bf16[2,1,3,24,384]{4,3,2,1,0:T(8,128)(2,1)}, bf16[2,1,3,24,384]{4,3,2,1,0:T(8,128)(2,1)S(1)}, u32[]{:S(2)}, u32[]{:S(2)}) collective-permute-start(bf16[2,1,3,24,384]{4,3,2,1,0:T(8,128)(2,1)} %get-tuple-element.305), channel_id=1, source_target_pairs={{0,24},{2,26},{4,28},{6,30},{8,16},{10,18},{12,20},{14,22},{16,8},... | collective-permute-start | bytes 331784 | tf_op jit(solution)/shard_map/ppermute | solution.py:522
  196.1 14.2 %collective-permute-start.30 = (bf16[2,1,24,1920]{3,2,1,0:T(8,128)(2,1)}, bf16[2,1,24,1920]{3,2,1,0:T(8,128)(2,1)S(1)}, u32[]{:S(2)}, u32[]{:S(2)}) collective-permute-start(bf16[2,1,24,1920]{3,2,1,0:T(8,128)(2,1)} %get-tuple-element.302), channel_id=1, source_target_pairs={{0,16},{2,18},{4,20},{6,22},{8,24},{10,26},{12,28},{14,30},{16,0},... | collective-permute-start | bytes 552968 | tf_op jit(solution)/shard_map/ppermute | solution.py:522
  (52 other events, 245.2 us)

commit v5 on v4

--- a/solution.py
+++ b/solution.py
@@ -20,18 +20,6 @@
 light = pl.CostEstimate(flops=1024, transcendentals=0, bytes_accessed=1024)
 
 
-def layer_norm(values, gain_row):
-    center = values - jnp.mean(values, axis=-1, keepdims=True)
-    spread = jnp.mean(center * center, axis=-1, keepdims=True)
-    inv_std = lax.rsqrt(spread + norm_eps)
-    normed = center * inv_std
-    return (normed * gain_row, normed, inv_std)
-
-
-def low_dot(left_side, right_side):
-    return jnp.dot(left_side, right_side, preferred_element_type=f32)
-
-
 def gelu_tanh(values):
     return jax.nn.gelu(values, approximate=True)
 
@@ -74,14 +62,77 @@
     return (lane // HEAD == row).astype(f32)
 
 
-def probe_kernel(probe_ref, query_ref, key_ref, row_ref, key_probe_ref):
-    row = wide_row(nn, probe_ref[...], query_ref[...])
+FIRST, SECOND, FINAL, PROBE = range(4)
+
+
+def norm_rows(values):
+    center = values - jnp.mean(values, axis=-1, keepdims=True)
+    inv = lax.rsqrt(jnp.mean(center * center, axis=-1, keepdims=True) + norm_eps)
+    return center * inv, inv
+
+
+def front_kernel(count, *refs):
+    tokens_ref, vectors_ref = refs[:2]
+    weight_refs = refs[2 : 2 + count]
+    low_ref, unit_ref, inv_ref = refs[2 + count : 5 + count]
+
+    @pl.when(pl.program_id(0) == 0)
+    def _():
+        unit, inv = norm_rows(tokens_ref[...].astype(f32))
+        unit_ref[...] = unit
+        inv_ref[...] = inv
+        low_ref[...] = (unit * vectors_ref[FIRST : FIRST + 1]).astype(bf16)
+
+    low = low_ref[...]
+    for weight_ref, out_ref in zip(weight_refs, refs[5 + count :]):
+        out_ref[...] = nn(low, weight_ref[...]).astype(bf16)
+
+
+def vectors_kernel(first_ref, second_ref, final_ref, probe_ref, out_ref):
+    for row, ref in enumerate((first_ref, second_ref, final_ref, probe_ref)):
+        out_ref[row : row + 1] = ref[...].reshape(1, ref.shape[0])
+
+
+def vectors_call(*vectors):
+    return pl.pallas_call(
+        vectors_kernel,
+        out_shape=jax.ShapeDtypeStruct((len(vectors), vectors[0].shape[0]), f32),
+        cost_estimate=light,
+        name="vectors",
+    )(*vectors)
+
+
+def front_call(tokens, vectors, *weights):
+    rows, width = tokens.shape
+    chunk = width // 3
+    whole = lambda *shape: pl.BlockSpec(shape, lambda c: (0,) * len(shape))
+    count = len(weights)
+    return pl.pallas_call(
+        functools.partial(front_kernel, count),
+        grid=(3,),
+        in_specs=[whole(rows, width), whole(*vectors.shape)]
+        + [pl.BlockSpec((width, chunk), lambda c: (0, c))] * count,
+        out_specs=[whole(rows, width), whole(rows, width), whole(rows, 1)]
+        + [pl.BlockSpec((rows, chunk), lambda c: (0, c))] * count,
+        out_shape=[
+            jax.ShapeDtypeStruct((rows, width), bf16),
+            jax.ShapeDtypeStruct((rows, width), f32),
+            jax.ShapeDtypeStruct((rows, 1), f32),
+        ]
+        + [jax.ShapeDtypeStruct((rows, width), bf16)] * count,
+        cost_estimate=light,
+        name="front",
+    )(tokens, vectors, *weights)
+
+
+def probe_kernel(vectors_ref, query_ref, key_ref, row_ref, key_probe_ref):
+    row = wide_row(nn, vectors_ref[PROBE : PROBE + 1], query_ref[...])
     row_ref[...] = row
     key_probe_ref[...] = wide(nt, row * head_rows(row.shape[1]), key_ref[...])
 
 
-def probe_call(probe, pool_query, pool_key):
-    width = probe.shape[0]
+def probe_call(vectors, pool_query, pool_key):
+    width = vectors.shape[1]
     return pl.pallas_call(
         probe_kernel,
         out_shape=[
@@ -90,43 +141,89 @@
         ],
         cost_estimate=light,
         name="probe_rows",
-    )(probe[None], pool_query, pool_key)
-
-
-def pool_kernel(result_ref, gain_ref, key_probe_ref, low_ref, unit_ref, inv_ref, exp_ref, packed_ref):
-    result = result_ref[...]
-    width = result.shape[1]
-    center = result - jnp.mean(result, axis=-1, keepdims=True)
-    inv = lax.rsqrt(jnp.mean(center * center, axis=-1, keepdims=True) + norm_eps)
-    unit = center * inv
-    low = (unit * gain_ref[...]).astype(bf16)
-    low_ref[...] = low
-    unit_ref[...] = unit
-    inv_ref[...] = inv
-    scores = wide(nt, key_probe_ref[...], low) * 0.125
-    top = jnp.max(scores, axis=-1, keepdims=True)
-    exps = jnp.exp(scores - top)
-    exp_ref[...] = exps
-    packed_ref[:, :width] = wide(nn, exps, low)
-    lane = lax.broadcasted_iota(jnp.int32, (TOP, 128), 1)
-    total = jnp.sum(exps, axis=-1, keepdims=True)
-    packed_ref[:, width:] = jnp.where(lane == 0, top, jnp.where(lane == 1, total, 0.0))
-
-
-def pool_call(result, gain, key_probe):
-    rows, width = result.shape
-    return pl.pallas_call(
-        pool_kernel,
-        out_shape=[
-            jax.ShapeDtypeStruct((rows, width), bf16),
-            jax.ShapeDtypeStruct((rows, width), f32),
-            jax.ShapeDtypeStruct((rows, 1), f32),
-            jax.ShapeDtypeStruct((TOP, rows), f32),
-            jax.ShapeDtypeStruct((TOP, width + 128), f32),
+    )(vectors, pool_query, pool_key)
+
+
+def middle_kernel(
+    attended_ref, tokens_ref, vectors_ref, wo_ref, up_ref, down_ref, key_probe_ref,
+    low_two_ref, unit_two_ref, inv_two_ref, upward_ref, hidden_ref, block_ref,
+    low_ref, unit_ref, inv_ref, exp_ref, packed_ref, acc_ref,
+):
+    c = pl.program_id(0)
+
+    @pl.when(c == 0)
+    def _():
+        residual = tokens_ref[...].astype(f32) + nn(attended_ref[...], wo_ref[...])
+        acc_ref[...] = residual
+        unit, inv = norm_rows(residual)
+        unit_two_ref[...] = unit
+        inv_two_ref[...] = inv
+        low_two_ref[...] = (unit * vectors_ref[SECOND : SECOND + 1]).astype(bf16)
+
+    upward = nn(low_two_ref[...], up_ref[...])
+    upward_ref[...] = upward
+    hidden = gelu_tanh(upward).astype(bf16)
+    hidden_ref[...] = hidden
+    acc_ref[...] += nn(hidden, down_ref[...])
+
+    @pl.when(c == pl.num_programs(0) - 1)
+    def _():
+        result = acc_ref[...]
+        width = result.shape[1]
+        block_ref[...] = result.astype(bf16)
+        unit, inv = norm_rows(result)
+        low = (unit * vectors_ref[FINAL : FINAL + 1]).astype(bf16)
+        low_ref[...] = low
+        unit_ref[...] = unit
+        inv_ref[...] = inv
+        scores = wide(nt, key_probe_ref[...], low) * 0.125
+        top = jnp.max(scores, axis=-1, keepdims=True)
+        exps = jnp.exp(scores - top)
+        exp_ref[...] = exps
+        packed_ref[:, :width] = wide(nn, exps, low)
+        lane = lax.broadcasted_iota(jnp.int32, (TOP, 128), 1)
+        total = jnp.sum(exps, axis=-1, keepdims=True)
+        packed_ref[:, width:] = jnp.where(lane == 0, top, jnp.where(lane == 1, total, 0.0))
+
+
+def middle_call(attended, tokens, vectors, w_output, w_up, w_down, key_probe):
+    rows, width = tokens.shape
+    depth = w_up.shape[1]
+    steps = 4
+    chunk = depth // steps
+    whole = lambda *shape: pl.BlockSpec(shape, lambda c: (0,) * len(shape))
+    cut = pl.BlockSpec((rows, chunk), lambda c: (0, c))
+    outs = [
+        (whole(rows, width), (rows, width), bf16),
+        (whole(rows, width), (rows, width), f32),
+        (whole(rows, 1), (rows, 1), f32),
+        (cut, (rows, depth), f32),
+        (cut, (rows, depth), bf16),
+        (whole(rows, width), (rows, width), bf16),
+        (whole(rows, width), (rows, width), bf16),
+        (whole(rows, width), (rows, width), f32),
+        (whole(rows, 1), (rows, 1), f32),
+        (whole(TOP, rows), (TOP, rows), f32),
+        (whole(TOP, width + 128), (TOP, width + 128), f32),
+    ]
+    return pl.pallas_call(
+        middle_kernel,
+        grid=(steps,),
+        in_specs=[
+            whole(rows, width),
+            whole(rows, width),
+            whole(*vectors.shape),
+            whole(width, width),
+            pl.BlockSpec((width, chunk), lambda c: (0, c)),
+            pl.BlockSpec((chunk, width), lambda c: (c, 0)),
+            whole(TOP, width),
         ],
-        cost_estimate=light,
-        name="pool_local",
-    )(result, gain[None], key_probe)
+        out_specs=[spec for spec, _, _ in outs],
+        out_shape=[jax.ShapeDtypeStruct(shape, dtype) for _, shape, dtype in outs],
+        scratch_shapes=[pltpu.VMEM((rows, width), f32)],
+        cost_estimate=light,
+        name="middle",
+    )(attended, tokens, vectors, w_output, w_up, w_down, key_probe)
 
 
 def pool_back_kernel(
@@ -143,7 +240,7 @@
     low_ref,
     unit_ref,
     inv_ref,
-    gain_ref,
+    vectors_ref,
     key_probe_ref,
     value_ref,
     output_ref,
@@ -215,7 +312,7 @@
     )
 
     unit = unit_ref[...]
-    scaled = pool_grad * gain_ref[...]
+    scaled = pool_grad * vectors_ref[FINAL : FINAL + 1]
     gain_grad = jnp.sum(pool_grad * unit, axis=0, keepdims=True)
     first_mean = jnp.mean(scaled, axis=-1, keepdims=True)
     second_mean = jnp.mean(scaled * unit, axis=-1, keepdims=True)
@@ -251,7 +348,7 @@
 
 
 def pool_back_call(
-    place, counts, pairs, log_temp, pair_bias, own, other, exps, low, unit, inv, gain, key_probe,
+    place, counts, pairs, log_temp, pair_bias, own, other, exps, low, unit, inv, vectors, key_probe,
     pool_value, pool_output, caps, images, seq_count,
 ):
     rows, width = low.shape
@@ -270,7 +367,7 @@
         name="pool_back",
     )(
         place, counts, pairs, log_temp[None], pair_bias[None], own, other, exps, low, unit, inv,
-        gain[None], key_probe, pool_value, pool_output, caps,
+        vectors, key_probe, pool_value, pool_output, caps,
     )
 
 
@@ -281,7 +378,7 @@
 
 
 def pool_weights_kernel(
-    images, place_ref, rows_ref, probe_ref, probe_query_ref, query_ref, key_ref, *out_refs
+    images, place_ref, rows_ref, vectors_ref, probe_query_ref, query_ref, key_ref, *out_refs
 ):
     query_out, key_out, value_out, output_out, probe_out, final_out = out_refs
     width = rows_ref.shape[1]
@@ -300,7 +397,7 @@
     pick = pick.astype(f32)
     rows = exact(((1,), (1,)), pick, rows_ref[...])
     probe_query_grad = jnp.sum(wide(nn, rows_ref[:TOP], key_ref[...]) * heads, axis=0, keepdims=True)
-    own_probe = jnp.sum(pick * probe_ref[...], axis=1, keepdims=True)
+    own_probe = jnp.sum(pick * vectors_ref[PROBE : PROBE + 1], axis=1, keepdims=True)
     query_out[...] = own_probe * mine(probe_query_grad)
     probe_out[...] = jnp.sum(query_ref[...].astype(f32) * probe_query_grad, axis=1, keepdims=True)
     final_out[...] = rows[:, HEADS : HEADS + 1]
@@ -319,7 +416,7 @@
     output_out[...] = exact(((1,), (0,)), left, jnp.concatenate(output_rights, axis=0))
 
 
-def pool_weights_call(place, rows, probe, probe_query, pool_query, pool_key, images):
+def pool_weights_call(place, rows, vectors, probe_query, pool_query, pool_key, images):
     width = rows.shape[1]
     block = width // images
     whole = lambda *shape: pl.BlockSpec(shape, lambda i, p: (0,) * len(shape))
@@ -331,9 +428,9 @@
             grid=(1,),
             in_specs=[
                 whole(*rows.shape),
+                whole(*vectors.shape),
                 whole(1, width),
-                whole(1, width),
-                whole(block, width),
+                pl.BlockSpec((None, block, width), lambda i, p: (p[0], 0, 0)),
                 whole(width, width),
             ],
             out_specs=[whole(*t) for t in grads],
@@ -341,7 +438,7 @@
         out_shape=[jax.ShapeDtypeStruct(t, f32) for t in grads],
         cost_estimate=light,
         name="pool_weights",
-    )(place, rows, probe, probe_query, pool_query, pool_key)
+    )(place, rows, vectors, probe_query, pool_query.reshape(images, block, width), pool_key)
 
 
 def attend_kernel(q_ref, ka_ref, kb_ref, va_ref, vb_ref, a_ref, lse_ref):
@@ -558,9 +655,9 @@
     return lambda p: 1 - ((p[4] >> bit) & 1)
 
 
-def fold_kernel(plan, gathers, place_ref, *refs):
+def fold_kernel(plan, gathers, products, place_ref, *refs):
     count = sum(sum(slots) for slots, _ in plan)
-    count += 2 * len(gathers)
+    count += 2 * len(gathers) + (1 + len(products) if products else 0)
     inputs = iter(refs[:count])
     outs = iter(refs[count:])
     for slots, join in plan:
@@ -602,9 +699,28 @@
             out[sums:rows] = own[sums:]
         if gather:
             out[rows:] = other[sums:]
-
-
-def fold(place, outputs, dtype, notes=()):
+    if products:
+        outs = refs[count:]
+        sums = refs[-1]
+        rows = outs[products[0][1]].shape[0]
+        vectors = next(inputs)[...]
+        pick = lax.broadcasted_iota(jnp.int32, (rows, vectors.shape[1]), 1) == (
+            lax.broadcasted_iota(jnp.int32, (rows, vectors.shape[1]), 0) + place_ref[0] * rows
+        )
+        eye = lax.broadcasted_iota(jnp.int32, (rows, 128), 1) == (
+            lax.broadcasted_iota(jnp.int32, (rows, 128), 0)
+        )
+        columns = {}
+        for row, output in products:
+            weight = next(inputs)[...].astype(f32)
+            part = jnp.sum(weight * outs[output][...], axis=1, keepdims=True)
+            columns[row] = columns[row] + part if row in columns else part
+        for row, column in columns.items():
+            gain = jnp.sum(jnp.where(pick, vectors[row : row + 1], 0.0), axis=1, keepdims=True)
+            sums[row : row + 1] = jnp.sum(jnp.where(eye, column / gain, 0.0), axis=0, keepdims=True)
+
+
+def fold(place, outputs, dtype, notes=(), products=(), vectors=None):
     arrays, specs, plan, shapes, gathers = [], [], [], [], []
     for slots, join in outputs:
         counts = []
@@ -638,8 +754,19 @@
         specs += [whole(own.shape)] * 2
         gathers.append(gather)
         shapes.append(((2 * rows - TOP if gather else rows, width), f32))
-    return pl.pallas_call(
-        functools.partial(fold_kernel, tuple(plan), tuple(gathers)),
+    if products:
+        arrays.append(vectors)
+        specs.append(whole(vectors.shape))
+    for _, output, weight in products:
+        rows, width = shapes[output][0]
+        arrays.append(weight.reshape(-1, rows, weight.shape[1]))
+        specs.append(pl.BlockSpec((None, rows, width), lambda i, p: (p[0], 0, p[1])))
+    if products:
+        shapes.append(((2, 128), f32))
+    return pl.pallas_call(
+        functools.partial(
+            fold_kernel, tuple(plan), tuple(gathers), tuple((c, o) for c, o, _ in products)
+        ),
         grid_spec=pltpu.PrefetchScalarGridSpec(
             num_scalar_prefetch=1,
             grid=(1,),
@@ -771,7 +898,7 @@
 
 
 def up_back_kernel(
-    block, place_ref, low_ref, du_ref, up_ref, unit_ref, inv_ref, gain_ref, above_ref, wo_ref,
+    block, place_ref, low_ref, du_ref, up_ref, unit_ref, inv_ref, vectors_ref, above_ref, wo_ref,
     a_ref, send_ref, keep_ref, grad_ref, heads_ref, acc_ref, out_ref,
 ):
     c = pl.program_id(0)
@@ -796,7 +923,7 @@
     @pl.when(c == steps - 1)
     def _():
         total = above_ref[...] + norm_back_rows(
-            acc_ref[...], unit_ref[...], inv_ref[...], gain_ref[...]
+            acc_ref[...], unit_ref[...], inv_ref[...], vectors_ref[SECOND : SECOND + 1]
         )
         grad_ref[...] = total
         branch = total.astype(bf16)
@@ -823,7 +950,7 @@
                 ref[0, 0, j, :, 2 * chunk :] = jnp.where(first, more[:size], more[size:]).astype(bf16)
 
 
-def up_back_call(place, low, du, w_up, unit, inv, gain, above, w_output, attended, images):
+def up_back_call(place, low, du, w_up, unit, inv, vectors, above, w_output, attended, images):
     rows, width = low.shape
     depth = du.shape[1]
     steps = 4
@@ -848,7 +975,7 @@
             pl.BlockSpec((width, chunk), lambda c: (0, jnp.minimum(c, steps - 1))),
             whole(rows, width),
             whole(rows, 1),
-            whole(1, width),
+            whole(*vectors.shape),
             whole(rows, width),
             whole(width, width),
             whole(rows, width),
@@ -871,7 +998,7 @@
         ],
         cost_estimate=light,
         name="up_back",
-    )(place, low, du, w_up, unit, inv, gain, above, w_output, attended)
+    )(place, low, du, w_up, unit, inv, vectors, above, w_output, attended)
 
 
 def parts_in_kernel(dq_ref, dk_ref, dv_ref, wq_ref, wk_ref, wv_ref, own_ref, other_ref):
@@ -894,19 +1021,20 @@
     )(dq, dk, dv, w_query, w_key, w_value)
 
 
-def own_in_kernel(own_ref, arrived_ref, unit_ref, inv_ref, gain_ref, above_ref, out_ref):
+def own_in_kernel(own_ref, arrived_ref, unit_ref, inv_ref, vectors_ref, above_ref, out_ref):
     grad = own_ref[...] + arrived_ref[...].astype(f32)
-    through = norm_back_rows(grad, unit_ref[...], inv_ref[...], gain_ref[...])
+    gain = vectors_ref[FIRST : FIRST + 1]
+    through = norm_back_rows(grad, unit_ref[...], inv_ref[...], gain)
     out_ref[...] = above_ref[...] + through
 
 
-def own_in_call(own, arrived, unit, inv, gain, above):
+def own_in_call(own, arrived, unit, inv, vectors, above):
     return pl.pallas_call(
         own_in_kernel,
         out_shape=jax.ShapeDtypeStruct(own.shape, f32),
         cost_estimate=light,
         name="own_in",
-    )(own, arrived, unit, inv, gain, above)
+    )(own, arrived, unit, inv, vectors, above)
 
 
 class Order:
@@ -951,11 +1079,9 @@
     caps = captions.shape[0]
     place = jnp.stack([me, seq_me, me & 1, (me >> 1) & 1, me >> 2]).astype(jnp.int32)
 
-    own_query = lax.dynamic_slice_in_dim(pool_query, me * (width // images), width // images, 0)
-    first_row, second_row = first_gain[None], second_gain[None]
-    place, own_query, first_row, second_row = tie(place, own_query, first_row, second_row)
-
     other_tokens = seq_swap(own_tokens)
+    vectors = vectors_call(first_gain, second_gain, final_gain, probe)
+    place, vectors = tie(place, vectors)
 
     gathered = captions[None]
 
@@ -964,41 +1090,31 @@
 
     gathered = gather_more(gathered, 0)
 
-    inputs = own_tokens.astype(f32)
-    normed_one, unit_one, scale_one = layer_norm(inputs, first_gain)
-    low_own = normed_one.astype(bf16)
-    queries = low_dot(low_own, w_query).astype(bf16)
-    keys_own = low_dot(low_own, w_key).astype(bf16)
-    values_own = low_dot(low_own, w_value).astype(bf16)
-    probe_query, key_probe = probe_call(probe, pool_query, pool_key)
+    low_own, unit_one, scale_one, queries, keys_own, values_own = front_call(
+        own_tokens, vectors, w_query, w_key, w_value
+    )
+    low_own, gathered, vectors = tie(low_own, gathered, vectors)
     gathered = gather_more(gathered, 1)
-
-    other_tokens, gathered, queries, keys_own, values_own, key_probe = tie(
-        other_tokens, gathered, queries, keys_own, values_own, key_probe
-    )
-    low_other = layer_norm(other_tokens.astype(f32), first_gain)[0].astype(bf16)
-    keys_other = low_dot(low_other, w_key).astype(bf16)
-    values_other = low_dot(low_other, w_value).astype(bf16)
+    probe_query, key_probe = probe_call(vectors, pool_query, pool_key)
+
+    other_tokens, gathered, key_probe = tie(other_tokens, gathered, key_probe)
     gathered = gather_more(gathered, 2)
+    low_other, _, _, keys_other, values_other = front_call(other_tokens, vectors, w_key, w_value)
     attended_low, log_totals = attend(queries, keys_own, keys_other, values_own, values_other)
     attended_low, gathered = tie(attended_low, gathered)
     for bit in range(3, bits):
         gathered = gather_more(gathered, bit)
-    residual = inputs + low_dot(attended_low, w_output)
-
-    normed_two, unit_two, scale_two = layer_norm(residual, second_gain)
-    second_low = normed_two.astype(bf16)
-    upward = low_dot(second_low, w_up)
-    hidden_low = gelu_tanh(upward).astype(bf16)
-    result = residual + low_dot(hidden_low, w_down)
-    block_out = result.astype(bf16)[None]
-
-    pool_low, unit_pool, inv_pool, exps, packed = pool_call(result, final_gain, key_probe)
+
+    (
+        second_low, unit_two, scale_two, upward, hidden_low, block_out,
+        pool_low, unit_pool, inv_pool, exps, packed,
+    ) = middle_call(attended_low, own_tokens, vectors, w_output, w_up, w_down, key_probe)
+    block_out = block_out[None]
     other_packed = seq_swap(packed)
     other_packed, gathered = tie(other_packed, gathered)
     result_grad, branch_grad, message = pool_back_call(
         place, caption_counts, positive_pairs, log_temp, pair_bias, packed, other_packed, exps,
-        pool_low, unit_pool, inv_pool, final_gain, key_probe, pool_value, pool_output,
+        pool_low, unit_pool, inv_pool, vectors, key_probe, pool_value, pool_output,
         gathered.reshape(images * caps, width), images, seq_count,
     )
 
@@ -1028,7 +1144,7 @@
     down_b.first = img_swap(send_b, 2)
     message_in = img_swap(message, 1)
     up_send, up_keep, residual_grad, attended_grad = up_back_call(
-        place, second_low, up_grad_low, w_up, unit_two, scale_two, second_row, result_grad,
+        place, second_low, up_grad_low, w_up, unit_two, scale_two, vectors, result_grad,
         w_output, attended_low, images,
     )
     attended_grad, up_send, message_in, down_a.first, down_b.first = step(
@@ -1115,7 +1231,7 @@
     for bit in range(4, bits):
         (message,) = fold(place, [], f32, [(message, img_swap(message, 1 << bit), True)])
     pool_grads = pool_weights_call(
-        place, message, probe[None], probe_query, own_query, pool_key, images
+        place, message, vectors, probe_query, pool_query, pool_key, images
     )
     pool_grads, three_a.second, three_b.second, arrived_part, up_in, down_in = step(
         pool_grads, three_a.second, three_b.second, arrived_part, up_in, down_in
@@ -1132,39 +1248,24 @@
     finish(place, down_a, down_b)
     (down_grad,) = fold(place, [([down_a.whole(), down_b.whole()], "rows")], f32)
     input_grad = own_in_call(
-        own_part, arrived_part, unit_one, scale_one, first_row, residual_grad
+        own_part, arrived_part, unit_one, scale_one, vectors, residual_grad
     )
     input_grad, down_grad, up_in, *three_in = step(input_grad, down_grad, up_in, *three_in)
     take(up_a, up_b, [up_in], 2)
     take(three_a, three_b, three_in, 2)
     finish(place, up_a, up_b)
     finish(place, three_a, three_b)
-    up_weight_grad, output_grad, query_weight_grad, key_weight_grad, value_weight_grad = fold(
+    up_weight_grad, output_grad, query_weight_grad, key_weight_grad, value_weight_grad, gains = fold(
         place,
         [([up_a.whole(), up_b.whole()], "wide")]
         + [([three_a.whole(m), three_b.whole(m)], "rows") for m in range(3)],
         f32,
-    )
-
+        products=[(SECOND, 0, w_up), (FIRST, 2, w_query), (FIRST, 3, w_key), (FIRST, 4, w_value)],
+        vectors=vectors,
+    )
+
+    gains = gains + seq_swap(gains)
     block = width // images
-
-    def own_product(weight, grad):
-        columns = grad.shape[1]
-        own = lax.dynamic_slice(weight, (me * block, seq_me * columns), (block, columns))
-        return jnp.sum(own.astype(f32) * grad, axis=1)
-
-    def own_rows(vector):
-        return lax.dynamic_slice_in_dim(vector, me * block, block)
-
-    gains = jnp.stack(
-        [
-            own_product(w_query, query_weight_grad)
-            + own_product(w_key, key_weight_grad)
-            + own_product(w_value, value_weight_grad),
-            own_product(w_up, up_weight_grad),
-        ]
-    )
-    gains = (gains + seq_swap(gains)) / jnp.stack([own_rows(first_gain), own_rows(second_gain)])
     query_pool_grad, key_pool_grad, value_pool_grad, out_pool_grad, probe_grad, final_grad = (
         pool_grads
     )
@@ -1177,8 +1278,8 @@
         output_grad,
         up_weight_grad,
         down_grad,
-        gains[0],
-        gains[1],
+        gains[FIRST, :block],
+        gains[SECOND, :block],
         final_grad[:, 0],
         probe_grad[:, 0],
         query_pool_grad,

time: 223 us -> 214 us (0.960)
  Pallas kernels: 103 us -> 122 us
  matrix products: 13.8 us -> 0 us
  other arithmetic: 11.9 us -> 2.01 us
  local copies, waits for them, and re-layouts: 15.3 us -> 9.63 us
  starting transfers between devices: 32.9 us -> 35.7 us
    pallas_call x1 -> x4, Pallas kernels: 2.58 us -> 21.7 us  [the longest x1 11 us: middle_call(): pl.pallas_call(middle_kernel, grid=(steps,), in_specs=[whole(rows, width)...]
    dot_general x8 -> x0, matrix products: 13.8 us -> none  [low_dot(): return jnp.dot(left_side, right_side, preferred_element_type=f32)]
    reduce_sum x8 -> x0, other arithmetic: 6.21 us -> none  [the longest x3 3.22 us: own_product(): return jnp.sum(own.astype(f32) * grad, axis=1)]
    broadcast_in_dim x4 -> x0, local copies, waits for them, and re-layouts: 2.33 us -> none  [the longest x2 1.17 us: layer_norm(): return (normed * gain_row, normed, inv_std)]
    unnamed x98 -> x66, local copies, waits for them, and re-layouts: 6.52 us -> 6.4 us
  transfers between devices with their start and end apart: 35 -> 35, of which waited for: 12 -> 11; matrix products, arithmetic and copies ran while one was open for 13% -> 2% of each run, Pallas kernels for 31% -> 41%
where the time goes in v5:
time: 214 us; the launch traced here: 213 us
  Pallas kernels  122 us (57%)
  waiting for transfers between devices  40.7 us (19%)
  starting transfers between devices  35.7 us (17%)
  local copies, waits for them, and re-layouts  9.63 us (5%)
  between operations  2.95 us (1%)
    pallas_call x9, Pallas kernels, fold(): pl.pallas_call(functools.partial(fold_kernel, tuple(plan), tuple(gathers)...  31.2 us
    ppermute x24, waiting for transfers between devices, img_swap(): return lax.ppermute(value, 'img', [(i, i ^ mask) for i in range(count)])  29.1 us
    ppermute x24, starting transfers between devices, img_swap(): return lax.ppermute(value, 'img', [(i, i ^ mask) for i in range(count)])  22.3 us
    ppermute x11, starting transfers between devices, seq_swap(): return lax.ppermute(value, 'seq', [(0, 1), (1, 0)])  13.4 us
    pallas_call x1, Pallas kernels, up_back_call(): pl.pallas_call(functools.partial(up_back_kernel, block), grid=(2 * steps,...  12.4 us
    ppermute x11, waiting for transfers between devices, seq_swap(): return lax.ppermute(value, 'seq', [(0, 1), (1, 0)])  11.6 us
    pallas_call x1, Pallas kernels, middle_call(): pl.pallas_call(middle_kernel, grid=(steps,), in_specs=[whole(rows, width)...  11 us
    pallas_call x1, Pallas kernels, attend_back(): pl.pallas_call(attend_back_kernel, grid=(pairs,), in_specs=[row_spec] * 6...  10.3 us
  transfers between devices with their start and end apart: 35, of which 11 were waited for; matrix products, arithmetic and copies ran while one was open for 2% of the time, Pallas kernels for 41%

profile of v5, /device:TPU:0, one launch (start us, length us, event | category | flops | bytes accessed | tf_op | source)
XLA Modules:
  0.0 212.7 jit_solution(7063770373860624577)
XLA Ops:
  0.7 3.1 %collective-permute-start = (bf16[256,768]{1,0:T(8,128)(2,1)}, bf16[256,768]{1,0:T(8,128)(2,1)S(1)}, u32[]{:S(2)}, u32[]{:S(2)}) collective-permute-start(bf16[256,768]{1,0:T(8,128)(2,1)} %bitcast.199), channel_id=1, source_target_pairs={{0,1},{1,0},{2,3},{3,2},{4,5},{5,4},{6,7},{7,6},{8,9},{9,8},{10,11... | collective-permute-start | bytes 1179656 | tf_op jit(solution)/shard_map/ppermute | solution.py:623
  5.7 4.9 %front.2 = (bf16[256,768]{1,0:T(8,128)(2,1)}, f32[256,768]{1,0:T(8,128)}, f32[256,1]{1,0:T(8,128)}, bf16[256,768]{1,0:T(8,128)(2,1)}, bf16[256,768]{1,0:T(8,128)(2,1)}, /*index=5*/bf16[256,768]{1,0:T(8,128)(2,1)}) custom-call(bf16[256,768]{1,0:T(8,128)(2,1)} %bitcast.200, f32[4,768]{1,0:T(4,128)} %vectors.1.refs_1_.vectors_ref.refs_54_, ...), custom_call_target="tpu_custom_call" | custom-call | flops 1024 | bytes 1024 | tf_op jit(solution)/shard_map/front/pallas_call | solution.py:110
  12.2 3.0 %probe_rows.1 = (f32[1,768]{1,0:T(1,128)}, f32[16,768]{1,0:T(8,128)}) custom-call(f32[4,768]{1,0:T(4,128)} %vectors.1.refs_1_.vectors_ref.refs_54_, bf16[768,768]{1,0:T(8,128)(2,1)} %query_ref.1, bf16[768,768]{1,0:T(8,128)(2,1)} %key_ref.3), custom_call_target="tpu_custom_call" | custom-call | flops 1024 | bytes 1024 | tf_op jit(solution)/shard_map/probe_rows/pallas_call | solution.py:136
  16.8 4.4 %front.3 = (bf16[256,768]{1,0:T(8,128)(2,1)}, f32[256,768]{1,0:T(8,128)}, f32[256,1]{1,0:T(8,128)}, bf16[256,768]{1,0:T(8,128)(2,1)}, bf16[256,768]{1,0:T(8,128)(2,1)}) custom-call(bf16[256,768]{1,0:T(8,128)(2,1)} %copy-done.23, f32[4,768]{1,0:T(4,128)} %vectors.1.refs_1_.vectors_ref.refs_54_, bf16[768,768]{1,0:T(8,128)(2,1)} %wk_ref.1, bf16[768,768]{1,0:T(8,128)(2,1)} %wv_ref.1), custom_call_target="tpu_custom_call" | custom-call | flops 1024 | bytes 1024 | tf_op jit(solution)/shard_map/front/pallas_call | solution.py:110
  21.2 7.9 %attend.1 = (bf16[256,768]{1,0:T(8,128)(2,1)}, f32[6,256,2]{2,1,0:T(8,128)}) custom-call(bf16[256,768]{1,0:T(8,128)(2,1)} %get-tuple-element.186.q_ref, bf16[256,768]{1,0:T(8,128)(2,1)} %get-tuple-element.187.ka_ref, bf16[256,768]{1,0:T(8,128)(2,1)} %get-tuple-element.193.kb_ref, bf16[256,768]{1,0:T(8,128)(2,1)} %get-tuple-element.194.va_ref, ...), custom_call_target="tpu_custom_call" | custom-call | flops 1024 | bytes 1024 | tf_op jit(solution)/shard_map/attend/pallas_call | solution.py:467
  29.1 2.6 %collective-permute-start.5 = (f32[8,5,768]{2,1,0:T(8,128)S(1)}, f32[8,5,768]{2,1,0:T(8,128)S(1)}, u32[]{:S(2)}, u32[]{:S(2)}) collective-permute-start(f32[8,5,768]{2,1,0:T(8,128)S(1)} %pad_maximum_fusion.1), channel_id=1, source_target_pairs={{0,16},{2,18},{4,20},{6,22},{8,24},{10,26},{12,28},{14,30},{16,0},... | collective-permute-start | bytes 368648 | tf_op jit(solution)/shard_map/ppermute | solution.py:619
  33.7 11.0 %middle.1 = (bf16[256,768]{1,0:T(8,128)(2,1)}, f32[256,768]{1,0:T(8,128)}, f32[256,1]{1,0:T(8,128)}, f32[256,3072]{1,0:T(8,128)}, bf16[256,3072]{1,0:T(8,128)(2,...) custom-call(bf16[256,768]{1,0:T(8,128)(2,1)} %get-tuple-element.198., ...), custom_call_target="tpu_custom_call" | custom-call | flops 1024 | bytes 1024 | tf_op jit(solution)/shard_map/middle/pallas_call | solution.py:209
  45.4 3.8 %collective-permute-done.4.other_ref = f32[16,896]{1,0:T(8,128)S(1)} collective-permute-done((f32[16,896]{1,0:T(8,128)}, f32[16,896]{1,0:T(8,128)S(1)}, u32[]{:S(2)}, u32[]{:S(2)}) %collective-permute-start.4) | collective-permute-done | bytes 57376 | tf_op jit(solution)/shard_map/ppermute | solution.py:623
  49.9 5.7 %pool_back.1 = (f32[256,768]{1,0:T(8,128)}, bf16[256,768]{1,0:T(8,128)(2,1)}, f32[24,768]{1,0:T(8,128)}) custom-call(s32[5]{0:T(128)} %stack.23.place_ref, s32[1]{0:T(128)S(6)} %copy.69.count_ref, s32[1,80]{1,0:T(1,128)} %pairs_ref.1, f32[1]{0:T(128)} %bitcast.86.temp_ref, f32[1]{0:T(128)} %bitcast.87.bias_ref, f32[16,896]{1,0:T(8,128)} %get-tuple-element.206.own_ref, ...), custom_call_target="tpu_custom_call" | custom-call | flops 1024 | bytes 1024 | tf_op jit(solution)/shard_map/pool_back/pallas_call | solution.py:357
  56.2 4.4 %wgrad.1 = (bf16[2,2,8,96,384]{4,3,2,1,0:T(8,128)(2,1)}, bf16[2,2,8,96,384]{4,3,2,1,0:T(8,128)(2,1)}) custom-call(s32[5]{0:T(128)} %stack.23.place_ref, bf16[256,3072]{1,0:T(8,128)(2,1)} %get-tuple-element.205.left_ref, bf16[256,768]{1,0:T(8,128)(2,1)} %get-tuple-element.218.right_ref.grad_ref), custom_call_target="tpu_custom_call" | custom-call | flops 1024 | bytes 1024 | tf_op jit(solution)/shard_map/wgrad/pallas_call | solution.py:557
  60.7 6.6 %gelu_back.1.du_ref = bf16[256,3072]{1,0:T(8,128)(2,1)} custom-call(bf16[256,768]{1,0:T(8,128)(2,1)} %get-tuple-element.218.right_ref.grad_ref, bf16[3072,768]{1,0:T(8,128)(2,1)} %down_ref.3, f32[256,3072]{1,0:T(8,128)} %get-tuple-element.219.up_ref), custom_call_target="tpu_custom_call" | custom-call | flops 1024 | bytes 1024 | tf_op jit(solution)/shard_map/gelu_back/pallas_call | solution.py:878
  68.7 3.5 %fold.9 = (bf16[8,96,384]{2,1,0:T(8,128)(2,1)}, bf16[2,4,96,384]{3,2,1,0:T(8,128)(2,1)}, f32[24,768]{1,0:T(8,128)}) custom-call(s32[5]{0:T(128)} %stack.23.place_ref, bf16[2,2,8,96,384]{4,3,2,1,0:T(8,128)(2,1)} %get-tuple-element.222.refs_0_, bf16[2,2,8,96,384]{4,3,2,1,0:T(8,128)(2,1)} %copy-done.2, bf16[2,2,4,2,96,384]{5,4,3,2,1,0:T(8,128)(2,1)} %bitcast.136, ...), custom_call_target="tpu_custom_call" | custom-call | flops 1024 | bytes 1024 | tf_op jit(solution)/shard_map/fold/pallas_call | solution.py:766
  74.9 12.4 %up_back.1 = (bf16[2,2,8,24,1920]{4,3,2,1,0:T(8,128)(2,1)}, bf16[2,2,8,24,1920]{4,3,2,1,0:T(8,128)(2,1)}, f32[256,768]{1,0:T(8,128)}, bf16[256,768]{1,0:T(8,128)(2,1)}) custom-call(s32[5]{0:T(128)} %stack.23.place_ref, bf16[256,768]{1,0:T(8,128)(2,1)} %get-tuple-element.204.low_ref, bf16[256,3072]{1,0:T(8,128)(2,1)} %gelu_back.1.du_ref, ...), custom_call_target="tpu_custom_call" | custom-call | flops 1024 | bytes 1024 | tf_op jit(solution)/shard_map/up_back/pallas_call | solution.py:968
  90.2 3.1 %fold.10 = (bf16[4,96,384]{2,1,0:T(8,128)(2,1)}, bf16[4,96,384]{2,1,0:T(8,128)(2,1)}, f32[32,768]{1,0:T(8,128)}) custom-call(s32[5]{0:T(128)} %stack.23.place_ref, bf16[2,2,4,2,96,384]{5,4,3,2,1,0:T(8,128)(2,1)} %bitcast.137, bf16[2,2,4,2,96,384]{5,4,3,2,1,0:T(8,128)(2,1)} %bitcast.146, bf16[4,2,96,384]{3,2,1,0:T(8,128)(2,1)} %bitcast.174, ...), custom_call_target="tpu_custom_call" | custom-call | flops 1024 | bytes 1024 | tf_op jit(solution)/shard_map/fold/pallas_call | solution.py:766
  95.8 10.3 %attend_back.1 = (bf16[256,768]{1,0:T(8,128)(2,1)}, bf16[512,768]{1,0:T(8,128)(2,1)}, bf16[512,768]{1,0:T(8,128)(2,1)}) custom-call(bf16[256,768]{1,0:T(8,128)(2,1)} %get-tuple-element.186.q_ref, bf16[256,768]{1,0:T(8,128)(2,1)} %get-tuple-element.187.ka_ref, bf16[256,768]{1,0:T(8,128)(2,1)} %get-tuple-element.193.kb_ref, ...), custom_call_target="tpu_custom_call" | custom-call | flops 1024 | bytes 1024 | tf_op jit(solution)/shard_map/attend_back/pallas_call | solution.py:515
  106.1 6.2 %wgrad_three.1 = (bf16[2,2,8,3,24,384]{5,4,3,2,1,0:T(8,128)(2,1)}, bf16[2,2,8,3,24,384]{5,4,3,2,1,0:T(8,128)(2,1)}) custom-call(s32[5]{0:T(128)} %stack.23.place_ref, bf16[256,768]{1,0:T(8,128)(2,1)} %get-tuple-element.202.na_ref, bf16[256,768]{1,0:T(8,128)(2,1)} %get-tuple-element.203.nb_ref, bf16[256,768]{1,0:T(8,128)(2,1)} %get-tuple-element.267.dq_ref, ...), custom_call_target="tpu_custom_call" | custom-call | flops 1024 | bytes 1024 | tf_op jit(solution)/shard_map/wgrad_three/pallas_call | solution.py:602
  112.3 4.3 %fold.11 = (bf16[2,4,24,1920]{3,2,1,0:T(8,128)(2,1)}, bf16[8,24,1920]{2,1,0:T(8,128)(2,1)}, bf16[2,2,96,384]{3,2,1,0:T(8,128)(2,1)}, f32[48,768]{1,0:T(8,128)}) custom-call(s32[5]{0:T(128)} %stack.23.place_ref, bf16[2,2,4,2,24,1920]{5,4,3,2,1,0:T(8,128)(2,1)} %bitcast.118, bf16[2,2,4,2,24,1920]{5,4,3,2,1,0:T(8,128)(2,1)} %bitcast.127, ...), custom_call_target="tpu_custom_call" | custom-call | flops 1024 | bytes 1024 | tf_op jit(solution)/shard_map/fold/pallas_call | solution.py:766
  121.4 5.2 %parts_in.1 = (f32[256,768]{1,0:T(8,128)}, bf16[256,768]{1,0:T(8,128)(2,1)}) custom-call(bf16[256,768]{1,0:T(8,128)(2,1)} %get-tuple-element.267.dq_ref, bf16[512,768]{1,0:T(8,128)(2,1)} %get-tuple-element.254.dk_ref, bf16[512,768]{1,0:T(8,128)(2,1)} %get-tuple-element.255.dv_ref, bf16[768,768]{1,0:T(8,128)(2,1)} %wq_ref.1, bf16[768,768]{1,0:T(8,128)(2,1)} %wk_ref.1, ...), custom_call_target="tpu_custom_call" | custom-call | flops 1024 | bytes 1024 | tf_op jit(solution)/shard_map/parts_in/pallas_call | solution.py:1013
  126.6 5.0 %collective-permute-done.19.refs_11_ = f32[48,768]{1,0:T(8,128)} collective-permute-done((f32[48,768]{1,0:T(8,128)}, f32[48,768]{1,0:T(8,128)}, u32[]{:S(2)}, u32[]{:S(2)}) %collective-permute-start.19) | collective-permute-done | bytes 147488 | tf_op jit(solution)/shard_map/ppermute | solution.py:619
  131.6 4.1 %collective-permute-done.16.refs_6_.refs_2_ = bf16[2,4,24,1920]{3,2,1,0:T(8,128)(2,1)S(1)} collective-permute-done((bf16[2,4,24,1920]{3,2,1,0:T(8,128)(2,1)}, bf16[2,4,24,1920]{3,2,1,0:T(8,128)(2,1)S(1)}, u32[]{:S(2)}, u32[]{:S(2)}) %collective-permute-start.16) | collective-permute-done | bytes 737312 | tf_op jit(solution)/shard_map/ppermute | solution.py:619
  138.0 4.2 %fold.12 = (bf16[2,4,3,24,384]{4,3,2,1,0:T(8,128)(2,1)}, bf16[8,3,24,384]{3,2,1,0:T(8,128)(2,1)}, bf16[4,24,1920]{2,1,0:T(8,128)(2,1)}, bf16[4,24,1920]{2,1,0:T(8,128)(2,1)}, f32[80,768]{1,0:T(8,128)}) custom-call(s32[5]{0:T(128)} %stack.23.place_ref, bf16[2,2,4,2,3,24,384]{6,5,4,3,2,1,0:T(8,128)(2,1)} %bitcast.88, ...), custom_call_target="tpu_custom_call" | custom-call | flops 1024 | bytes 1024 | tf_op jit(solution)/shard_map/fold/pallas_call | solution.py:766
  149.3 9.5 %collective-permute-done.20.refs_15_ = f32[80,768]{1,0:T(8,128)S(1)} collective-permute-done((f32[80,768]{1,0:T(8,128)}, f32[80,768]{1,0:T(8,128)S(1)}, u32[]{:S(2)}, u32[]{:S(2)}) %collective-permute-start.20) | collective-permute-done | bytes 245792 | tf_op jit(solution)/shard_map/ppermute | solution.py:619
  158.8 3.6 %collective-permute-done.23.refs_3_ = bf16[4,24,1920]{2,1,0:T(8,128)(2,1)S(1)} collective-permute-done((bf16[4,24,1920]{2,1,0:T(8,128)(2,1)}, bf16[4,24,1920]{2,1,0:T(8,128)(2,1)S(1)}, u32[]{:S(2)}, u32[]{:S(2)}) %collective-permute-start.23) | collective-permute-done | bytes 368672 | tf_op jit(solution)/shard_map/ppermute | solution.py:623
  163.5 4.1 %fold.14 = (bf16[4,3,24,384]{3,2,1,0:T(8,128)(2,1)}, bf16[4,3,24,384]{3,2,1,0:T(8,128)(2,1)}, bf16[2,2,24,1920]{3,2,1,0:T(8,128)(2,1)}, f32[144,768]{1,0:T(8,128)}) custom-call(s32[5]{0:T(128)} %stack.23.place_ref, bf16[2,2,4,2,3,24,384]{6,5,4,3,2,1,0:T(8,128)(2,1)} %bitcast.89, bf16[2,2,4,2,3,24,384]{6,5,4,3,2,1,0:T(8,128)(2,1)} %bitcast.104, ...), custom_call_target="tpu_custom_call" | custom-call | flops 1024 | bytes 1024 | tf_op jit(solution)/shard_map/fold/pallas_call | solution.py:766
  171.8 4.2 %pool_weights.1 = (f32[48,384]{1,0:T(8,128)}, f32[48,384]{1,0:T(8,128)}, f32[48,384]{1,0:T(8,128)}, f32[48,384]{1,0:T(8,128)}, f32[48,1]{1,0:T(8,128)}, /*index=5*/f32[48,1]{1,0:T(8,128)}) custom-call(s32[5]{0:T(128)} %stack.23.place_ref, f32[144,768]{1,0:T(8,128)} %get-tuple-element.304.rows_ref, f32[4,768]{1,0:T(4,128)} %vectors.1.refs_1_.vectors_ref.refs_54_, ...), custom_call_target="tpu_custom_call" | custom-call | flops 1024 | bytes 1024 | tf_op jit(solution)/shard_map/pool_weights/pallas_call | solution.py:424
  176.0 3.1 %collective-permute-done.29.refs_5_.refs_11_ = bf16[2,1,96,384]{3,2,1,0:T(8,128)(2,1)S(1)} collective-permute-done((bf16[2,1,96,384]{3,2,1,0:T(8,128)(2,1)S(1)}, bf16[2,1,96,384]{3,2,1,0:T(8,128)(2,1)S(1)}, u32[]{:S(2)}, u32[]{:S(2)}) %collective-permute-start.29) | collective-permute-done | bytes 147488 | tf_op jit(solution)/shard_map/ppermute | solution.py:619
  182.5 3.3 %fold.16 = (bf16[2,1,3,24,384]{4,3,2,1,0:T(8,128)(2,1)}, bf16[2,1,3,24,384]{4,3,2,1,0:T(8,128)(2,1)}, bf16[2,1,3,24,384]{4,3,2,1,0:T(8,128)(2,1)}, bf16[2,1,24,1920]{3,2,1,0:T(8,128)(2,1)}) custom-call(s32[5]{0:T(128)} %stack.23.place_ref, bf16[2,2,1,4,2,3,24,384]{7,6,5,4,3,2,1,0:T(8,128)(2,1)} %bitcast.91, ...), custom_call_target="tpu_custom_call" | custom-call | flops 1024 | bytes 1024 | tf_op jit(solution)/shard_map/fold/pallas_call | solution.py:766
  186.9 2.6 %collective-permute-start.32 = (bf16[2,1,3,24,384]{4,3,2,1,0:T(8,128)(2,1)}, bf16[2,1,3,24,384]{4,3,2,1,0:T(8,128)(2,1)S(1)}, u32[]{:S(2)}, u32[]{:S(2)}) collective-permute-start(bf16[2,1,3,24,384]{4,3,2,1,0:T(8,128)(2,1)} %get-tuple-element.331), channel_id=1, source_target_pairs={{0,16},{2,18},{4,20},{6,22},{8,24},{10,26},{12,28},{14,30},{16,0},... | collective-permute-start | bytes 331784 | tf_op jit(solution)/shard_map/ppermute | solution.py:619
  191.2 2.7 %fold.15 = f32[192,384]{1,0:T(8,128)} custom-call(s32[5]{0:T(128)} %stack.23.place_ref, bf16[2,2,4,2,96,384]{5,4,3,2,1,0:T(8,128)(2,1)} %bitcast.143, bf16[2,2,4,2,96,384]{5,4,3,2,1,0:T(8,128)(2,1)} %bitcast.152, bf16[4,2,96,384]{3,2,1,0:T(8,128)(2,1)} %bitcast.177, bf16[4,96,384]{2,1,0:T(8,128)(2,1)} %copy-done.18, bf16[2,2,96,384]{3,2,1,0:T(8,128)(2,1)} %copy-done.12, ...), custom_call_target="tpu_custom_call" | custom-call | flops 1024 | bytes 1024 | tf_op jit(solution)/shard_map/fold/pallas_call | solution.py:766
  193.9 3.1 %own_in.1 = f32[256,768]{1,0:T(8,128)} custom-call(f32[256,768]{1,0:T(8,128)} %get-tuple-element.275.own_ref, bf16[256,768]{1,0:T(8,128)(2,1)} %copy-done.22, f32[256,768]{1,0:T(8,128)} %get-tuple-element.318.unit_ref, f32[256,1]{1,0:T(8,128)} %get-tuple-element.319.inv_ref, f32[4,768]{1,0:T(4,128)} %vectors.1.refs_1_.vectors_ref.refs_54_, ...), custom_call_target="tpu_custom_call" | custom-call | flops 1024 | bytes 1024 | tf_op jit(solution)/shard_map/own_in/pallas_call | solution.py:1032
  197.1 6.1 %collective-permute-done.32.refs_17_.refs_24_.refs_31_.refs_38_.refs_45_.refs_52_ = bf16[2,1,3,24,384]{4,3,2,1,0:T(8,128)(2,1)S(1)} collective-permute-done((bf16[2,1,3,24,384]{4,3,2,1,0:T(8,128)(2,1)}, bf16[2,1,3,24,384]{4,3,2,1,0:T(8,128)(2,1)S(1)}, u32[]{:S(2)}, u32[]{:S(2)}) %collective-permute-start.32) | collective-permute-done | bytes 110624 | tf_op jit(solution)/shard_map/ppermute | solution.py:619
  203.9 3.4 %fold.17 = (f32[48,1536]{1,0:T(8,128)}, f32[48,384]{1,0:T(8,128)}, f32[48,384]{1,0:T(8,128)}, f32[48,384]{1,0:T(8,128)}, f32[48,384]{1,0:T(8,128)}, /*index=5*/f32[2,128]{1,0:T(2,128)}) custom-call(s32[5]{0:T(128)} %stack.23.place_ref, bf16[2,2,4,2,24,1920]{5,4,3,2,1,0:T(8,128)(2,1)} %bitcast.125, bf16[2,2,4,2,24,1920]{5,4,3,2,1,0:T(8,128)(2,1)} %bitcast.134, ...), custom_call_target="tpu_custom_call" | custom-call | flops 1024 | bytes 1024 | tf_op jit(solution)/shard_map/fold/pallas_call | solution.py:766
  (139 shorter events, 48.4 us)
Async XLA Ops:
  0.7 14.5 %collective-permute-start = (bf16[256,768]{1,0:T(8,128)(2,1)}, bf16[256,768]{1,0:T(8,128)(2,1)S(1)}, u32[]{:S(2)}, u32[]{:S(2)}) collective-permute-start(bf16[256,768]{1,0:T(8,128)(2,1)} %bitcast.199), channel_id=1, source_target_pairs={{0,1},{1,0},{2,3},{3,2},{4,5},{5,4},{6,7},{7,6},{8,9},{9,8},{10,11... | collective-permute-start | bytes 1179656 | tf_op jit(solution)/shard_map/ppermute | solution.py:623
  3.7 6.9 %collective-permute-start.1 = (f32[1,5,768]{2,1,0:T(8,128)}, f32[1,5,768]{2,1,0:T(8,128)S(1)}, u32[]{:S(2)}, u32[]{:S(2)}) collective-permute-start(f32[1,5,768]{2,1,0:T(8,128)} %bitcast.203), channel_id=1, source_target_pairs={{0,2},{2,0},{4,6},{6,4},{8,10},{10,8},{12,14},{14,12},{16,18},{18,... | collective-permute-start | bytes 46088 | tf_op jit(solution)/shard_map/ppermute | solution.py:619
  15.2 13.9 %collective-permute-start.3 = (f32[4,5,768]{2,1,0:T(8,128)S(1)}, f32[4,5,768]{2,1,0:T(8,128)S(1)}, u32[]{:S(2)}, u32[]{:S(2)}) collective-permute-start(f32[4,5,768]{2,1,0:T(8,128)S(1)} %pad_maximum_fusion.2), channel_id=1, source_target_pairs={{0,8},{2,10},{4,12},{6,14},{8,0},{10,2},{12,4},{14,6},{16,24},{18,... | collective-permute-start | bytes 184328 | tf_op jit(solution)/shard_map/ppermute | solution.py:619
  29.1 16.2 %collective-permute-start.5 = (f32[8,5,768]{2,1,0:T(8,128)S(1)}, f32[8,5,768]{2,1,0:T(8,128)S(1)}, u32[]{:S(2)}, u32[]{:S(2)}) collective-permute-start(f32[8,5,768]{2,1,0:T(8,128)S(1)} %pad_maximum_fusion.1), channel_id=1, source_target_pairs={{0,16},{2,18},{4,20},{6,22},{8,24},{10,26},{12,28},{14,30},{16,0},... | collective-permute-start | bytes 368648 | tf_op jit(solution)/shard_map/ppermute | solution.py:619
  55.7 4.9 %collective-permute-start.6 = (f32[24,768]{1,0:T(8,128)}, f32[24,768]{1,0:T(8,128)S(1)}, u32[]{:S(2)}, u32[]{:S(2)}) collective-permute-start(f32[24,768]{1,0:T(8,128)} %get-tuple-element.217.refs_4_), channel_id=1, source_target_pairs={{0,1},{1,0},{2,3},{3,2},{4,5},{5,4},{6,7},{7,6},{8,9},{9,8},{10,11... | collective-permute-start | bytes 221192 | tf_op jit(solution)/shard_map/ppermute | solution.py:623
  60.6 6.7 %collective-permute-start.7 = (bf16[2,2,8,96,384]{4,3,2,1,0:T(8,128)(2,1)}, bf16[2,2,8,96,384]{4,3,2,1,0:T(8,128)(2,1)S(1)}, u32[]{:S(2)}, u32[]{:S(2)}) collective-permute-start(bf16[2,2,8,96,384]{4,3,2,1,0:T(8,128)(2,1)} %get-tuple-element.220), channel_id=1, source_target_pairs={{0,2},{2,0},{4,6},{6,4},{8,10},{10,8},{12,14},{14,12},{16,18},{18,... | collective-permute-start | bytes 7077896 | tf_op jit(solution)/shard_map/ppermute | solution.py:619
  72.2 15.9 %collective-permute-start.9 = (bf16[8,96,384]{2,1,0:T(8,128)(2,1)}, bf16[8,96,384]{2,1,0:T(8,128)(2,1)S(1)}, u32[]{:S(2)}, u32[]{:S(2)}) collective-permute-start(bf16[8,96,384]{2,1,0:T(8,128)(2,1)} %get-tuple-element.235), channel_id=1, source_target_pairs={{0,1},{1,0},{2,3},{3,2},{4,5},{5,4},{6,7},{7,6},{8,9},{9,8},{10,11... | collective-permute-start | bytes 1769480 | tf_op jit(solution)/shard_map/ppermute | solution.py:623
  73.7 15.6 %collective-permute-start.10 = (bf16[2,4,96,384]{3,2,1,0:T(8,128)(2,1)}, bf16[2,4,96,384]{3,2,1,0:T(8,128)(2,1)S(1)}, u32[]{:S(2)}, u32[]{:S(2)}) collective-permute-start(bf16[2,4,96,384]{3,2,1,0:T(8,128)(2,1)} %get-tuple-element.236), channel_id=1, source_target_pairs={{0,4},{2,6},{4,0},{6,2},{8,12},{10,14},{12,8},{14,10},{16,20},{18,... | collective-permute-start | bytes 1769480 | tf_op jit(solution)/shard_map/ppermute | solution.py:619
  74.9 12.4 %collective-permute-start.8 = (f32[24,768]{1,0:T(8,128)}, f32[24,768]{1,0:T(8,128)S(1)}, u32[]{:S(2)}, u32[]{:S(2)}) collective-permute-start(f32[24,768]{1,0:T(8,128)} %get-tuple-element.234.refs_6_), channel_id=1, source_target_pairs={{0,2},{2,0},{4,6},{6,4},{8,10},{10,8},{12,14},{14,12},{16,18},{18,... | collective-permute-start | bytes 221192 | tf_op jit(solution)/shard_map/ppermute | solution.py:619
  90.1 15.9 %collective-permute-start.11 = (bf16[2,2,8,24,1920]{4,3,2,1,0:T(8,128)(2,1)}, bf16[2,2,8,24,1920]{4,3,2,1,0:T(8,128)(2,1)S(1)}, u32[]{:S(2)}, u32[]{:S(2)}) collective-permute-start(bf16[2,2,8,24,1920]{4,3,2,1,0:T(8,128)(2,1)} %get-tuple-element.249), channel_id=1, source_target_pairs={{0,2},{2,0},{4,6},{6,4},{8,10},{10,8},{12,14},{14,12},{16,18},{18,... | collective-permute-start | bytes 8847368 | tf_op jit(solution)/shard_map/ppermute | solution.py:619
  93.2 12.8 %collective-permute-start.13 = (bf16[4,96,384]{2,1,0:T(8,128)(2,1)}, bf16[4,96,384]{2,1,0:T(8,128)(2,1)S(1)}, u32[]{:S(2)}, u32[]{:S(2)}) collective-permute-start(bf16[4,96,384]{2,1,0:T(8,128)(2,1)} %get-tuple-element.251), channel_id=1, source_target_pairs={{0,4},{2,6},{4,0},{6,2},{8,12},{10,14},{12,8},{14,10},{16,20},{18,... | collective-permute-start | bytes 884744 | tf_op jit(solution)/shard_map/ppermute | solution.py:619
  94.4 11.6 %collective-permute-start.14 = (bf16[4,96,384]{2,1,0:T(8,128)(2,1)}, bf16[4,96,384]{2,1,0:T(8,128)(2,1)S(1)}, u32[]{:S(2)}, u32[]{:S(2)}) collective-permute-start(bf16[4,96,384]{2,1,0:T(8,128)(2,1)} %get-tuple-element.252), channel_id=1, source_target_pairs={{0,1},{1,0},{2,3},{3,2},{4,5},{5,4},{6,7},{7,6},{8,9},{9,8},{10,11... | collective-permute-start | bytes 884744 | tf_op jit(solution)/shard_map/ppermute | solution.py:623
  95.0 11.1 %collective-permute-start.12 = (f32[32,768]{1,0:T(8,128)}, f32[32,768]{1,0:T(8,128)}, u32[]{:S(2)}, u32[]{:S(2)}) collective-permute-start(f32[32,768]{1,0:T(8,128)} %get-tuple-element.250.refs_12_), channel_id=1, source_target_pairs={{0,4},{2,6},{4,0},{6,2},{8,12},{10,14},{12,8},{14,10},{16,20},{18,... | collective-permute-start | bytes 294920 | tf_op jit(solution)/shard_map/ppermute | solution.py:619
  116.6 20.0 %collective-permute-start.15 = (bf16[2,2,8,3,24,384]{5,4,3,2,1,0:T(8,128)(2,1)}, bf16[2,2,8,3,24,384]{5,4,3,2,1,0:T(8,128)(2,1)S(1)}, u32[]{:S(2)}, u32[]{:S(2)}) collective-permute-start(bf16[2,2,8,3,24,384]{5,4,3,2,1,0:T(8,128)(2,1)} %get-tuple-element.270), channel_id=1, source_target_pairs={{0,2},{2,0},{4,6},{6,4},{8,10},{10,8},{12,14},{14,12},{16,18},{18,... | collective-permute-start | bytes 5308424 | tf_op jit(solution)/shard_map/ppermute | solution.py:619
  116.6 19.1 %collective-permute-start.16 = (bf16[2,4,24,1920]{3,2,1,0:T(8,128)(2,1)}, bf16[2,4,24,1920]{3,2,1,0:T(8,128)(2,1)S(1)}, u32[]{:S(2)}, u32[]{:S(2)}) collective-permute-start(bf16[2,4,24,1920]{3,2,1,0:T(8,128)(2,1)} %get-tuple-element.271), channel_id=1, source_target_pairs={{0,4},{2,6},{4,0},{6,2},{8,12},{10,14},{12,8},{14,10},{16,20},{18,... | collective-permute-start | bytes 2211848 | tf_op jit(solution)/shard_map/ppermute | solution.py:619
  117.9 18.8 %collective-permute-start.17 = (bf16[8,24,1920]{2,1,0:T(8,128)(2,1)}, bf16[8,24,1920]{2,1,0:T(8,128)(2,1)S(1)}, u32[]{:S(2)}, u32[]{:S(2)}) collective-permute-start(bf16[8,24,1920]{2,1,0:T(8,128)(2,1)} %get-tuple-element.272), channel_id=1, source_target_pairs={{0,1},{1,0},{2,3},{3,2},{4,5},{5,4},{6,7},{7,6},{8,9},{9,8},{10,11... | collective-permute-start | bytes 2211848 | tf_op jit(solution)/shard_map/ppermute | solution.py:623
  119.4 12.3 %collective-permute-start.18 = (bf16[2,2,96,384]{3,2,1,0:T(8,128)(2,1)}, bf16[2,2,96,384]{3,2,1,0:T(8,128)(2,1)S(1)}, u32[]{:S(2)}, u32[]{:S(2)}) collective-permute-start(bf16[2,2,96,384]{3,2,1,0:T(8,128)(2,1)} %get-tuple-element.273), channel_id=1, source_target_pairs={{0,8},{2,10},{4,12},{6,14},{8,0},{10,2},{12,4},{14,6},{16,24},{18,... | collective-permute-start | bytes 884744 | tf_op jit(solution)/shard_map/ppermute | solution.py:619
  120.0 11.6 %collective-permute-start.19 = (f32[48,768]{1,0:T(8,128)}, f32[48,768]{1,0:T(8,128)}, u32[]{:S(2)}, u32[]{:S(2)}) collective-permute-start(f32[48,768]{1,0:T(8,128)} %get-tuple-element.274.refs_10_), channel_id=1, source_target_pairs={{0,8},{2,10},{4,12},{6,14},{8,0},{10,2},{12,4},{14,6},{16,24},{18,... | collective-permute-start | bytes 442376 | tf_op jit(solution)/shard_map/ppermute | solution.py:619
  142.2 20.1 %collective-permute-start.21 = (bf16[2,4,3,24,384]{4,3,2,1,0:T(8,128)(2,1)}, bf16[2,4,3,24,384]{4,3,2,1,0:T(8,128)(2,1)S(1)}, u32[]{:S(2)}, u32[]{:S(2)}) collective-permute-start(bf16[2,4,3,24,384]{4,3,2,1,0:T(8,128)(2,1)} %get-tuple-element.290), channel_id=1, source_target_pairs={{0,4},{2,6},{4,0},{6,2},{8,12},{10,14},{12,8},{14,10},{16,20},{18,... | collective-permute-start | bytes 1327112 | tf_op jit(solution)/shard_map/ppermute | solution.py:619
  143.1 19.3 %collective-permute-start.22 = (bf16[8,3,24,384]{3,2,1,0:T(8,128)(2,1)}, bf16[8,3,24,384]{3,2,1,0:T(8,128)(2,1)S(1)}, u32[]{:S(2)}, u32[]{:S(2)}) collective-permute-start(bf16[8,3,24,384]{3,2,1,0:T(8,128)(2,1)} %get-tuple-element.291), channel_id=1, source_target_pairs={{0,1},{1,0},{2,3},{3,2},{4,5},{5,4},{6,7},{7,6},{8,9},{9,8},{10,11... | collective-permute-start | bytes 1327112 | tf_op jit(solution)/shard_map/ppermute | solution.py:623
  144.6 17.7 %collective-permute-start.23 = (bf16[4,24,1920]{2,1,0:T(8,128)(2,1)}, bf16[4,24,1920]{2,1,0:T(8,128)(2,1)S(1)}, u32[]{:S(2)}, u32[]{:S(2)}) collective-permute-start(bf16[4,24,1920]{2,1,0:T(8,128)(2,1)} %get-tuple-element.292), channel_id=1, source_target_pairs={{0,1},{1,0},{2,3},{3,2},{4,5},{5,4},{6,7},{7,6},{8,9},{9,8},{10,11... | collective-permute-start | bytes 1105928 | tf_op jit(solution)/shard_map/ppermute | solution.py:623
  145.1 17.2 %collective-permute-start.24 = (bf16[4,24,1920]{2,1,0:T(8,128)(2,1)}, bf16[4,24,1920]{2,1,0:T(8,128)(2,1)S(1)}, u32[]{:S(2)}, u32[]{:S(2)}) collective-permute-start(bf16[4,24,1920]{2,1,0:T(8,128)(2,1)} %get-tuple-element.293), channel_id=1, source_target_pairs={{0,4},{2,6},{4,0},{6,2},{8,12},{10,14},{12,8},{14,10},{16,20},{18,... | collective-permute-start | bytes 1105928 | tf_op jit(solution)/shard_map/ppermute | solution.py:619
  146.3 12.4 %collective-permute-start.20 = (f32[80,768]{1,0:T(8,128)}, f32[80,768]{1,0:T(8,128)S(1)}, u32[]{:S(2)}, u32[]{:S(2)}) collective-permute-start(f32[80,768]{1,0:T(8,128)} %get-tuple-element.289.refs_14_), channel_id=1, source_target_pairs={{0,16},{2,18},{4,20},{6,22},{8,24},{10,26},{12,28},{14,30},{16,0},... | collective-permute-start | bytes 737288 | tf_op jit(solution)/shard_map/ppermute | solution.py:619
  167.6 14.1 %collective-permute-start.27 = (bf16[256,768]{1,0:T(8,128)(2,1)S(1)}, bf16[256,768]{1,0:T(8,128)(2,1)S(1)}, u32[]{:S(2)}, u32[]{:S(2)}) collective-permute-start(bf16[256,768]{1,0:T(8,128)(2,1)S(1)} %copy-done.32), channel_id=1, source_target_pairs={{0,1},{1,0},{2,3},{3,2},{4,5},{5,4},{6,7},{7,6},{8,9},{9,8},{10,11... | collective-permute-start | bytes 1179656 | tf_op jit(solution)/shard_map/ppermute | solution.py:623
  169.2 12.5 %collective-permute-start.28 = (bf16[2,2,24,1920]{3,2,1,0:T(8,128)(2,1)}, bf16[2,2,24,1920]{3,2,1,0:T(8,128)(2,1)S(1)}, u32[]{:S(2)}, u32[]{:S(2)}) collective-permute-start(bf16[2,2,24,1920]{3,2,1,0:T(8,128)(2,1)} %get-tuple-element.315), channel_id=1, source_target_pairs={{0,8},{2,10},{4,12},{6,14},{8,0},{10,2},{12,4},{14,6},{16,24},{18,... | collective-permute-start | bytes 1105928 | tf_op jit(solution)/shard_map/ppermute | solution.py:619
  169.8 11.8 %collective-permute-start.25 = (bf16[4,3,24,384]{3,2,1,0:T(8,128)(2,1)}, bf16[4,3,24,384]{3,2,1,0:T(8,128)(2,1)S(1)}, u32[]{:S(2)}, u32[]{:S(2)}) collective-permute-start(bf16[4,3,24,384]{3,2,1,0:T(8,128)(2,1)} %get-tuple-element.312), channel_id=1, source_target_pairs={{0,1},{1,0},{2,3},{3,2},{4,5},{5,4},{6,7},{7,6},{8,9},{9,8},{10,11... | collective-permute-start | bytes 663560 | tf_op jit(solution)/shard_map/ppermute | solution.py:623
  170.3 11.3 %collective-permute-start.26 = (bf16[4,3,24,384]{3,2,1,0:T(8,128)(2,1)}, bf16[4,3,24,384]{3,2,1,0:T(8,128)(2,1)S(1)}, u32[]{:S(2)}, u32[]{:S(2)}) collective-permute-start(bf16[4,3,24,384]{3,2,1,0:T(8,128)(2,1)} %get-tuple-element.313), channel_id=1, source_target_pairs={{0,4},{2,6},{4,0},{6,2},{8,12},{10,14},{12,8},{14,10},{16,20},{18,... | collective-permute-start | bytes 663560 | tf_op jit(solution)/shard_map/ppermute | solution.py:619
  171.5 7.6 %collective-permute-start.29 = (bf16[2,1,96,384]{3,2,1,0:T(8,128)(2,1)S(1)}, bf16[2,1,96,384]{3,2,1,0:T(8,128)(2,1)S(1)}, u32[]{:S(2)}, u32[]{:S(2)}) collective-permute-start(bf16[2,1,96,384]{3,2,1,0:T(8,128)(2,1)S(1)} %copy-done.25), channel_id=1, source_target_pairs={{0,16},{2,18},{4,20},{6,22},{8,24},{10,26},{12,28},{14,30},{16,0},... | collective-permute-start | bytes 442376 | tf_op jit(solution)/shard_map/ppermute | solution.py:619
  185.9 17.3 %collective-permute-start.30 = (bf16[2,1,24,1920]{3,2,1,0:T(8,128)(2,1)}, bf16[2,1,24,1920]{3,2,1,0:T(8,128)(2,1)S(1)}, u32[]{:S(2)}, u32[]{:S(2)}) collective-permute-start(bf16[2,1,24,1920]{3,2,1,0:T(8,128)(2,1)} %get-tuple-element.329), channel_id=1, source_target_pairs={{0,16},{2,18},{4,20},{6,22},{8,24},{10,26},{12,28},{14,30},{16,0},... | collective-permute-start | bytes 552968 | tf_op jit(solution)/shard_map/ppermute | solution.py:619
  186.8 10.2 %collective-permute-start.31 = (bf16[2,1,3,24,384]{4,3,2,1,0:T(8,128)(2,1)}, bf16[2,1,3,24,384]{4,3,2,1,0:T(8,128)(2,1)S(1)}, u32[]{:S(2)}, u32[]{:S(2)}) collective-permute-start(bf16[2,1,3,24,384]{4,3,2,1,0:T(8,128)(2,1)} %get-tuple-element.330), channel_id=1, source_target_pairs={{0,8},{2,10},{4,12},{6,14},{8,0},{10,2},{12,4},{14,6},{16,24},{18,... | collective-permute-start | bytes 331784 | tf_op jit(solution)/shard_map/ppermute | solution.py:619
  186.9 16.3 %collective-permute-start.32 = (bf16[2,1,3,24,384]{4,3,2,1,0:T(8,128)(2,1)}, bf16[2,1,3,24,384]{4,3,2,1,0:T(8,128)(2,1)S(1)}, u32[]{:S(2)}, u32[]{:S(2)}) collective-permute-start(bf16[2,1,3,24,384]{4,3,2,1,0:T(8,128)(2,1)} %get-tuple-element.331), channel_id=1, source_target_pairs={{0,16},{2,18},{4,20},{6,22},{8,24},{10,26},{12,28},{14,30},{16,0},... | collective-permute-start | bytes 331784 | tf_op jit(solution)/shard_map/ppermute | solution.py:619
  189.5 13.7 %collective-permute-start.33 = (bf16[2,1,3,24,384]{4,3,2,1,0:T(8,128)(2,1)}, bf16[2,1,3,24,384]{4,3,2,1,0:T(8,128)(2,1)S(1)}, u32[]{:S(2)}, u32[]{:S(2)}) collective-permute-start(bf16[2,1,3,24,384]{4,3,2,1,0:T(8,128)(2,1)} %get-tuple-element.332), channel_id=1, source_target_pairs={{0,24},{2,26},{4,28},{6,30},{8,16},{10,18},{12,20},{14,22},{16,8},... | collective-permute-start | bytes 331784 | tf_op jit(solution)/shard_map/ppermute | solution.py:619
  (36 other events, 120.2 us)

commit v6 on v5

--- a/solution.py
+++ b/solution.py
@@ -72,7 +72,7 @@
 
 
 def front_kernel(count, *refs):
-    tokens_ref, vectors_ref = refs[:2]
+    tokens_ref, gain_ref = refs[:2]
     weight_refs = refs[2 : 2 + count]
     low_ref, unit_ref, inv_ref = refs[2 + count : 5 + count]
 
@@ -81,7 +81,7 @@
         unit, inv = norm_rows(tokens_ref[...].astype(f32))
         unit_ref[...] = unit
         inv_ref[...] = inv
-        low_ref[...] = (unit * vectors_ref[FIRST : FIRST + 1]).astype(bf16)
+        low_ref[...] = (unit * gain_ref[...].reshape(1, gain_ref.shape[0])).astype(bf16)
 
     low = low_ref[...]
     for weight_ref, out_ref in zip(weight_refs, refs[5 + count :]):
@@ -102,7 +102,7 @@
     )(*vectors)
 
 
-def front_call(tokens, vectors, *weights):
+def front_call(tokens, gain, *weights):
     rows, width = tokens.shape
     chunk = width // 3
     whole = lambda *shape: pl.BlockSpec(shape, lambda c: (0,) * len(shape))
@@ -110,7 +110,7 @@
     return pl.pallas_call(
         functools.partial(front_kernel, count),
         grid=(3,),
-        in_specs=[whole(rows, width), whole(*vectors.shape)]
+        in_specs=[whole(rows, width), whole(width)]
         + [pl.BlockSpec((width, chunk), lambda c: (0, c))] * count,
         out_specs=[whole(rows, width), whole(rows, width), whole(rows, 1)]
         + [pl.BlockSpec((rows, chunk), lambda c: (0, c))] * count,
@@ -122,31 +122,12 @@
         + [jax.ShapeDtypeStruct((rows, width), bf16)] * count,
         cost_estimate=light,
         name="front",
-    )(tokens, vectors, *weights)
-
-
-def probe_kernel(vectors_ref, query_ref, key_ref, row_ref, key_probe_ref):
-    row = wide_row(nn, vectors_ref[PROBE : PROBE + 1], query_ref[...])
-    row_ref[...] = row
-    key_probe_ref[...] = wide(nt, row * head_rows(row.shape[1]), key_ref[...])
-
-
-def probe_call(vectors, pool_query, pool_key):
-    width = vectors.shape[1]
-    return pl.pallas_call(
-        probe_kernel,
-        out_shape=[
-            jax.ShapeDtypeStruct((1, width), f32),
-            jax.ShapeDtypeStruct((TOP, width), f32),
-        ],
-        cost_estimate=light,
-        name="probe_rows",
-    )(vectors, pool_query, pool_key)
+    )(tokens, gain, *weights)
 
 
 def middle_kernel(
-    attended_ref, tokens_ref, vectors_ref, wo_ref, up_ref, down_ref, key_probe_ref,
-    low_two_ref, unit_two_ref, inv_two_ref, upward_ref, hidden_ref, block_ref,
+    attended_ref, tokens_ref, vectors_ref, wo_ref, up_ref, down_ref, query_ref, key_ref,
+    row_ref, key_probe_ref, low_two_ref, unit_two_ref, inv_two_ref, upward_ref, hidden_ref, block_ref,
     low_ref, unit_ref, inv_ref, exp_ref, packed_ref, acc_ref,
 ):
     c = pl.program_id(0)
@@ -159,6 +140,12 @@
         unit_two_ref[...] = unit
         inv_two_ref[...] = inv
         low_two_ref[...] = (unit * vectors_ref[SECOND : SECOND + 1]).astype(bf16)
+
+    @pl.when(c == 1)
+    def _():
+        row = wide_row(nn, vectors_ref[PROBE : PROBE + 1], query_ref[...])
+        row_ref[...] = row
+        key_probe_ref[...] = wide(nt, row * head_rows(row.shape[1]), key_ref[...])
 
     upward = nn(low_two_ref[...], up_ref[...])
     upward_ref[...] = upward
@@ -186,7 +173,7 @@
         packed_ref[:, width:] = jnp.where(lane == 0, top, jnp.where(lane == 1, total, 0.0))
 
 
-def middle_call(attended, tokens, vectors, w_output, w_up, w_down, key_probe):
+def middle_call(attended, tokens, vectors, w_output, w_up, w_down, pool_query, pool_key):
     rows, width = tokens.shape
     depth = w_up.shape[1]
     steps = 4
@@ -194,6 +181,8 @@
     whole = lambda *shape: pl.BlockSpec(shape, lambda c: (0,) * len(shape))
     cut = pl.BlockSpec((rows, chunk), lambda c: (0, c))
     outs = [
+        (whole(1, width), (1, width), f32),
+        (whole(TOP, width), (TOP, width), f32),
         (whole(rows, width), (rows, width), bf16),
         (whole(rows, width), (rows, width), f32),
         (whole(rows, 1), (rows, 1), f32),
@@ -216,14 +205,15 @@
             whole(width, width),
             pl.BlockSpec((width, chunk), lambda c: (0, c)),
             pl.BlockSpec((chunk, width), lambda c: (c, 0)),
-            whole(TOP, width),
+            whole(width, width),
+            whole(width, width),
         ],
         out_specs=[spec for spec, _, _ in outs],
         out_shape=[jax.ShapeDtypeStruct(shape, dtype) for _, shape, dtype in outs],
         scratch_shapes=[pltpu.VMEM((rows, width), f32)],
         cost_estimate=light,
         name="middle",
-    )(attended, tokens, vectors, w_output, w_up, w_down, key_probe)
+    )(attended, tokens, vectors, w_output, w_up, w_down, pool_query, pool_key)
 
 
 def pool_back_kernel(
@@ -380,7 +370,7 @@
 def pool_weights_kernel(
     images, place_ref, rows_ref, vectors_ref, probe_query_ref, query_ref, key_ref, *out_refs
 ):
-    query_out, key_out, value_out, output_out, probe_out, final_out = out_refs
+    query_out, key_out, value_out, output_out, small_out = out_refs
     width = rows_ref.shape[1]
     block = width // images
     half = width // 2
@@ -399,8 +389,13 @@
     probe_query_grad = jnp.sum(wide(nn, rows_ref[:TOP], key_ref[...]) * heads, axis=0, keepdims=True)
     own_probe = jnp.sum(pick * vectors_ref[PROBE : PROBE + 1], axis=1, keepdims=True)
     query_out[...] = own_probe * mine(probe_query_grad)
-    probe_out[...] = jnp.sum(query_ref[...].astype(f32) * probe_query_grad, axis=1, keepdims=True)
-    final_out[...] = rows[:, HEADS : HEADS + 1]
+    eye = lax.broadcasted_iota(jnp.int32, (block, 128), 1) == (
+        lax.broadcasted_iota(jnp.int32, (block, 128), 0)
+    )
+    probe_grad = jnp.sum(query_ref[...].astype(f32) * probe_query_grad, axis=1, keepdims=True)
+    for at_row, column in enumerate((probe_grad, rows[:, HEADS : HEADS + 1])):
+        small_out[at_row : at_row + 1] = jnp.sum(jnp.where(eye, column, 0.0), axis=0, keepdims=True)
+    small_out[2:3] = rows_ref[HEADS + 1 : HEADS + 2, :128]
     key_out[...] = exact(((1,), (0,)), rows[:, :TOP], mine(probe_query_ref[...] * heads))
     row = lax.broadcasted_iota(jnp.int32, (8, half), 0)
     lane = lax.broadcasted_iota(jnp.int32, (8, half), 1)
@@ -420,7 +415,7 @@
     width = rows.shape[1]
     block = width // images
     whole = lambda *shape: pl.BlockSpec(shape, lambda i, p: (0,) * len(shape))
-    grads = [(block, width // 2)] * 4 + [(block, 1)] * 2
+    grads = [(block, width // 2)] * 4 + [(3, 128)]
     return pl.pallas_call(
         functools.partial(pool_weights_kernel, images),
         grid_spec=pltpu.PrefetchScalarGridSpec(
@@ -569,13 +564,14 @@
     )(place, left, right)
 
 
-def wgrad_three_kernel(
-    block, place_ref, na_ref, nb_ref, dq_ref, dk_ref, dv_ref, send_ref, keep_ref
+def wgrad_four_kernel(
+    block, place_ref, na_ref, nb_ref, a_ref, dq_ref, dk_ref, dv_ref, dx_ref, send_ref, keep_ref
 ):
     na = na_ref[...]
     both = jnp.concatenate([na, nb_ref[...]], axis=0)
     low = block // 2
-    for m, (left, right_ref) in enumerate(((na, dq_ref), (both, dk_ref), (both, dv_ref))):
+    pairs = ((na, dq_ref), (both, dk_ref), (both, dv_ref), (a_ref[...], dx_ref))
+    for m, (left, right_ref) in enumerate(pairs):
         grad = tn(left, right_ref[...])
         columns = grad.shape[1] // 2
         for j in range(grad.shape[0] // (2 * block)):
@@ -586,13 +582,13 @@
                         ref[g, y, j, m] = mine[g * low : (g + 1) * low].astype(bf16)
 
 
-def wgrad_three(place, na, nb, dq, dk, dv, images):
+def wgrad_four(place, na, nb, a, dq, dk, dv, dx, images):
     rows, depth = na.shape
     columns = dq.shape[1]
     block = depth // images
     chunk = depth // 2
     pairs = chunk // (2 * block)
-    cut = (3, block // 2, columns // 2)
+    cut = (4, block // 2, columns // 2)
     left = pl.BlockSpec((rows, chunk), lambda i: (0, i))
     right = pl.BlockSpec((rows, columns), lambda i: (0, 0))
     right_all = pl.BlockSpec((2 * rows, columns), lambda i: (0, 0))
@@ -600,14 +596,14 @@
     out_shape = jax.ShapeDtypeStruct((2, 2, images // 2, *cut), bf16)
     smem = pl.BlockSpec(memory_space=pltpu.SMEM)
     return pl.pallas_call(
-        functools.partial(wgrad_three_kernel, block),
+        functools.partial(wgrad_four_kernel, block),
         grid=(2,),
-        in_specs=[smem, left, left, right, right_all, right_all],
+        in_specs=[smem, left, left, left, right, right_all, right_all, right],
         out_specs=[out_spec, out_spec],
         out_shape=[out_shape, out_shape],
         cost_estimate=light,
-        name="wgrad_three",
-    )(place, na, nb, dq, dk, dv)
+        name="wgrad_four",
+    )(place, na, nb, a, dq, dk, dv, dx)
 
 
 def img_bits():
@@ -657,12 +653,13 @@
 
 def fold_kernel(plan, gathers, products, place_ref, *refs):
     count = sum(sum(slots) for slots, _ in plan)
-    count += 2 * len(gathers) + (1 + len(products) if products else 0)
+    count += sum(1 + others for others, _ in gathers)
+    if products:
+        count += 1 + len(products) + sum(output is None for _, output in products)
     inputs = iter(refs[:count])
     outs = iter(refs[count:])
     for slots, join in plan:
         out = next(outs)
-        extra = next(outs) if join == "wide" else None
         start = 0
         for slot, parts in enumerate(slots):
             total = next(inputs)[...].astype(f32)
@@ -683,18 +680,19 @@
                     out[start : start + size] = total
                 start += size
             else:
-                size, half = total.shape[0], extra.shape[1]
-                chunk = (total.shape[1] - half) // 2
-                for piece in range(2):
-                    out[piece * size : (piece + 1) * size, slot * chunk : (slot + 1) * chunk] = (
-                        total[:, piece * chunk : (piece + 1) * chunk]
-                    )
-                extra[slot * size : (slot + 1) * size] = total[:, 2 * chunk :]
-    for gather in gathers:
-        own, other, out = next(inputs), next(inputs), next(outs)
+                size = total.shape[1]
+                out[:, start : start + size] = total
+                start += size
+    for others, gather in gathers:
+        own = next(inputs)
+        rest = [next(inputs) for _ in range(others)]
+        other, out = rest[0], next(outs)
         rows = own.shape[0]
         sums = min(TOP, rows)
-        out[:sums] = own[:sums] + other[:sums]
+        total = own[:sums]
+        for more in rest:
+            total = total + more[:sums]
+        out[:sums] = total
         if rows > sums:
             out[sums:rows] = own[sums:]
         if gather:
@@ -702,7 +700,7 @@
     if products:
         outs = refs[count:]
         sums = refs[-1]
-        rows = outs[products[0][1]].shape[0]
+        rows = outs[products[-1][1]].shape[0]
         vectors = next(inputs)[...]
         pick = lax.broadcasted_iota(jnp.int32, (rows, vectors.shape[1]), 1) == (
             lax.broadcasted_iota(jnp.int32, (rows, vectors.shape[1]), 0) + place_ref[0] * rows
@@ -713,7 +711,8 @@
         columns = {}
         for row, output in products:
             weight = next(inputs)[...].astype(f32)
-            part = jnp.sum(weight * outs[output][...], axis=1, keepdims=True)
+            grad = next(inputs)[...] if output is None else outs[output][...]
+            part = jnp.sum(weight * grad, axis=1, keepdims=True)
             columns[row] = columns[row] + part if row in columns else part
         for row, column in columns.items():
             gain = jnp.sum(jnp.where(pick, vectors[row : row + 1], 0.0), axis=1, keepdims=True)
@@ -742,25 +741,28 @@
             shape = (len(slots), *shape)
         elif join == "rows":
             shape = (*shape[:-2], len(slots) * shape[-2], shape[-1])
-        elif join == "wide":
-            size, total = shape
-            shapes.append(((2 * size, 2 * ((total - total // 5) // 2)), dtype))
-            shape = (2 * size, total // 5)
+        elif join == "columns":
+            shape = (shape[0], len(slots) * shape[1])
         shapes.append((shape, dtype))
     whole = lambda t: pl.BlockSpec(t, lambda i, p: (0,) * len(t))
-    for own, other, gather in notes:
+    for own, others, gather in notes:
         rows, width = own.shape
-        arrays += [own, other]
-        specs += [whole(own.shape)] * 2
-        gathers.append(gather)
+        arrays += [own, *others]
+        specs += [whole(own.shape)] * (1 + len(others))
+        gathers.append((len(others), gather))
         shapes.append(((2 * rows - TOP if gather else rows, width), f32))
     if products:
         arrays.append(vectors)
         specs.append(whole(vectors.shape))
-    for _, output, weight in products:
-        rows, width = shapes[output][0]
+    for n, (row, output, weight) in enumerate(products):
+        given = not isinstance(output, int)
+        rows, width = output.shape if given else shapes[output][0]
         arrays.append(weight.reshape(-1, rows, weight.shape[1]))
         specs.append(pl.BlockSpec((None, rows, width), lambda i, p: (p[0], 0, p[1])))
+        if given:
+            arrays.append(output)
+            specs.append(whole(output.shape))
+            products[n] = (row, None, weight)
     if products:
         shapes.append(((2, 128), f32))
     return pl.pallas_call(
@@ -859,7 +861,9 @@
         take(first, second, [img_swap(send, 1 << bit)], bit - 1)
 
 
-def gelu_back_kernel(grad_ref, down_ref, up_ref, out_ref):
+def gelu_back_kernel(
+    block, place_ref, grad_ref, down_ref, up_ref, low_ref, out_ref, send_ref, keep_ref
+):
     hidden_grad = nt(grad_ref[...], down_ref[...])
     u = up_ref[...]
     factor = math.sqrt(2.0 / math.pi)
@@ -868,26 +872,39 @@
     slope = 0.5 * (1.0 + t) + 0.5 * u * (1.0 - t * t) * (
         factor * (1.0 + (3.0 * 0.044715) * square)
     )
-    out_ref[...] = (hidden_grad * slope).astype(bf16)
-
-
-def gelu_back_call(grad, w_down, upward):
+    du = (hidden_grad * slope).astype(bf16)
+    out_ref[...] = du
+    grad = tn(low_ref[...], du)
+    for j in range(grad.shape[0] // (2 * block)):
+        send, keep = halves(place_ref[2], grad, block, j)
+        send_ref[0, 0, j] = send.astype(bf16)
+        keep_ref[0, 0, j] = keep.astype(bf16)
+
+
+def gelu_back_call(place, grad, w_down, upward, low, images):
     rows, width = grad.shape
     depth = upward.shape[1]
     chunk = depth // 4
+    block = width // images
+    half_spec = pl.BlockSpec(
+        (1, 1, images // 2, block, chunk), lambda c: (c % 2, c // 2, 0, 0, 0)
+    )
+    half_shape = jax.ShapeDtypeStruct((2, 2, images // 2, block, chunk), bf16)
     return pl.pallas_call(
-        gelu_back_kernel,
+        functools.partial(gelu_back_kernel, block),
         grid=(4,),
         in_specs=[
+            pl.BlockSpec(memory_space=pltpu.SMEM),
             pl.BlockSpec((rows, width), lambda c: (0, 0)),
             pl.BlockSpec((chunk, width), lambda c: (c, 0)),
             pl.BlockSpec((rows, chunk), lambda c: (0, c)),
+            pl.BlockSpec((rows, width), lambda c: (0, 0)),
         ],
-        out_specs=pl.BlockSpec((rows, chunk), lambda c: (0, c)),
-        out_shape=jax.ShapeDtypeStruct((rows, depth), bf16),
+        out_specs=[pl.BlockSpec((rows, chunk), lambda c: (0, c)), half_spec, half_spec],
+        out_shape=[jax.ShapeDtypeStruct((rows, depth), bf16), half_shape, half_shape],
         cost_estimate=light,
         name="gelu_back",
-    )(grad, w_down, upward)
+    )(place, grad, w_down, upward, low)
 
 
 def norm_back_rows(grad, unit, inv, gain):
@@ -898,107 +915,59 @@
 
 
 def up_back_kernel(
-    block, place_ref, low_ref, du_ref, up_ref, unit_ref, inv_ref, vectors_ref, above_ref, wo_ref,
-    a_ref, send_ref, keep_ref, grad_ref, heads_ref, acc_ref, out_ref,
+    du_ref, up_ref, unit_ref, inv_ref, vectors_ref, above_ref, wo_ref,
+    grad_ref, branch_ref, heads_ref, acc_ref,
 ):
     c = pl.program_id(0)
-    steps = pl.num_programs(0) // 2
-    du = du_ref[...]
-    chunk = du.shape[1]
-    half = out_ref.shape[2]
-    size = block // 2
-
-    @pl.when(c < steps)
+    back = nt(du_ref[...], up_ref[...])
+
+    @pl.when(c == 0)
     def _():
-        back = nt(du, up_ref[...])
-
-        @pl.when(c == 0)
-        def _():
-            acc_ref[...] = back
-
-        @pl.when(c > 0)
-        def _():
-            acc_ref[...] += back
-
-    @pl.when(c == steps - 1)
+        acc_ref[...] = back
+
+    @pl.when(c > 0)
+    def _():
+        acc_ref[...] += back
+
+    @pl.when(c == pl.num_programs(0) - 1)
     def _():
         total = above_ref[...] + norm_back_rows(
             acc_ref[...], unit_ref[...], inv_ref[...], vectors_ref[SECOND : SECOND + 1]
         )
         grad_ref[...] = total
         branch = total.astype(bf16)
+        branch_ref[...] = branch
         heads_ref[...] = nt(branch, wo_ref[...]).astype(bf16)
-        out_grad = tn(a_ref[...], branch)
-        for y in range(2):
-            out_ref[y] = out_grad[:, y * half : (y + 1) * half]
-
-    @pl.when(c >= steps)
-    def _():
-        grad = tn(low_ref[...], du)
-        out_grad = out_ref[(c - steps) // 2]
-        first = (c - steps) % 2 == 0
-        for j in range(grad.shape[0] // (2 * block)):
-            for ref, part, more in zip(
-                (send_ref, keep_ref),
-                halves(place_ref[2], grad, block, j),
-                halves(place_ref[2], out_grad, block, j),
-            ):
-                for piece in range(2):
-                    ref[0, 0, j, :, piece * chunk : (piece + 1) * chunk] = part[
-                        piece * size : (piece + 1) * size
-                    ].astype(bf16)
-                ref[0, 0, j, :, 2 * chunk :] = jnp.where(first, more[:size], more[size:]).astype(bf16)
-
-
-def up_back_call(place, low, du, w_up, unit, inv, vectors, above, w_output, attended, images):
-    rows, width = low.shape
-    depth = du.shape[1]
+
+
+def up_back_call(du, w_up, unit, inv, vectors, above, w_output):
+    rows, depth = du.shape
+    width = w_up.shape[0]
     steps = 4
     chunk = depth // steps
-    block = width // images
-    wide = 2 * chunk + width // 2
     whole = lambda *shape: pl.BlockSpec(shape, lambda c: (0,) * len(shape))
-
-    def half_index(c):
-        k = jnp.maximum(c - steps, 0)
-        return (k % 2, k // 2, 0, 0, 0)
-
-    half_spec = pl.BlockSpec((1, 1, images // 2, block // 2, wide), half_index)
-    half_shape = jax.ShapeDtypeStruct((2, 2, images // 2, block // 2, wide), bf16)
     return pl.pallas_call(
-        functools.partial(up_back_kernel, block),
-        grid=(2 * steps,),
+        up_back_kernel,
+        grid=(steps,),
         in_specs=[
-            pl.BlockSpec(memory_space=pltpu.SMEM),
-            whole(rows, width),
-            pl.BlockSpec((rows, chunk), lambda c: (0, c % steps)),
-            pl.BlockSpec((width, chunk), lambda c: (0, jnp.minimum(c, steps - 1))),
+            pl.BlockSpec((rows, chunk), lambda c: (0, c)),
+            pl.BlockSpec((width, chunk), lambda c: (0, c)),
             whole(rows, width),
             whole(rows, 1),
             whole(*vectors.shape),
             whole(rows, width),
             whole(width, width),
-            whole(rows, width),
         ],
-        out_specs=[
-            half_spec,
-            half_spec,
-            whole(rows, width),
-            whole(rows, width),
-        ],
+        out_specs=[whole(rows, width)] * 3,
         out_shape=[
-            half_shape,
-            half_shape,
             jax.ShapeDtypeStruct((rows, width), f32),
             jax.ShapeDtypeStruct((rows, width), bf16),
+            jax.ShapeDtypeStruct((rows, width), bf16),
         ],
-        scratch_shapes=[
-            pltpu.VMEM((rows, width), f32),
-            pltpu.VMEM((2, width, width // 2), f32),
-        ],
+        scratch_shapes=[pltpu.VMEM((rows, width), f32)],
         cost_estimate=light,
         name="up_back",
-    )(place, low, du, w_up, unit, inv, vectors, above, w_output, attended)
+    )(du, w_up, unit, inv, vectors, above, w_output)
 
 
 def parts_in_kernel(dq_ref, dk_ref, dv_ref, wq_ref, wk_ref, wv_ref, own_ref, other_ref):
@@ -1080,9 +1049,6 @@
     place = jnp.stack([me, seq_me, me & 1, (me >> 1) & 1, me >> 2]).astype(jnp.int32)
 
     other_tokens = seq_swap(own_tokens)
-    vectors = vectors_call(first_gain, second_gain, final_gain, probe)
-    place, vectors = tie(place, vectors)
-
     gathered = captions[None]
 
     def gather_more(gathered, bit):
@@ -1091,24 +1057,28 @@
     gathered = gather_more(gathered, 0)
 
     low_own, unit_one, scale_one, queries, keys_own, values_own = front_call(
-        own_tokens, vectors, w_query, w_key, w_value
-    )
-    low_own, gathered, vectors = tie(low_own, gathered, vectors)
+        own_tokens, first_gain, w_query, w_key, w_value
+    )
+    low_own, gathered, place, first, second, final, own_probe = tie(
+        low_own, gathered, place, first_gain, second_gain, final_gain, probe
+    )
     gathered = gather_more(gathered, 1)
-    probe_query, key_probe = probe_call(vectors, pool_query, pool_key)
-
-    other_tokens, gathered, key_probe = tie(other_tokens, gathered, key_probe)
+    vectors = vectors_call(first, second, final, own_probe)
+
+    other_tokens, gathered, vectors, place = tie(other_tokens, gathered, vectors, place)
     gathered = gather_more(gathered, 2)
-    low_other, _, _, keys_other, values_other = front_call(other_tokens, vectors, w_key, w_value)
+    low_other, _, _, keys_other, values_other = front_call(other_tokens, first, w_key, w_value)
     attended_low, log_totals = attend(queries, keys_own, keys_other, values_own, values_other)
     attended_low, gathered = tie(attended_low, gathered)
     for bit in range(3, bits):
         gathered = gather_more(gathered, bit)
 
     (
-        second_low, unit_two, scale_two, upward, hidden_low, block_out,
+        probe_query, key_probe, second_low, unit_two, scale_two, upward, hidden_low, block_out,
         pool_low, unit_pool, inv_pool, exps, packed,
-    ) = middle_call(attended_low, own_tokens, vectors, w_output, w_up, w_down, key_probe)
+    ) = middle_call(
+        attended_low, own_tokens, vectors, w_output, w_up, w_down, pool_query, pool_key
+    )
     block_out = block_out[None]
     other_packed = seq_swap(packed)
     other_packed, gathered = tie(other_packed, gathered)
@@ -1125,8 +1095,13 @@
         down_send, down_keep, branch_grad, message_in
     )
     down_core = img_swap(down_send, 1)
-    up_grad_low = gelu_back_call(branch_grad, w_down, upward)
-    up_grad_low, down_core = step(up_grad_low, down_core)
+    messages = [img_swap(message, 1), message_in, img_swap(message_in, 1)]
+    up_grad_low, up_send, up_keep = gelu_back_call(
+        place, branch_grad, w_down, upward, second_low, images
+    )
+    up_grad_low, up_send, up_keep, down_core, *messages = step(
+        up_grad_low, up_send, up_keep, down_core, *messages
+    )
     down_a = Staged(0, True, down_keep, down_core)
     down_b = Staged(1, False, down_keep, down_core)
 
@@ -1137,138 +1112,143 @@
         return [([first.stage_two()], None), ([second.stage_two()], None)]
 
     send_a, send_b, message = fold(
-        place, first_stage(down_a, down_b), bf16, [(message, message_in, False)]
-    )
-    up_grad_low, send_a, send_b, message = step(up_grad_low, send_a, send_b, message)
+        place, first_stage(down_a, down_b), bf16, [(message, messages, True)]
+    )
+    up_grad_low, up_send, send_a, send_b, message = step(
+        up_grad_low, up_send, send_a, send_b, message
+    )
+
+    up_core = img_swap(up_send, 1)
     down_a.first = seq_swap(send_a)
     down_b.first = img_swap(send_b, 2)
-    message_in = img_swap(message, 1)
-    up_send, up_keep, residual_grad, attended_grad = up_back_call(
-        place, second_low, up_grad_low, w_up, unit_two, scale_two, vectors, result_grad,
-        w_output, attended_low, images,
-    )
-    attended_grad, up_send, message_in, down_a.first, down_b.first = step(
-        attended_grad, up_send, message_in, down_a.first, down_b.first
-    )
-    up_core = img_swap(up_send, 1)
-    send_a, send_b, message = fold(
-        place, second_stage(down_a, down_b), bf16, [(message, message_in, True)]
-    )
-    attended_grad, send_a, send_b, message = step(attended_grad, send_a, send_b, message)
-    down_a.second = img_swap(send_a, 2)
-    down_b.second = seq_swap(send_b)
-    message_in = img_swap(message, 2)
-
+    message_in = img_swap(message, 8)
+    residual_grad, attn_branch, attended_grad = up_back_call(
+        up_grad_low, w_up, unit_two, scale_two, vectors, result_grad, w_output
+    )
+    attended_grad, up_core, message_in, down_a.first, down_b.first = step(
+        attended_grad, up_core, message_in, down_a.first, down_b.first
+    )
+    up_a = Staged(0, False, up_keep, up_core)
+    up_b = Staged(1, True, up_keep, up_core)
+    send_a, send_b, send_c, send_d, message = fold(
+        place,
+        first_stage(up_a, up_b) + second_stage(down_a, down_b),
+        bf16,
+        [(message, [message_in], True)],
+    )
+    attended_grad, send_a, send_b, send_c, send_d, message = step(
+        attended_grad, send_a, send_b, send_c, send_d, message
+    )
+
+    up_a.first = img_swap(send_a, 2)
+    up_b.first = seq_swap(send_b)
+    message_in = img_swap(message, 4)
     query_grad, key_part, value_part = attend_back(
         queries, keys_own, keys_other, values_own, values_other, attended_grad, log_totals
     )
-    query_grad, key_part, value_part, up_core, message_in, down_a.second, down_b.second = step(
-        query_grad, key_part, value_part, up_core, message_in, down_a.second, down_b.second
-    )
-    up_a = Staged(0, False, up_keep, up_core)
-    up_b = Staged(1, True, up_keep, up_core)
-    three_send, three_keep = wgrad_three(
-        place, low_own, low_other, query_grad, key_part, value_part, images
+    query_grad, key_part, value_part, up_a.first, up_b.first, message_in, send_c, send_d = step(
+        query_grad, key_part, value_part, up_a.first, up_b.first, message_in, send_c, send_d
+    )
+
+    down_a.second = img_swap(send_c, 2)
+    down_b.second = seq_swap(send_d)
+    four_send, four_keep = wgrad_four(
+        place, low_own, low_other, attended_low, query_grad, key_part, value_part, attn_branch, images
+    )
+    four_send, four_keep, query_grad, down_a.second, down_b.second = step(
+        four_send, four_keep, query_grad, down_a.second, down_b.second
     )
     send_a, send_b, down_send, message = fold(
         place,
-        first_stage(up_a, up_b) + far_send(down_a, down_b, 0),
+        second_stage(up_a, up_b) + far_send(down_a, down_b, 0),
         bf16,
-        [(message, message_in, True)],
-    )
-    three_send, three_keep, query_grad, send_a, send_b, down_send, message = step(
-        three_send, three_keep, query_grad, send_a, send_b, down_send, message
-    )
-
-    three_core = img_swap(three_send, 1)
-    up_a.first = img_swap(send_a, 2)
-    up_b.first = seq_swap(send_b)
+        [(message, [message_in], True)],
+    )
+    four_send, query_grad, send_a, send_b, down_send, message = step(
+        four_send, query_grad, send_a, send_b, down_send, message
+    )
+
+    four_core = img_swap(four_send, 1)
+    up_a.second = seq_swap(send_a)
+    up_b.second = img_swap(send_b, 2)
     down_in = img_swap(down_send, 4)
-    message_in = img_swap(message, 4)
     own_part, other_part = parts_in_call(
         query_grad, key_part, value_part, w_query, w_key, w_value
     )
-    own_part, other_part, three_core, up_a.first, up_b.first, down_in, message_in = step(
-        own_part, other_part, three_core, up_a.first, up_b.first, down_in, message_in
+    own_part, other_part, four_core, up_a.second, up_b.second, down_in = step(
+        own_part, other_part, four_core, up_a.second, up_b.second, down_in
     )
     take(down_a, down_b, [down_in], 1)
-    three_a = Staged(0, False, three_keep, three_core)
-    three_b = Staged(1, True, three_keep, three_core)
-    send_a, send_b, send_c, send_d, message = fold(
+    four_a = Staged(0, False, four_keep, four_core)
+    four_b = Staged(1, True, four_keep, four_core)
+    send_a, send_b, up_send, down_send = fold(
         place,
-        first_stage(three_a, three_b) + second_stage(up_a, up_b),
+        first_stage(four_a, four_b) + far_send(up_a, up_b, 0) + far_send(down_a, down_b, 1),
         bf16,
-        [(message, message_in, True)],
-    )
-    send_a, send_b, send_c, send_d, message, other_part = step(
-        send_a, send_b, send_c, send_d, message, other_part
-    )
-
-    three_a.first = img_swap(send_a, 2)
-    three_b.first = seq_swap(send_b)
-    up_a.second = seq_swap(send_c)
-    up_b.second = img_swap(send_d, 2)
-    message_in = img_swap(message, 8)
-    (down_send,) = fold(place, far_send(down_a, down_b, 1), bf16)
-    down_send, message_in, three_a.first, three_b.first, up_a.second, up_b.second = step(
-        down_send, message_in, three_a.first, three_b.first, up_a.second, up_b.second
-    )
-    send_a, send_b, up_send, message = fold(
-        place,
-        second_stage(three_a, three_b) + far_send(up_a, up_b, 0),
-        bf16,
-        [(message, message_in, True)],
-    )
-    other_part, send_a, send_b, up_send, down_send, message = step(
-        other_part, send_a, send_b, up_send, down_send, message
-    )
-
-    three_a.second = seq_swap(send_a)
-    three_b.second = img_swap(send_b, 2)
+    )
+    send_a, send_b, up_send, down_send, message, other_part = step(
+        send_a, send_b, up_send, down_send, message, other_part
+    )
+
+    four_a.first = img_swap(send_a, 2)
+    four_b.first = seq_swap(send_b)
     up_in = img_swap(up_send, 4)
     down_in = img_swap(down_send, 8)
+    four_a.first, four_b.first, up_in, down_in = step(four_a.first, four_b.first, up_in, down_in)
+    take(up_a, up_b, [up_in], 1)
+    take(down_a, down_b, [down_in], 2)
+    send_a, send_b, up_send = fold(
+        place, second_stage(four_a, four_b) + far_send(up_a, up_b, 1), bf16
+    )
+    send_a, send_b, up_send, message, other_part = step(
+        send_a, send_b, up_send, message, other_part
+    )
+
+    four_a.second = seq_swap(send_a)
+    four_b.second = img_swap(send_b, 2)
+    up_in = img_swap(up_send, 8)
+    message_in = img_swap(message, 2)
+    finish(place, down_a, down_b)
+    (down_grad,) = fold(place, [([down_a.whole(), down_b.whole()], "rows")], f32)
+    down_grad, four_a.second, four_b.second, up_in, message_in = step(
+        down_grad, four_a.second, four_b.second, up_in, message_in
+    )
+    take(up_a, up_b, [up_in], 2)
+    *four_sends, message = fold(
+        place, near_sends(four_a, four_b), bf16, [(message, [message_in], True)]
+    )
+    message, other_part, *four_sends = step(message, other_part, *four_sends)
+
+    four_in = near_swap(four_sends)
     arrived_part = seq_swap(other_part)
+    finish(place, up_a, up_b)
+    (up_weight_grad,) = fold(place, [([up_a.whole(), up_b.whole()], "columns")], f32)
     for bit in range(4, bits):
-        (message,) = fold(place, [], f32, [(message, img_swap(message, 1 << bit), True)])
+        (message,) = fold(place, [], f32, [(message, [img_swap(message, 1 << bit)], True)])
     pool_grads = pool_weights_call(
         place, message, vectors, probe_query, pool_query, pool_key, images
     )
-    pool_grads, three_a.second, three_b.second, arrived_part, up_in, down_in = step(
-        pool_grads, three_a.second, three_b.second, arrived_part, up_in, down_in
-    )
-    take(up_a, up_b, [up_in], 1)
-    take(down_a, down_b, [down_in], 2)
-    *three_sends, up_send = fold(
-        place, near_sends(three_a, three_b) + far_send(up_a, up_b, 1), bf16
-    )
-    up_send, *three_sends = step(up_send, *three_sends)
-
-    three_in = near_swap(three_sends)
-    up_in = img_swap(up_send, 8)
-    finish(place, down_a, down_b)
-    (down_grad,) = fold(place, [([down_a.whole(), down_b.whole()], "rows")], f32)
+    up_weight_grad, pool_grads, arrived_part, *four_in = step(
+        up_weight_grad, pool_grads, arrived_part, *four_in
+    )
+    take(four_a, four_b, four_in, 2)
+    finish(place, four_a, four_b)
+    query_weight_grad, key_weight_grad, value_weight_grad, output_grad, gains = fold(
+        place,
+        [([four_a.whole(m), four_b.whole(m)], "rows") for m in range(4)],
+        f32,
+        products=[
+            (SECOND, up_weight_grad, w_up), (FIRST, 0, w_query), (FIRST, 1, w_key), (FIRST, 2, w_value)
+        ],
+        vectors=vectors,
+    )
     input_grad = own_in_call(
         own_part, arrived_part, unit_one, scale_one, vectors, residual_grad
     )
-    input_grad, down_grad, up_in, *three_in = step(input_grad, down_grad, up_in, *three_in)
-    take(up_a, up_b, [up_in], 2)
-    take(three_a, three_b, three_in, 2)
-    finish(place, up_a, up_b)
-    finish(place, three_a, three_b)
-    up_weight_grad, output_grad, query_weight_grad, key_weight_grad, value_weight_grad, gains = fold(
-        place,
-        [([up_a.whole(), up_b.whole()], "wide")]
-        + [([three_a.whole(m), three_b.whole(m)], "rows") for m in range(3)],
-        f32,
-        products=[(SECOND, 0, w_up), (FIRST, 2, w_query), (FIRST, 3, w_key), (FIRST, 4, w_value)],
-        vectors=vectors,
-    )
 
     gains = gains + seq_swap(gains)
     block = width // images
-    query_pool_grad, key_pool_grad, value_pool_grad, out_pool_grad, probe_grad, final_grad = (
-        pool_grads
-    )
+    query_pool_grad, key_pool_grad, value_pool_grad, out_pool_grad, small = pool_grads
     return (
         block_out,
         input_grad[None],
@@ -1280,15 +1260,15 @@
         down_grad,
         gains[FIRST, :block],
         gains[SECOND, :block],
-        final_grad[:, 0],
-        probe_grad[:, 0],
+        small[1, :block],
+        small[0, :block],
         query_pool_grad,
         key_pool_grad,
         value_pool_grad,
         out_pool_grad,
-        message[HEADS + 1, 0],
-        message[HEADS + 1, 1],
-        message[HEADS + 1, 2],
+        small[2, 0],
+        small[2, 1],
+        small[2, 2],
     )
 
 

time: 214 us -> 203 us (0.949)
  waiting for transfers between devices: 40.7 us -> 35.1 us
  Pallas kernels: 122 us -> 117 us
    pallas_call x4 -> x3, Pallas kernels: 28.2 us -> 21.7 us  [the longest x1 8.54 us: gelu_back_call(): pl.pallas_call(functools.partial(gelu_back_kernel, block), grid=(4,), in_...]
    ppermute x24 -> x25, waiting for transfers between devices: 29.1 us -> 23.8 us  [img_swap(): return lax.ppermute(value, 'img', [(i, i ^ mask) for i in range(count)])]
    unnamed x66 -> x74, local copies, waits for them, and re-layouts: 6.4 us -> 7.01 us
    ppermute x24 -> x25, starting transfers between devices: 22.3 us -> 22.3 us  [img_swap(): return lax.ppermute(value, 'img', [(i, i ^ mask) for i in range(count)])]
  transfers between devices with their start and end apart: 35 -> 36, of which waited for: 11 -> 16; matrix products, arithmetic and copies ran while one was open for 2% -> 1% of each run, Pallas kernels for 41% -> 42%
where the time goes in v6:
time: 203 us; the launch traced here: 202 us
  Pallas kernels  117 us (58%)
  starting transfers between devices  36.3 us (18%)
  waiting for transfers between devices  35.1 us (17%)
  local copies, waits for them, and re-layouts  10.7 us (5%)
  between operations  2.94 us (1%)
    pallas_call x9, Pallas kernels, fold(): pl.pallas_call(functools.partial(fold_kernel, tuple(plan), tuple(gathers)...  31.2 us
    ppermute x25, waiting for transfers between devices, img_swap(): return lax.ppermute(value, 'img', [(i, i ^ mask) for i in range(count)])  23.8 us
    ppermute x25, starting transfers between devices, img_swap(): return lax.ppermute(value, 'img', [(i, i ^ mask) for i in range(count)])  22.3 us
    ppermute x11, starting transfers between devices, seq_swap(): return lax.ppermute(value, 'seq', [(0, 1), (1, 0)])  14 us
    pallas_call x1, Pallas kernels, middle_call(): pl.pallas_call(middle_kernel, grid=(steps,), in_specs=[whole(rows, width)...  12.3 us
    ppermute x11, waiting for transfers between devices, seq_swap(): return lax.ppermute(value, 'seq', [(0, 1), (1, 0)])  11.2 us
    pallas_call x1, Pallas kernels, attend_back(): pl.pallas_call(attend_back_kernel, grid=(pairs,), in_specs=[row_spec] * 6...  10.3 us
    pallas_call x2, Pallas kernels, front_call(): pl.pallas_call(functools.partial(front_kernel, count), grid=(3,), in_spec...  9.29 us
  transfers between devices with their start and end apart: 36, of which 16 were waited for; matrix products, arithmetic and copies ran while one was open for 1% of the time, Pallas kernels for 42%

profile of v6, /device:TPU:0, one launch (start us, length us, event | category | flops | bytes accessed | tf_op | source)
XLA Modules:
  0.0 201.7 jit_solution(10977519925443880324)
XLA Ops:
  0.7 3.1 %collective-permute-start = (bf16[256,768]{1,0:T(8,128)(2,1)}, bf16[256,768]{1,0:T(8,128)(2,1)S(1)}, u32[]{:S(2)}, u32[]{:S(2)}) collective-permute-start(bf16[256,768]{1,0:T(8,128)(2,1)} %bitcast.208), channel_id=1, source_target_pairs={{0,1},{1,0},{2,3},{3,2},{4,5},{5,4},{6,7},{7,6},{8,9},{9,8},{10,11... | collective-permute-start | bytes 1179656 | tf_op jit(solution)/shard_map/ppermute | solution.py:619
  3.7 4.9 %front.2 = (bf16[256,768]{1,0:T(8,128)(2,1)}, f32[256,768]{1,0:T(8,128)}, f32[256,1]{1,0:T(8,128)}, bf16[256,768]{1,0:T(8,128)(2,1)}, bf16[256,768]{1,0:T(8,128)(2,1)}, /*index=5*/bf16[256,768]{1,0:T(8,128)(2,1)}) custom-call(bf16[256,768]{1,0:T(8,128)(2,1)} %bitcast.209, f32[768]{0:T(1024)} %refs_1_.2, bf16[768,768]{1,0:T(8,128)(2,1)} %wq_ref.1, ...), custom_call_target="tpu_custom_call" | custom-call | flops 1024 | bytes 1024 | tf_op jit(solution)/shard_map/front/pallas_call | solution.py:110
  13.5 1.6 collective-permute-start.3
  15.2 4.3 %front.3 = (bf16[256,768]{1,0:T(8,128)(2,1)}, f32[256,768]{1,0:T(8,128)}, f32[256,1]{1,0:T(8,128)}, bf16[256,768]{1,0:T(8,128)(2,1)}, bf16[256,768]{1,0:T(8,128)(2,1)}) custom-call(bf16[256,768]{1,0:T(8,128)(2,1)} %copy-done.23, f32[768]{0:T(1024)} %refs_1_.2, bf16[768,768]{1,0:T(8,128)(2,1)} %wk_ref.1, bf16[768,768]{1,0:T(8,128)(2,1)} %wv_ref.1), custom_call_target="tpu_custom_call" | custom-call | flops 1024 | bytes 1024 | tf_op jit(solution)/shard_map/front/pallas_call | solution.py:110
  19.5 7.8 %attend.1 = (bf16[256,768]{1,0:T(8,128)(2,1)}, f32[6,256,2]{2,1,0:T(8,128)}) custom-call(bf16[256,768]{1,0:T(8,128)(2,1)} %get-tuple-element.196.q_ref, bf16[256,768]{1,0:T(8,128)(2,1)} %get-tuple-element.197.ka_ref, bf16[256,768]{1,0:T(8,128)(2,1)} %get-tuple-element.206.kb_ref, bf16[256,768]{1,0:T(8,128)(2,1)} %get-tuple-element.207.va_ref, ...), custom_call_target="tpu_custom_call" | custom-call | flops 1024 | bytes 1024 | tf_op jit(solution)/shard_map/attend/pallas_call | solution.py:462
  27.4 2.7 %collective-permute-start.5 = (f32[8,5,768]{2,1,0:T(8,128)S(1)}, f32[8,5,768]{2,1,0:T(8,128)S(1)}, u32[]{:S(2)}, u32[]{:S(2)}) collective-permute-start(f32[8,5,768]{2,1,0:T(8,128)S(1)} %pad_maximum_fusion.1), channel_id=1, source_target_pairs={{0,16},{2,18},{4,20},{6,22},{8,24},{10,26},{12,28},{14,30},{16,0},... | collective-permute-start | bytes 368648 | tf_op jit(solution)/shard_map/ppermute | solution.py:615
  32.0 12.3 %middle.1 = (f32[1,768]{1,0:T(1,128)}, f32[16,768]{1,0:T(8,128)}, bf16[256,768]{1,0:T(8,128)(2,1)}, f32[256,768]{1,0:T(8,128)}, f32[256,1]{1,0:T(8,128)}, /*inde...) custom-call(bf16[256,768]{1,0:T(8,128)(2,1)} %get-tuple-element.211., ...), custom_call_target="tpu_custom_call" | custom-call | flops 1024 | bytes 1024 | tf_op jit(solution)/shard_map/middle/pallas_call | solution.py:198
  45.6 3.2 %collective-permute-done.4.other_ref = f32[16,896]{1,0:T(8,128)S(1)} collective-permute-done((f32[16,896]{1,0:T(8,128)}, f32[16,896]{1,0:T(8,128)S(1)}, u32[]{:S(2)}, u32[]{:S(2)}) %collective-permute-start.4) | collective-permute-done | bytes 57376 | tf_op jit(solution)/shard_map/ppermute | solution.py:619
  49.5 5.7 %pool_back.1 = (f32[256,768]{1,0:T(8,128)}, bf16[256,768]{1,0:T(8,128)(2,1)}, f32[24,768]{1,0:T(8,128)}) custom-call(s32[5]{0:T(128)} %stack.23.place_ref, s32[1]{0:T(128)S(6)} %copy.69.count_ref, s32[1,80]{1,0:T(1,128)} %pairs_ref.1, f32[1]{0:T(128)} %bitcast.90.temp_ref, f32[1]{0:T(128)} %bitcast.91.bias_ref, f32[16,896]{1,0:T(8,128)} %get-tuple-element.218.own_ref, ...), custom_call_target="tpu_custom_call" | custom-call | flops 1024 | bytes 1024 | tf_op jit(solution)/shard_map/pool_back/pallas_call | solution.py:347
  56.4 4.4 %wgrad.1 = (bf16[2,2,8,96,384]{4,3,2,1,0:T(8,128)(2,1)}, bf16[2,2,8,96,384]{4,3,2,1,0:T(8,128)(2,1)}) custom-call(s32[5]{0:T(128)} %stack.23.place_ref, bf16[256,3072]{1,0:T(8,128)(2,1)} %get-tuple-element.217.left_ref, bf16[256,768]{1,0:T(8,128)(2,1)} %get-tuple-element.231.right_ref.grad_ref), custom_call_target="tpu_custom_call" | custom-call | flops 1024 | bytes 1024 | tf_op jit(solution)/shard_map/wgrad/pallas_call | solution.py:552
  61.4 8.5 %gelu_back.1 = (bf16[256,3072]{1,0:T(8,128)(2,1)}, bf16[2,2,8,48,768]{4,3,2,1,0:T(8,128)(2,1)}, bf16[2,2,8,48,768]{4,3,2,1,0:T(8,128)(2,1)}) custom-call(s32[5]{0:T(128)} %stack.23.place_ref, bf16[256,768]{1,0:T(8,128)(2,1)} %get-tuple-element.231.right_ref.grad_ref, bf16[3072,768]{1,0:T(8,128)(2,1)} %down_ref.3, f32[256,3072]{1,0:T(8,128)} %get-tuple-element.232.up_ref, ...), custom_call_target="tpu_custom_call" | custom-call | flops 1024 | bytes 1024 | tf_op jit(solution)/shard_map/gelu_back/pallas_call | solution.py:893
  71.4 3.6 %fold.9 = (bf16[8,96,384]{2,1,0:T(8,128)(2,1)}, bf16[2,4,96,384]{3,2,1,0:T(8,128)(2,1)}, f32[32,768]{1,0:T(8,128)}) custom-call(s32[5]{0:T(128)} %stack.23.place_ref, bf16[2,2,8,96,384]{4,3,2,1,0:T(8,128)(2,1)} %get-tuple-element.241.refs_0_, bf16[2,2,8,96,384]{4,3,2,1,0:T(8,128)(2,1)} %copy-done.2, bf16[2,2,4,2,96,384]{5,4,3,2,1,0:T(8,128)(2,1)} %bitcast.144, ...), custom_call_target="tpu_custom_call" | custom-call | flops 1024 | bytes 1024 | tf_op jit(solution)/shard_map/fold/pallas_call | solution.py:768
  78.1 7.5 %up_back.1 = (f32[256,768]{1,0:T(8,128)}, bf16[256,768]{1,0:T(8,128)(2,1)}, bf16[256,768]{1,0:T(8,128)(2,1)}) custom-call(bf16[256,3072]{1,0:T(8,128)(2,1)} %get-tuple-element.249.du_ref, bf16[768,3072]{1,0:T(8,128)(2,1)} %up_ref.3, f32[256,768]{1,0:T(8,128)} %get-tuple-element.250.unit_ref, f32[256,1]{1,0:T(8,128)} %get-tuple-element.251.inv_ref, ...), custom_call_target="tpu_custom_call" | custom-call | flops 1024 | bytes 1024 | tf_op jit(solution)/shard_map/up_back/pallas_call | solution.py:949
  85.7 5.3 %collective-permute-done.12 = bf16[8,96,384]{2,1,0:T(8,128)(2,1)S(1)} collective-permute-done((bf16[8,96,384]{2,1,0:T(8,128)(2,1)}, bf16[8,96,384]{2,1,0:T(8,128)(2,1)S(1)}, u32[]{:S(2)}, u32[]{:S(2)}) %collective-permute-start.12) | collective-permute-done | bytes 589856 | tf_op jit(solution)/shard_map/ppermute | solution.py:619
  93.2 4.2 %fold.10 = (bf16[2,4,48,768]{3,2,1,0:T(8,128)(2,1)}, bf16[8,48,768]{2,1,0:T(8,128)(2,1)}, bf16[4,96,384]{2,1,0:T(8,128)(2,1)}, bf16[4,96,384]{2,1,0:T(8,128)(2,1)}, f32[48,768]{1,0:T(8,128)}) custom-call(s32[5]{0:T(128)} %stack.23.place_ref, bf16[2,2,4,2,48,768]{5,4,3,2,1,0:T(8,128)(2,1)} %bitcast.126, bf16[2,2,4,2,48,768]{5,4,3,2,1,0:T(8,128)(2,1)} %bitcast.135, ...), custom_call_target="tpu_custom_call" | custom-call | flops 1024 | bytes 1024 | tf_op jit(solution)/shard_map/fold/pallas_call | solution.py:768
  100.9 10.3 %attend_back.1 = (bf16[256,768]{1,0:T(8,128)(2,1)}, bf16[512,768]{1,0:T(8,128)(2,1)}, bf16[512,768]{1,0:T(8,128)(2,1)}) custom-call(bf16[256,768]{1,0:T(8,128)(2,1)} %get-tuple-element.196.q_ref, bf16[256,768]{1,0:T(8,128)(2,1)} %get-tuple-element.197.ka_ref, bf16[256,768]{1,0:T(8,128)(2,1)} %get-tuple-element.206.kb_ref, ...), custom_call_target="tpu_custom_call" | custom-call | flops 1024 | bytes 1024 | tf_op jit(solution)/shard_map/attend_back/pallas_call | solution.py:510
  114.8 5.7 %wgrad_four.1 = (bf16[2,2,8,4,24,384]{5,4,3,2,1,0:T(8,128)(2,1)}, bf16[2,2,8,4,24,384]{5,4,3,2,1,0:T(8,128)(2,1)}) custom-call(s32[5]{0:T(128)} %stack.23.place_ref, bf16[256,768]{1,0:T(8,128)(2,1)} %get-tuple-element.215.na_ref, bf16[256,768]{1,0:T(8,128)(2,1)} %get-tuple-element.216.nb_ref, bf16[256,768]{1,0:T(8,128)(2,1)} %get-tuple-element.211.attended_ref.a_ref, ...), custom_call_target="tpu_custom_call" | custom-call | flops 1024 | bytes 1024 | tf_op jit(solution)/shard_map/wgrad_four/pallas_call | solution.py:598
  121.3 3.7 %fold.11 = (bf16[4,48,768]{2,1,0:T(8,128)(2,1)}, bf16[4,48,768]{2,1,0:T(8,128)(2,1)}, bf16[2,2,96,384]{3,2,1,0:T(8,128)(2,1)}, f32[80,768]{1,0:T(8,128)}) custom-call(s32[5]{0:T(128)} %stack.23.place_ref, bf16[2,2,4,2,48,768]{5,4,3,2,1,0:T(8,128)(2,1)} %bitcast.127, bf16[2,2,4,2,48,768]{5,4,3,2,1,0:T(8,128)(2,1)} %bitcast.136, ...), custom_call_target="tpu_custom_call" | custom-call | flops 1024 | bytes 1024 | tf_op jit(solution)/shard_map/fold/pallas_call | solution.py:768
  128.2 5.2 %parts_in.1 = (f32[256,768]{1,0:T(8,128)}, bf16[256,768]{1,0:T(8,128)(2,1)}) custom-call(bf16[256,768]{1,0:T(8,128)(2,1)} %get-tuple-element.298.dq_ref, bf16[512,768]{1,0:T(8,128)(2,1)} %get-tuple-element.280.dk_ref, bf16[512,768]{1,0:T(8,128)(2,1)} %get-tuple-element.281.dv_ref, bf16[768,768]{1,0:T(8,128)(2,1)} %wq_ref.1, bf16[768,768]{1,0:T(8,128)(2,1)} %wk_ref.1, ...), custom_call_target="tpu_custom_call" | custom-call | flops 1024 | bytes 1024 | tf_op jit(solution)/shard_map/parts_in/pallas_call | solution.py:982
  138.0 4.1 %fold.12 = (bf16[2,4,4,24,384]{4,3,2,1,0:T(8,128)(2,1)}, bf16[8,4,24,384]{3,2,1,0:T(8,128)(2,1)}, bf16[2,2,48,768]{3,2,1,0:T(8,128)(2,1)}, bf16[2,1,96,384]{3,2,1,0:T(8,128)(2,1)}) custom-call(s32[5]{0:T(128)} %stack.23.place_ref, bf16[2,2,4,2,4,24,384]{6,5,4,3,2,1,0:T(8,128)(2,1)} %bitcast.92, bf16[2,2,4,2,4,24,384]{6,5,4,3,2,1,0:T(8,128)(2,1)} %bitcast.109, ...), custom_call_target="tpu_custom_call" | custom-call | flops 1024 | bytes 1024 | tf_op jit(solution)/shard_map/fold/pallas_call | solution.py:768
  144.9 8.1 %collective-permute-done.26.refs_5_.refs_11_ = bf16[2,1,96,384]{3,2,1,0:T(8,128)(2,1)S(1)} collective-permute-done((bf16[2,1,96,384]{3,2,1,0:T(8,128)(2,1)}, bf16[2,1,96,384]{3,2,1,0:T(8,128)(2,1)S(1)}, u32[]{:S(2)}, u32[]{:S(2)}) %collective-permute-start.26) | collective-permute-done | bytes 147488 | tf_op jit(solution)/shard_map/ppermute | solution.py:615
  154.6 2.0 collective-permute-done.23.refs_2_.refs_16_.refs_30_.refs_44_
  157.8 3.4 %fold.14 = (bf16[4,4,24,384]{3,2,1,0:T(8,128)(2,1)}, bf16[4,4,24,384]{3,2,1,0:T(8,128)(2,1)}, bf16[2,1,48,768]{3,2,1,0:T(8,128)(2,1)}) custom-call(s32[5]{0:T(128)} %stack.23.place_ref, bf16[2,2,4,2,4,24,384]{6,5,4,3,2,1,0:T(8,128)(2,1)} %bitcast.93, bf16[2,2,4,2,4,24,384]{6,5,4,3,2,1,0:T(8,128)(2,1)} %bitcast.110, bf16[2,4,4,24,384]{4,3,2,1,0:T(8,128)(2,1)} %copy-done.3, ...), custom_call_target="tpu_custom_call" | custom-call | flops 1024 | bytes 1024 | tf_op jit(solution)/shard_map/fold/pallas_call | solution.py:768
  164.7 2.7 %fold.13 = f32[192,384]{1,0:T(8,128)} custom-call(s32[5]{0:T(128)} %stack.23.place_ref, bf16[2,2,4,2,96,384]{5,4,3,2,1,0:T(8,128)(2,1)} %bitcast.151, bf16[2,2,4,2,96,384]{5,4,3,2,1,0:T(8,128)(2,1)} %bitcast.160, bf16[4,2,96,384]{3,2,1,0:T(8,128)(2,1)} %bitcast.188, bf16[4,96,384]{2,1,0:T(8,128)(2,1)} %copy-done.18, bf16[2,2,96,384]{3,2,1,0:T(8,128)(2,1)} %copy-done.15, ...), custom_call_target="tpu_custom_call" | custom-call | flops 1024 | bytes 1024 | tf_op jit(solution)/shard_map/fold/pallas_call | solution.py:768
  167.5 4.8 %collective-permute-done.29.refs_5_.refs_11_ = bf16[2,1,48,768]{3,2,1,0:T(8,128)(2,1)S(1)} collective-permute-done((bf16[2,1,48,768]{3,2,1,0:T(8,128)(2,1)}, bf16[2,1,48,768]{3,2,1,0:T(8,128)(2,1)S(1)}, u32[]{:S(2)}, u32[]{:S(2)}) %collective-permute-start.29) | collective-permute-done | bytes 147488 | tf_op jit(solution)/shard_map/ppermute | solution.py:615
  172.2 2.2 %collective-permute-done.30.refs_25_ = f32[80,768]{1,0:T(8,128)S(1)} collective-permute-done((f32[80,768]{1,0:T(8,128)S(1)}, f32[80,768]{1,0:T(8,128)S(1)}, u32[]{:S(2)}, u32[]{:S(2)}) %collective-permute-start.30) | collective-permute-done | bytes 245792 | tf_op jit(solution)/shard_map/ppermute | solution.py:615
  175.4 3.5 %fold.16 = (bf16[2,1,4,24,384]{4,3,2,1,0:T(8,128)(2,1)}, bf16[2,1,4,24,384]{4,3,2,1,0:T(8,128)(2,1)}, bf16[2,1,4,24,384]{4,3,2,1,0:T(8,128)(2,1)}, f32[144,768]{1,0:T(8,128)}) custom-call(s32[5]{0:T(128)} %stack.23.place_ref, bf16[2,2,1,4,2,4,24,384]{7,6,5,4,3,2,1,0:T(8,128)(2,1)} %bitcast.95, bf16[2,2,1,4,2,4,24,384]{7,6,5,4,3,2,1,0:T(8,128)(2,1)} %bitcast.112, ...), custom_call_target="tpu_custom_call" | custom-call | flops 1024 | bytes 1024 | tf_op jit(solution)/shard_map/fold/pallas_call | solution.py:768
  181.1 3.3 %collective-permute-start.34 = (bf16[2,1,4,24,384]{4,3,2,1,0:T(8,128)(2,1)}, bf16[2,1,4,24,384]{4,3,2,1,0:T(8,128)(2,1)S(1)}, u32[]{:S(2)}, u32[]{:S(2)}) collective-permute-start(bf16[2,1,4,24,384]{4,3,2,1,0:T(8,128)(2,1)} %get-tuple-element.353), channel_id=1, source_target_pairs={{0,24},{2,26},{4,28},{6,30},{8,16},{10,18},{12,20},{14,22},{16,8},... | collective-permute-start | bytes 442376 | tf_op jit(solution)/shard_map/ppermute | solution.py:615
  184.4 2.7 %fold.15.refs_58_ = f32[48,1536]{1,0:T(8,128)} custom-call(s32[5]{0:T(128)} %stack.23.place_ref, bf16[2,2,4,2,48,768]{5,4,3,2,1,0:T(8,128)(2,1)} %bitcast.133, bf16[2,2,4,2,48,768]{5,4,3,2,1,0:T(8,128)(2,1)} %bitcast.142, bf16[2,4,48,768]{3,2,1,0:T(8,128)(2,1)} %copy-done.10, bf16[4,48,768]{2,1,0:T(8,128)(2,1)} %copy-done.16, ...), custom_call_target="tpu_custom_call" | custom-call | flops 1024 | bytes 1024 | tf_op jit(solution)/shard_map/fold/pallas_call | solution.py:768
  187.1 4.2 %pool_weights.1 = (f32[48,384]{1,0:T(8,128)}, f32[48,384]{1,0:T(8,128)}, f32[48,384]{1,0:T(8,128)}, f32[48,384]{1,0:T(8,128)}, f32[3,128]{1,0:T(4,128)}) custom-call(s32[5]{0:T(128)} %stack.23.place_ref, f32[144,768]{1,0:T(8,128)} %get-tuple-element.343.rows_ref, f32[4,768]{1,0:T(4,128)} %vectors.1.vectors_ref.refs_56_, ...), custom_call_target="tpu_custom_call" | custom-call | flops 1024 | bytes 1024 | tf_op jit(solution)/shard_map/pool_weights/pallas_call | solution.py:419
  193.2 3.1 %fold.17 = (f32[48,384]{1,0:T(8,128)}, f32[48,384]{1,0:T(8,128)}, f32[48,384]{1,0:T(8,128)}, f32[48,384]{1,0:T(8,128)}, f32[2,128]{1,0:T(2,128)}) custom-call(s32[5]{0:T(128)} %stack.23.place_ref, bf16[2,2,4,2,4,24,384]{6,5,4,3,2,1,0:T(8,128)(2,1)} %bitcast.101, bf16[2,2,4,2,4,24,384]{6,5,4,3,2,1,0:T(8,128)(2,1)} %bitcast.118, ...), custom_call_target="tpu_custom_call" | custom-call | flops 1024 | bytes 1024 | tf_op jit(solution)/shard_map/fold/pallas_call | solution.py:768
  198.1 3.1 %own_in.1 = f32[256,768]{1,0:T(8,128)} custom-call(f32[256,768]{1,0:T(8,128)} %get-tuple-element.305.own_ref, bf16[256,768]{1,0:T(8,128)(2,1)} %copy-done.22, f32[256,768]{1,0:T(8,128)} %get-tuple-element.355.unit_ref, f32[256,1]{1,0:T(8,128)} %get-tuple-element.356.inv_ref, f32[4,768]{1,0:T(4,128)} %vectors.1.vectors_ref.refs_56_, ...), custom_call_target="tpu_custom_call" | custom-call | flops 1024 | bytes 1024 | tf_op jit(solution)/shard_map/own_in/pallas_call | solution.py:1001
  (147 shorter events, 47.1 us)
Async XLA Ops:
  0.7 12.9 %collective-permute-start = (bf16[256,768]{1,0:T(8,128)(2,1)}, bf16[256,768]{1,0:T(8,128)(2,1)S(1)}, u32[]{:S(2)}, u32[]{:S(2)}) collective-permute-start(bf16[256,768]{1,0:T(8,128)(2,1)} %bitcast.208), channel_id=1, source_target_pairs={{0,1},{1,0},{2,3},{3,2},{4,5},{5,4},{6,7},{7,6},{8,9},{9,8},{10,11... | collective-permute-start | bytes 1179656 | tf_op jit(solution)/shard_map/ppermute | solution.py:619
  3.7 5.5 %collective-permute-start.1 = (f32[1,5,768]{2,1,0:T(8,128)}, f32[1,5,768]{2,1,0:T(8,128)S(1)}, u32[]{:S(2)}, u32[]{:S(2)}) collective-permute-start(f32[1,5,768]{2,1,0:T(8,128)} %bitcast.212), channel_id=1, source_target_pairs={{0,2},{2,0},{4,6},{6,4},{8,10},{10,8},{12,14},{14,12},{16,18},{18,... | collective-permute-start | bytes 46088 | tf_op jit(solution)/shard_map/ppermute | solution.py:615
  13.5 13.8 %collective-permute-start.3 = (f32[4,5,768]{2,1,0:T(8,128)S(1)}, f32[4,5,768]{2,1,0:T(8,128)S(1)}, u32[]{:S(2)}, u32[]{:S(2)}) collective-permute-start(f32[4,5,768]{2,1,0:T(8,128)S(1)} %pad_maximum_fusion.2), channel_id=1, source_target_pairs={{0,8},{2,10},{4,12},{6,14},{8,0},{10,2},{12,4},{14,6},{16,24},{18,... | collective-permute-start | bytes 184328 | tf_op jit(solution)/shard_map/ppermute | solution.py:615
  27.4 18.1 %collective-permute-start.5 = (f32[8,5,768]{2,1,0:T(8,128)S(1)}, f32[8,5,768]{2,1,0:T(8,128)S(1)}, u32[]{:S(2)}, u32[]{:S(2)}) collective-permute-start(f32[8,5,768]{2,1,0:T(8,128)S(1)} %pad_maximum_fusion.1), channel_id=1, source_target_pairs={{0,16},{2,18},{4,20},{6,22},{8,24},{10,26},{12,28},{14,30},{16,0},... | collective-permute-start | bytes 368648 | tf_op jit(solution)/shard_map/ppermute | solution.py:615
  60.8 9.2 %collective-permute-start.7 = (bf16[2,2,8,96,384]{4,3,2,1,0:T(8,128)(2,1)}, bf16[2,2,8,96,384]{4,3,2,1,0:T(8,128)(2,1)S(1)}, u32[]{:S(2)}, u32[]{:S(2)}) collective-permute-start(bf16[2,2,8,96,384]{4,3,2,1,0:T(8,128)(2,1)} %get-tuple-element.237), channel_id=1, source_target_pairs={{0,2},{2,0},{4,6},{6,4},{8,10},{10,8},{12,14},{14,12},{16,18},{18,... | collective-permute-start | bytes 7077896 | tf_op jit(solution)/shard_map/ppermute | solution.py:615
  60.9 9.1 %collective-permute-start.8 = (f32[24,768]{1,0:T(8,128)}, f32[24,768]{1,0:T(8,128)S(1)}, u32[]{:S(2)}, u32[]{:S(2)}) collective-permute-start(f32[24,768]{1,0:T(8,128)} %get-tuple-element.230.refs_4_), channel_id=1, source_target_pairs={{0,2},{2,0},{4,6},{6,4},{8,10},{10,8},{12,14},{14,12},{16,18},{18,... | collective-permute-start | bytes 221192 | tf_op jit(solution)/shard_map/ppermute | solution.py:615
  61.4 8.6 %collective-permute-start.9 = (f32[24,768]{1,0:T(8,128)S(1)}, f32[24,768]{1,0:T(8,128)S(1)}, u32[]{:S(2)}, u32[]{:S(2)}) collective-permute-start(f32[24,768]{1,0:T(8,128)S(1)} %collective-permute-done.6.refs_6_), channel_id=1, source_target_pairs={{0,2},{2,0},{4,6},{6,4},{8,10},{10,8},{12,14},{14,12},{16,18},{18,... | collective-permute-start | bytes 221192 | tf_op jit(solution)/shard_map/ppermute | solution.py:615
  75.0 16.6 %collective-permute-start.10 = (bf16[2,2,8,48,768]{4,3,2,1,0:T(8,128)(2,1)}, bf16[2,2,8,48,768]{4,3,2,1,0:T(8,128)(2,1)S(1)}, u32[]{:S(2)}, u32[]{:S(2)}) collective-permute-start(bf16[2,2,8,48,768]{4,3,2,1,0:T(8,128)(2,1)} %get-tuple-element.254), channel_id=1, source_target_pairs={{0,2},{2,0},{4,6},{6,4},{8,10},{10,8},{12,14},{14,12},{16,18},{18,... | collective-permute-start | bytes 7077896 | tf_op jit(solution)/shard_map/ppermute | solution.py:615
  75.5 15.5 %collective-permute-start.12 = (bf16[8,96,384]{2,1,0:T(8,128)(2,1)}, bf16[8,96,384]{2,1,0:T(8,128)(2,1)S(1)}, u32[]{:S(2)}, u32[]{:S(2)}) collective-permute-start(bf16[8,96,384]{2,1,0:T(8,128)(2,1)} %get-tuple-element.256), channel_id=1, source_target_pairs={{0,1},{1,0},{2,3},{3,2},{4,5},{5,4},{6,7},{7,6},{8,9},{9,8},{10,11... | collective-permute-start | bytes 1769480 | tf_op jit(solution)/shard_map/ppermute | solution.py:619
  76.3 15.2 %collective-permute-start.13 = (bf16[2,4,96,384]{3,2,1,0:T(8,128)(2,1)}, bf16[2,4,96,384]{3,2,1,0:T(8,128)(2,1)S(1)}, u32[]{:S(2)}, u32[]{:S(2)}) collective-permute-start(bf16[2,4,96,384]{3,2,1,0:T(8,128)(2,1)} %get-tuple-element.257), channel_id=1, source_target_pairs={{0,4},{2,6},{4,0},{6,2},{8,12},{10,14},{12,8},{14,10},{16,20},{18,... | collective-permute-start | bytes 1769480 | tf_op jit(solution)/shard_map/ppermute | solution.py:615
  77.8 7.9 %collective-permute-start.11 = (f32[32,768]{1,0:T(8,128)}, f32[32,768]{1,0:T(8,128)}, u32[]{:S(2)}, u32[]{:S(2)}) collective-permute-start(f32[32,768]{1,0:T(8,128)} %get-tuple-element.255.refs_10_), channel_id=1, source_target_pairs={{0,16},{2,18},{4,20},{6,22},{8,24},{10,26},{12,28},{14,30},{16,0},... | collective-permute-start | bytes 294920 | tf_op jit(solution)/shard_map/ppermute | solution.py:615
  97.4 14.5 %collective-permute-start.14 = (bf16[2,4,48,768]{3,2,1,0:T(8,128)(2,1)}, bf16[2,4,48,768]{3,2,1,0:T(8,128)(2,1)S(1)}, u32[]{:S(2)}, u32[]{:S(2)}) collective-permute-start(bf16[2,4,48,768]{3,2,1,0:T(8,128)(2,1)} %get-tuple-element.274), channel_id=1, source_target_pairs={{0,4},{2,6},{4,0},{6,2},{8,12},{10,14},{12,8},{14,10},{16,20},{18,... | collective-permute-start | bytes 1769480 | tf_op jit(solution)/shard_map/ppermute | solution.py:615
  98.9 14.1 %collective-permute-start.15 = (bf16[8,48,768]{2,1,0:T(8,128)(2,1)}, bf16[8,48,768]{2,1,0:T(8,128)(2,1)S(1)}, u32[]{:S(2)}, u32[]{:S(2)}) collective-permute-start(bf16[8,48,768]{2,1,0:T(8,128)(2,1)} %get-tuple-element.275), channel_id=1, source_target_pairs={{0,1},{1,0},{2,3},{3,2},{4,5},{5,4},{6,7},{7,6},{8,9},{9,8},{10,11... | collective-permute-start | bytes 1769480 | tf_op jit(solution)/shard_map/ppermute | solution.py:619
  100.1 11.0 %collective-permute-start.16 = (f32[48,768]{1,0:T(8,128)}, f32[48,768]{1,0:T(8,128)S(1)}, u32[]{:S(2)}, u32[]{:S(2)}) collective-permute-start(f32[48,768]{1,0:T(8,128)} %get-tuple-element.276.refs_14_), channel_id=1, source_target_pairs={{0,8},{2,10},{4,12},{6,14},{8,0},{10,2},{12,4},{14,6},{16,24},{18,... | collective-permute-start | bytes 442376 | tf_op jit(solution)/shard_map/ppermute | solution.py:615
  113.1 7.4 %collective-permute-start.17 = (bf16[4,96,384]{2,1,0:T(8,128)(2,1)S(1)}, bf16[4,96,384]{2,1,0:T(8,128)(2,1)S(1)}, u32[]{:S(2)}, u32[]{:S(2)}) collective-permute-start(bf16[4,96,384]{2,1,0:T(8,128)(2,1)S(1)} %copy-done.36), channel_id=1, source_target_pairs={{0,4},{2,6},{4,0},{6,2},{8,12},{10,14},{12,8},{14,10},{16,20},{18,... | collective-permute-start | bytes 884744 | tf_op jit(solution)/shard_map/ppermute | solution.py:615
  113.6 6.8 %collective-permute-start.18 = (bf16[4,96,384]{2,1,0:T(8,128)(2,1)S(1)}, bf16[4,96,384]{2,1,0:T(8,128)(2,1)S(1)}, u32[]{:S(2)}, u32[]{:S(2)}) collective-permute-start(bf16[4,96,384]{2,1,0:T(8,128)(2,1)S(1)} %copy-done.35), channel_id=1, source_target_pairs={{0,1},{1,0},{2,3},{3,2},{4,5},{5,4},{6,7},{7,6},{8,9},{9,8},{10,11... | collective-permute-start | bytes 884744 | tf_op jit(solution)/shard_map/ppermute | solution.py:619
  125.0 11.5 %collective-permute-start.19 = (bf16[2,2,8,4,24,384]{5,4,3,2,1,0:T(8,128)(2,1)}, bf16[2,2,8,4,24,384]{5,4,3,2,1,0:T(8,128)(2,1)S(1)}, u32[]{:S(2)}, u32[]{:S(2)}) collective-permute-start(bf16[2,2,8,4,24,384]{5,4,3,2,1,0:T(8,128)(2,1)} %get-tuple-element.301), channel_id=1, source_target_pairs={{0,2},{2,0},{4,6},{6,4},{8,10},{10,8},{12,14},{14,12},{16,18},{18,... | collective-permute-start | bytes 7077896 | tf_op jit(solution)/shard_map/ppermute | solution.py:615
  125.0 9.6 %collective-permute-start.20 = (bf16[4,48,768]{2,1,0:T(8,128)(2,1)}, bf16[4,48,768]{2,1,0:T(8,128)(2,1)S(1)}, u32[]{:S(2)}, u32[]{:S(2)}) collective-permute-start(bf16[4,48,768]{2,1,0:T(8,128)(2,1)} %get-tuple-element.302), channel_id=1, source_target_pairs={{0,1},{1,0},{2,3},{3,2},{4,5},{5,4},{6,7},{7,6},{8,9},{9,8},{10,11... | collective-permute-start | bytes 884744 | tf_op jit(solution)/shard_map/ppermute | solution.py:619
  126.0 9.3 %collective-permute-start.21 = (bf16[4,48,768]{2,1,0:T(8,128)(2,1)}, bf16[4,48,768]{2,1,0:T(8,128)(2,1)S(1)}, u32[]{:S(2)}, u32[]{:S(2)}) collective-permute-start(bf16[4,48,768]{2,1,0:T(8,128)(2,1)} %get-tuple-element.303), channel_id=1, source_target_pairs={{0,4},{2,6},{4,0},{6,2},{8,12},{10,14},{12,8},{14,10},{16,20},{18,... | collective-permute-start | bytes 884744 | tf_op jit(solution)/shard_map/ppermute | solution.py:615
  127.5 9.0 %collective-permute-start.22 = (bf16[2,2,96,384]{3,2,1,0:T(8,128)(2,1)}, bf16[2,2,96,384]{3,2,1,0:T(8,128)(2,1)S(1)}, u32[]{:S(2)}, u32[]{:S(2)}) collective-permute-start(bf16[2,2,96,384]{3,2,1,0:T(8,128)(2,1)} %get-tuple-element.304), channel_id=1, source_target_pairs={{0,8},{2,10},{4,12},{6,14},{8,0},{10,2},{12,4},{14,6},{16,24},{18,... | collective-permute-start | bytes 884744 | tf_op jit(solution)/shard_map/ppermute | solution.py:615
  142.1 14.5 %collective-permute-start.23 = (bf16[2,4,4,24,384]{4,3,2,1,0:T(8,128)(2,1)}, bf16[2,4,4,24,384]{4,3,2,1,0:T(8,128)(2,1)S(1)}, u32[]{:S(2)}, u32[]{:S(2)}) collective-permute-start(bf16[2,4,4,24,384]{4,3,2,1,0:T(8,128)(2,1)} %get-tuple-element.317), channel_id=1, source_target_pairs={{0,4},{2,6},{4,0},{6,2},{8,12},{10,14},{12,8},{14,10},{16,20},{18,... | collective-permute-start | bytes 1769480 | tf_op jit(solution)/shard_map/ppermute | solution.py:615
  142.7 14.3 %collective-permute-start.24 = (bf16[8,4,24,384]{3,2,1,0:T(8,128)(2,1)}, bf16[8,4,24,384]{3,2,1,0:T(8,128)(2,1)S(1)}, u32[]{:S(2)}, u32[]{:S(2)}) collective-permute-start(bf16[8,4,24,384]{3,2,1,0:T(8,128)(2,1)} %get-tuple-element.318), channel_id=1, source_target_pairs={{0,1},{1,0},{2,3},{3,2},{4,5},{5,4},{6,7},{7,6},{8,9},{9,8},{10,11... | collective-permute-start | bytes 1769480 | tf_op jit(solution)/shard_map/ppermute | solution.py:619
  143.8 10.9 %collective-permute-start.25 = (bf16[2,2,48,768]{3,2,1,0:T(8,128)(2,1)}, bf16[2,2,48,768]{3,2,1,0:T(8,128)(2,1)S(1)}, u32[]{:S(2)}, u32[]{:S(2)}) collective-permute-start(bf16[2,2,48,768]{3,2,1,0:T(8,128)(2,1)} %get-tuple-element.319), channel_id=1, source_target_pairs={{0,8},{2,10},{4,12},{6,14},{8,0},{10,2},{12,4},{14,6},{16,24},{18,... | collective-permute-start | bytes 884744 | tf_op jit(solution)/shard_map/ppermute | solution.py:615
  144.5 8.5 %collective-permute-start.26 = (bf16[2,1,96,384]{3,2,1,0:T(8,128)(2,1)}, bf16[2,1,96,384]{3,2,1,0:T(8,128)(2,1)S(1)}, u32[]{:S(2)}, u32[]{:S(2)}) collective-permute-start(bf16[2,1,96,384]{3,2,1,0:T(8,128)(2,1)} %get-tuple-element.320), channel_id=1, source_target_pairs={{0,16},{2,18},{4,20},{6,22},{8,24},{10,26},{12,28},{14,30},{16,0},... | collective-permute-start | bytes 442376 | tf_op jit(solution)/shard_map/ppermute | solution.py:615
  161.2 13.2 %collective-permute-start.27 = (bf16[4,4,24,384]{3,2,1,0:T(8,128)(2,1)}, bf16[4,4,24,384]{3,2,1,0:T(8,128)(2,1)S(1)}, u32[]{:S(2)}, u32[]{:S(2)}) collective-permute-start(bf16[4,4,24,384]{3,2,1,0:T(8,128)(2,1)} %get-tuple-element.330), channel_id=1, source_target_pairs={{0,1},{1,0},{2,3},{3,2},{4,5},{5,4},{6,7},{7,6},{8,9},{9,8},{10,11... | collective-permute-start | bytes 884744 | tf_op jit(solution)/shard_map/ppermute | solution.py:619
  162.4 12.1 %collective-permute-start.28 = (bf16[4,4,24,384]{3,2,1,0:T(8,128)(2,1)}, bf16[4,4,24,384]{3,2,1,0:T(8,128)(2,1)S(1)}, u32[]{:S(2)}, u32[]{:S(2)}) collective-permute-start(bf16[4,4,24,384]{3,2,1,0:T(8,128)(2,1)} %get-tuple-element.331), channel_id=1, source_target_pairs={{0,4},{2,6},{4,0},{6,2},{8,12},{10,14},{12,8},{14,10},{16,20},{18,... | collective-permute-start | bytes 884744 | tf_op jit(solution)/shard_map/ppermute | solution.py:615
  163.8 10.7 %collective-permute-start.30 = (f32[80,768]{1,0:T(8,128)S(1)}, f32[80,768]{1,0:T(8,128)S(1)}, u32[]{:S(2)}, u32[]{:S(2)}) collective-permute-start(f32[80,768]{1,0:T(8,128)S(1)} %copy-done.24), channel_id=1, source_target_pairs={{0,4},{2,6},{4,0},{6,2},{8,12},{10,14},{12,8},{14,10},{16,20},{18,... | collective-permute-start | bytes 737288 | tf_op jit(solution)/shard_map/ppermute | solution.py:615
  164.4 7.8 %collective-permute-start.29 = (bf16[2,1,48,768]{3,2,1,0:T(8,128)(2,1)}, bf16[2,1,48,768]{3,2,1,0:T(8,128)(2,1)S(1)}, u32[]{:S(2)}, u32[]{:S(2)}) collective-permute-start(bf16[2,1,48,768]{3,2,1,0:T(8,128)(2,1)} %get-tuple-element.332), channel_id=1, source_target_pairs={{0,16},{2,18},{4,20},{6,22},{8,24},{10,26},{12,28},{14,30},{16,0},... | collective-permute-start | bytes 442376 | tf_op jit(solution)/shard_map/ppermute | solution.py:615
  179.0 12.9 %collective-permute-start.31 = (bf16[256,768]{1,0:T(8,128)(2,1)S(1)}, bf16[256,768]{1,0:T(8,128)(2,1)S(1)}, u32[]{:S(2)}, u32[]{:S(2)}) collective-permute-start(bf16[256,768]{1,0:T(8,128)(2,1)S(1)} %copy-done.34), channel_id=1, source_target_pairs={{0,1},{1,0},{2,3},{3,2},{4,5},{5,4},{6,7},{7,6},{8,9},{9,8},{10,11... | collective-permute-start | bytes 1179656 | tf_op jit(solution)/shard_map/ppermute | solution.py:619
  180.0 11.3 %collective-permute-start.32 = (bf16[2,1,4,24,384]{4,3,2,1,0:T(8,128)(2,1)}, bf16[2,1,4,24,384]{4,3,2,1,0:T(8,128)(2,1)S(1)}, u32[]{:S(2)}, u32[]{:S(2)}) collective-permute-start(bf16[2,1,4,24,384]{4,3,2,1,0:T(8,128)(2,1)} %get-tuple-element.351), channel_id=1, source_target_pairs={{0,8},{2,10},{4,12},{6,14},{8,0},{10,2},{12,4},{14,6},{16,24},{18,... | collective-permute-start | bytes 442376 | tf_op jit(solution)/shard_map/ppermute | solution.py:615
  180.8 11.1 %collective-permute-start.33 = (bf16[2,1,4,24,384]{4,3,2,1,0:T(8,128)(2,1)}, bf16[2,1,4,24,384]{4,3,2,1,0:T(8,128)(2,1)S(1)}, u32[]{:S(2)}, u32[]{:S(2)}) collective-permute-start(bf16[2,1,4,24,384]{4,3,2,1,0:T(8,128)(2,1)} %get-tuple-element.352), channel_id=1, source_target_pairs={{0,16},{2,18},{4,20},{6,22},{8,24},{10,26},{12,28},{14,30},{16,0},... | collective-permute-start | bytes 442376 | tf_op jit(solution)/shard_map/ppermute | solution.py:615
  181.1 10.8 %collective-permute-start.34 = (bf16[2,1,4,24,384]{4,3,2,1,0:T(8,128)(2,1)}, bf16[2,1,4,24,384]{4,3,2,1,0:T(8,128)(2,1)S(1)}, u32[]{:S(2)}, u32[]{:S(2)}) collective-permute-start(bf16[2,1,4,24,384]{4,3,2,1,0:T(8,128)(2,1)} %get-tuple-element.353), channel_id=1, source_target_pairs={{0,24},{2,26},{4,28},{6,30},{8,16},{10,18},{12,20},{14,22},{16,8},... | collective-permute-start | bytes 442376 | tf_op jit(solution)/shard_map/ppermute | solution.py:615
  (41 other events, 158.2 us)

commit v7 on v6

--- a/solution.py
+++ b/solution.py
@@ -264,11 +264,16 @@
     caps = caps_ref[...]
     unit_caps = caps * lax.rsqrt(jnp.sum(caps * caps, axis=-1, keepdims=True) + norm_eps)
     similar = jnp.sum(unit_caps * embedding, axis=-1, keepdims=True)
+
+    def over_pairs(value):
+        return jnp.sum(jnp.sum(value, axis=0), axis=0, keepdims=True)
+
     temper = jnp.exp(jnp.full((1, 1), temp_ref[0], f32))
     logits = temper * similar + bias_ref[0]
-    slot = lax.broadcasted_iota(jnp.int32, similar.shape, 0)
+    per_image = caps.shape[1]
+    slot = lax.broadcasted_iota(jnp.int32, similar.shape, 0) * per_image
+    slot = slot + lax.broadcasted_iota(jnp.int32, similar.shape, 1)
     pair = jnp.zeros(similar.shape, jnp.int32)
-    per_image = caps.shape[0] // images
     for j in range(per_image):
         pair = jnp.where(slot == j, pairs_ref[0, place_ref[0] * per_image + j], pair)
     positive = pair == 1
@@ -278,11 +283,11 @@
     decay = jnp.exp(-jnp.abs(signed))
     log_sigmoid = jnp.minimum(signed, 0.0) - jnp.log1p(decay)
     against = jnp.where(signed >= 0, decay, 1.0) / (1.0 + decay)
-    row_loss = -jnp.sum(weight * log_sigmoid, axis=0, keepdims=True) / images
+    row_loss = -over_pairs(weight * log_sigmoid) / images
     logit_grad = -(weight / images) * sign * against
-    temp_row = jnp.sum(logit_grad * temper * similar, axis=0, keepdims=True)
-    bias_row = jnp.sum(logit_grad, axis=0, keepdims=True)
-    embed_grad = temper * jnp.sum(logit_grad * unit_caps, axis=0, keepdims=True)
+    temp_row = over_pairs(logit_grad * temper * similar)
+    bias_row = over_pairs(logit_grad)
+    embed_grad = temper * over_pairs(logit_grad * unit_caps)
     pooled_grad = scale * (
         embed_grad - embedding * jnp.sum(embedding * embed_grad, axis=-1, keepdims=True)
     )
@@ -1045,7 +1050,6 @@
     me = lax.axis_index("img")
     seq_me = lax.axis_index("seq")
     half = width // seq_count
-    caps = captions.shape[0]
     place = jnp.stack([me, seq_me, me & 1, (me >> 1) & 1, me >> 2]).astype(jnp.int32)
 
     other_tokens = seq_swap(own_tokens)
@@ -1054,7 +1058,7 @@
     def gather_more(gathered, bit):
         return jnp.concatenate([gathered, img_swap(gathered, 1 << bit)], axis=0)
 
-    gathered = gather_more(gathered, 0)
+    gathered = gather_more(gathered, 1)
 
     low_own, unit_one, scale_one, queries, keys_own, values_own = front_call(
         own_tokens, first_gain, w_query, w_key, w_value
@@ -1062,7 +1066,7 @@
     low_own, gathered, place, first, second, final, own_probe = tie(
         low_own, gathered, place, first_gain, second_gain, final_gain, probe
     )
-    gathered = gather_more(gathered, 1)
+    gathered = gather_more(gathered, 0)
     vectors = vectors_call(first, second, final, own_probe)
 
     other_tokens, gathered, vectors, place = tie(other_tokens, gathered, vectors, place)
@@ -1085,7 +1089,7 @@
     result_grad, branch_grad, message = pool_back_call(
         place, caption_counts, positive_pairs, log_temp, pair_bias, packed, other_packed, exps,
         pool_low, unit_pool, inv_pool, vectors, key_probe, pool_value, pool_output,
-        gathered.reshape(images * caps, width), images, seq_count,
+        gathered, images, seq_count,
     )
 
     step = Order(place)
@@ -1095,7 +1099,7 @@
         down_send, down_keep, branch_grad, message_in
     )
     down_core = img_swap(down_send, 1)
-    messages = [img_swap(message, 1), message_in, img_swap(message_in, 1)]
+    messages = [img_swap(message, 2), message_in, img_swap(message_in, 2)]
     up_grad_low, up_send, up_keep = gelu_back_call(
         place, branch_grad, w_down, upward, second_low, images
     )
@@ -1172,19 +1176,21 @@
     up_a.second = seq_swap(send_a)
     up_b.second = img_swap(send_b, 2)
     down_in = img_swap(down_send, 4)
+    message_in = img_swap(message, 1)
     own_part, other_part = parts_in_call(
         query_grad, key_part, value_part, w_query, w_key, w_value
     )
-    own_part, other_part, four_core, up_a.second, up_b.second, down_in = step(
-        own_part, other_part, four_core, up_a.second, up_b.second, down_in
+    own_part, other_part, four_core, up_a.second, up_b.second, down_in, message_in = step(
+        own_part, other_part, four_core, up_a.second, up_b.second, down_in, message_in
     )
     take(down_a, down_b, [down_in], 1)
     four_a = Staged(0, False, four_keep, four_core)
     four_b = Staged(1, True, four_keep, four_core)
-    send_a, send_b, up_send, down_send = fold(
+    send_a, send_b, up_send, down_send, message = fold(
         place,
         first_stage(four_a, four_b) + far_send(up_a, up_b, 0) + far_send(down_a, down_b, 1),
         bf16,
+        [(message, [message_in], True)],
     )
     send_a, send_b, up_send, down_send, message, other_part = step(
         send_a, send_b, up_send, down_send, message, other_part
@@ -1194,43 +1200,45 @@
     four_b.first = seq_swap(send_b)
     up_in = img_swap(up_send, 4)
     down_in = img_swap(down_send, 8)
-    four_a.first, four_b.first, up_in, down_in = step(four_a.first, four_b.first, up_in, down_in)
+    for bit in range(4, bits):
+        (message,) = fold(place, [], f32, [(message, [img_swap(message, 1 << bit)], True)])
+    pool_grads = pool_weights_call(
+        place, message, vectors, probe_query, pool_query, pool_key, images
+    )
+    pool_grads, four_a.first, four_b.first, up_in, down_in = step(
+        pool_grads, four_a.first, four_b.first, up_in, down_in
+    )
     take(up_a, up_b, [up_in], 1)
     take(down_a, down_b, [down_in], 2)
     send_a, send_b, up_send = fold(
         place, second_stage(four_a, four_b) + far_send(up_a, up_b, 1), bf16
     )
-    send_a, send_b, up_send, message, other_part = step(
-        send_a, send_b, up_send, message, other_part
-    )
+    send_a, send_b, up_send, other_part = step(send_a, send_b, up_send, other_part)
 
     four_a.second = seq_swap(send_a)
     four_b.second = img_swap(send_b, 2)
     up_in = img_swap(up_send, 8)
-    message_in = img_swap(message, 2)
     finish(place, down_a, down_b)
     (down_grad,) = fold(place, [([down_a.whole(), down_b.whole()], "rows")], f32)
-    down_grad, four_a.second, four_b.second, up_in, message_in = step(
-        down_grad, four_a.second, four_b.second, up_in, message_in
+    query_pool_grad, key_pool_grad, value_pool_grad, out_pool_grad, small = pool_grads
+    block = width // images
+    small = (small[1, :block], small[0, :block], small[2, 0], small[2, 1], small[2, 2])
+    down_grad, small, four_a.second, four_b.second, up_in = step(
+        down_grad, small, four_a.second, four_b.second, up_in
     )
     take(up_a, up_b, [up_in], 2)
-    *four_sends, message = fold(
-        place, near_sends(four_a, four_b), bf16, [(message, [message_in], True)]
-    )
-    message, other_part, *four_sends = step(message, other_part, *four_sends)
+    four_sends = fold(place, near_sends(four_a, four_b), bf16)
+    other_part, *four_sends = step(other_part, *four_sends)
 
     four_in = near_swap(four_sends)
     arrived_part = seq_swap(other_part)
     finish(place, up_a, up_b)
     (up_weight_grad,) = fold(place, [([up_a.whole(), up_b.whole()], "columns")], f32)
-    for bit in range(4, bits):
-        (message,) = fold(place, [], f32, [(message, [img_swap(message, 1 << bit)], True)])
-    pool_grads = pool_weights_call(
-        place, message, vectors, probe_query, pool_query, pool_key, images
-    )
-    up_weight_grad, pool_grads, arrived_part, *four_in = step(
-        up_weight_grad, pool_grads, arrived_part, *four_in
-    )
+    up_weight_grad, arrived_part = step(up_weight_grad, arrived_part)
+    input_grad = own_in_call(
+        own_part, arrived_part, unit_one, scale_one, vectors, residual_grad
+    )
+    input_grad, *four_in = step(input_grad, *four_in)
     take(four_a, four_b, four_in, 2)
     finish(place, four_a, four_b)
     query_weight_grad, key_weight_grad, value_weight_grad, output_grad, gains = fold(
@@ -1242,13 +1250,7 @@
         ],
         vectors=vectors,
     )
-    input_grad = own_in_call(
-        own_part, arrived_part, unit_one, scale_one, vectors, residual_grad
-    )
-
     gains = gains + seq_swap(gains)
-    block = width // images
-    query_pool_grad, key_pool_grad, value_pool_grad, out_pool_grad, small = pool_grads
     return (
         block_out,
         input_grad[None],
@@ -1260,15 +1262,13 @@
         down_grad,
         gains[FIRST, :block],
         gains[SECOND, :block],
-        small[1, :block],
-        small[0, :block],
+        small[0],
+        small[1],
         query_pool_grad,
         key_pool_grad,
         value_pool_grad,
         out_pool_grad,
-        small[2, 0],
-        small[2, 1],
-        small[2, 2],
+        *small[2:],
     )
 
 

time: 203 us -> 200 us (0.985)
  waiting for transfers between devices: 35.1 us -> 28.9 us
    ppermute x25, waiting for transfers between devices: 23.8 us -> 14.5 us  [img_swap(): return lax.ppermute(value, 'img', [(i, i ^ mask) for i in range(count)])]
    ppermute x11, waiting for transfers between devices: 11.2 us -> 14.4 us  [seq_swap(): return lax.ppermute(value, 'seq', [(0, 1), (1, 0)])]
    unnamed x74 -> x70, local copies, waits for them, and re-layouts: 7.01 us -> 9.15 us
  transfers between devices with their start and end apart: 36 -> 36, of which waited for: 16 -> 17; matrix products, arithmetic and copies ran while one was open for 1% -> 1% of each run, Pallas kernels for 42% -> 43%
where the time goes in v7:
time: 200 us; the launch traced here: 199 us
  Pallas kernels  117 us (58%)
  starting transfers between devices  37.6 us (19%)
  waiting for transfers between devices  28.9 us (14%)
  local copies, waits for them, and re-layouts  11.4 us (6%)
  between operations  2.89 us (1%)
    pallas_call x9, Pallas kernels, fold(): pl.pallas_call(functools.partial(fold_kernel, tuple(plan), tuple(gathers)...  31.1 us
    ppermute x25, starting transfers between devices, img_swap(): return lax.ppermute(value, 'img', [(i, i ^ mask) for i in range(count)])  22.9 us
    ppermute x11, starting transfers between devices, seq_swap(): return lax.ppermute(value, 'seq', [(0, 1), (1, 0)])  14.8 us
    ppermute x25, waiting for transfers between devices, img_swap(): return lax.ppermute(value, 'img', [(i, i ^ mask) for i in range(count)])  14.5 us
    ppermute x11, waiting for transfers between devices, seq_swap(): return lax.ppermute(value, 'seq', [(0, 1), (1, 0)])  14.4 us
    pallas_call x1, Pallas kernels, middle_call(): pl.pallas_call(middle_kernel, grid=(steps,), in_specs=[whole(rows, width)...  12.3 us
    pallas_call x1, Pallas kernels, attend_back(): pl.pallas_call(attend_back_kernel, grid=(pairs,), in_specs=[row_spec] * 6...  10.2 us
    pallas_call x2, Pallas kernels, front_call(): pl.pallas_call(functools.partial(front_kernel, count), grid=(3,), in_spec...  9.34 us
  transfers between devices with their start and end apart: 36, of which 17 were waited for; matrix products, arithmetic and copies ran while one was open for 1% of the time, Pallas kernels for 43%

profile of v7, /device:TPU:0, one launch (start us, length us, event | category | flops | bytes accessed | tf_op | source)
XLA Modules:
  0.0 199.1 jit_solution(8411043111434065159)
XLA Ops:
  0.7 3.1 %collective-permute-start = (bf16[256,768]{1,0:T(8,128)(2,1)}, bf16[256,768]{1,0:T(8,128)(2,1)S(1)}, u32[]{:S(2)}, u32[]{:S(2)}) collective-permute-start(bf16[256,768]{1,0:T(8,128)(2,1)} %bitcast.208), channel_id=1, source_target_pairs={{0,1},{1,0},{2,3},{3,2},{4,5},{5,4},{6,7},{7,6},{8,9},{9,8},{10,11... | collective-permute-start | bytes 1179656 | tf_op jit(solution)/shard_map/ppermute | solution.py:624
  5.2 5.0 %front.2 = (bf16[256,768]{1,0:T(8,128)(2,1)}, f32[256,768]{1,0:T(8,128)}, f32[256,1]{1,0:T(8,128)}, bf16[256,768]{1,0:T(8,128)(2,1)}, bf16[256,768]{1,0:T(8,128)(2,1)}, /*index=5*/bf16[256,768]{1,0:T(8,128)(2,1)}) custom-call(bf16[256,768]{1,0:T(8,128)(2,1)} %bitcast.209, f32[768]{0:T(1024)} %refs_1_.2, bf16[768,768]{1,0:T(8,128)(2,1)} %wq_ref.1, ...), custom_call_target="tpu_custom_call" | custom-call | flops 1024 | bytes 1024 | tf_op jit(solution)/shard_map/front/pallas_call | solution.py:110
  13.1 1.8 collective-permute-start.3
  14.9 4.3 %front.3 = (bf16[256,768]{1,0:T(8,128)(2,1)}, f32[256,768]{1,0:T(8,128)}, f32[256,1]{1,0:T(8,128)}, bf16[256,768]{1,0:T(8,128)(2,1)}, bf16[256,768]{1,0:T(8,128)(2,1)}) custom-call(bf16[256,768]{1,0:T(8,128)(2,1)} %copy-done.22, f32[768]{0:T(1024)} %refs_1_.2, bf16[768,768]{1,0:T(8,128)(2,1)} %wk_ref.1, bf16[768,768]{1,0:T(8,128)(2,1)} %wv_ref.1), custom_call_target="tpu_custom_call" | custom-call | flops 1024 | bytes 1024 | tf_op jit(solution)/shard_map/front/pallas_call | solution.py:110
  19.2 7.8 %attend.1 = (bf16[256,768]{1,0:T(8,128)(2,1)}, f32[6,256,2]{2,1,0:T(8,128)}) custom-call(bf16[256,768]{1,0:T(8,128)(2,1)} %get-tuple-element.201.q_ref, bf16[256,768]{1,0:T(8,128)(2,1)} %get-tuple-element.202.ka_ref, bf16[256,768]{1,0:T(8,128)(2,1)} %get-tuple-element.211.kb_ref, bf16[256,768]{1,0:T(8,128)(2,1)} %get-tuple-element.212.va_ref, ...), custom_call_target="tpu_custom_call" | custom-call | flops 1024 | bytes 1024 | tf_op jit(solution)/shard_map/attend/pallas_call | solution.py:467
  27.1 2.7 %collective-permute-start.5 = (f32[8,5,768]{2,1,0:T(8,128)S(1)}, f32[8,5,768]{2,1,0:T(8,128)S(1)}, u32[]{:S(2)}, u32[]{:S(2)}) collective-permute-start(f32[8,5,768]{2,1,0:T(8,128)S(1)} %pad_maximum_fusion.1), channel_id=1, source_target_pairs={{0,16},{2,18},{4,20},{6,22},{8,24},{10,26},{12,28},{14,30},{16,0},... | collective-permute-start | bytes 368648 | tf_op jit(solution)/shard_map/ppermute | solution.py:620
  31.7 12.3 %middle.1 = (f32[1,768]{1,0:T(1,128)}, f32[16,768]{1,0:T(8,128)}, bf16[256,768]{1,0:T(8,128)(2,1)}, f32[256,768]{1,0:T(8,128)}, f32[256,1]{1,0:T(8,128)}, /*inde...) custom-call(bf16[256,768]{1,0:T(8,128)(2,1)} %get-tuple-element.216., ...), custom_call_target="tpu_custom_call" | custom-call | flops 1024 | bytes 1024 | tf_op jit(solution)/shard_map/middle/pallas_call | solution.py:198
  46.4 2.1 %collective-permute-done.4.other_ref = f32[16,896]{1,0:T(8,128)S(1)} collective-permute-done((f32[16,896]{1,0:T(8,128)}, f32[16,896]{1,0:T(8,128)S(1)}, u32[]{:S(2)}, u32[]{:S(2)}) %collective-permute-start.4) | collective-permute-done | bytes 57376 | tf_op jit(solution)/shard_map/ppermute | solution.py:624
  49.0 5.8 %pool_back.1 = (f32[256,768]{1,0:T(8,128)}, bf16[256,768]{1,0:T(8,128)(2,1)}, f32[24,768]{1,0:T(8,128)}) custom-call(s32[5]{0:T(128)} %stack.23.place_ref, s32[1]{0:T(128)S(6)} %copy.54.count_ref, s32[1,80]{1,0:T(1,128)} %pairs_ref.1, f32[1]{0:T(128)} %bitcast.90.temp_ref, f32[1]{0:T(128)} %bitcast.91.bias_ref, f32[16,896]{1,0:T(8,128)} %get-tuple-element.223.own_ref, ...), custom_call_target="tpu_custom_call" | custom-call | flops 1024 | bytes 1024 | tf_op jit(solution)/shard_map/pool_back/pallas_call | solution.py:352
  56.4 4.4 %wgrad.1 = (bf16[2,2,8,96,384]{4,3,2,1,0:T(8,128)(2,1)}, bf16[2,2,8,96,384]{4,3,2,1,0:T(8,128)(2,1)}) custom-call(s32[5]{0:T(128)} %stack.23.place_ref, bf16[256,3072]{1,0:T(8,128)(2,1)} %get-tuple-element.222.left_ref, bf16[256,768]{1,0:T(8,128)(2,1)} %get-tuple-element.236.right_ref.grad_ref), custom_call_target="tpu_custom_call" | custom-call | flops 1024 | bytes 1024 | tf_op jit(solution)/shard_map/wgrad/pallas_call | solution.py:557
  63.0 8.6 %gelu_back.1 = (bf16[256,3072]{1,0:T(8,128)(2,1)}, bf16[2,2,8,48,768]{4,3,2,1,0:T(8,128)(2,1)}, bf16[2,2,8,48,768]{4,3,2,1,0:T(8,128)(2,1)}) custom-call(s32[5]{0:T(128)} %stack.23.place_ref, bf16[256,768]{1,0:T(8,128)(2,1)} %get-tuple-element.236.right_ref.grad_ref, bf16[3072,768]{1,0:T(8,128)(2,1)} %down_ref.3, f32[256,3072]{1,0:T(8,128)} %get-tuple-element.237.up_ref, ...), custom_call_target="tpu_custom_call" | custom-call | flops 1024 | bytes 1024 | tf_op jit(solution)/shard_map/gelu_back/pallas_call | solution.py:898
  73.2 3.6 %fold.9 = (bf16[8,96,384]{2,1,0:T(8,128)(2,1)}, bf16[2,4,96,384]{3,2,1,0:T(8,128)(2,1)}, f32[32,768]{1,0:T(8,128)}) custom-call(s32[5]{0:T(128)} %stack.23.place_ref, bf16[2,2,8,96,384]{4,3,2,1,0:T(8,128)(2,1)} %get-tuple-element.247.refs_0_, bf16[2,2,8,96,384]{4,3,2,1,0:T(8,128)(2,1)} %copy-done.2, bf16[2,2,4,2,96,384]{5,4,3,2,1,0:T(8,128)(2,1)} %bitcast.144, ...), custom_call_target="tpu_custom_call" | custom-call | flops 1024 | bytes 1024 | tf_op jit(solution)/shard_map/fold/pallas_call | solution.py:773
  79.1 7.4 %up_back.1 = (f32[256,768]{1,0:T(8,128)}, bf16[256,768]{1,0:T(8,128)(2,1)}, bf16[256,768]{1,0:T(8,128)(2,1)}) custom-call(bf16[256,3072]{1,0:T(8,128)(2,1)} %get-tuple-element.255.du_ref, bf16[768,3072]{1,0:T(8,128)(2,1)} %up_ref.3, f32[256,768]{1,0:T(8,128)} %get-tuple-element.256.unit_ref, f32[256,1]{1,0:T(8,128)} %get-tuple-element.257.inv_ref, ...), custom_call_target="tpu_custom_call" | custom-call | flops 1024 | bytes 1024 | tf_op jit(solution)/shard_map/up_back/pallas_call | solution.py:954
  86.7 6.0 %collective-permute-done.12 = bf16[8,96,384]{2,1,0:T(8,128)(2,1)S(1)} collective-permute-done((bf16[8,96,384]{2,1,0:T(8,128)(2,1)}, bf16[8,96,384]{2,1,0:T(8,128)(2,1)S(1)}, u32[]{:S(2)}, u32[]{:S(2)}) %collective-permute-start.12) | collective-permute-done | bytes 589856 | tf_op jit(solution)/shard_map/ppermute | solution.py:624
  94.6 4.2 %fold.10 = (bf16[2,4,48,768]{3,2,1,0:T(8,128)(2,1)}, bf16[8,48,768]{2,1,0:T(8,128)(2,1)}, bf16[4,96,384]{2,1,0:T(8,128)(2,1)}, bf16[4,96,384]{2,1,0:T(8,128)(2,1)}, f32[48,768]{1,0:T(8,128)}) custom-call(s32[5]{0:T(128)} %stack.23.place_ref, bf16[2,2,4,2,48,768]{5,4,3,2,1,0:T(8,128)(2,1)} %bitcast.126, bf16[2,2,4,2,48,768]{5,4,3,2,1,0:T(8,128)(2,1)} %bitcast.135, ...), custom_call_target="tpu_custom_call" | custom-call | flops 1024 | bytes 1024 | tf_op jit(solution)/shard_map/fold/pallas_call | solution.py:773
  102.6 10.2 %attend_back.1 = (bf16[256,768]{1,0:T(8,128)(2,1)}, bf16[512,768]{1,0:T(8,128)(2,1)}, bf16[512,768]{1,0:T(8,128)(2,1)}) custom-call(bf16[256,768]{1,0:T(8,128)(2,1)} %get-tuple-element.201.q_ref, bf16[256,768]{1,0:T(8,128)(2,1)} %get-tuple-element.202.ka_ref, bf16[256,768]{1,0:T(8,128)(2,1)} %get-tuple-element.211.kb_ref, ...), custom_call_target="tpu_custom_call" | custom-call | flops 1024 | bytes 1024 | tf_op jit(solution)/shard_map/attend_back/pallas_call | solution.py:515
  117.0 5.8 %wgrad_four.1 = (bf16[2,2,8,4,24,384]{5,4,3,2,1,0:T(8,128)(2,1)}, bf16[2,2,8,4,24,384]{5,4,3,2,1,0:T(8,128)(2,1)}) custom-call(s32[5]{0:T(128)} %stack.23.place_ref, bf16[256,768]{1,0:T(8,128)(2,1)} %get-tuple-element.220.na_ref, bf16[256,768]{1,0:T(8,128)(2,1)} %get-tuple-element.221.nb_ref, bf16[256,768]{1,0:T(8,128)(2,1)} %get-tuple-element.216.attended_ref.a_ref, ...), custom_call_target="tpu_custom_call" | custom-call | flops 1024 | bytes 1024 | tf_op jit(solution)/shard_map/wgrad_four/pallas_call | solution.py:603
  123.6 3.7 %fold.11 = (bf16[4,48,768]{2,1,0:T(8,128)(2,1)}, bf16[4,48,768]{2,1,0:T(8,128)(2,1)}, bf16[2,2,96,384]{3,2,1,0:T(8,128)(2,1)}, f32[80,768]{1,0:T(8,128)}) custom-call(s32[5]{0:T(128)} %stack.23.place_ref, bf16[2,2,4,2,48,768]{5,4,3,2,1,0:T(8,128)(2,1)} %bitcast.127, bf16[2,2,4,2,48,768]{5,4,3,2,1,0:T(8,128)(2,1)} %bitcast.136, ...), custom_call_target="tpu_custom_call" | custom-call | flops 1024 | bytes 1024 | tf_op jit(solution)/shard_map/fold/pallas_call | solution.py:773
  130.5 5.2 %parts_in.1 = (f32[256,768]{1,0:T(8,128)}, bf16[256,768]{1,0:T(8,128)(2,1)}) custom-call(bf16[256,768]{1,0:T(8,128)(2,1)} %get-tuple-element.304.dq_ref, bf16[512,768]{1,0:T(8,128)(2,1)} %get-tuple-element.286.dk_ref, bf16[512,768]{1,0:T(8,128)(2,1)} %get-tuple-element.287.dv_ref, bf16[768,768]{1,0:T(8,128)(2,1)} %wq_ref.1, bf16[768,768]{1,0:T(8,128)(2,1)} %wk_ref.1, ...), custom_call_target="tpu_custom_call" | custom-call | flops 1024 | bytes 1024 | tf_op jit(solution)/shard_map/parts_in/pallas_call | solution.py:987
  140.3 4.4 %fold.12 = (bf16[2,4,4,24,384]{4,3,2,1,0:T(8,128)(2,1)}, bf16[8,4,24,384]{3,2,1,0:T(8,128)(2,1)}, bf16[2,2,48,768]{3,2,1,0:T(8,128)(2,1)}, bf16[2,1,96,384]{3,2,1,0:T(8,128)(2,1)}, f32[144,768]{1,0:T(8,128)}) custom-call(s32[5]{0:T(128)} %stack.23.place_ref, bf16[2,2,4,2,4,24,384]{6,5,4,3,2,1,0:T(8,128)(2,1)} %bitcast.92, ...), custom_call_target="tpu_custom_call" | custom-call | flops 1024 | bytes 1024 | tf_op jit(solution)/shard_map/fold/pallas_call | solution.py:773
  147.6 4.2 %pool_weights.1 = (f32[48,384]{1,0:T(8,128)}, f32[48,384]{1,0:T(8,128)}, f32[48,384]{1,0:T(8,128)}, f32[48,384]{1,0:T(8,128)}, f32[3,128]{1,0:T(4,128)}) custom-call(s32[5]{0:T(128)} %stack.23.place_ref, f32[144,768]{1,0:T(8,128)} %get-tuple-element.325.rows_ref, f32[4,768]{1,0:T(4,128)} %vectors.1.vectors_ref.refs_56_, ...), custom_call_target="tpu_custom_call" | custom-call | flops 1024 | bytes 1024 | tf_op jit(solution)/shard_map/pool_weights/pallas_call | solution.py:424
  151.8 3.8 %collective-permute-done.27.refs_5_.refs_11_ = bf16[2,1,96,384]{3,2,1,0:T(8,128)(2,1)S(1)} collective-permute-done((bf16[2,1,96,384]{3,2,1,0:T(8,128)(2,1)}, bf16[2,1,96,384]{3,2,1,0:T(8,128)(2,1)S(1)}, u32[]{:S(2)}, u32[]{:S(2)}) %collective-permute-start.27) | collective-permute-done | bytes 147488 | tf_op jit(solution)/shard_map/ppermute | solution.py:620
  157.2 2.0 %collective-permute-done.24.refs_2_.refs_16_.refs_30_.refs_44_ = bf16[2,4,4,24,384]{4,3,2,1,0:T(8,128)(2,1)S(1)} collective-permute-done((bf16[2,4,4,24,384]{4,3,2,1,0:T(8,128)(2,1)}, bf16[2,4,4,24,384]{4,3,2,1,0:T(8,128)(2,1)S(1)}, u32[]{:S(2)}, u32[]{:S(2)}) %collective-permute-start.24) | collective-permute-done | bytes 589856 | tf_op jit(solution)/shard_map/ppermute | solution.py:620
  160.5 3.4 %fold.14 = (bf16[4,4,24,384]{3,2,1,0:T(8,128)(2,1)}, bf16[4,4,24,384]{3,2,1,0:T(8,128)(2,1)}, bf16[2,1,48,768]{3,2,1,0:T(8,128)(2,1)}) custom-call(s32[5]{0:T(128)} %stack.23.place_ref, bf16[2,2,4,2,4,24,384]{6,5,4,3,2,1,0:T(8,128)(2,1)} %bitcast.93, bf16[2,2,4,2,4,24,384]{6,5,4,3,2,1,0:T(8,128)(2,1)} %bitcast.110, bf16[2,4,4,24,384]{4,3,2,1,0:T(8,128)(2,1)} %copy-done.3, ...), custom_call_target="tpu_custom_call" | custom-call | flops 1024 | bytes 1024 | tf_op jit(solution)/shard_map/fold/pallas_call | solution.py:773
  167.3 2.7 %fold.13 = f32[192,384]{1,0:T(8,128)} custom-call(s32[5]{0:T(128)} %stack.23.place_ref, bf16[2,2,4,2,96,384]{5,4,3,2,1,0:T(8,128)(2,1)} %bitcast.151, bf16[2,2,4,2,96,384]{5,4,3,2,1,0:T(8,128)(2,1)} %bitcast.160, bf16[4,2,96,384]{3,2,1,0:T(8,128)(2,1)} %bitcast.192, bf16[4,96,384]{2,1,0:T(8,128)(2,1)} %copy-done.18, bf16[2,2,96,384]{3,2,1,0:T(8,128)(2,1)} %copy-done.14, ...), custom_call_target="tpu_custom_call" | custom-call | flops 1024 | bytes 1024 | tf_op jit(solution)/shard_map/fold/pallas_call | solution.py:773
  170.6 3.6 %collective-permute-done.30.refs_5_.refs_11_ = bf16[2,1,48,768]{3,2,1,0:T(8,128)(2,1)S(1)} collective-permute-done((bf16[2,1,48,768]{3,2,1,0:T(8,128)(2,1)}, bf16[2,1,48,768]{3,2,1,0:T(8,128)(2,1)S(1)}, u32[]{:S(2)}, u32[]{:S(2)}) %collective-permute-start.30) | collective-permute-done | bytes 147488 | tf_op jit(solution)/shard_map/ppermute | solution.py:620
  175.1 3.2 %fold.16 = (bf16[2,1,4,24,384]{4,3,2,1,0:T(8,128)(2,1)}, bf16[2,1,4,24,384]{4,3,2,1,0:T(8,128)(2,1)}, bf16[2,1,4,24,384]{4,3,2,1,0:T(8,128)(2,1)}) custom-call(s32[5]{0:T(128)} %stack.23.place_ref, bf16[2,2,1,4,2,4,24,384]{7,6,5,4,3,2,1,0:T(8,128)(2,1)} %bitcast.95, bf16[2,2,1,4,2,4,24,384]{7,6,5,4,3,2,1,0:T(8,128)(2,1)} %bitcast.112, ...), custom_call_target="tpu_custom_call" | custom-call | flops 1024 | bytes 1024 | tf_op jit(solution)/shard_map/fold/pallas_call | solution.py:773
  180.5 3.3 %collective-permute-start.34 = (bf16[2,1,4,24,384]{4,3,2,1,0:T(8,128)(2,1)}, bf16[2,1,4,24,384]{4,3,2,1,0:T(8,128)(2,1)S(1)}, u32[]{:S(2)}, u32[]{:S(2)}) collective-permute-start(bf16[2,1,4,24,384]{4,3,2,1,0:T(8,128)(2,1)} %get-tuple-element.362), channel_id=1, source_target_pairs={{0,24},{2,26},{4,28},{6,30},{8,16},{10,18},{12,20},{14,22},{16,8},... | collective-permute-start | bytes 442376 | tf_op jit(solution)/shard_map/ppermute | solution.py:620
  183.8 2.7 %fold.15.refs_58_ = f32[48,1536]{1,0:T(8,128)} custom-call(s32[5]{0:T(128)} %stack.23.place_ref, bf16[2,2,4,2,48,768]{5,4,3,2,1,0:T(8,128)(2,1)} %bitcast.133, bf16[2,2,4,2,48,768]{5,4,3,2,1,0:T(8,128)(2,1)} %bitcast.142, bf16[2,4,48,768]{3,2,1,0:T(8,128)(2,1)} %copy-done.10, bf16[4,48,768]{2,1,0:T(8,128)(2,1)} %copy-done.16, ...), custom_call_target="tpu_custom_call" | custom-call | flops 1024 | bytes 1024 | tf_op jit(solution)/shard_map/fold/pallas_call | solution.py:773
  187.3 3.1 %own_in.1 = f32[256,768]{1,0:T(8,128)} custom-call(f32[256,768]{1,0:T(8,128)} %get-tuple-element.312.own_ref, bf16[256,768]{1,0:T(8,128)(2,1)} %copy-done.23, f32[256,768]{1,0:T(8,128)} %get-tuple-element.357.unit_ref, f32[256,1]{1,0:T(8,128)} %get-tuple-element.358.inv_ref, f32[4,768]{1,0:T(4,128)} %vectors.1.vectors_ref.refs_56_, ...), custom_call_target="tpu_custom_call" | custom-call | flops 1024 | bytes 1024 | tf_op jit(solution)/shard_map/own_in/pallas_call | solution.py:1006
  191.1 3.0 %fold.17 = (f32[48,384]{1,0:T(8,128)}, f32[48,384]{1,0:T(8,128)}, f32[48,384]{1,0:T(8,128)}, f32[48,384]{1,0:T(8,128)}, f32[2,128]{1,0:T(2,128)}) custom-call(s32[5]{0:T(128)} %stack.23.place_ref, bf16[2,2,4,2,4,24,384]{6,5,4,3,2,1,0:T(8,128)(2,1)} %bitcast.101, bf16[2,2,4,2,4,24,384]{6,5,4,3,2,1,0:T(8,128)(2,1)} %bitcast.118, ...), custom_call_target="tpu_custom_call" | custom-call | flops 1024 | bytes 1024 | tf_op jit(solution)/shard_map/fold/pallas_call | solution.py:773
  195.3 2.6 %collective-permute-done.35 = f32[2,128]{1,0:T(2,128)S(1)} collective-permute-done((f32[2,128]{1,0:T(2,128)}, f32[2,128]{1,0:T(2,128)S(1)}, u32[]{:S(2)}, u32[]{:S(2)}) %collective-permute-start.35) | collective-permute-done | bytes 1056 | tf_op jit(solution)/shard_map/ppermute | solution.py:624
  (142 shorter events, 49.8 us)
Async XLA Ops:
  0.7 12.4 %collective-permute-start = (bf16[256,768]{1,0:T(8,128)(2,1)}, bf16[256,768]{1,0:T(8,128)(2,1)S(1)}, u32[]{:S(2)}, u32[]{:S(2)}) collective-permute-start(bf16[256,768]{1,0:T(8,128)(2,1)} %bitcast.208), channel_id=1, source_target_pairs={{0,1},{1,0},{2,3},{3,2},{4,5},{5,4},{6,7},{7,6},{8,9},{9,8},{10,11... | collective-permute-start | bytes 1179656 | tf_op jit(solution)/shard_map/ppermute | solution.py:624
  3.7 7.1 %collective-permute-start.1 = (f32[1,5,768]{2,1,0:T(8,128)}, f32[1,5,768]{2,1,0:T(8,128)S(1)}, u32[]{:S(2)}, u32[]{:S(2)}) collective-permute-start(f32[1,5,768]{2,1,0:T(8,128)} %bitcast.212), channel_id=1, source_target_pairs={{0,4},{2,6},{4,0},{6,2},{8,12},{10,14},{12,8},{14,10},{16,20},{18,... | collective-permute-start | bytes 46088 | tf_op jit(solution)/shard_map/ppermute | solution.py:620
  13.1 14.0 %collective-permute-start.3 = (f32[4,5,768]{2,1,0:T(8,128)S(1)}, f32[4,5,768]{2,1,0:T(8,128)S(1)}, u32[]{:S(2)}, u32[]{:S(2)}) collective-permute-start(f32[4,5,768]{2,1,0:T(8,128)S(1)} %pad_maximum_fusion.2), channel_id=1, source_target_pairs={{0,8},{2,10},{4,12},{6,14},{8,0},{10,2},{12,4},{14,6},{16,24},{18,... | collective-permute-start | bytes 184328 | tf_op jit(solution)/shard_map/ppermute | solution.py:620
  27.1 18.5 %collective-permute-start.5 = (f32[8,5,768]{2,1,0:T(8,128)S(1)}, f32[8,5,768]{2,1,0:T(8,128)S(1)}, u32[]{:S(2)}, u32[]{:S(2)}) collective-permute-start(f32[8,5,768]{2,1,0:T(8,128)S(1)} %pad_maximum_fusion.1), channel_id=1, source_target_pairs={{0,16},{2,18},{4,20},{6,22},{8,24},{10,26},{12,28},{14,30},{16,0},... | collective-permute-start | bytes 368648 | tf_op jit(solution)/shard_map/ppermute | solution.py:620
  54.9 5.9 %collective-permute-start.6 = (f32[24,768]{1,0:T(8,128)}, f32[24,768]{1,0:T(8,128)S(1)}, u32[]{:S(2)}, u32[]{:S(2)}) collective-permute-start(f32[24,768]{1,0:T(8,128)} %get-tuple-element.235.refs_4_), channel_id=1, source_target_pairs={{0,1},{1,0},{2,3},{3,2},{4,5},{5,4},{6,7},{7,6},{8,9},{9,8},{10,11... | collective-permute-start | bytes 221192 | tf_op jit(solution)/shard_map/ppermute | solution.py:624
  60.8 10.8 %collective-permute-start.7 = (bf16[2,2,8,96,384]{4,3,2,1,0:T(8,128)(2,1)}, bf16[2,2,8,96,384]{4,3,2,1,0:T(8,128)(2,1)S(1)}, u32[]{:S(2)}, u32[]{:S(2)}) collective-permute-start(bf16[2,2,8,96,384]{4,3,2,1,0:T(8,128)(2,1)} %get-tuple-element.242), channel_id=1, source_target_pairs={{0,2},{2,0},{4,6},{6,4},{8,10},{10,8},{12,14},{14,12},{16,18},{18,... | collective-permute-start | bytes 7077896 | tf_op jit(solution)/shard_map/ppermute | solution.py:620
  60.9 10.7 %collective-permute-start.8 = (f32[24,768]{1,0:T(8,128)}, f32[24,768]{1,0:T(8,128)S(1)}, u32[]{:S(2)}, u32[]{:S(2)}) collective-permute-start(f32[24,768]{1,0:T(8,128)} %get-tuple-element.235.refs_4_), channel_id=1, source_target_pairs={{0,4},{2,6},{4,0},{6,2},{8,12},{10,14},{12,8},{14,10},{16,20},{18,... | collective-permute-start | bytes 221192 | tf_op jit(solution)/shard_map/ppermute | solution.py:620
  62.4 9.2 %collective-permute-start.9 = (f32[24,768]{1,0:T(8,128)S(1)}, f32[24,768]{1,0:T(8,128)S(1)}, u32[]{:S(2)}, u32[]{:S(2)}) collective-permute-start(f32[24,768]{1,0:T(8,128)S(1)} %collective-permute-done.6.refs_6_), channel_id=1, source_target_pairs={{0,4},{2,6},{4,0},{6,2},{8,12},{10,14},{12,8},{14,10},{16,20},{18,... | collective-permute-start | bytes 221192 | tf_op jit(solution)/shard_map/ppermute | solution.py:620
  76.8 16.2 %collective-permute-start.10 = (bf16[2,2,8,48,768]{4,3,2,1,0:T(8,128)(2,1)}, bf16[2,2,8,48,768]{4,3,2,1,0:T(8,128)(2,1)S(1)}, u32[]{:S(2)}, u32[]{:S(2)}) collective-permute-start(bf16[2,2,8,48,768]{4,3,2,1,0:T(8,128)(2,1)} %get-tuple-element.260), channel_id=1, source_target_pairs={{0,2},{2,0},{4,6},{6,4},{8,10},{10,8},{12,14},{14,12},{16,18},{18,... | collective-permute-start | bytes 7077896 | tf_op jit(solution)/shard_map/ppermute | solution.py:620
  76.8 16.0 %collective-permute-start.12 = (bf16[8,96,384]{2,1,0:T(8,128)(2,1)}, bf16[8,96,384]{2,1,0:T(8,128)(2,1)S(1)}, u32[]{:S(2)}, u32[]{:S(2)}) collective-permute-start(bf16[8,96,384]{2,1,0:T(8,128)(2,1)} %get-tuple-element.262), channel_id=1, source_target_pairs={{0,1},{1,0},{2,3},{3,2},{4,5},{5,4},{6,7},{7,6},{8,9},{9,8},{10,11... | collective-permute-start | bytes 1769480 | tf_op jit(solution)/shard_map/ppermute | solution.py:624
  77.3 15.7 %collective-permute-start.13 = (bf16[2,4,96,384]{3,2,1,0:T(8,128)(2,1)}, bf16[2,4,96,384]{3,2,1,0:T(8,128)(2,1)S(1)}, u32[]{:S(2)}, u32[]{:S(2)}) collective-permute-start(bf16[2,4,96,384]{3,2,1,0:T(8,128)(2,1)} %get-tuple-element.263), channel_id=1, source_target_pairs={{0,4},{2,6},{4,0},{6,2},{8,12},{10,14},{12,8},{14,10},{16,20},{18,... | collective-permute-start | bytes 1769480 | tf_op jit(solution)/shard_map/ppermute | solution.py:620
  78.8 8.0 %collective-permute-start.11 = (f32[32,768]{1,0:T(8,128)}, f32[32,768]{1,0:T(8,128)}, u32[]{:S(2)}, u32[]{:S(2)}) collective-permute-start(f32[32,768]{1,0:T(8,128)} %get-tuple-element.261.refs_10_), channel_id=1, source_target_pairs={{0,16},{2,18},{4,20},{6,22},{8,24},{10,26},{12,28},{14,30},{16,0},... | collective-permute-start | bytes 294920 | tf_op jit(solution)/shard_map/ppermute | solution.py:620
  98.8 15.2 %collective-permute-start.14 = (bf16[2,4,48,768]{3,2,1,0:T(8,128)(2,1)}, bf16[2,4,48,768]{3,2,1,0:T(8,128)(2,1)S(1)}, u32[]{:S(2)}, u32[]{:S(2)}) collective-permute-start(bf16[2,4,48,768]{3,2,1,0:T(8,128)(2,1)} %get-tuple-element.280), channel_id=1, source_target_pairs={{0,4},{2,6},{4,0},{6,2},{8,12},{10,14},{12,8},{14,10},{16,20},{18,... | collective-permute-start | bytes 1769480 | tf_op jit(solution)/shard_map/ppermute | solution.py:620
  100.3 14.8 %collective-permute-start.15 = (bf16[8,48,768]{2,1,0:T(8,128)(2,1)}, bf16[8,48,768]{2,1,0:T(8,128)(2,1)S(1)}, u32[]{:S(2)}, u32[]{:S(2)}) collective-permute-start(bf16[8,48,768]{2,1,0:T(8,128)(2,1)} %get-tuple-element.281), channel_id=1, source_target_pairs={{0,1},{1,0},{2,3},{3,2},{4,5},{5,4},{6,7},{7,6},{8,9},{9,8},{10,11... | collective-permute-start | bytes 1769480 | tf_op jit(solution)/shard_map/ppermute | solution.py:624
  101.8 11.0 %collective-permute-start.16 = (f32[48,768]{1,0:T(8,128)}, f32[48,768]{1,0:T(8,128)S(1)}, u32[]{:S(2)}, u32[]{:S(2)}) collective-permute-start(f32[48,768]{1,0:T(8,128)} %get-tuple-element.282.refs_14_), channel_id=1, source_target_pairs={{0,8},{2,10},{4,12},{6,14},{8,0},{10,2},{12,4},{14,6},{16,24},{18,... | collective-permute-start | bytes 442376 | tf_op jit(solution)/shard_map/ppermute | solution.py:620
  115.1 7.6 %collective-permute-start.17 = (bf16[4,96,384]{2,1,0:T(8,128)(2,1)S(1)}, bf16[4,96,384]{2,1,0:T(8,128)(2,1)S(1)}, u32[]{:S(2)}, u32[]{:S(2)}) collective-permute-start(bf16[4,96,384]{2,1,0:T(8,128)(2,1)S(1)} %copy-done.34), channel_id=1, source_target_pairs={{0,4},{2,6},{4,0},{6,2},{8,12},{10,14},{12,8},{14,10},{16,20},{18,... | collective-permute-start | bytes 884744 | tf_op jit(solution)/shard_map/ppermute | solution.py:620
  115.7 7.2 %collective-permute-start.18 = (bf16[4,96,384]{2,1,0:T(8,128)(2,1)S(1)}, bf16[4,96,384]{2,1,0:T(8,128)(2,1)S(1)}, u32[]{:S(2)}, u32[]{:S(2)}) collective-permute-start(bf16[4,96,384]{2,1,0:T(8,128)(2,1)S(1)} %copy-done.33), channel_id=1, source_target_pairs={{0,1},{1,0},{2,3},{3,2},{4,5},{5,4},{6,7},{7,6},{8,9},{9,8},{10,11... | collective-permute-start | bytes 884744 | tf_op jit(solution)/shard_map/ppermute | solution.py:624
  127.3 11.5 %collective-permute-start.19 = (bf16[2,2,8,4,24,384]{5,4,3,2,1,0:T(8,128)(2,1)}, bf16[2,2,8,4,24,384]{5,4,3,2,1,0:T(8,128)(2,1)S(1)}, u32[]{:S(2)}, u32[]{:S(2)}) collective-permute-start(bf16[2,2,8,4,24,384]{5,4,3,2,1,0:T(8,128)(2,1)} %get-tuple-element.307), channel_id=1, source_target_pairs={{0,2},{2,0},{4,6},{6,4},{8,10},{10,8},{12,14},{14,12},{16,18},{18,... | collective-permute-start | bytes 7077896 | tf_op jit(solution)/shard_map/ppermute | solution.py:620
  127.4 9.6 %collective-permute-start.20 = (bf16[4,48,768]{2,1,0:T(8,128)(2,1)}, bf16[4,48,768]{2,1,0:T(8,128)(2,1)S(1)}, u32[]{:S(2)}, u32[]{:S(2)}) collective-permute-start(bf16[4,48,768]{2,1,0:T(8,128)(2,1)} %get-tuple-element.308), channel_id=1, source_target_pairs={{0,1},{1,0},{2,3},{3,2},{4,5},{5,4},{6,7},{7,6},{8,9},{9,8},{10,11... | collective-permute-start | bytes 884744 | tf_op jit(solution)/shard_map/ppermute | solution.py:624
  128.4 9.3 %collective-permute-start.21 = (bf16[4,48,768]{2,1,0:T(8,128)(2,1)}, bf16[4,48,768]{2,1,0:T(8,128)(2,1)S(1)}, u32[]{:S(2)}, u32[]{:S(2)}) collective-permute-start(bf16[4,48,768]{2,1,0:T(8,128)(2,1)} %get-tuple-element.309), channel_id=1, source_target_pairs={{0,4},{2,6},{4,0},{6,2},{8,12},{10,14},{12,8},{14,10},{16,20},{18,... | collective-permute-start | bytes 884744 | tf_op jit(solution)/shard_map/ppermute | solution.py:620
  129.8 9.0 %collective-permute-start.22 = (bf16[2,2,96,384]{3,2,1,0:T(8,128)(2,1)}, bf16[2,2,96,384]{3,2,1,0:T(8,128)(2,1)S(1)}, u32[]{:S(2)}, u32[]{:S(2)}) collective-permute-start(bf16[2,2,96,384]{3,2,1,0:T(8,128)(2,1)} %get-tuple-element.310), channel_id=1, source_target_pairs={{0,8},{2,10},{4,12},{6,14},{8,0},{10,2},{12,4},{14,6},{16,24},{18,... | collective-permute-start | bytes 884744 | tf_op jit(solution)/shard_map/ppermute | solution.py:620
  144.7 14.5 %collective-permute-start.24 = (bf16[2,4,4,24,384]{4,3,2,1,0:T(8,128)(2,1)}, bf16[2,4,4,24,384]{4,3,2,1,0:T(8,128)(2,1)S(1)}, u32[]{:S(2)}, u32[]{:S(2)}) collective-permute-start(bf16[2,4,4,24,384]{4,3,2,1,0:T(8,128)(2,1)} %get-tuple-element.332), channel_id=1, source_target_pairs={{0,4},{2,6},{4,0},{6,2},{8,12},{10,14},{12,8},{14,10},{16,20},{18,... | collective-permute-start | bytes 1769480 | tf_op jit(solution)/shard_map/ppermute | solution.py:620
  145.4 14.2 %collective-permute-start.25 = (bf16[8,4,24,384]{3,2,1,0:T(8,128)(2,1)}, bf16[8,4,24,384]{3,2,1,0:T(8,128)(2,1)S(1)}, u32[]{:S(2)}, u32[]{:S(2)}) collective-permute-start(bf16[8,4,24,384]{3,2,1,0:T(8,128)(2,1)} %get-tuple-element.333), channel_id=1, source_target_pairs={{0,1},{1,0},{2,3},{3,2},{4,5},{5,4},{6,7},{7,6},{8,9},{9,8},{10,11... | collective-permute-start | bytes 1769480 | tf_op jit(solution)/shard_map/ppermute | solution.py:624
  146.5 10.8 %collective-permute-start.26 = (bf16[2,2,48,768]{3,2,1,0:T(8,128)(2,1)}, bf16[2,2,48,768]{3,2,1,0:T(8,128)(2,1)S(1)}, u32[]{:S(2)}, u32[]{:S(2)}) collective-permute-start(bf16[2,2,48,768]{3,2,1,0:T(8,128)(2,1)} %get-tuple-element.334), channel_id=1, source_target_pairs={{0,8},{2,10},{4,12},{6,14},{8,0},{10,2},{12,4},{14,6},{16,24},{18,... | collective-permute-start | bytes 884744 | tf_op jit(solution)/shard_map/ppermute | solution.py:620
  147.2 8.4 %collective-permute-start.27 = (bf16[2,1,96,384]{3,2,1,0:T(8,128)(2,1)}, bf16[2,1,96,384]{3,2,1,0:T(8,128)(2,1)S(1)}, u32[]{:S(2)}, u32[]{:S(2)}) collective-permute-start(bf16[2,1,96,384]{3,2,1,0:T(8,128)(2,1)} %get-tuple-element.335), channel_id=1, source_target_pairs={{0,16},{2,18},{4,20},{6,22},{8,24},{10,26},{12,28},{14,30},{16,0},... | collective-permute-start | bytes 442376 | tf_op jit(solution)/shard_map/ppermute | solution.py:620
  163.9 10.3 %collective-permute-start.28 = (bf16[4,4,24,384]{3,2,1,0:T(8,128)(2,1)}, bf16[4,4,24,384]{3,2,1,0:T(8,128)(2,1)S(1)}, u32[]{:S(2)}, u32[]{:S(2)}) collective-permute-start(bf16[4,4,24,384]{3,2,1,0:T(8,128)(2,1)} %get-tuple-element.345), channel_id=1, source_target_pairs={{0,1},{1,0},{2,3},{3,2},{4,5},{5,4},{6,7},{7,6},{8,9},{9,8},{10,11... | collective-permute-start | bytes 884744 | tf_op jit(solution)/shard_map/ppermute | solution.py:624
  165.0 9.2 %collective-permute-start.29 = (bf16[4,4,24,384]{3,2,1,0:T(8,128)(2,1)}, bf16[4,4,24,384]{3,2,1,0:T(8,128)(2,1)S(1)}, u32[]{:S(2)}, u32[]{:S(2)}) collective-permute-start(bf16[4,4,24,384]{3,2,1,0:T(8,128)(2,1)} %get-tuple-element.346), channel_id=1, source_target_pairs={{0,4},{2,6},{4,0},{6,2},{8,12},{10,14},{12,8},{14,10},{16,20},{18,... | collective-permute-start | bytes 884744 | tf_op jit(solution)/shard_map/ppermute | solution.py:620
  166.4 7.8 %collective-permute-start.30 = (bf16[2,1,48,768]{3,2,1,0:T(8,128)(2,1)}, bf16[2,1,48,768]{3,2,1,0:T(8,128)(2,1)S(1)}, u32[]{:S(2)}, u32[]{:S(2)}) collective-permute-start(bf16[2,1,48,768]{3,2,1,0:T(8,128)(2,1)} %get-tuple-element.347), channel_id=1, source_target_pairs={{0,16},{2,18},{4,20},{6,22},{8,24},{10,26},{12,28},{14,30},{16,0},... | collective-permute-start | bytes 442376 | tf_op jit(solution)/shard_map/ppermute | solution.py:620
  178.3 8.2 %collective-permute-start.31 = (bf16[256,768]{1,0:T(8,128)(2,1)S(1)}, bf16[256,768]{1,0:T(8,128)(2,1)S(1)}, u32[]{:S(2)}, u32[]{:S(2)}) collective-permute-start(bf16[256,768]{1,0:T(8,128)(2,1)S(1)} %copy-done.32), channel_id=1, source_target_pairs={{0,1},{1,0},{2,3},{3,2},{4,5},{5,4},{6,7},{7,6},{8,9},{9,8},{10,11... | collective-permute-start | bytes 1179656 | tf_op jit(solution)/shard_map/ppermute | solution.py:624
  179.4 11.0 %collective-permute-start.32 = (bf16[2,1,4,24,384]{4,3,2,1,0:T(8,128)(2,1)}, bf16[2,1,4,24,384]{4,3,2,1,0:T(8,128)(2,1)S(1)}, u32[]{:S(2)}, u32[]{:S(2)}) collective-permute-start(bf16[2,1,4,24,384]{4,3,2,1,0:T(8,128)(2,1)} %get-tuple-element.360), channel_id=1, source_target_pairs={{0,8},{2,10},{4,12},{6,14},{8,0},{10,2},{12,4},{14,6},{16,24},{18,... | collective-permute-start | bytes 442376 | tf_op jit(solution)/shard_map/ppermute | solution.py:620
  179.4 11.0 %collective-permute-start.33 = (bf16[2,1,4,24,384]{4,3,2,1,0:T(8,128)(2,1)}, bf16[2,1,4,24,384]{4,3,2,1,0:T(8,128)(2,1)S(1)}, u32[]{:S(2)}, u32[]{:S(2)}) collective-permute-start(bf16[2,1,4,24,384]{4,3,2,1,0:T(8,128)(2,1)} %get-tuple-element.361), channel_id=1, source_target_pairs={{0,16},{2,18},{4,20},{6,22},{8,24},{10,26},{12,28},{14,30},{16,0},... | collective-permute-start | bytes 442376 | tf_op jit(solution)/shard_map/ppermute | solution.py:620
  180.5 9.9 %collective-permute-start.34 = (bf16[2,1,4,24,384]{4,3,2,1,0:T(8,128)(2,1)}, bf16[2,1,4,24,384]{4,3,2,1,0:T(8,128)(2,1)S(1)}, u32[]{:S(2)}, u32[]{:S(2)}) collective-permute-start(bf16[2,1,4,24,384]{4,3,2,1,0:T(8,128)(2,1)} %get-tuple-element.362), channel_id=1, source_target_pairs={{0,24},{2,26},{4,28},{6,30},{8,16},{10,18},{12,20},{14,22},{16,8},... | collective-permute-start | bytes 442376 | tf_op jit(solution)/shard_map/ppermute | solution.py:620
  (39 other events, 144.5 us)

commit v8 on v7

--- a/solution.py
+++ b/solution.py
@@ -656,7 +656,7 @@
     return lambda p: 1 - ((p[4] >> bit) & 1)
 
 
-def fold_kernel(plan, gathers, products, place_ref, *refs):
+def last_fold_kernel(plan, gathers, products, place_ref, *refs):
     count = sum(sum(slots) for slots, _ in plan)
     count += sum(1 + others for others, _ in gathers)
     if products:
@@ -724,7 +724,7 @@
             sums[row : row + 1] = jnp.sum(jnp.where(eye, column / gain, 0.0), axis=0, keepdims=True)
 
 
-def fold(place, outputs, dtype, notes=(), products=(), vectors=None):
+def last_fold(place, outputs, dtype, notes=(), products=(), vectors=None):
     arrays, specs, plan, shapes, gathers = [], [], [], [], []
     for slots, join in outputs:
         counts = []
@@ -772,13 +772,146 @@
         shapes.append(((2, 128), f32))
     return pl.pallas_call(
         functools.partial(
-            fold_kernel, tuple(plan), tuple(gathers), tuple((c, o) for c, o, _ in products)
+            last_fold_kernel, tuple(plan), tuple(gathers), tuple((c, o) for c, o, _ in products)
         ),
         grid_spec=pltpu.PrefetchScalarGridSpec(
             num_scalar_prefetch=1,
             grid=(1,),
             in_specs=specs,
             out_specs=[whole(t) for t, _ in shapes],
+        ),
+        out_shape=[jax.ShapeDtypeStruct(t, d) for t, d in shapes],
+        cost_estimate=light,
+        name="last_fold",
+    )(place, *arrays)
+
+
+def fold_kernel(plan, gathers, place_ref, *refs):
+    count = sum(len(picks) for slots, _ in plan for picks in slots)
+    refs = list(refs)
+
+    def next_refs(number):
+        taken = refs[:number]
+        del refs[:number]
+        return taken
+
+    parts = next_refs(count)
+    note_refs = next_refs(sum(1 + more for more, _ in gathers))
+    outs = next_refs(len(plan))
+    small_outs = next_refs(len(gathers))
+    buffers = next_refs(count)
+    note_buffers = next_refs(len(note_refs))
+    totals = next_refs(len(plan))
+    note_totals = next_refs(len(gathers))
+    in_sems, out_sems = refs
+
+    copies = []
+    for slots, _ in plan:
+        for slot in slots:
+            for picks in slot:
+                n = len(copies)
+                where = tuple(slice(None) if c is None else c(place_ref) for c in picks)
+                copies.append(
+                    pltpu.make_async_copy(parts[n].at[where], buffers[n], in_sems.at[n])
+                )
+    for n, ref in enumerate(note_refs):
+        copies.append(pltpu.make_async_copy(ref, note_buffers[n], in_sems.at[count + n]))
+    for copy in copies:
+        copy.start()
+
+    small = iter(small_outs)
+    n = 0
+    leaving = []
+    for at_out, (slots, join) in enumerate(plan):
+        out = totals[at_out]
+        start = 0
+        for at_slot, slot in enumerate(slots):
+            total = None
+            for _ in slot:
+                copies[n].wait()
+                part = buffers[n][...].astype(f32)
+                total = part if total is None else total + part
+                n += 1
+            total = total.astype(out.dtype)
+            if join is None:
+                out[...] = total
+            elif join == "stack":
+                out[at_slot] = total
+            elif join == "rows":
+                size = total.shape[0]
+                out[start : start + size] = total
+                start += size
+            else:
+                size = total.shape[1]
+                out[:, start : start + size] = total
+                start += size
+        leaving.append(pltpu.make_async_copy(out, outs[at_out], out_sems.at[at_out]))
+        leaving[-1].start()
+
+    for at_note, (more, gather) in enumerate(gathers):
+        own, *rest = note_buffers[n - count : n - count + 1 + more]
+        for _ in range(1 + more):
+            copies[n].wait()
+            n += 1
+        out = note_totals[at_note]
+        rows = own.shape[0]
+        sums = min(TOP, rows)
+        total = own[:sums]
+        for other in rest:
+            total = total + other[:sums]
+        out[:sums] = total
+        if rows > sums:
+            out[sums:rows] = own[sums:]
+        if gather:
+            out[rows:] = rest[0][sums:]
+        leaving.append(
+            pltpu.make_async_copy(out, next(small), out_sems.at[len(plan) + at_note])
+        )
+        leaving[-1].start()
+
+    for copy in leaving:
+        copy.wait()
+
+
+def fold(place, outputs, dtype, notes=()):
+    arrays, buffers, plan, shapes, gathers = [], [], [], [], []
+    for slots, join in outputs:
+        picked = []
+        for slot in slots:
+            picked.append([])
+            for array, picks in slot:
+                picks = picks + (None,) * (array.ndim - len(picks))
+                shape = tuple(d for d, choose in zip(array.shape, picks) if choose is None)
+                arrays.append(array)
+                buffers.append(pltpu.VMEM(shape, array.dtype))
+                picked[-1].append(picks)
+        plan.append((picked, join))
+        if join == "stack":
+            shape = (len(slots), *shape)
+        elif join == "rows":
+            shape = (len(slots) * shape[0], *shape[1:])
+        elif join == "columns":
+            shape = (shape[0], len(slots) * shape[1])
+        shapes.append((shape, dtype))
+    far = pl.BlockSpec(memory_space=pltpu.HBM)
+    specs = [far] * len(arrays)
+    for own, others, gather in notes:
+        rows, width = own.shape
+        arrays += [own, *others]
+        specs += [far] * (1 + len(others))
+        buffers += [pltpu.VMEM(own.shape, f32)] * (1 + len(others))
+        gathers.append((len(others), gather))
+        shapes.append(((2 * rows - TOP if gather else rows, width), f32))
+    totals = [pltpu.VMEM(t, d) for t, d in shapes]
+    sems = [pltpu.SemaphoreType.DMA((max(len(v), 1),)) for v in (arrays, shapes)]
+    return pl.pallas_call(
+        functools.partial(fold_kernel, plan, gathers),
+        grid_spec=pltpu.PrefetchScalarGridSpec(
+            num_scalar_prefetch=1,
+            grid=(1,),
+            in_specs=specs,
+            out_specs=[far] * len(shapes),
+            scratch_shapes=buffers + totals + sems,
         ),
         out_shape=[jax.ShapeDtypeStruct(t, d) for t, d in shapes],
         cost_estimate=light,
@@ -1241,7 +1374,7 @@
     input_grad, *four_in = step(input_grad, *four_in)
     take(four_a, four_b, four_in, 2)
     finish(place, four_a, four_b)
-    query_weight_grad, key_weight_grad, value_weight_grad, output_grad, gains = fold(
+    query_weight_grad, key_weight_grad, value_weight_grad, output_grad, gains = last_fold(
         place,
         [([four_a.whole(m), four_b.whole(m)], "rows") for m in range(4)],
         f32,
@@ -1250,7 +1383,7 @@
         ],
         vectors=vectors,
     )
-    gains = gains + seq_swap(gains)
+    gains_in = seq_swap(gains)
     return (
         block_out,
         input_grad[None],
@@ -1260,8 +1393,8 @@
         output_grad,
         up_weight_grad,
         down_grad,
-        gains[FIRST, :block],
-        gains[SECOND, :block],
+        gains[FIRST, :block] + gains_in[FIRST, :block],
+        gains[SECOND, :block] + gains_in[SECOND, :block],
         small[0],
         small[1],
         query_pool_grad,

time: 200 us -> 199 us (level)
  Pallas kernels: 117 us -> 115 us
where the time goes in v8:
time: 199 us; the launch traced here: 198 us
  Pallas kernels  115 us (58%)
  starting transfers between devices  37.9 us (19%)
  waiting for transfers between devices  28.6 us (14%)
  local copies, waits for them, and re-layouts  10.9 us (5%)
  between operations  2.99 us (2%)
  other arithmetic  2.11 us (1%)
    pallas_call x8, Pallas kernels, fold(): pl.pallas_call(functools.partial(fold_kernel, plan, gathers), grid_spec=p...  26.7 us
    ppermute x25, starting transfers between devices, img_swap(): return lax.ppermute(value, 'img', [(i, i ^ mask) for i in range(count)])  23 us
    ppermute x11, starting transfers between devices, seq_swap(): return lax.ppermute(value, 'seq', [(0, 1), (1, 0)])  14.9 us
    ppermute x25, waiting for transfers between devices, img_swap(): return lax.ppermute(value, 'img', [(i, i ^ mask) for i in range(count)])  14.3 us
    ppermute x11, waiting for transfers between devices, seq_swap(): return lax.ppermute(value, 'seq', [(0, 1), (1, 0)])  14.2 us
    pallas_call x1, Pallas kernels, middle_call(): pl.pallas_call(middle_kernel, grid=(steps,), in_specs=[whole(rows, width)...  12.3 us
    pallas_call x1, Pallas kernels, attend_back(): pl.pallas_call(attend_back_kernel, grid=(pairs,), in_specs=[row_spec] * 6...  10.2 us
    pallas_call x2, Pallas kernels, front_call(): pl.pallas_call(functools.partial(front_kernel, count), grid=(3,), in_spec...  9.34 us
  transfers between devices with their start and end apart: 36, of which 17 were waited for; matrix products, arithmetic and copies ran while one was open for 1% of the time, Pallas kernels for 43%

profile of v8, /device:TPU:0, one launch (start us, length us, event | category | flops | bytes accessed | tf_op | source)
XLA Modules:
  0.0 197.7 jit_solution(10536033682199249489)
XLA Ops:
  0.7 3.1 %collective-permute-start = (bf16[256,768]{1,0:T(8,128)(2,1)}, bf16[256,768]{1,0:T(8,128)(2,1)S(1)}, u32[]{:S(2)}, u32[]{:S(2)}) collective-permute-start(bf16[256,768]{1,0:T(8,128)(2,1)} %bitcast.208), channel_id=1, source_target_pairs={{0,1},{1,0},{2,3},{3,2},{4,5},{5,4},{6,7},{7,6},{8,9},{9,8},{10,11... | collective-permute-start | bytes 1179656 | tf_op jit(solution)/shard_map/ppermute | solution.py:624
  5.2 5.0 %front.2 = (bf16[256,768]{1,0:T(8,128)(2,1)}, f32[256,768]{1,0:T(8,128)}, f32[256,1]{1,0:T(8,128)}, bf16[256,768]{1,0:T(8,128)(2,1)}, bf16[256,768]{1,0:T(8,128)(2,1)}, /*index=5*/bf16[256,768]{1,0:T(8,128)(2,1)}) custom-call(bf16[256,768]{1,0:T(8,128)(2,1)} %bitcast.209, f32[768]{0:T(1024)} %refs_1_.2, bf16[768,768]{1,0:T(8,128)(2,1)} %wq_ref.1, ...), custom_call_target="tpu_custom_call" | custom-call | flops 1024 | bytes 1024 | tf_op jit(solution)/shard_map/front/pallas_call | solution.py:110
  13.1 1.8 collective-permute-start.3
  14.9 4.3 %front.3 = (bf16[256,768]{1,0:T(8,128)(2,1)}, f32[256,768]{1,0:T(8,128)}, f32[256,1]{1,0:T(8,128)}, bf16[256,768]{1,0:T(8,128)(2,1)}, bf16[256,768]{1,0:T(8,128)(2,1)}) custom-call(bf16[256,768]{1,0:T(8,128)(2,1)} %copy-done.22, f32[768]{0:T(1024)} %refs_1_.2, bf16[768,768]{1,0:T(8,128)(2,1)} %wk_ref.1, bf16[768,768]{1,0:T(8,128)(2,1)} %wv_ref.1), custom_call_target="tpu_custom_call" | custom-call | flops 1024 | bytes 1024 | tf_op jit(solution)/shard_map/front/pallas_call | solution.py:110
  19.2 7.8 %attend.1 = (bf16[256,768]{1,0:T(8,128)(2,1)}, f32[6,256,2]{2,1,0:T(8,128)}) custom-call(bf16[256,768]{1,0:T(8,128)(2,1)} %get-tuple-element.201.q_ref, bf16[256,768]{1,0:T(8,128)(2,1)} %get-tuple-element.202.ka_ref, bf16[256,768]{1,0:T(8,128)(2,1)} %get-tuple-element.211.kb_ref, bf16[256,768]{1,0:T(8,128)(2,1)} %get-tuple-element.212.va_ref, ...), custom_call_target="tpu_custom_call" | custom-call | flops 1024 | bytes 1024 | tf_op jit(solution)/shard_map/attend/pallas_call | solution.py:467
  27.1 2.7 %collective-permute-start.5 = (f32[8,5,768]{2,1,0:T(8,128)S(1)}, f32[8,5,768]{2,1,0:T(8,128)S(1)}, u32[]{:S(2)}, u32[]{:S(2)}) collective-permute-start(f32[8,5,768]{2,1,0:T(8,128)S(1)} %pad_maximum_fusion.1), channel_id=1, source_target_pairs={{0,16},{2,18},{4,20},{6,22},{8,24},{10,26},{12,28},{14,30},{16,0},... | collective-permute-start | bytes 368648 | tf_op jit(solution)/shard_map/ppermute | solution.py:620
  31.7 12.3 %middle.1 = (f32[1,768]{1,0:T(1,128)}, f32[16,768]{1,0:T(8,128)}, bf16[256,768]{1,0:T(8,128)(2,1)}, f32[256,768]{1,0:T(8,128)}, f32[256,1]{1,0:T(8,128)}, /*inde...) custom-call(bf16[256,768]{1,0:T(8,128)(2,1)} %get-tuple-element.216., ...), custom_call_target="tpu_custom_call" | custom-call | flops 1024 | bytes 1024 | tf_op jit(solution)/shard_map/middle/pallas_call | solution.py:198
  46.4 2.1 %collective-permute-done.4.other_ref = f32[16,896]{1,0:T(8,128)S(1)} collective-permute-done((f32[16,896]{1,0:T(8,128)}, f32[16,896]{1,0:T(8,128)S(1)}, u32[]{:S(2)}, u32[]{:S(2)}) %collective-permute-start.4) | collective-permute-done | bytes 57376 | tf_op jit(solution)/shard_map/ppermute | solution.py:624
  49.0 5.8 %pool_back.1 = (f32[256,768]{1,0:T(8,128)}, bf16[256,768]{1,0:T(8,128)(2,1)}, f32[24,768]{1,0:T(8,128)}) custom-call(s32[5]{0:T(128)} %stack.23.place_ref, s32[1]{0:T(128)S(6)} %copy.54.count_ref, s32[1,80]{1,0:T(1,128)} %pairs_ref.1, f32[1]{0:T(128)} %bitcast.90.temp_ref, f32[1]{0:T(128)} %bitcast.91.bias_ref, f32[16,896]{1,0:T(8,128)} %get-tuple-element.223.own_ref, ...), custom_call_target="tpu_custom_call" | custom-call | flops 1024 | bytes 1024 | tf_op jit(solution)/shard_map/pool_back/pallas_call | solution.py:352
  56.4 4.4 %wgrad.1 = (bf16[2,2,8,96,384]{4,3,2,1,0:T(8,128)(2,1)}, bf16[2,2,8,96,384]{4,3,2,1,0:T(8,128)(2,1)}) custom-call(s32[5]{0:T(128)} %stack.23.place_ref, bf16[256,3072]{1,0:T(8,128)(2,1)} %get-tuple-element.222.left_ref, bf16[256,768]{1,0:T(8,128)(2,1)} %get-tuple-element.236.right_ref.grad_ref), custom_call_target="tpu_custom_call" | custom-call | flops 1024 | bytes 1024 | tf_op jit(solution)/shard_map/wgrad/pallas_call | solution.py:557
  63.0 8.6 %gelu_back.1 = (bf16[256,3072]{1,0:T(8,128)(2,1)}, bf16[2,2,8,48,768]{4,3,2,1,0:T(8,128)(2,1)}, bf16[2,2,8,48,768]{4,3,2,1,0:T(8,128)(2,1)}) custom-call(s32[5]{0:T(128)} %stack.23.place_ref, bf16[256,768]{1,0:T(8,128)(2,1)} %get-tuple-element.236.right_ref.grad_ref, bf16[3072,768]{1,0:T(8,128)(2,1)} %down_ref.3, f32[256,3072]{1,0:T(8,128)} %get-tuple-element.237.up_ref, ...), custom_call_target="tpu_custom_call" | custom-call | flops 1024 | bytes 1024 | tf_op jit(solution)/shard_map/gelu_back/pallas_call | solution.py:1031
  73.2 3.3 %fold.8 = (bf16[8,96,384]{2,1,0:T(8,128)(2,1)}, bf16[2,4,96,384]{3,2,1,0:T(8,128)(2,1)}, f32[32,768]{1,0:T(8,128)}) custom-call(s32[5]{0:T(128)} %stack.23.place_ref, bf16[2,2,8,96,384]{4,3,2,1,0:T(8,128)(2,1)} %get-tuple-element.247.refs_0_, bf16[2,2,8,96,384]{4,3,2,1,0:T(8,128)(2,1)} %copy-done.2, bf16[2,2,4,2,96,384]{5,4,3,2,1,0:T(8,128)(2,1)} %bitcast.144, ...), custom_call_target="tpu_custom_call" | custom-call | flops 1024 | bytes 1024 | tf_op jit(solution)/shard_map/fold/pallas_call | solution.py:907
  79.0 7.4 %up_back.1 = (f32[256,768]{1,0:T(8,128)}, bf16[256,768]{1,0:T(8,128)(2,1)}, bf16[256,768]{1,0:T(8,128)(2,1)}) custom-call(bf16[256,3072]{1,0:T(8,128)(2,1)} %get-tuple-element.255.du_ref, bf16[768,3072]{1,0:T(8,128)(2,1)} %up_ref.3, f32[256,768]{1,0:T(8,128)} %get-tuple-element.256.unit_ref, f32[256,1]{1,0:T(8,128)} %get-tuple-element.257.inv_ref, ...), custom_call_target="tpu_custom_call" | custom-call | flops 1024 | bytes 1024 | tf_op jit(solution)/shard_map/up_back/pallas_call | solution.py:1087
  86.5 6.0 %collective-permute-done.12 = bf16[8,96,384]{2,1,0:T(8,128)(2,1)S(1)} collective-permute-done((bf16[8,96,384]{2,1,0:T(8,128)(2,1)}, bf16[8,96,384]{2,1,0:T(8,128)(2,1)S(1)}, u32[]{:S(2)}, u32[]{:S(2)}) %collective-permute-start.12) | collective-permute-done | bytes 589856 | tf_op jit(solution)/shard_map/ppermute | solution.py:624
  94.4 3.7 %fold.9 = (bf16[2,4,48,768]{3,2,1,0:T(8,128)(2,1)}, bf16[8,48,768]{2,1,0:T(8,128)(2,1)}, bf16[4,96,384]{2,1,0:T(8,128)(2,1)}, bf16[4,96,384]{2,1,0:T(8,128)(2,1)}, f32[48,768]{1,0:T(8,128)}) custom-call(s32[5]{0:T(128)} %stack.23.place_ref, bf16[2,2,4,2,48,768]{5,4,3,2,1,0:T(8,128)(2,1)} %bitcast.126, bf16[2,2,4,2,48,768]{5,4,3,2,1,0:T(8,128)(2,1)} %bitcast.135, ...), custom_call_target="tpu_custom_call" | custom-call | flops 1024 | bytes 1024 | tf_op jit(solution)/shard_map/fold/pallas_call | solution.py:907
  101.9 10.2 %attend_back.1 = (bf16[256,768]{1,0:T(8,128)(2,1)}, bf16[512,768]{1,0:T(8,128)(2,1)}, bf16[512,768]{1,0:T(8,128)(2,1)}) custom-call(bf16[256,768]{1,0:T(8,128)(2,1)} %get-tuple-element.201.q_ref, bf16[256,768]{1,0:T(8,128)(2,1)} %get-tuple-element.202.ka_ref, bf16[256,768]{1,0:T(8,128)(2,1)} %get-tuple-element.211.kb_ref, ...), custom_call_target="tpu_custom_call" | custom-call | flops 1024 | bytes 1024 | tf_op jit(solution)/shard_map/attend_back/pallas_call | solution.py:515
  116.2 5.8 %wgrad_four.1 = (bf16[2,2,8,4,24,384]{5,4,3,2,1,0:T(8,128)(2,1)}, bf16[2,2,8,4,24,384]{5,4,3,2,1,0:T(8,128)(2,1)}) custom-call(s32[5]{0:T(128)} %stack.23.place_ref, bf16[256,768]{1,0:T(8,128)(2,1)} %get-tuple-element.220.na_ref, bf16[256,768]{1,0:T(8,128)(2,1)} %get-tuple-element.221.nb_ref, bf16[256,768]{1,0:T(8,128)(2,1)} %get-tuple-element.216.attended_ref.a_ref, ...), custom_call_target="tpu_custom_call" | custom-call | flops 1024 | bytes 1024 | tf_op jit(solution)/shard_map/wgrad_four/pallas_call | solution.py:603
  122.8 3.4 %fold.10 = (bf16[4,48,768]{2,1,0:T(8,128)(2,1)}, bf16[4,48,768]{2,1,0:T(8,128)(2,1)}, bf16[2,2,96,384]{3,2,1,0:T(8,128)(2,1)}, f32[80,768]{1,0:T(8,128)}) custom-call(s32[5]{0:T(128)} %stack.23.place_ref, bf16[2,2,4,2,48,768]{5,4,3,2,1,0:T(8,128)(2,1)} %bitcast.127, bf16[2,2,4,2,48,768]{5,4,3,2,1,0:T(8,128)(2,1)} %bitcast.136, ...), custom_call_target="tpu_custom_call" | custom-call | flops 1024 | bytes 1024 | tf_op jit(solution)/shard_map/fold/pallas_call | solution.py:907
  129.5 5.2 %parts_in.1 = (f32[256,768]{1,0:T(8,128)}, bf16[256,768]{1,0:T(8,128)(2,1)}) custom-call(bf16[256,768]{1,0:T(8,128)(2,1)} %get-tuple-element.304.dq_ref, bf16[512,768]{1,0:T(8,128)(2,1)} %get-tuple-element.286.dk_ref, bf16[512,768]{1,0:T(8,128)(2,1)} %get-tuple-element.287.dv_ref, bf16[768,768]{1,0:T(8,128)(2,1)} %wq_ref.1, bf16[768,768]{1,0:T(8,128)(2,1)} %wk_ref.1, ...), custom_call_target="tpu_custom_call" | custom-call | flops 1024 | bytes 1024 | tf_op jit(solution)/shard_map/parts_in/pallas_call | solution.py:1120
  139.2 4.2 %fold.11 = (bf16[2,4,4,24,384]{4,3,2,1,0:T(8,128)(2,1)}, bf16[8,4,24,384]{3,2,1,0:T(8,128)(2,1)}, bf16[2,2,48,768]{3,2,1,0:T(8,128)(2,1)}, bf16[2,1,96,384]{3,2,1,0:T(8,128)(2,1)}, f32[144,768]{1,0:T(8,128)}) custom-call(s32[5]{0:T(128)} %stack.23.place_ref, bf16[2,2,4,2,4,24,384]{6,5,4,3,2,1,0:T(8,128)(2,1)} %bitcast.92, ...), custom_call_target="tpu_custom_call" | custom-call | flops 1024 | bytes 1024 | tf_op jit(solution)/shard_map/fold/pallas_call | solution.py:907
  146.3 4.2 %pool_weights.1 = (f32[48,384]{1,0:T(8,128)}, f32[48,384]{1,0:T(8,128)}, f32[48,384]{1,0:T(8,128)}, f32[48,384]{1,0:T(8,128)}, f32[3,128]{1,0:T(4,128)}) custom-call(s32[5]{0:T(128)} %stack.23.place_ref, f32[144,768]{1,0:T(8,128)} %get-tuple-element.325.rows_ref, f32[4,768]{1,0:T(4,128)} %vectors.1.vectors_ref.refs_56_, ...), custom_call_target="tpu_custom_call" | custom-call | flops 1024 | bytes 1024 | tf_op jit(solution)/shard_map/pool_weights/pallas_call | solution.py:424
  150.5 3.9 %collective-permute-done.27.refs_5_.refs_11_ = bf16[2,1,96,384]{3,2,1,0:T(8,128)(2,1)S(1)} collective-permute-done((bf16[2,1,96,384]{3,2,1,0:T(8,128)(2,1)}, bf16[2,1,96,384]{3,2,1,0:T(8,128)(2,1)S(1)}, u32[]{:S(2)}, u32[]{:S(2)}) %collective-permute-start.27) | collective-permute-done | bytes 147488 | tf_op jit(solution)/shard_map/ppermute | solution.py:620
  156.0 2.0 collective-permute-done.24.refs_2_.refs_16_.refs_30_.refs_44_
  159.2 3.3 %fold.13 = (bf16[4,4,24,384]{3,2,1,0:T(8,128)(2,1)}, bf16[4,4,24,384]{3,2,1,0:T(8,128)(2,1)}, bf16[2,1,48,768]{3,2,1,0:T(8,128)(2,1)}) custom-call(s32[5]{0:T(128)} %stack.23.place_ref, bf16[2,2,4,2,4,24,384]{6,5,4,3,2,1,0:T(8,128)(2,1)} %bitcast.93, bf16[2,2,4,2,4,24,384]{6,5,4,3,2,1,0:T(8,128)(2,1)} %bitcast.110, bf16[2,4,4,24,384]{4,3,2,1,0:T(8,128)(2,1)} %copy-done.3, ...), custom_call_target="tpu_custom_call" | custom-call | flops 1024 | bytes 1024 | tf_op jit(solution)/shard_map/fold/pallas_call | solution.py:907
  165.9 2.7 %fold.12 = f32[192,384]{1,0:T(8,128)} custom-call(s32[5]{0:T(128)} %stack.23.place_ref, bf16[2,2,4,2,96,384]{5,4,3,2,1,0:T(8,128)(2,1)} %bitcast.151, bf16[2,2,4,2,96,384]{5,4,3,2,1,0:T(8,128)(2,1)} %bitcast.160, bf16[4,2,96,384]{3,2,1,0:T(8,128)(2,1)} %bitcast.192, bf16[4,96,384]{2,1,0:T(8,128)(2,1)} %copy-done.18, bf16[2,2,96,384]{3,2,1,0:T(8,128)(2,1)} %copy-done.14, ...), custom_call_target="tpu_custom_call" | custom-call | flops 1024 | bytes 1024 | tf_op jit(solution)/shard_map/fold/pallas_call | solution.py:907
  169.2 3.6 %collective-permute-done.30.refs_5_.refs_11_ = bf16[2,1,48,768]{3,2,1,0:T(8,128)(2,1)S(1)} collective-permute-done((bf16[2,1,48,768]{3,2,1,0:T(8,128)(2,1)}, bf16[2,1,48,768]{3,2,1,0:T(8,128)(2,1)S(1)}, u32[]{:S(2)}, u32[]{:S(2)}) %collective-permute-start.30) | collective-permute-done | bytes 147488 | tf_op jit(solution)/shard_map/ppermute | solution.py:620
  173.7 3.2 %fold.15 = (bf16[2,1,4,24,384]{4,3,2,1,0:T(8,128)(2,1)}, bf16[2,1,4,24,384]{4,3,2,1,0:T(8,128)(2,1)}, bf16[2,1,4,24,384]{4,3,2,1,0:T(8,128)(2,1)}) custom-call(s32[5]{0:T(128)} %stack.23.place_ref, bf16[2,2,1,4,2,4,24,384]{7,6,5,4,3,2,1,0:T(8,128)(2,1)} %bitcast.95, bf16[2,2,1,4,2,4,24,384]{7,6,5,4,3,2,1,0:T(8,128)(2,1)} %bitcast.112, ...), custom_call_target="tpu_custom_call" | custom-call | flops 1024 | bytes 1024 | tf_op jit(solution)/shard_map/fold/pallas_call | solution.py:907
  179.0 3.3 %collective-permute-start.34 = (bf16[2,1,4,24,384]{4,3,2,1,0:T(8,128)(2,1)}, bf16[2,1,4,24,384]{4,3,2,1,0:T(8,128)(2,1)S(1)}, u32[]{:S(2)}, u32[]{:S(2)}) collective-permute-start(bf16[2,1,4,24,384]{4,3,2,1,0:T(8,128)(2,1)} %get-tuple-element.362), channel_id=1, source_target_pairs={{0,24},{2,26},{4,28},{6,30},{8,16},{10,18},{12,20},{14,22},{16,8},... | collective-permute-start | bytes 442376 | tf_op jit(solution)/shard_map/ppermute | solution.py:620
  182.3 2.7 %fold.14.refs_58_ = f32[48,1536]{1,0:T(8,128)} custom-call(s32[5]{0:T(128)} %stack.23.place_ref, bf16[2,2,4,2,48,768]{5,4,3,2,1,0:T(8,128)(2,1)} %bitcast.133, bf16[2,2,4,2,48,768]{5,4,3,2,1,0:T(8,128)(2,1)} %bitcast.142, bf16[2,4,48,768]{3,2,1,0:T(8,128)(2,1)} %copy-done.10, bf16[4,48,768]{2,1,0:T(8,128)(2,1)} %copy-done.16, ...), custom_call_target="tpu_custom_call" | custom-call | flops 1024 | bytes 1024 | tf_op jit(solution)/shard_map/fold/pallas_call | solution.py:907
  185.9 3.1 %own_in.1 = f32[256,768]{1,0:T(8,128)} custom-call(f32[256,768]{1,0:T(8,128)} %get-tuple-element.312.own_ref, bf16[256,768]{1,0:T(8,128)(2,1)} %copy-done.23, f32[256,768]{1,0:T(8,128)} %get-tuple-element.357.unit_ref, f32[256,1]{1,0:T(8,128)} %get-tuple-element.358.inv_ref, f32[4,768]{1,0:T(4,128)} %vectors.1.vectors_ref.refs_56_, ...), custom_call_target="tpu_custom_call" | custom-call | flops 1024 | bytes 1024 | tf_op jit(solution)/shard_map/own_in/pallas_call | solution.py:1139
  189.7 3.0 %last_fold.1 = (f32[48,384]{1,0:T(8,128)}, f32[48,384]{1,0:T(8,128)}, f32[48,384]{1,0:T(8,128)}, f32[48,384]{1,0:T(8,128)}, f32[2,128]{1,0:T(2,128)}) custom-call(s32[5]{0:T(128)} %stack.23.place_ref, bf16[2,2,4,2,4,24,384]{6,5,4,3,2,1,0:T(8,128)(2,1)} %bitcast.101, bf16[2,2,4,2,4,24,384]{6,5,4,3,2,1,0:T(8,128)(2,1)} %bitcast.118, ...), custom_call_target="tpu_custom_call" | custom-call | flops 1024 | bytes 1024 | tf_op jit(solution)/shard_map/last_fold/pallas_call | solution.py:773
  193.9 2.5 %collective-permute-done.35 = f32[2,128]{1,0:T(2,128)S(1)} collective-permute-done((f32[2,128]{1,0:T(2,128)}, f32[2,128]{1,0:T(2,128)S(1)}, u32[]{:S(2)}, u32[]{:S(2)}) %collective-permute-start.35) | collective-permute-done | bytes 1056 | tf_op jit(solution)/shard_map/ppermute | solution.py:624
  (141 shorter events, 49.9 us)
Async XLA Ops:
  0.7 12.4 %collective-permute-start = (bf16[256,768]{1,0:T(8,128)(2,1)}, bf16[256,768]{1,0:T(8,128)(2,1)S(1)}, u32[]{:S(2)}, u32[]{:S(2)}) collective-permute-start(bf16[256,768]{1,0:T(8,128)(2,1)} %bitcast.208), channel_id=1, source_target_pairs={{0,1},{1,0},{2,3},{3,2},{4,5},{5,4},{6,7},{7,6},{8,9},{9,8},{10,11... | collective-permute-start | bytes 1179656 | tf_op jit(solution)/shard_map/ppermute | solution.py:624
  3.7 7.1 %collective-permute-start.1 = (f32[1,5,768]{2,1,0:T(8,128)}, f32[1,5,768]{2,1,0:T(8,128)S(1)}, u32[]{:S(2)}, u32[]{:S(2)}) collective-permute-start(f32[1,5,768]{2,1,0:T(8,128)} %bitcast.212), channel_id=1, source_target_pairs={{0,4},{2,6},{4,0},{6,2},{8,12},{10,14},{12,8},{14,10},{16,20},{18,... | collective-permute-start | bytes 46088 | tf_op jit(solution)/shard_map/ppermute | solution.py:620
  13.1 14.0 %collective-permute-start.3 = (f32[4,5,768]{2,1,0:T(8,128)S(1)}, f32[4,5,768]{2,1,0:T(8,128)S(1)}, u32[]{:S(2)}, u32[]{:S(2)}) collective-permute-start(f32[4,5,768]{2,1,0:T(8,128)S(1)} %pad_maximum_fusion.2), channel_id=1, source_target_pairs={{0,8},{2,10},{4,12},{6,14},{8,0},{10,2},{12,4},{14,6},{16,24},{18,... | collective-permute-start | bytes 184328 | tf_op jit(solution)/shard_map/ppermute | solution.py:620
  27.1 18.5 %collective-permute-start.5 = (f32[8,5,768]{2,1,0:T(8,128)S(1)}, f32[8,5,768]{2,1,0:T(8,128)S(1)}, u32[]{:S(2)}, u32[]{:S(2)}) collective-permute-start(f32[8,5,768]{2,1,0:T(8,128)S(1)} %pad_maximum_fusion.1), channel_id=1, source_target_pairs={{0,16},{2,18},{4,20},{6,22},{8,24},{10,26},{12,28},{14,30},{16,0},... | collective-permute-start | bytes 368648 | tf_op jit(solution)/shard_map/ppermute | solution.py:620
  54.9 5.9 %collective-permute-start.6 = (f32[24,768]{1,0:T(8,128)}, f32[24,768]{1,0:T(8,128)S(1)}, u32[]{:S(2)}, u32[]{:S(2)}) collective-permute-start(f32[24,768]{1,0:T(8,128)} %get-tuple-element.235.refs_4_), channel_id=1, source_target_pairs={{0,1},{1,0},{2,3},{3,2},{4,5},{5,4},{6,7},{7,6},{8,9},{9,8},{10,11... | collective-permute-start | bytes 221192 | tf_op jit(solution)/shard_map/ppermute | solution.py:624
  60.8 10.8 %collective-permute-start.7 = (bf16[2,2,8,96,384]{4,3,2,1,0:T(8,128)(2,1)}, bf16[2,2,8,96,384]{4,3,2,1,0:T(8,128)(2,1)S(1)}, u32[]{:S(2)}, u32[]{:S(2)}) collective-permute-start(bf16[2,2,8,96,384]{4,3,2,1,0:T(8,128)(2,1)} %get-tuple-element.242), channel_id=1, source_target_pairs={{0,2},{2,0},{4,6},{6,4},{8,10},{10,8},{12,14},{14,12},{16,18},{18,... | collective-permute-start | bytes 7077896 | tf_op jit(solution)/shard_map/ppermute | solution.py:620
  60.9 10.7 %collective-permute-start.8 = (f32[24,768]{1,0:T(8,128)}, f32[24,768]{1,0:T(8,128)S(1)}, u32[]{:S(2)}, u32[]{:S(2)}) collective-permute-start(f32[24,768]{1,0:T(8,128)} %get-tuple-element.235.refs_4_), channel_id=1, source_target_pairs={{0,4},{2,6},{4,0},{6,2},{8,12},{10,14},{12,8},{14,10},{16,20},{18,... | collective-permute-start | bytes 221192 | tf_op jit(solution)/shard_map/ppermute | solution.py:620
  62.4 9.2 %collective-permute-start.9 = (f32[24,768]{1,0:T(8,128)S(1)}, f32[24,768]{1,0:T(8,128)S(1)}, u32[]{:S(2)}, u32[]{:S(2)}) collective-permute-start(f32[24,768]{1,0:T(8,128)S(1)} %collective-permute-done.6.refs_6_), channel_id=1, source_target_pairs={{0,4},{2,6},{4,0},{6,2},{8,12},{10,14},{12,8},{14,10},{16,20},{18,... | collective-permute-start | bytes 221192 | tf_op jit(solution)/shard_map/ppermute | solution.py:620
  76.5 16.3 %collective-permute-start.10 = (bf16[2,2,8,48,768]{4,3,2,1,0:T(8,128)(2,1)}, bf16[2,2,8,48,768]{4,3,2,1,0:T(8,128)(2,1)S(1)}, u32[]{:S(2)}, u32[]{:S(2)}) collective-permute-start(bf16[2,2,8,48,768]{4,3,2,1,0:T(8,128)(2,1)} %get-tuple-element.260), channel_id=1, source_target_pairs={{0,2},{2,0},{4,6},{6,4},{8,10},{10,8},{12,14},{14,12},{16,18},{18,... | collective-permute-start | bytes 7077896 | tf_op jit(solution)/shard_map/ppermute | solution.py:620
  76.6 15.9 %collective-permute-start.12 = (bf16[8,96,384]{2,1,0:T(8,128)(2,1)}, bf16[8,96,384]{2,1,0:T(8,128)(2,1)S(1)}, u32[]{:S(2)}, u32[]{:S(2)}) collective-permute-start(bf16[8,96,384]{2,1,0:T(8,128)(2,1)} %get-tuple-element.262), channel_id=1, source_target_pairs={{0,1},{1,0},{2,3},{3,2},{4,5},{5,4},{6,7},{7,6},{8,9},{9,8},{10,11... | collective-permute-start | bytes 1769480 | tf_op jit(solution)/shard_map/ppermute | solution.py:624
  77.2 15.6 %collective-permute-start.13 = (bf16[2,4,96,384]{3,2,1,0:T(8,128)(2,1)}, bf16[2,4,96,384]{3,2,1,0:T(8,128)(2,1)S(1)}, u32[]{:S(2)}, u32[]{:S(2)}) collective-permute-start(bf16[2,4,96,384]{3,2,1,0:T(8,128)(2,1)} %get-tuple-element.263), channel_id=1, source_target_pairs={{0,4},{2,6},{4,0},{6,2},{8,12},{10,14},{12,8},{14,10},{16,20},{18,... | collective-permute-start | bytes 1769480 | tf_op jit(solution)/shard_map/ppermute | solution.py:620
  78.6 7.9 %collective-permute-start.11 = (f32[32,768]{1,0:T(8,128)}, f32[32,768]{1,0:T(8,128)}, u32[]{:S(2)}, u32[]{:S(2)}) collective-permute-start(f32[32,768]{1,0:T(8,128)} %get-tuple-element.261.refs_10_), channel_id=1, source_target_pairs={{0,16},{2,18},{4,20},{6,22},{8,24},{10,26},{12,28},{14,30},{16,0},... | collective-permute-start | bytes 294920 | tf_op jit(solution)/shard_map/ppermute | solution.py:620
  98.1 15.1 %collective-permute-start.14 = (bf16[2,4,48,768]{3,2,1,0:T(8,128)(2,1)}, bf16[2,4,48,768]{3,2,1,0:T(8,128)(2,1)S(1)}, u32[]{:S(2)}, u32[]{:S(2)}) collective-permute-start(bf16[2,4,48,768]{3,2,1,0:T(8,128)(2,1)} %get-tuple-element.280), channel_id=1, source_target_pairs={{0,4},{2,6},{4,0},{6,2},{8,12},{10,14},{12,8},{14,10},{16,20},{18,... | collective-permute-start | bytes 1769480 | tf_op jit(solution)/shard_map/ppermute | solution.py:620
  99.7 14.7 %collective-permute-start.15 = (bf16[8,48,768]{2,1,0:T(8,128)(2,1)}, bf16[8,48,768]{2,1,0:T(8,128)(2,1)S(1)}, u32[]{:S(2)}, u32[]{:S(2)}) collective-permute-start(bf16[8,48,768]{2,1,0:T(8,128)(2,1)} %get-tuple-element.281), channel_id=1, source_target_pairs={{0,1},{1,0},{2,3},{3,2},{4,5},{5,4},{6,7},{7,6},{8,9},{9,8},{10,11... | collective-permute-start | bytes 1769480 | tf_op jit(solution)/shard_map/ppermute | solution.py:624
  101.2 11.0 %collective-permute-start.16 = (f32[48,768]{1,0:T(8,128)}, f32[48,768]{1,0:T(8,128)S(1)}, u32[]{:S(2)}, u32[]{:S(2)}) collective-permute-start(f32[48,768]{1,0:T(8,128)} %get-tuple-element.282.refs_14_), channel_id=1, source_target_pairs={{0,8},{2,10},{4,12},{6,14},{8,0},{10,2},{12,4},{14,6},{16,24},{18,... | collective-permute-start | bytes 442376 | tf_op jit(solution)/shard_map/ppermute | solution.py:620
  114.4 7.6 %collective-permute-start.17 = (bf16[4,96,384]{2,1,0:T(8,128)(2,1)S(1)}, bf16[4,96,384]{2,1,0:T(8,128)(2,1)S(1)}, u32[]{:S(2)}, u32[]{:S(2)}) collective-permute-start(bf16[4,96,384]{2,1,0:T(8,128)(2,1)S(1)} %copy-done.34), channel_id=1, source_target_pairs={{0,4},{2,6},{4,0},{6,2},{8,12},{10,14},{12,8},{14,10},{16,20},{18,... | collective-permute-start | bytes 884744 | tf_op jit(solution)/shard_map/ppermute | solution.py:620
  115.0 7.1 %collective-permute-start.18 = (bf16[4,96,384]{2,1,0:T(8,128)(2,1)S(1)}, bf16[4,96,384]{2,1,0:T(8,128)(2,1)S(1)}, u32[]{:S(2)}, u32[]{:S(2)}) collective-permute-start(bf16[4,96,384]{2,1,0:T(8,128)(2,1)S(1)} %copy-done.33), channel_id=1, source_target_pairs={{0,1},{1,0},{2,3},{3,2},{4,5},{5,4},{6,7},{7,6},{8,9},{9,8},{10,11... | collective-permute-start | bytes 884744 | tf_op jit(solution)/shard_map/ppermute | solution.py:624
  126.2 11.5 %collective-permute-start.19 = (bf16[2,2,8,4,24,384]{5,4,3,2,1,0:T(8,128)(2,1)}, bf16[2,2,8,4,24,384]{5,4,3,2,1,0:T(8,128)(2,1)S(1)}, u32[]{:S(2)}, u32[]{:S(2)}) collective-permute-start(bf16[2,2,8,4,24,384]{5,4,3,2,1,0:T(8,128)(2,1)} %get-tuple-element.307), channel_id=1, source_target_pairs={{0,2},{2,0},{4,6},{6,4},{8,10},{10,8},{12,14},{14,12},{16,18},{18,... | collective-permute-start | bytes 7077896 | tf_op jit(solution)/shard_map/ppermute | solution.py:620
  126.3 9.6 %collective-permute-start.20 = (bf16[4,48,768]{2,1,0:T(8,128)(2,1)}, bf16[4,48,768]{2,1,0:T(8,128)(2,1)S(1)}, u32[]{:S(2)}, u32[]{:S(2)}) collective-permute-start(bf16[4,48,768]{2,1,0:T(8,128)(2,1)} %get-tuple-element.308), channel_id=1, source_target_pairs={{0,1},{1,0},{2,3},{3,2},{4,5},{5,4},{6,7},{7,6},{8,9},{9,8},{10,11... | collective-permute-start | bytes 884744 | tf_op jit(solution)/shard_map/ppermute | solution.py:624
  127.4 9.3 %collective-permute-start.21 = (bf16[4,48,768]{2,1,0:T(8,128)(2,1)}, bf16[4,48,768]{2,1,0:T(8,128)(2,1)S(1)}, u32[]{:S(2)}, u32[]{:S(2)}) collective-permute-start(bf16[4,48,768]{2,1,0:T(8,128)(2,1)} %get-tuple-element.309), channel_id=1, source_target_pairs={{0,4},{2,6},{4,0},{6,2},{8,12},{10,14},{12,8},{14,10},{16,20},{18,... | collective-permute-start | bytes 884744 | tf_op jit(solution)/shard_map/ppermute | solution.py:620
  128.7 9.0 %collective-permute-start.22 = (bf16[2,2,96,384]{3,2,1,0:T(8,128)(2,1)}, bf16[2,2,96,384]{3,2,1,0:T(8,128)(2,1)S(1)}, u32[]{:S(2)}, u32[]{:S(2)}) collective-permute-start(bf16[2,2,96,384]{3,2,1,0:T(8,128)(2,1)} %get-tuple-element.310), channel_id=1, source_target_pairs={{0,8},{2,10},{4,12},{6,14},{8,0},{10,2},{12,4},{14,6},{16,24},{18,... | collective-permute-start | bytes 884744 | tf_op jit(solution)/shard_map/ppermute | solution.py:620
  143.4 14.5 %collective-permute-start.24 = (bf16[2,4,4,24,384]{4,3,2,1,0:T(8,128)(2,1)}, bf16[2,4,4,24,384]{4,3,2,1,0:T(8,128)(2,1)S(1)}, u32[]{:S(2)}, u32[]{:S(2)}) collective-permute-start(bf16[2,4,4,24,384]{4,3,2,1,0:T(8,128)(2,1)} %get-tuple-element.332), channel_id=1, source_target_pairs={{0,4},{2,6},{4,0},{6,2},{8,12},{10,14},{12,8},{14,10},{16,20},{18,... | collective-permute-start | bytes 1769480 | tf_op jit(solution)/shard_map/ppermute | solution.py:620
  144.1 14.2 %collective-permute-start.25 = (bf16[8,4,24,384]{3,2,1,0:T(8,128)(2,1)}, bf16[8,4,24,384]{3,2,1,0:T(8,128)(2,1)S(1)}, u32[]{:S(2)}, u32[]{:S(2)}) collective-permute-start(bf16[8,4,24,384]{3,2,1,0:T(8,128)(2,1)} %get-tuple-element.333), channel_id=1, source_target_pairs={{0,1},{1,0},{2,3},{3,2},{4,5},{5,4},{6,7},{7,6},{8,9},{9,8},{10,11... | collective-permute-start | bytes 1769480 | tf_op jit(solution)/shard_map/ppermute | solution.py:624
  145.2 10.8 %collective-permute-start.26 = (bf16[2,2,48,768]{3,2,1,0:T(8,128)(2,1)}, bf16[2,2,48,768]{3,2,1,0:T(8,128)(2,1)S(1)}, u32[]{:S(2)}, u32[]{:S(2)}) collective-permute-start(bf16[2,2,48,768]{3,2,1,0:T(8,128)(2,1)} %get-tuple-element.334), channel_id=1, source_target_pairs={{0,8},{2,10},{4,12},{6,14},{8,0},{10,2},{12,4},{14,6},{16,24},{18,... | collective-permute-start | bytes 884744 | tf_op jit(solution)/shard_map/ppermute | solution.py:620
  145.9 8.4 %collective-permute-start.27 = (bf16[2,1,96,384]{3,2,1,0:T(8,128)(2,1)}, bf16[2,1,96,384]{3,2,1,0:T(8,128)(2,1)S(1)}, u32[]{:S(2)}, u32[]{:S(2)}) collective-permute-start(bf16[2,1,96,384]{3,2,1,0:T(8,128)(2,1)} %get-tuple-element.335), channel_id=1, source_target_pairs={{0,16},{2,18},{4,20},{6,22},{8,24},{10,26},{12,28},{14,30},{16,0},... | collective-permute-start | bytes 442376 | tf_op jit(solution)/shard_map/ppermute | solution.py:620
  162.4 10.4 %collective-permute-start.28 = (bf16[4,4,24,384]{3,2,1,0:T(8,128)(2,1)}, bf16[4,4,24,384]{3,2,1,0:T(8,128)(2,1)S(1)}, u32[]{:S(2)}, u32[]{:S(2)}) collective-permute-start(bf16[4,4,24,384]{3,2,1,0:T(8,128)(2,1)} %get-tuple-element.345), channel_id=1, source_target_pairs={{0,1},{1,0},{2,3},{3,2},{4,5},{5,4},{6,7},{7,6},{8,9},{9,8},{10,11... | collective-permute-start | bytes 884744 | tf_op jit(solution)/shard_map/ppermute | solution.py:624
  163.6 9.2 %collective-permute-start.29 = (bf16[4,4,24,384]{3,2,1,0:T(8,128)(2,1)}, bf16[4,4,24,384]{3,2,1,0:T(8,128)(2,1)S(1)}, u32[]{:S(2)}, u32[]{:S(2)}) collective-permute-start(bf16[4,4,24,384]{3,2,1,0:T(8,128)(2,1)} %get-tuple-element.346), channel_id=1, source_target_pairs={{0,4},{2,6},{4,0},{6,2},{8,12},{10,14},{12,8},{14,10},{16,20},{18,... | collective-permute-start | bytes 884744 | tf_op jit(solution)/shard_map/ppermute | solution.py:620
  165.0 7.8 %collective-permute-start.30 = (bf16[2,1,48,768]{3,2,1,0:T(8,128)(2,1)}, bf16[2,1,48,768]{3,2,1,0:T(8,128)(2,1)S(1)}, u32[]{:S(2)}, u32[]{:S(2)}) collective-permute-start(bf16[2,1,48,768]{3,2,1,0:T(8,128)(2,1)} %get-tuple-element.347), channel_id=1, source_target_pairs={{0,16},{2,18},{4,20},{6,22},{8,24},{10,26},{12,28},{14,30},{16,0},... | collective-permute-start | bytes 442376 | tf_op jit(solution)/shard_map/ppermute | solution.py:620
  177.0 8.1 %collective-permute-start.31 = (bf16[256,768]{1,0:T(8,128)(2,1)S(1)}, bf16[256,768]{1,0:T(8,128)(2,1)S(1)}, u32[]{:S(2)}, u32[]{:S(2)}) collective-permute-start(bf16[256,768]{1,0:T(8,128)(2,1)S(1)} %copy-done.32), channel_id=1, source_target_pairs={{0,1},{1,0},{2,3},{3,2},{4,5},{5,4},{6,7},{7,6},{8,9},{9,8},{10,11... | collective-permute-start | bytes 1179656 | tf_op jit(solution)/shard_map/ppermute | solution.py:624
  177.9 11.0 %collective-permute-start.32 = (bf16[2,1,4,24,384]{4,3,2,1,0:T(8,128)(2,1)}, bf16[2,1,4,24,384]{4,3,2,1,0:T(8,128)(2,1)S(1)}, u32[]{:S(2)}, u32[]{:S(2)}) collective-permute-start(bf16[2,1,4,24,384]{4,3,2,1,0:T(8,128)(2,1)} %get-tuple-element.360), channel_id=1, source_target_pairs={{0,8},{2,10},{4,12},{6,14},{8,0},{10,2},{12,4},{14,6},{16,24},{18,... | collective-permute-start | bytes 442376 | tf_op jit(solution)/shard_map/ppermute | solution.py:620
  177.9 11.0 %collective-permute-start.33 = (bf16[2,1,4,24,384]{4,3,2,1,0:T(8,128)(2,1)}, bf16[2,1,4,24,384]{4,3,2,1,0:T(8,128)(2,1)S(1)}, u32[]{:S(2)}, u32[]{:S(2)}) collective-permute-start(bf16[2,1,4,24,384]{4,3,2,1,0:T(8,128)(2,1)} %get-tuple-element.361), channel_id=1, source_target_pairs={{0,16},{2,18},{4,20},{6,22},{8,24},{10,26},{12,28},{14,30},{16,0},... | collective-permute-start | bytes 442376 | tf_op jit(solution)/shard_map/ppermute | solution.py:620
  179.0 9.9 %collective-permute-start.34 = (bf16[2,1,4,24,384]{4,3,2,1,0:T(8,128)(2,1)}, bf16[2,1,4,24,384]{4,3,2,1,0:T(8,128)(2,1)S(1)}, u32[]{:S(2)}, u32[]{:S(2)}) collective-permute-start(bf16[2,1,4,24,384]{4,3,2,1,0:T(8,128)(2,1)} %get-tuple-element.362), channel_id=1, source_target_pairs={{0,24},{2,26},{4,28},{6,30},{8,16},{10,18},{12,20},{14,22},{16,8},... | collective-permute-start | bytes 442376 | tf_op jit(solution)/shard_map/ppermute | solution.py:620
  (39 other events, 143.7 us)
